TPU v7x, 256 devices: a whole 4x4x8 slice. The times are simulated.
256 devices in a mesh: gx: 32 (over z, x), gy: 8 (over y, core).
Axes of the slice: x: 4, y: 4, z: 8, core: 2. Of those that a mesh axis runs over, the one named last changes fastest.
Arguments:
- fine_disp: float32 [3, 512, 128, 128], P(None, 'gx', 'gy'), may hold values from -12 to 12
- fine_prev: float32 [3, 512, 128, 128], P(None, 'gx', 'gy'), may hold values from -12 to 12
- coarse_disp: float32 [3, 256, 64, 256], P(None, 'gx', 'gy'), may hold values from -12 to 12
- coarse_prev: float32 [3, 256, 64, 256], P(None, 'gx', 'gy'), may hold values from -12 to 12
- fine_density: float32 [512, 128, 128], P('gx', 'gy'), may hold values from 0.6 to 1.8
- fine_lame: float32 [512, 128, 128], P('gx', 'gy'), may hold values from 0.5 to 2
- fine_rigidity: float32 [512, 128, 128], P('gx', 'gy'), may hold values from 0.3 to 1.5
- fine_metric: float32 [512, 128, 128], P('gx', 'gy'), may hold values from 0.7 to 1.4
- coarse_density: float32 [256, 64, 256], P('gx', 'gy'), may hold values from 0.6 to 1.8
- coarse_lame: float32 [256, 64, 256], P('gx', 'gy'), may hold values from 0.5 to 2
- coarse_rigidity: float32 [256, 64, 256], P('gx', 'gy'), may hold values from 0.3 to 1.5
- coarse_metric: float32 [256, 64, 256], P('gx', 'gy'), may hold values from 0.7 to 1.4
- offsets: int32 [2, 512, 128], P(None, 'gx', 'gy'), may hold values from -1 to 1
Outputs:
- fine_final: float32 [3, 512, 128, 128], P(None, 'gx', 'gy')
- coarse_final: float32 [3, 256, 64, 256], P(None, 'gx', 'gy')
- energy: float32 [3, 2], replicated
All inputs are finite; a program needn't handle non-finite values.
Results may differ from a plain program's by a relative error of at most 0.00021.
Values sent between devices are 32-bit elements; how exact they have to be, the bound alone decides.
No kernel may reach another device: no remote copies, remote signals or barrier semaphores. Data moves between devices by JAX's collectives and lax.ppermute only.
A program may use at most 64 MiB of HBM per device.

v0:
```python
import jax
import jax.numpy as jnp
from jax import lax
from jax.sharding import Mesh
from jax.sharding import PartitionSpec as P

STEPS = 3
GX_GY = ("gx_0", "gx_1", "gy_0", "gy_1")
GX = ("gx_0", "gx_1")
GY = ("gy_0", "gy_1")


step_factor = 0.15


def padded(x, sides, width):
    for axis, dim in sides:
        count, length = (lax.axis_size(axis), x.shape[dim])
        up = [(i, (i + 1) % count) for i in range(count - 1)]
        down = [(j, i) for i, j in up]
        last = lax.slice_in_dim(x, length - width, length, axis=dim)
        initial = lax.slice_in_dim(x, 0, width, axis=dim)
        before = lax.ppermute(last, axis, up)
        after = lax.ppermute(initial, axis, down)
        x = jnp.concatenate([before, x, after], axis=dim)
    return x


def by_axis(x, axes):
    for axis in axes:
        x = lax.psum(x, axis)
    return x


def vertical_slope(values):
    middle = 0.5 * (values[..., 2:] - values[..., :-2])
    first = values[..., 1:2] - values[..., 0:1]
    final = values[..., -1:] - values[..., -2:-1]
    return jnp.concatenate([first, middle, final], axis=-1)


def divergence(along_x, along_y, along_z, inverse):
    return (
        0.5 * (along_x[2:] - along_x[:-2])
        + 0.5 * (along_y[:, 2:] - along_y[:, :-2])
        + inverse * vertical_slope(along_z)
    )


def interpolate(plane_ext, offsets):
    coarse_x = plane_ext.shape[1] - 4
    coarse_y = plane_ext.shape[2] - 4
    near_x = jnp.where(jnp.arange(2 * coarse_x) % 2 == 0, 0.75, 0.25)[:, None]
    near_y = jnp.where(jnp.arange(2 * coarse_y) % 2 == 0, 0.75, 0.25)[None, :]
    offset_x = offsets[0]
    offset_y = offsets[1]
    summed = jnp.zeros((3, 2 * coarse_x, 2 * coarse_y), plane_ext.dtype)
    for shift_x in (-1, 0, 1, 2):
        weight_x = jnp.where(offset_x == shift_x, near_x, 0.0) + jnp.where(
            offset_x + 1 == shift_x, 1.0 - near_x, 0.0
        )
        row_band = jnp.repeat(plane_ext[:, 2 + shift_x : 2 + shift_x + coarse_x, :], 2, axis=1)
        for shift_y in (-1, 0, 1, 2):
            weight_y = jnp.where(offset_y == shift_y, near_y, 0.0) + jnp.where(
                offset_y + 1 == shift_y, 1.0 - near_y, 0.0
            )
            tile_band = jnp.repeat(row_band[:, :, 2 + shift_y : 2 + shift_y + coarse_y], 2, axis=2)
            summed = summed + (weight_x * weight_y)[None] * tile_band
    return summed


def restrict(plane):
    half_x = plane.shape[1] // 2
    half_y = plane.shape[2] // 2
    return 0.25 * jnp.sum(plane.reshape(3, half_x, 2, half_y, 2), axis=(2, 4))


def elastic_rate(
    extended, mats_ext, div_ext, displace, top_ghost, bottom_ghost, density, lame_first, rigidity
):
    wide_ext = mats_ext[0]
    inverse = mats_ext[1, 1:-1, 1:-1]
    face_x = 0.5 * (wide_ext[:-1, 1:-1] + wide_ext[1:, 1:-1])
    flux_x = face_x * (extended[:, 1:, 1:-1] - extended[:, :-1, 1:-1])
    face_y = 0.5 * (wide_ext[1:-1, :-1] + wide_ext[1:-1, 1:])
    flux_y = face_y * (extended[:, 1:-1, 1:] - extended[:, 1:-1, :-1])
    vertical = rigidity * inverse
    face_z = jnp.concatenate(
        [vertical[:, :, :1], 0.5 * (vertical[:, :, :-1] + vertical[:, :, 1:]), vertical[:, :, -1:]],
        axis=2,
    )
    column = jnp.concatenate(
        [top_ghost[:, :, :, None], displace, bottom_ghost[:, :, :, None]], axis=3
    )
    flux_z = face_z * (column[:, :, :, 1:] - column[:, :, :, :-1])
    spread = (
        flux_x[:, 1:]
        - flux_x[:, :-1]
        + (flux_y[:, :, 1:] - flux_y[:, :, :-1])
        + (flux_z[:, :, :, 1:] - flux_z[:, :, :, :-1])
    )
    grad_x = 0.5 * (div_ext[2:, 1:-1] - div_ext[:-2, 1:-1])
    grad_y = 0.5 * (div_ext[1:-1, 2:] - div_ext[1:-1, :-2])
    grad_z = inverse * vertical_slope(div_ext[1:-1, 1:-1])
    gradient = jnp.stack([grad_x, grad_y, grad_z])
    return spread * (inverse / density) + (lame_first + rigidity) / density * gradient


def energy_part(updated, displace, rate, density, metric, cell_count):
    change = updated - displace
    inner_sum = jnp.sum(change * change - step_factor * updated * rate, axis=0)
    return jnp.sum(density * metric * inner_sum) / cell_count


def inside_mask(length, place, count):
    position = place * length + jnp.arange(length + 2) - 1
    return (position >= 0) & (position < length * count)


def wide_parts(bigger, inverse_ext, inside):
    div_full = divergence(
        bigger[0, :, 1:-1], bigger[1, 1:-1, :], bigger[2, 1:-1, 1:-1], inverse_ext
    )
    return (bigger[:, 1:-1, 1:-1], jnp.where(inside[:, :, None], div_full, 0.0))


def per_device(
    fine_disp,
    fine_prev,
    coarse_disp,
    coarse_prev,
    fine_density,
    fine_lame,
    fine_rigidity,
    fine_metric,
    coarse_density,
    coarse_lame,
    coarse_rigidity,
    coarse_metric,
    offsets,
):
    fine_mats = padded(
        jnp.stack([fine_rigidity * fine_metric, 1.0 / fine_metric]), ((GX, 1), (GY, 2)), 1
    )
    coarse_mats = padded(
        jnp.stack([coarse_rigidity * coarse_metric, 1.0 / coarse_metric]), ((GX, 1), (GY, 2)), 1
    )
    count_x = lax.axis_size(GX)
    count_y = lax.axis_size(GY)
    place_x = lax.axis_index(GX)
    place_y = lax.axis_index(GY)
    fine_cells = fine_disp.shape[1] * count_x * fine_disp.shape[2] * count_y * fine_disp.shape[3]
    coarse_cells = (
        coarse_disp.shape[1] * count_x * coarse_disp.shape[2] * count_y * coarse_disp.shape[3]
    )
    inside_fine = (
        inside_mask(fine_disp.shape[1], place_x, count_x)[:, None]
        & inside_mask(fine_disp.shape[2], place_y, count_y)[None, :]
    )
    inside_coarse = (
        inside_mask(coarse_disp.shape[1], place_x, count_x)[:, None]
        & inside_mask(coarse_disp.shape[2], place_y, count_y)[None, :]
    )
    partials = []
    for step_index in range(STEPS):
        fine_big = padded(fine_disp, ((GX, 1), (GY, 2)), 2)
        coarse_big = padded(coarse_disp, ((GX, 1), (GY, 2)), 2)
        fine_ext, fine_div_ext = wide_parts(fine_big, fine_mats[1], inside_fine)
        coarse_ext, coarse_div_ext = wide_parts(coarse_big, coarse_mats[1], inside_coarse)
        plane_ext = coarse_big[:, :, :, 0]
        fine_bottom = interpolate(plane_ext, offsets)
        fine_top = fine_disp[:, :, :, 0]
        coarse_top = restrict(fine_disp[:, :, :, -1])
        coarse_bottom = jnp.zeros_like(coarse_top)
        fine_rate = elastic_rate(
            fine_ext,
            fine_mats,
            fine_div_ext,
            fine_disp,
            fine_top,
            fine_bottom,
            fine_density,
            fine_lame,
            fine_rigidity,
        )
        coarse_rate = elastic_rate(
            coarse_ext,
            coarse_mats,
            coarse_div_ext,
            coarse_disp,
            coarse_top,
            coarse_bottom,
            coarse_density,
            coarse_lame,
            coarse_rigidity,
        )
        fine_new = 2.0 * fine_disp - fine_prev + step_factor * fine_rate
        coarse_new = 2.0 * coarse_disp - coarse_prev + step_factor * coarse_rate
        level_pair = jnp.stack(
            [
                energy_part(fine_new, fine_disp, fine_rate, fine_density, fine_metric, fine_cells),
                energy_part(
                    coarse_new,
                    coarse_disp,
                    coarse_rate,
                    coarse_density,
                    coarse_metric,
                    coarse_cells,
                ),
            ]
        )
        partials.append(level_pair)
        fine_prev, fine_disp = (fine_disp, fine_new)
        coarse_prev, coarse_disp = (coarse_disp, coarse_new)
    energy = by_axis(jnp.stack(partials), GX_GY)
    return (fine_disp, coarse_disp, energy)


def solution(mesh):
    finer = Mesh(mesh.devices.reshape(8, 4, 4, 2), ("gx_0", "gx_1", "gy_0", "gy_1"))
    in_specs = (
        P(None, GX, GY, None),
        P(None, GX, GY, None),
        P(None, GX, GY, None),
        P(None, GX, GY, None),
        P(GX, GY, None),
        P(GX, GY, None),
        P(GX, GY, None),
        P(GX, GY, None),
        P(GX, GY, None),
        P(GX, GY, None),
        P(GX, GY, None),
        P(GX, GY, None),
        P(None, GX, GY),
    )
    out_specs = (P(None, GX, GY, None), P(None, GX, GY, None), P())
    return jax.shard_map(
        per_device, mesh=finer, in_specs=in_specs, out_specs=out_specs, check_vma=False
    )
```

profile of v0, /device:TPU:1, one launch (start us, length us, event | category | flops | bytes accessed | tf_op | source)
XLA Modules:
  0.0 237.2 jit_solution(7720606352309467459)
XLA Ops:
  1.5 3.9 %collective-permute-start.5 = (f32[3,2,16,128]{3,2,1,0:T(8,128)S(1)}, f32[3,2,16,128]{3,2,1,0:T(8,128)S(1)}, u32[]{:S(2)}, u32[]{:S(2)}) collective-permute-start(f32[3,2,16,128]{3,2,1,0:T(8,128)S(1)} %get-tuple-element.84), channel_id=1, source_target_pairs={{0,8},{8,16},{16,24},{24,32},{32,40},{40,48},{48,56},{56,64},{64,7... | collective-permute-start | bytes 147464 | tf_op jit(solution)/shard_map/ppermute | solution.py:23
  10.0 4.6 %collective-permute-start = (f32[2,1,16,128]{3,2,1,0:T(8,128)S(1)}, f32[2,1,16,128]{3,2,1,0:T(8,128)S(1)}, u32[]{:S(2)}, u32[]{:S(2)}) collective-permute-start(f32[2,1,16,128]{3,2,1,0:T(8,128)S(1)} %get-tuple-element.95), channel_id=1, source_target_pairs={{0,8},{8,16},{16,24},{24,32},{32,40},{40,48},{48,56},{56,64},{64,7... | collective-permute-start | bytes 49160 | tf_op jit(solution)/shard_map/ppermute | solution.py:23
  14.6 3.4 %collective-permute-start.8 = (f32[3,2,8,256]{3,2,1,0:T(8,128)S(1)}, f32[3,2,8,256]{3,2,1,0:T(8,128)S(1)}, u32[]{:S(2)}, u32[]{:S(2)}) collective-permute-start(f32[3,2,8,256]{3,2,1,0:T(8,128)S(1)} %get-tuple-element.120), channel_id=1, source_target_pairs={{0,8},{8,16},{16,24},{24,32},{32,40},{40,48},{48,56},{56,64},{64,7... | collective-permute-start | bytes 147464 | tf_op jit(solution)/shard_map/ppermute | solution.py:23
  31.3 4.0 %collective-permute-start.16 = (f32[2,1,8,256]{3,2,1,0:T(8,128)S(1)}, f32[2,1,8,256]{3,2,1,0:T(8,128)S(1)}, u32[]{:S(2)}, u32[]{:S(2)}) collective-permute-start(f32[2,1,8,256]{3,2,1,0:T(8,128)S(1)} %get-tuple-element.143), channel_id=1, source_target_pairs={{0,8},{8,16},{16,24},{24,32},{32,40},{40,48},{48,56},{56,64},{64,7... | collective-permute-start | bytes 49160 | tf_op jit(solution)/shard_map/ppermute | solution.py:23
  35.4 4.5 %collective-permute-start.3 = (f32[2,18,1,128]{3,2,1,0:T(1,128)S(1)}, f32[2,18,1,128]{3,2,1,0:T(1,128)S(1)}, u32[]{:S(2)}, u32[]{:S(2)}) collective-permute-start(f32[2,18,1,128]{3,2,1,0:T(1,128)S(1)} %get-tuple-element.92), channel_id=1, source_target_pairs={{1,0},{2,1},{3,2},{4,3},{5,4},{6,5},{7,6},{9,8},{10,9},{11,10},{12... | collective-permute-start | bytes 55304 | tf_op jit(solution)/shard_map/ppermute | solution.py:24
  39.9 3.1 %collective-permute-start.2 = (f32[2,18,1,128]{3,2,1,0:T(1,128)S(1)}, f32[2,18,1,128]{3,2,1,0:T(1,128)S(1)}, u32[]{:S(2)}, u32[]{:S(2)}) collective-permute-start(f32[2,18,1,128]{3,2,1,0:T(1,128)S(1)} %get-tuple-element.91), channel_id=1, source_target_pairs={{0,1},{1,2},{2,3},{3,4},{4,5},{5,6},{6,7},{8,9},{9,10},{10,11},{11... | collective-permute-start | bytes 55304 | tf_op jit(solution)/shard_map/ppermute | solution.py:23
  43.1 1.9 collective-permute-start.19
  45.1 3.6 %collective-permute-start.18 = (f32[2,10,1,256]{3,0,2,1:T(2,128)S(1)}, f32[2,10,1,256]{3,0,2,1:T(2,128)S(1)}, u32[]{:S(2)}, u32[]{:S(2)}) collective-permute-start(f32[2,10,1,256]{3,0,2,1:T(2,128)S(1)} %copy.352), channel_id=1, source_target_pairs={{0,1},{1,2},{2,3},{3,4},{4,5},{5,6},{6,7},{8,9},{9,10},{10,11},{11... | collective-permute-start | bytes 61448 | tf_op jit(solution)/shard_map/ppermute | solution.py:23
  50.6 1.9 collective-permute-start.6
  52.5 3.6 %collective-permute-start.7 = (f32[3,20,2,128]{3,2,1,0:T(2,128)S(1)}, f32[3,20,2,128]{3,2,1,0:T(2,128)S(1)}, u32[]{:S(2)}, u32[]{:S(2)}) collective-permute-start(f32[3,20,2,128]{3,2,1,0:T(2,128)S(1)} %get-tuple-element.71), channel_id=1, source_target_pairs={{0,1},{1,2},{2,3},{3,4},{4,5},{5,6},{6,7},{8,9},{9,10},{10,11},{11... | collective-permute-start | bytes 184328 | tf_op jit(solution)/shard_map/ppermute | solution.py:23
  56.3 1.9 collective-permute-start.11
  58.2 3.6 %collective-permute-start.10 = (f32[3,12,2,256]{3,2,1,0:T(2,128)S(1)}, f32[3,12,2,256]{3,2,1,0:T(2,128)S(1)}, u32[]{:S(2)}, u32[]{:S(2)}) collective-permute-start(f32[3,12,2,256]{3,2,1,0:T(2,128)S(1)} %get-tuple-element.89), channel_id=1, source_target_pairs={{0,1},{1,2},{2,3},{3,4},{4,5},{5,6},{6,7},{8,9},{9,10},{10,11},{11... | collective-permute-start | bytes 221192 | tf_op jit(solution)/shard_map/ppermute | solution.py:23
  79.6 5.7 %collective-permute-start.13 = (f32[3,2,16,128]{3,2,1,0:T(8,128)}, f32[3,2,16,128]{3,2,1,0:T(8,128)S(1)}, u32[]{:S(2)}, u32[]{:S(2)}) collective-permute-start(f32[3,2,16,128]{3,2,1,0:T(8,128)} %get-tuple-element.81), channel_id=1, source_target_pairs={{0,8},{8,16},{16,24},{24,32},{32,40},{40,48},{48,56},{56,64},{64,7... | collective-permute-start | bytes 147464 | tf_op jit(solution)/shard_map/ppermute | solution.py:23
  89.5 4.3 %collective-permute-start.20 = (f32[3,2,8,256]{3,2,1,0:T(8,128)S(1)}, f32[3,2,8,256]{3,2,1,0:T(8,128)S(1)}, u32[]{:S(2)}, u32[]{:S(2)}) collective-permute-start(f32[3,2,8,256]{3,2,1,0:T(8,128)S(1)} %get-tuple-element.117), channel_id=1, source_target_pairs={{0,8},{8,16},{16,24},{24,32},{32,40},{40,48},{48,56},{56,64},{64,7... | collective-permute-start | bytes 147464 | tf_op jit(solution)/shard_map/ppermute | solution.py:23
  97.1 3.6 %collective-permute-start.15 = (f32[3,20,2,128]{3,2,1,0:T(2,128)S(1)}, f32[3,20,2,128]{3,2,1,0:T(2,128)S(1)}, u32[]{:S(2)}, u32[]{:S(2)}) collective-permute-start(f32[3,20,2,128]{3,2,1,0:T(2,128)S(1)} %get-tuple-element.69), channel_id=1, source_target_pairs={{0,1},{1,2},{2,3},{3,4},{4,5},{5,6},{6,7},{8,9},{9,10},{10,11},{11... | collective-permute-start | bytes 184328 | tf_op jit(solution)/shard_map/ppermute | solution.py:23
  102.7 4.0 %collective-permute-start.22 = (f32[3,12,2,256]{3,2,1,0:T(2,128)S(1)}, f32[3,12,2,256]{3,2,1,0:T(2,128)S(1)}, u32[]{:S(2)}, u32[]{:S(2)}) collective-permute-start(f32[3,12,2,256]{3,2,1,0:T(2,128)S(1)} %get-tuple-element.87), channel_id=1, source_target_pairs={{0,1},{1,2},{2,3},{3,4},{4,5},{5,6},{6,7},{8,9},{9,10},{10,11},{11... | collective-permute-start | bytes 221192 | tf_op jit(solution)/shard_map/ppermute | solution.py:23
  125.9 6.2 %collective-permute-start.25 = (f32[3,2,16,128]{3,2,1,0:T(8,128)}, f32[3,2,16,128]{3,2,1,0:T(8,128)S(1)}, u32[]{:S(2)}, u32[]{:S(2)}) collective-permute-start(f32[3,2,16,128]{3,2,1,0:T(8,128)} %get-tuple-element.75), channel_id=1, source_target_pairs={{0,8},{8,16},{16,24},{24,32},{32,40},{40,48},{48,56},{56,64},{64,7... | collective-permute-start | bytes 147464 | tf_op jit(solution)/shard_map/ppermute | solution.py:23
  136.3 6.1 %collective-permute-start.28 = (f32[3,2,8,256]{3,2,1,0:T(8,128)S(1)}, f32[3,2,8,256]{3,2,1,0:T(8,128)S(1)}, u32[]{:S(2)}, u32[]{:S(2)}) collective-permute-start(f32[3,2,8,256]{3,2,1,0:T(8,128)S(1)} %get-tuple-element.115), channel_id=1, source_target_pairs={{0,8},{8,16},{16,24},{24,32},{32,40},{40,48},{48,56},{56,64},{64,7... | collective-permute-start | bytes 147464 | tf_op jit(solution)/shard_map/ppermute | solution.py:23
  147.0 3.8 %collective-permute-start.27 = (f32[3,20,2,128]{3,2,1,0:T(2,128)S(1)}, f32[3,20,2,128]{3,2,1,0:T(2,128)S(1)}, u32[]{:S(2)}, u32[]{:S(2)}) collective-permute-start(f32[3,20,2,128]{3,2,1,0:T(2,128)S(1)} %get-tuple-element.68), channel_id=1, source_target_pairs={{0,1},{1,2},{2,3},{3,4},{4,5},{5,6},{6,7},{8,9},{9,10},{10,11},{11... | collective-permute-start | bytes 184328 | tf_op jit(solution)/shard_map/ppermute | solution.py:23
  152.8 3.6 %collective-permute-start.30 = (f32[3,12,2,256]{3,2,1,0:T(2,128)S(1)}, f32[3,12,2,256]{3,2,1,0:T(2,128)S(1)}, u32[]{:S(2)}, u32[]{:S(2)}) collective-permute-start(f32[3,12,2,256]{3,2,1,0:T(2,128)S(1)} %get-tuple-element.85), channel_id=1, source_target_pairs={{0,1},{1,2},{2,3},{3,4},{4,5},{5,6},{6,7},{8,9},{9,10},{10,11},{11... | collective-permute-start | bytes 221192 | tf_op jit(solution)/shard_map/ppermute | solution.py:23
  181.7 26.6 %psum.28 = f32[3,2]{1,0:T(4,128)S(1)} all-reduce(f32[3,2]{1,0:T(4,128)S(1)} %pad_maximum_fusion.74), channel_id=1, replica_groups=mesh['gx_0'=8,'gx_1'=4,'gy_0'=4,'gy_1'=2] {'gx_0'}, use_global_device_ids=true, to_apply=%region_15.16 | all-reduce | flops 6 | bytes 48 | tf_op jit(solution)/shard_map/psum | solution.py:31
  208.3 10.8 %psum.29 = f32[3,2]{1,0:T(4,128)S(1)} all-reduce(f32[3,2]{1,0:T(4,128)S(1)} %psum.28), channel_id=1, replica_groups=mesh['gx_0'=8,'gx_1'=4,'gy_0'=4,'gy_1'=2] {'gx_1'}, use_global_device_ids=true, to_apply=%region_16.17 | all-reduce | flops 6 | bytes 48 | tf_op jit(solution)/shard_map/psum | solution.py:31
  219.0 7.3 %psum.30 = f32[3,2]{1,0:T(4,128)S(1)} all-reduce(f32[3,2]{1,0:T(4,128)S(1)} %psum.29), channel_id=1, replica_groups=mesh['gx_0'=8,'gx_1'=4,'gy_0'=4,'gy_1'=2] {'gy_0'}, use_global_device_ids=true, to_apply=%region_17.18 | all-reduce | flops 6 | bytes 48 | tf_op jit(solution)/shard_map/psum | solution.py:31
  226.3 10.3 %psum.31 = f32[3,2]{1,0:T(4,128)S(1)} all-reduce(f32[3,2]{1,0:T(4,128)S(1)} %psum.30), channel_id=1, replica_groups=mesh['gx_0'=8,'gx_1'=4,'gy_0'=4,'gy_1'=2] {'gy_1'}, use_global_device_ids=true, to_apply=%region_18.19 | all-reduce | flops 6 | bytes 48 | tf_op jit(solution)/shard_map/psum | solution.py:31
  (672 shorter events, 97.3 us)
Async XLA Ops:
  1.5 49.0 %collective-permute-start.5 = (f32[3,2,16,128]{3,2,1,0:T(8,128)S(1)}, f32[3,2,16,128]{3,2,1,0:T(8,128)S(1)}, u32[]{:S(2)}, u32[]{:S(2)}) collective-permute-start(f32[3,2,16,128]{3,2,1,0:T(8,128)S(1)} %get-tuple-element.84), channel_id=1, source_target_pairs={{0,8},{8,16},{16,24},{24,32},{32,40},{40,48},{48,56},{56,64},{64,7... | collective-permute-start | bytes 147464 | tf_op jit(solution)/shard_map/ppermute | solution.py:23
  5.4 45.1 %collective-permute-start.4 = (f32[3,2,16,128]{3,2,1,0:T(8,128)S(1)}, f32[3,2,16,128]{3,2,1,0:T(8,128)S(1)}, u32[]{:S(2)}, u32[]{:S(2)}) collective-permute-start(f32[3,2,16,128]{3,2,1,0:T(8,128)S(1)} %get-tuple-element.83), channel_id=1, source_target_pairs={{8,0},{16,8},{24,16},{32,24},{40,32},{48,40},{56,48},{64,56},{72,6... | collective-permute-start | bytes 147464 | tf_op jit(solution)/shard_map/ppermute | solution.py:24
  8.5 21.5 %collective-permute-start.1 = (f32[2,1,16,128]{3,2,1,0:T(8,128)S(1)}, f32[2,1,16,128]{3,2,1,0:T(8,128)S(1)}, u32[]{:S(2)}, u32[]{:S(2)}) collective-permute-start(f32[2,1,16,128]{3,2,1,0:T(8,128)S(1)} %get-tuple-element.96), channel_id=1, source_target_pairs={{8,0},{16,8},{24,16},{32,24},{40,32},{48,40},{56,48},{64,56},{72,6... | collective-permute-start | bytes 49160 | tf_op jit(solution)/shard_map/ppermute | solution.py:24
  10.0 21.3 %collective-permute-start = (f32[2,1,16,128]{3,2,1,0:T(8,128)S(1)}, f32[2,1,16,128]{3,2,1,0:T(8,128)S(1)}, u32[]{:S(2)}, u32[]{:S(2)}) collective-permute-start(f32[2,1,16,128]{3,2,1,0:T(8,128)S(1)} %get-tuple-element.95), channel_id=1, source_target_pairs={{0,8},{8,16},{16,24},{24,32},{32,40},{40,48},{48,56},{56,64},{64,7... | collective-permute-start | bytes 49160 | tf_op jit(solution)/shard_map/ppermute | solution.py:23
  14.6 41.6 %collective-permute-start.8 = (f32[3,2,8,256]{3,2,1,0:T(8,128)S(1)}, f32[3,2,8,256]{3,2,1,0:T(8,128)S(1)}, u32[]{:S(2)}, u32[]{:S(2)}) collective-permute-start(f32[3,2,8,256]{3,2,1,0:T(8,128)S(1)} %get-tuple-element.120), channel_id=1, source_target_pairs={{0,8},{8,16},{16,24},{24,32},{32,40},{40,48},{48,56},{56,64},{64,7... | collective-permute-start | bytes 147464 | tf_op jit(solution)/shard_map/ppermute | solution.py:23
  50.6 12.1 %collective-permute-start.6 = (f32[3,20,2,128]{3,2,1,0:T(2,128)S(1)}, f32[3,20,2,128]{3,2,1,0:T(2,128)S(1)}, u32[]{:S(2)}, u32[]{:S(2)}) collective-permute-start(f32[3,20,2,128]{3,2,1,0:T(2,128)S(1)} %get-tuple-element.72), channel_id=1, source_target_pairs={{1,0},{2,1},{3,2},{4,3},{5,4},{6,5},{7,6},{9,8},{10,9},{11,10},{12... | collective-permute-start | bytes 184328 | tf_op jit(solution)/shard_map/ppermute | solution.py:24
  52.5 10.2 %collective-permute-start.7 = (f32[3,20,2,128]{3,2,1,0:T(2,128)S(1)}, f32[3,20,2,128]{3,2,1,0:T(2,128)S(1)}, u32[]{:S(2)}, u32[]{:S(2)}) collective-permute-start(f32[3,20,2,128]{3,2,1,0:T(2,128)S(1)} %get-tuple-element.71), channel_id=1, source_target_pairs={{0,1},{1,2},{2,3},{3,4},{4,5},{5,6},{6,7},{8,9},{9,10},{10,11},{11... | collective-permute-start | bytes 184328 | tf_op jit(solution)/shard_map/ppermute | solution.py:23
  56.3 10.0 %collective-permute-start.11 = (f32[3,12,2,256]{3,2,1,0:T(2,128)S(1)}, f32[3,12,2,256]{3,2,1,0:T(2,128)S(1)}, u32[]{:S(2)}, u32[]{:S(2)}) collective-permute-start(f32[3,12,2,256]{3,2,1,0:T(2,128)S(1)} %get-tuple-element.90), channel_id=1, source_target_pairs={{1,0},{2,1},{3,2},{4,3},{5,4},{6,5},{7,6},{9,8},{10,9},{11,10},{12... | collective-permute-start | bytes 221192 | tf_op jit(solution)/shard_map/ppermute | solution.py:24
  78.3 16.7 %collective-permute-start.12 = (f32[3,2,16,128]{3,2,1,0:T(8,128)}, f32[3,2,16,128]{3,2,1,0:T(8,128)S(1)}, u32[]{:S(2)}, u32[]{:S(2)}) collective-permute-start(f32[3,2,16,128]{3,2,1,0:T(8,128)} %get-tuple-element.82), channel_id=1, source_target_pairs={{8,0},{16,8},{24,16},{32,24},{40,32},{48,40},{56,48},{64,56},{72,6... | collective-permute-start | bytes 147464 | tf_op jit(solution)/shard_map/ppermute | solution.py:24
  79.6 15.4 %collective-permute-start.13 = (f32[3,2,16,128]{3,2,1,0:T(8,128)}, f32[3,2,16,128]{3,2,1,0:T(8,128)S(1)}, u32[]{:S(2)}, u32[]{:S(2)}) collective-permute-start(f32[3,2,16,128]{3,2,1,0:T(8,128)} %get-tuple-element.81), channel_id=1, source_target_pairs={{0,8},{8,16},{16,24},{24,32},{32,40},{40,48},{48,56},{56,64},{64,7... | collective-permute-start | bytes 147464 | tf_op jit(solution)/shard_map/ppermute | solution.py:23
  88.2 12.5 %collective-permute-start.21 = (f32[3,2,8,256]{3,2,1,0:T(8,128)S(1)}, f32[3,2,8,256]{3,2,1,0:T(8,128)S(1)}, u32[]{:S(2)}, u32[]{:S(2)}) collective-permute-start(f32[3,2,8,256]{3,2,1,0:T(8,128)S(1)} %get-tuple-element.118), channel_id=1, source_target_pairs={{8,0},{16,8},{24,16},{32,24},{40,32},{48,40},{56,48},{64,56},{72,6... | collective-permute-start | bytes 147464 | tf_op jit(solution)/shard_map/ppermute | solution.py:24
  89.5 11.2 %collective-permute-start.20 = (f32[3,2,8,256]{3,2,1,0:T(8,128)S(1)}, f32[3,2,8,256]{3,2,1,0:T(8,128)S(1)}, u32[]{:S(2)}, u32[]{:S(2)}) collective-permute-start(f32[3,2,8,256]{3,2,1,0:T(8,128)S(1)} %get-tuple-element.117), channel_id=1, source_target_pairs={{0,8},{8,16},{16,24},{24,32},{32,40},{40,48},{48,56},{56,64},{64,7... | collective-permute-start | bytes 147464 | tf_op jit(solution)/shard_map/ppermute | solution.py:23
  95.1 12.4 %collective-permute-start.14 = (f32[3,20,2,128]{3,2,1,0:T(2,128)S(1)}, f32[3,20,2,128]{3,2,1,0:T(2,128)S(1)}, u32[]{:S(2)}, u32[]{:S(2)}) collective-permute-start(f32[3,20,2,128]{3,2,1,0:T(2,128)S(1)} %get-tuple-element.70), channel_id=1, source_target_pairs={{1,0},{2,1},{3,2},{4,3},{5,4},{6,5},{7,6},{9,8},{10,9},{11,10},{12... | collective-permute-start | bytes 184328 | tf_op jit(solution)/shard_map/ppermute | solution.py:24
  97.1 10.5 %collective-permute-start.15 = (f32[3,20,2,128]{3,2,1,0:T(2,128)S(1)}, f32[3,20,2,128]{3,2,1,0:T(2,128)S(1)}, u32[]{:S(2)}, u32[]{:S(2)}) collective-permute-start(f32[3,20,2,128]{3,2,1,0:T(2,128)S(1)} %get-tuple-element.69), channel_id=1, source_target_pairs={{0,1},{1,2},{2,3},{3,4},{4,5},{5,6},{6,7},{8,9},{9,10},{10,11},{11... | collective-permute-start | bytes 184328 | tf_op jit(solution)/shard_map/ppermute | solution.py:23
  100.8 11.2 %collective-permute-start.23 = (f32[3,12,2,256]{3,2,1,0:T(2,128)S(1)}, f32[3,12,2,256]{3,2,1,0:T(2,128)S(1)}, u32[]{:S(2)}, u32[]{:S(2)}) collective-permute-start(f32[3,12,2,256]{3,2,1,0:T(2,128)S(1)} %get-tuple-element.88), channel_id=1, source_target_pairs={{1,0},{2,1},{3,2},{4,3},{5,4},{6,5},{7,6},{9,8},{10,9},{11,10},{12... | collective-permute-start | bytes 221192 | tf_op jit(solution)/shard_map/ppermute | solution.py:24
  102.7 9.3 %collective-permute-start.22 = (f32[3,12,2,256]{3,2,1,0:T(2,128)S(1)}, f32[3,12,2,256]{3,2,1,0:T(2,128)S(1)}, u32[]{:S(2)}, u32[]{:S(2)}) collective-permute-start(f32[3,12,2,256]{3,2,1,0:T(2,128)S(1)} %get-tuple-element.87), channel_id=1, source_target_pairs={{0,1},{1,2},{2,3},{3,4},{4,5},{5,6},{6,7},{8,9},{9,10},{10,11},{11... | collective-permute-start | bytes 221192 | tf_op jit(solution)/shard_map/ppermute | solution.py:23
  124.6 19.8 %collective-permute-start.24 = (f32[3,2,16,128]{3,2,1,0:T(8,128)}, f32[3,2,16,128]{3,2,1,0:T(8,128)S(1)}, u32[]{:S(2)}, u32[]{:S(2)}) collective-permute-start(f32[3,2,16,128]{3,2,1,0:T(8,128)} %get-tuple-element.76), channel_id=1, source_target_pairs={{8,0},{16,8},{24,16},{32,24},{40,32},{48,40},{56,48},{64,56},{72,6... | collective-permute-start | bytes 147464 | tf_op jit(solution)/shard_map/ppermute | solution.py:24
  125.9 18.5 %collective-permute-start.25 = (f32[3,2,16,128]{3,2,1,0:T(8,128)}, f32[3,2,16,128]{3,2,1,0:T(8,128)S(1)}, u32[]{:S(2)}, u32[]{:S(2)}) collective-permute-start(f32[3,2,16,128]{3,2,1,0:T(8,128)} %get-tuple-element.75), channel_id=1, source_target_pairs={{0,8},{8,16},{16,24},{24,32},{32,40},{40,48},{48,56},{56,64},{64,7... | collective-permute-start | bytes 147464 | tf_op jit(solution)/shard_map/ppermute | solution.py:23
  135.0 15.8 %collective-permute-start.29 = (f32[3,2,8,256]{3,2,1,0:T(8,128)S(1)}, f32[3,2,8,256]{3,2,1,0:T(8,128)S(1)}, u32[]{:S(2)}, u32[]{:S(2)}) collective-permute-start(f32[3,2,8,256]{3,2,1,0:T(8,128)S(1)} %get-tuple-element.116), channel_id=1, source_target_pairs={{8,0},{16,8},{24,16},{32,24},{40,32},{48,40},{56,48},{64,56},{72,6... | collective-permute-start | bytes 147464 | tf_op jit(solution)/shard_map/ppermute | solution.py:24
  136.3 14.5 %collective-permute-start.28 = (f32[3,2,8,256]{3,2,1,0:T(8,128)S(1)}, f32[3,2,8,256]{3,2,1,0:T(8,128)S(1)}, u32[]{:S(2)}, u32[]{:S(2)}) collective-permute-start(f32[3,2,8,256]{3,2,1,0:T(8,128)S(1)} %get-tuple-element.115), channel_id=1, source_target_pairs={{0,8},{8,16},{16,24},{24,32},{32,40},{40,48},{48,56},{56,64},{64,7... | collective-permute-start | bytes 147464 | tf_op jit(solution)/shard_map/ppermute | solution.py:23
  145.0 12.2 %collective-permute-start.26 = (f32[3,20,2,128]{3,2,1,0:T(2,128)S(1)}, f32[3,20,2,128]{3,2,1,0:T(2,128)S(1)}, u32[]{:S(2)}, u32[]{:S(2)}) collective-permute-start(f32[3,20,2,128]{3,2,1,0:T(2,128)S(1)} %get-tuple-element.67), channel_id=1, source_target_pairs={{1,0},{2,1},{3,2},{4,3},{5,4},{6,5},{7,6},{9,8},{10,9},{11,10},{12... | collective-permute-start | bytes 184328 | tf_op jit(solution)/shard_map/ppermute | solution.py:24
  147.0 10.3 %collective-permute-start.27 = (f32[3,20,2,128]{3,2,1,0:T(2,128)S(1)}, f32[3,20,2,128]{3,2,1,0:T(2,128)S(1)}, u32[]{:S(2)}, u32[]{:S(2)}) collective-permute-start(f32[3,20,2,128]{3,2,1,0:T(2,128)S(1)} %get-tuple-element.68), channel_id=1, source_target_pairs={{0,1},{1,2},{2,3},{3,4},{4,5},{5,6},{6,7},{8,9},{9,10},{10,11},{11... | collective-permute-start | bytes 184328 | tf_op jit(solution)/shard_map/ppermute | solution.py:23
  150.8 11.0 %collective-permute-start.31 = (f32[3,12,2,256]{3,2,1,0:T(2,128)S(1)}, f32[3,12,2,256]{3,2,1,0:T(2,128)S(1)}, u32[]{:S(2)}, u32[]{:S(2)}) collective-permute-start(f32[3,12,2,256]{3,2,1,0:T(2,128)S(1)} %get-tuple-element.86), channel_id=1, source_target_pairs={{1,0},{2,1},{3,2},{4,3},{5,4},{6,5},{7,6},{9,8},{10,9},{11,10},{12... | collective-permute-start | bytes 221192 | tf_op jit(solution)/shard_map/ppermute | solution.py:24
  152.8 9.0 %collective-permute-start.30 = (f32[3,12,2,256]{3,2,1,0:T(2,128)S(1)}, f32[3,12,2,256]{3,2,1,0:T(2,128)S(1)}, u32[]{:S(2)}, u32[]{:S(2)}) collective-permute-start(f32[3,12,2,256]{3,2,1,0:T(2,128)S(1)} %get-tuple-element.85), channel_id=1, source_target_pairs={{0,1},{1,2},{2,3},{3,4},{4,5},{5,6},{6,7},{8,9},{9,10},{10,11},{11... | collective-permute-start | bytes 221192 | tf_op jit(solution)/shard_map/ppermute | solution.py:23
  (170 other events, 1134.9 us)
where the time goes:
time: 239 us; the launch traced here: 237 us
  starting transfers between devices  95.6 us (40%)
  blocking collectives  54.9 us (23%)
  other arithmetic  39.9 us (17%)
  local copies, waits for them, and re-layouts  39.2 us (16%)
  between operations  7.58 us (3%)
    ppermute x16, starting transfers between devices, padded(): before = lax.ppermute(last, axis, up)  67.2 us
    psum x4, blocking collectives, by_axis(): x = lax.psum(x, axis)  54.9 us
    ppermute x16, starting transfers between devices, padded(): after = lax.ppermute(initial, axis, down)  28.4 us
    unnamed x328, local copies, waits for them, and re-layouts  18.2 us
    another operation x12, other arithmetic, elastic_rate(): gradient = jnp.stack([grad_x, grad_y, grad_z])  6.96 us
    mul x16, local copies, waits for them, and re-layouts, interpolate(): summed = summed + (weight_x * weight_y)[None] * tile_band  6.48 us
    mul x6, other arithmetic, elastic_rate(): flux_z = face_z * (column[:, :, :, 1:] - column[:, :, :, :-1])  5.73 us
  transfers between devices with their start and end apart: 32, of which 0 were waited for; matrix products, arithmetic and copies ran while one was open for 13% of the time, Pallas kernels for 0%

commit v1 on v0

v1 whole, which is shorter than its diff:
```python
import functools

import jax
import jax.numpy as jnp
from jax import lax
from jax.experimental import pallas as pl
from jax.experimental.pallas import tpu as pltpu
from jax.sharding import Mesh
from jax.sharding import PartitionSpec as P

STEPS = 3
GX = ("gx_0", "gx_1")
GY = ("gy_0", "gy_1")
ALL = GX + GY
STEP = 0.15
LANES = 128
VMEM_LIMIT = 20 * 1024 * 1024

EVEN_X, HAS_XM, HAS_XP, EVEN_Y, HAS_YM, HAS_YP = range(6)


class Sizes:
    def __init__(self, fine, coarse):
        self.fx, self.fy, self.fz = fine
        self.cx, self.cy, self.cz = coarse
        self.halves = self.cz // LANES
        self.x_fine = 0
        self.x_coarse = 6 * self.fy
        self.x_rows = self.x_coarse + self.halves * 6 * self.cy
        self.x_fine_mats = self.x_rows
        self.x_coarse_mats = self.x_fine_mats + 2 * self.fy
        self.x_rows_mats = self.x_coarse_mats + 2 * self.halves * self.cy
        self.fe, self.ce = self.fx + 4, self.cx + 4
        self.y_coarse = 3 * self.fe
        self.y_rows = self.y_coarse + self.halves * 3 * self.ce
        self.y_fine_mats = self.y_rows
        self.y_coarse_mats = self.y_fine_mats + self.fx
        self.y_rows_mats = self.y_coarse_mats + self.halves * self.cx


def lanes_of(h):
    return slice(h * LANES, (h + 1) * LANES)


def put_x(s, flags, outs, fine, coarse, mats):
    even = flags[EVEN_X] == 1
    for k, out in enumerate(outs):
        far = even if k == 0 else jnp.logical_not(even)
        start_f = jnp.where(far, s.fx - 2, 0)
        start_c = jnp.where(far, s.cx - 2, 0)
        out[0 : s.x_coarse, :] = fine[:, pl.ds(start_f, 2), :, :].reshape(6 * s.fy, LANES)
        strip = coarse[:, pl.ds(start_c, 2), :, :]
        for h in range(s.halves):
            base = s.x_coarse + h * 6 * s.cy
            out[base : base + 6 * s.cy, :] = strip[:, :, :, lanes_of(h)].reshape(6 * s.cy, LANES)
        if mats is None:
            continue
        edge_f = jnp.where(far, s.fx - 1, 0)
        edge_c = jnp.where(far, s.cx - 1, 0)
        for m in range(2):
            base = s.x_fine_mats + m * s.fy
            out[base : base + s.fy, :] = mats[m][edge_f]
            line = mats[2 + m][edge_c]
            for h in range(s.halves):
                base = s.x_coarse_mats + (m * s.halves + h) * s.cy
                out[base : base + s.cy, :] = line[:, lanes_of(h)]


def first_kernel(s, flags, fine, coarse, rig_f, met_f, rig_c, met_c, out_a, out_b):
    put_x(s, flags, (out_a, out_b), fine, coarse, (rig_f, met_f, rig_c, met_c))


def sides(flags, even, has_low, has_high, a, b):
    low = jnp.where(flags[even] == 1, b, a)
    high = jnp.where(flags[even] == 1, a, b)
    low = jnp.where(flags[has_low] == 1, low, 0.0)
    high = jnp.where(flags[has_high] == 1, high, 0.0)
    return low, high


def middle_kernel(s, with_mats, flags, *refs):
    if with_mats:
        fine, coarse, rig_f, met_f, rig_c, met_c, in_a, in_b, out_a, out_b = refs
    else:
        fine, coarse, in_a, in_b, out_a, out_b = refs
    even = flags[EVEN_Y] == 1

    def put(index, low, high):
        out_a[index] = jnp.where(even, high, low)
        out_b[index] = jnp.where(even, low, high)

    for c in range(3):
        own = pl.ds(c * s.fe + 2, s.fx)
        put(own, fine[c, :, 0:2, :], fine[c, :, s.fy - 2 : s.fy, :])
        for k in range(2):
            base = (c * 2 + k) * s.fy
            pieces = []
            for first in (0, s.fy - 2):
                rows = slice(base + first, base + first + 2)
                pieces.append(sides(flags, EVEN_X, HAS_XM, HAS_XP, in_a[rows, :], in_b[rows, :]))
            for side in range(2):
                place = c * s.fe + (k if side == 0 else s.fx + 2 + k)
                put(place, pieces[0][side], pieces[1][side])
        for h in range(s.halves):
            origin = s.y_coarse + (h * 3 + c) * s.ce
            own = pl.ds(origin + 2, s.cx)
            put(own, coarse[c, :, 0:2, lanes_of(h)], coarse[c, :, s.cy - 2 : s.cy, lanes_of(h)])
            for k in range(2):
                base = s.x_coarse + (h * 6 + c * 2 + k) * s.cy
                pieces = []
                for first in (0, s.cy - 2):
                    rows = slice(base + first, base + first + 2)
                    pieces.append(
                        sides(flags, EVEN_X, HAS_XM, HAS_XP, in_a[rows, :], in_b[rows, :])
                    )
                for side in range(2):
                    place = origin + (k if side == 0 else s.cx + 2 + k)
                    put(place, pieces[0][side], pieces[1][side])
    if not with_mats:
        return
    for m, (of_f, of_c) in enumerate(((rig_f, rig_c), (met_f, met_c))):
        low, high = of_f[:, 0:1, :], of_f[:, s.fy - 1 : s.fy, :]
        where = pl.ds(s.y_fine_mats, s.fx)
        out_a[where, m : m + 1, :] = jnp.where(even, high, low)
        out_b[where, m : m + 1, :] = jnp.where(even, low, high)
        for h in range(s.halves):
            low, high = of_c[:, 0:1, lanes_of(h)], of_c[:, s.cy - 1 : s.cy, lanes_of(h)]
            where = pl.ds(s.y_coarse_mats + h * s.cx, s.cx)
            out_a[where, m : m + 1, :] = jnp.where(even, high, low)
            out_b[where, m : m + 1, :] = jnp.where(even, low, high)


def up_one(x):
    return pltpu.roll(x, x.shape[-1] - 1, x.ndim - 1)


def down_one(x):
    return pltpu.roll(x, 1, x.ndim - 1)


def own_kernel(density, lame, rigidity, metric, inverse, c1, c2, weight, above, below):
    inv = 1.0 / metric[...]
    inverse[...] = inv
    over = 1.0 / density[...]
    c1[...] = inv * over
    c2[...] = (lame[...] + rigidity[...]) * over
    weight[...] = density[...] * metric[...]
    v = rigidity[...] * inv
    lane = lax.broadcasted_iota(jnp.int32, v.shape, 2)
    above[...] = jnp.where(lane == v.shape[2] - 1, v, 0.5 * (v + up_one(v)))
    below[...] = jnp.where(lane == 0, v, 0.5 * (v + down_one(v)))


def slope(f, up, down, lane):
    last = f.shape[-1] - 1
    return jnp.where(lane == 0, up - f, jnp.where(lane == last, f - down, 0.5 * (up - down)))


def fill_displacement(s, flags, own, ext, x_in, y_in, fine):
    x, y, e = (s.fx, s.fy, s.fe) if fine else (s.cx, s.cy, s.ce)
    ext[:, 2 : 2 + x, 8 : 8 + y, :] = own[...]
    for h in range(1 if fine else s.halves):
        base = s.x_fine if fine else s.x_coarse + h * 6 * y
        rows = slice(base, base + 6 * y)
        low, high = sides(flags, EVEN_X, HAS_XM, HAS_XP, x_in[0][rows, :], x_in[1][rows, :])
        ext[:, 0:2, 8 : 8 + y, lanes_of(h)] = low.reshape(3, 2, y, LANES)
        ext[:, x + 2 : x + 4, 8 : 8 + y, lanes_of(h)] = high.reshape(3, 2, y, LANES)
        for c in range(3):
            start = c * e if fine else s.y_coarse + (h * 3 + c) * e
            rows = slice(start, start + e)
            low, high = sides(flags, EVEN_Y, HAS_YM, HAS_YP, y_in[0][rows], y_in[1][rows])
            ext[c, :, 6:8, lanes_of(h)] = low
            ext[c, :, 8 + y : 10 + y, lanes_of(h)] = high


def fill_materials(s, flags, rigidity, metric, inverse, wide_ext, inv_ext, x_in, y_in, fine):
    x, y = (s.fx, s.fy) if fine else (s.cx, s.cy)
    wide_ext[1 : 1 + x, 8 : 8 + y, :] = rigidity[...] * metric[...]
    inv_ext[1 : 1 + x, 8 : 8 + y, :] = inverse[...]
    for h in range(1 if fine else s.halves):
        at = lanes_of(h)
        got = []
        for m in range(2):
            base = s.x_fine_mats + m * y if fine else s.x_coarse_mats + (m * s.halves + h) * y
            rows = slice(base, base + y)
            even = flags[EVEN_X] == 1
            a, b = x_in[0][rows, :], x_in[1][rows, :]
            got.append((jnp.where(even, b, a), jnp.where(even, a, b)))
        for side, (flag, place) in enumerate(((HAS_XM, 0), (HAS_XP, x + 1))):
            rig, met = got[0][side], got[1][side]
            wide_ext[place, 8 : 8 + y, at] = jnp.where(flags[flag] == 1, rig * met, 0.0)
            inv_ext[place, 8 : 8 + y, at] = jnp.where(flags[flag] == 1, 1.0 / met, 0.0)
        start = s.y_fine_mats if fine else s.y_coarse_mats + h * x
        rows = slice(start, start + x)
        got = []
        for m in range(2):
            even = flags[EVEN_Y] == 1
            a, b = y_in[0][rows, m : m + 1, :], y_in[1][rows, m : m + 1, :]
            got.append((jnp.where(even, b, a), jnp.where(even, a, b)))
        for side, (flag, place) in enumerate(((HAS_YM, 7), (HAS_YP, 8 + y))):
            rig, met = got[0][side], got[1][side]
            wide_ext[1 : 1 + x, place : place + 1, at] = jnp.where(flags[flag] == 1, rig * met, 0.0)
            inv_ext[1 : 1 + x, place : place + 1, at] = jnp.where(flags[flag] == 1, 1.0 / met, 0.0)


def fill_divergence(x, y, ext, inv_ext, div):
    z = ext.shape[-1]
    lane = lax.broadcasted_iota(jnp.int32, (y + 2, z), 1)

    def row(r, carry):
        along_x = ext[0, r + 2, 7 : 9 + y, :] - ext[0, r, 7 : 9 + y, :]
        along_y = ext[1, r + 1, 8 : 10 + y, :] - ext[1, r + 1, 6 : 8 + y, :]
        f = ext[2, r + 1, 7 : 9 + y, :]
        inv = inv_ext[r, 7 : 9 + y, :]
        total = 0.5 * along_x + 0.5 * along_y + inv * slope(f, up_one(f), down_one(f), lane)
        div[r, 7 : 9 + y, :] = jnp.where(inv > 0.0, total, 0.0)
        return carry

    lax.fori_loop(0, x + 2, row, 0)


def update(x, y, ext, wide_ext, inv_ext, div, prev, coef, new, ghosts):
    c1, c2, weight, above, below = coef
    z = ext.shape[-1]
    lane = lax.broadcasted_iota(jnp.int32, (y, z), 1)
    mid, left, right = slice(8, 8 + y), slice(7, 7 + y), slice(9, 9 + y)

    def row(i, total):
        wide = wide_ext[i + 1, mid, :]
        w_xp = 0.5 * (wide + wide_ext[i + 2, mid, :])
        w_xm = 0.5 * (wide_ext[i, mid, :] + wide)
        w_yp = 0.5 * (wide + wide_ext[i + 1, right, :])
        w_ym = 0.5 * (wide_ext[i + 1, left, :] + wide)
        inv = inv_ext[i + 1, mid, :]
        f = div[i + 1, mid, :]
        gradient = (
            0.5 * (div[i + 2, mid, :] - div[i, mid, :]),
            0.5 * (div[i + 1, right, :] - div[i + 1, left, :]),
            inv * slope(f, up_one(f), down_one(f), lane),
        )
        top, bottom = ghosts(i)
        k1, k2, dm, va, vb = c1[i], c2[i], weight[i], above[i], below[i]
        inner = jnp.zeros((y, z), jnp.float32)
        for c in range(3):
            u = ext[c, i + 2, mid, :]
            up = jnp.where(lane == z - 1, bottom(c), up_one(u))
            down = jnp.where(lane == 0, u if top is None else top(c), down_one(u))
            flux = w_xp * (ext[c, i + 3, mid, :] - u) - w_xm * (u - ext[c, i + 1, mid, :])
            flux += w_yp * (ext[c, i + 2, right, :] - u) - w_ym * (u - ext[c, i + 2, left, :])
            flux += va * (up - u) - vb * (u - down)
            rate = flux * k1 + k2 * gradient[c]
            updated = 2.0 * u - prev[c, i] + STEP * rate
            change = updated - u
            inner += change * change - STEP * updated * rate
            new[c, i] = updated
        return total + dm * inner

    return lax.fori_loop(0, x, row, jnp.zeros((y, z), jnp.float32))


def step_kernel(s, step, flags, *refs):
    refs = list(refs)

    def take(n):
        out = refs[:n]
        del refs[:n]
        return out

    fine, coarse, fine_prev, coarse_prev, offs = take(5)
    coef_f, coef_c = take(5), take(5)
    first, final = step == 0, step == STEPS - 1
    if first:
        rig_f, met_f, inverse_f, rig_c, met_c, inverse_c = take(6)
    else:
        wide_f, inv_f, wide_c, inv_c, energy_in = take(5)
    x_in, y_in = take(2), take(2)
    new_f, new_c, energy = take(3)
    if not final:
        x_out = take(2)
    if first:
        wide_f, inv_f, wide_c, inv_c = take(4)
    ext_f, ext_c, div_f, div_c, double, pairs = take(6)

    fill_displacement(s, flags, fine, ext_f, x_in, y_in, True)
    fill_displacement(s, flags, coarse, ext_c, x_in, y_in, False)
    if first:
        fill_materials(s, flags, rig_f, met_f, inverse_f, wide_f, inv_f, x_in, y_in, True)
        fill_materials(s, flags, rig_c, met_c, inverse_c, wide_c, inv_c, x_in, y_in, False)

    lane = lax.broadcasted_iota(jnp.int32, (s.cy + 4, LANES), 1)
    for i in range(s.ce):
        e0, e1, e2 = (ext_c[c, i, 6 : 10 + s.cy, 0:LANES] for c in range(3))
        e1, e2 = pltpu.roll(e1, 1, 1), pltpu.roll(e2, 2, 1)
        plane = jnp.where(lane == 0, e0, jnp.where(lane == 1, e1, e2))
        for j in range(s.cy + 4):
            double[i, 2 * j : 2 * j + 2, :] = jnp.broadcast_to(plane[j : j + 1, :], (2, LANES))
    for c in range(3):
        for i in range(s.cx):
            pairs[c, i] = fine[c, 2 * i] + fine[c, 2 * i + 1]

    fill_divergence(s.fx, s.fy, ext_f, inv_f, div_f)
    fill_divergence(s.cx, s.cy, ext_c, inv_c, div_c)

    odd_y = lax.broadcasted_iota(jnp.int32, (s.fy, LANES), 0) % 2
    near_y = jnp.where(odd_y == 0, 0.75, 0.25)

    def fine_ghosts(i):
        half = i // 2
        near_x = jnp.where(i % 2 == 0, 0.75, 0.25)
        off_x, off_y = offs[0, i], offs[1, i]
        total = jnp.zeros((s.fy, LANES), jnp.float32)
        weights = []
        for shift in (-1, 0, 1, 2):
            weights.append(
                jnp.where(off_y == shift, near_y, 0.0)
                + jnp.where(off_y == shift - 1, 1.0 - near_y, 0.0)
            )
        for shift in (-1, 0, 1, 2):
            weight_x = jnp.where(off_x == shift, near_x, 0.0) + jnp.where(
                off_x == shift - 1, 1.0 - near_x, 0.0
            )
            line = jnp.zeros((s.fy, LANES), jnp.float32)
            for k in range(4):
                line += weights[k] * double[half + 2 + shift, 2 * k + 2 : 2 * k + 2 + s.fy, :]
            total += weight_x * line
        return None, lambda c: pltpu.roll(total, LANES - 1 - c, 1)

    def coarse_ghosts(i):
        def top(c):
            both = pairs[c, i, pl.ds(0, s.cy, stride=2), :] + pairs[c, i, pl.ds(1, s.cy, stride=2), :]
            column = pltpu.roll(0.25 * both, 1, 1)
            return jnp.concatenate([column] * s.halves, axis=1)

        return top, lambda c: jnp.zeros((s.cy, s.cz), jnp.float32)

    sum_f = update(s.fx, s.fy, ext_f, wide_f, inv_f, div_f, fine_prev, coef_f, new_f, fine_ghosts)
    sum_c = update(
        s.cx, s.cy, ext_c, wide_c, inv_c, div_c, coarse_prev, coef_c, new_c, coarse_ghosts
    )
    place = lax.broadcasted_iota(jnp.int32, (8, LANES), 0)
    before = jnp.zeros((8, LANES), jnp.float32) if first else energy_in[...]
    before = jnp.where(place == 2 * step, jnp.sum(sum_f), before)
    energy[...] = jnp.where(place == 2 * step + 1, jnp.sum(sum_c), before)
    if not final:
        put_x(s, flags, x_out, new_f, new_c, None)


VMEM = pl.BlockSpec(memory_space=pltpu.VMEM)
SMEM = pl.BlockSpec(memory_space=pltpu.SMEM)


def call(kernel, shapes, flops, *args, scratch=(), name=None, table=True):
    shapes = [jax.ShapeDtypeStruct(shape, jnp.float32) for shape in shapes]
    return pl.pallas_call(
        kernel,
        out_shape=shapes,
        in_specs=([SMEM] if table else []) + [VMEM] * (len(args) - table),
        out_specs=[VMEM] * len(shapes),
        scratch_shapes=[pltpu.VMEM(shape, jnp.float32) for shape in scratch],
        compiler_params=pltpu.CompilerParams(vmem_limit_bytes=VMEM_LIMIT),
        cost_estimate=pl.CostEstimate(flops=flops, bytes_accessed=1 << 20, transcendentals=0),
        name=name,
    )(*args)


def across(i, n):
    return (i + 1) % n if i % 2 else (i - 1) % n


def opposite(i, n):
    return (i - 3) % n if i % 2 else (i + 3) % n


def device_pairs(mesh, axes, move):
    sizes = dict(mesh.shape)
    names = list(sizes)
    total = 1
    for name in names:
        total *= sizes[name]
    count = 1
    for name in axes:
        count *= sizes[name]
    pairs = []
    for source in range(total):
        rest, at = source, {}
        for name in reversed(names):
            at[name] = rest % sizes[name]
            rest //= sizes[name]
        index = 0
        for name in axes:
            index = index * sizes[name] + at[name]
        index = move(index, count)
        for name in reversed(axes):
            at[name] = index % sizes[name]
            index //= sizes[name]
        target = 0
        for name in names:
            target = target * sizes[name] + at[name]
        pairs.append((source, target))
    return pairs


def beside(i, n):
    return i ^ 1


def total_over_mesh(value, swap):
    lane = lax.broadcasted_iota(jnp.int32, (8, LANES), 1)

    def ring_of_eight(value, axes):
        value = value + swap(value, axes, beside)
        pair = lax.axis_index(axes) // 2
        slots = jnp.where(lane == pair, value, 0.0)
        slots = slots + swap(slots, axes, across)
        slots = slots + swap(slots, axes, opposite)
        return jnp.broadcast_to(jnp.sum(slots[:, 0:4], axis=1, keepdims=True), (8, LANES))

    value = ring_of_eight(value, GY)
    value = value + swap(value, ("gx_1",), beside)
    value = value + swap(value, ("gx_1",), across)
    return ring_of_eight(value, ("gx_0",))


def per_device(
    mesh,
    fine_disp,
    fine_prev,
    coarse_disp,
    coarse_prev,
    fine_density,
    fine_lame,
    fine_rigidity,
    fine_metric,
    coarse_density,
    coarse_lame,
    coarse_rigidity,
    coarse_metric,
    offsets,
):
    fine_shape, coarse_shape = fine_metric.shape, coarse_metric.shape
    s = Sizes(fine_shape, coarse_shape)
    count_x, count_y = lax.axis_size(GX), lax.axis_size(GY)
    place_x, place_y = lax.axis_index(GX), lax.axis_index(GY)
    flags = jnp.stack(
        [
            (place_x % 2 == 0).astype(jnp.int32),
            (place_x > 0).astype(jnp.int32),
            (place_x < count_x - 1).astype(jnp.int32),
            (place_y % 2 == 0).astype(jnp.int32),
            (place_y > 0).astype(jnp.int32),
            (place_y < count_y - 1).astype(jnp.int32),
        ]
    )

    def swap(value, axes, move):
        return lax.ppermute(value, ALL, device_pairs(mesh, axes, move))

    def swap_both(pair, axes):
        second = swap(pair[1], axes, across)
        return swap(pair[0], axes, beside), second

    offs = jnp.broadcast_to(offsets[..., None], offsets.shape + (LANES,))
    x_out = call(
        functools.partial(first_kernel, s),
        [(s.x_rows_mats, LANES)] * 2,
        1000,
        flags,
        fine_disp,
        coarse_disp,
        fine_rigidity,
        fine_metric,
        coarse_rigidity,
        coarse_metric,
        name="first_strips",
    )
    own = []
    for tag, density, lame, rigidity, metric in (
        ("fine", fine_density, fine_lame, fine_rigidity, fine_metric),
        ("coarse", coarse_density, coarse_lame, coarse_rigidity, coarse_metric),
    ):
        own.append(
            call(
                own_kernel,
                [metric.shape] * 6,
                2_000_000,
                density,
                lame,
                rigidity,
                metric,
                name=f"own_{tag}",
                table=False,
            )
        )
    inverse_f, *coef_f = own[0]
    inverse_c, *coef_c = own[1]

    fine, coarse = fine_disp, coarse_disp
    fine_ext = (s.fx + 2, s.fy + 16, s.fz)
    coarse_ext = (s.cx + 2, s.cy + 16, s.cz)
    scratch = [
        (3, s.fe, s.fy + 16, s.fz),
        (3, s.ce, s.cy + 16, s.cz),
        fine_ext,
        coarse_ext,
        (s.ce, 2 * (s.cy + 4), LANES),
        (3, s.cx, s.fy, LANES),
    ]
    energy = None
    for step in range(STEPS):
        first, final = step == 0, step == STEPS - 1
        raw = [fine_rigidity, fine_metric, coarse_rigidity, coarse_metric] if first else []
        x_in = swap_both(x_out, GX)
        y_out = call(
            functools.partial(middle_kernel, s, first),
            [(s.y_rows_mats if first else s.y_rows, 2, LANES)] * 2,
            1000,
            flags,
            fine,
            coarse,
            *raw,
            *x_in,
            name=f"corner_strips_{step}",
        )
        y_in = swap_both(y_out, GY)
        if first:
            extra = [fine_rigidity, fine_metric, inverse_f, coarse_rigidity, coarse_metric, inverse_c]
        else:
            extra = [*ext_mats, energy]
        shapes = [fine.shape, coarse.shape, (8, LANES)]
        if not final:
            shapes += [(s.x_rows, LANES)] * 2
        if first:
            shapes += [fine_ext, fine_ext, coarse_ext, coarse_ext]
        outs = call(
            functools.partial(step_kernel, s, step),
            shapes,
            4_000_000,
            flags,
            fine,
            coarse,
            fine_prev,
            coarse_prev,
            offs,
            *coef_f,
            *coef_c,
            *extra,
            *x_in,
            *y_in,
            scratch=scratch,
            name=f"step_{step}",
        )
        fine_prev, coarse_prev = fine, coarse
        fine, coarse, energy = outs[:3]
        if not final:
            x_out = outs[3:5]
        if first:
            ext_mats = outs[5:9]
    total = total_over_mesh(energy, swap)
    cells = [count_x * count_y * s.fx * s.fy * s.fz, count_x * count_y * s.cx * s.cy * s.cz]
    energy = total[: 2 * STEPS, 0].reshape(STEPS, 2) / jnp.array(cells, jnp.float32)
    return fine, coarse, energy


def solution(mesh):
    finer = Mesh(mesh.devices.reshape(8, 4, 4, 2), ALL)
    level, cell = P(None, GX, GY, None), P(GX, GY, None)
    in_specs = (level,) * 4 + (cell,) * 8 + (P(None, GX, GY),)
    return jax.shard_map(
        functools.partial(per_device, finer),
        mesh=finer,
        in_specs=in_specs,
        out_specs=(level, level, P()),
        check_vma=False,
    )
```

time: 239 us -> 110 us (0.46)
  the two profiles are of different devices: /device:TPU:1 before, /device:TPU:6 now
where the time goes in v1:
time: 110 us; the launch traced here: 109 us
  waiting for transfers between devices  43.1 us (39%)
  starting transfers between devices  33.4 us (30%)
  Pallas kernels  22.9 us (21%)
  local copies, waits for them, and re-layouts  8.71 us (8%)
    ppermute x20, waiting for transfers between devices, swap(): return lax.ppermute(value, ALL, device_pairs(mesh, axes, move))  43.1 us
    ppermute x20, starting transfers between devices, swap(): return lax.ppermute(value, ALL, device_pairs(mesh, axes, move))  33.4 us
    pallas_call x9, Pallas kernels, call(): pl.pallas_call(kernel, out_shape=shapes, in_specs=([SMEM] if table else [...  22.9 us
    unnamed x47, local copies, waits for them, and re-layouts  8.33 us
  transfers between devices with their start and end apart: 20, of which 17 were waited for; matrix products, arithmetic and copies ran while one was open for 0% of the time, Pallas kernels for 0%

profile of v1, /device:TPU:6, one launch (start us, length us, event | category | flops | bytes accessed | tf_op | source)
XLA Modules:
  0.0 109.5 jit_solution(5026170769002790245)
XLA Ops:
  7.5 2.5 %collective-permute-start.1 = (f32[256,128]{1,0:T(8,128)S(1)}, f32[256,128]{1,0:T(8,128)S(1)}, u32[]{:S(2)}, u32[]{:S(2)}) collective-permute-start(f32[256,128]{1,0:T(8,128)S(1)} %get-tuple-element.53), channel_id=1, source_target_pairs={{0,248},{1,249},{2,250},{3,251},{4,252},{5,253},{6,254},{7,255},{8... | collective-permute-start | bytes 393224 | tf_op jit(solution)/shard_map/ppermute | solution.py:456
  11.9 2.7 %collective-permute-done.1.refs_7_.refs_22_ = f32[256,128]{1,0:T(8,128)S(1)} collective-permute-done((f32[256,128]{1,0:T(8,128)S(1)}, f32[256,128]{1,0:T(8,128)S(1)}, u32[]{:S(2)}, u32[]{:S(2)}) %collective-permute-start.1) | collective-permute-done | bytes 131104 | tf_op jit(solution)/shard_map/ppermute | solution.py:456
  15.5 3.1 %collective-permute-start.3 = (f32[164,2,128]{2,1,0:T(2,128)S(1)}, f32[164,2,128]{2,1,0:T(2,128)S(1)}, u32[]{:S(2)}, u32[]{:S(2)}) collective-permute-start(f32[164,2,128]{2,1,0:T(2,128)S(1)} %get-tuple-element.55), channel_id=1, source_target_pairs={{0,7},{1,2},{2,1},{3,4},{4,3},{5,6},{6,5},{7,0},{8,15},{9,10},{10,... | collective-permute-start | bytes 503816 | tf_op jit(solution)/shard_map/ppermute | solution.py:456
  18.9 2.7 %collective-permute-done.3.refs_24_ = f32[164,2,128]{2,1,0:T(2,128)S(1)} collective-permute-done((f32[164,2,128]{2,1,0:T(2,128)S(1)}, f32[164,2,128]{2,1,0:T(2,128)S(1)}, u32[]{:S(2)}, u32[]{:S(2)}) %collective-permute-start.3) | collective-permute-done | bytes 167968 | tf_op jit(solution)/shard_map/ppermute | solution.py:456
  21.8 6.2 %step_0.1 = (f32[3,16,16,128]{3,2,1,0:T(8,128)S(1)}, f32[3,8,8,256]{3,2,1,0:T(8,128)S(1)}, f32[8,128]{1,0:T(8,128)S(1)}, f32[192,128]{1,0:T(8,128)S(1)}, f32[192...) custom-call(s32[6]{0:T(128)S(1)} %stack.36.flags, ...), custom_call_target="tpu_custom_call" | custom-call | flops 4000000 | bytes 1048576 | tf_op jit(solution)/shard_map/step_0/pallas_call | solution.py:354
  28.1 2.6 %collective-permute-start.5 = (f32[192,128]{1,0:T(8,128)S(1)}, f32[192,128]{1,0:T(8,128)S(1)}, u32[]{:S(2)}, u32[]{:S(2)}) collective-permute-start(f32[192,128]{1,0:T(8,128)S(1)} %get-tuple-element.64), channel_id=1, source_target_pairs={{0,248},{1,249},{2,250},{3,251},{4,252},{5,253},{6,254},{7,255},{8... | collective-permute-start | bytes 294920 | tf_op jit(solution)/shard_map/ppermute | solution.py:456
  30.7 2.0 %collective-permute-done.4.refs_2_.refs_20_ = f32[192,128]{1,0:T(8,128)S(1)} collective-permute-done((f32[192,128]{1,0:T(8,128)S(1)}, f32[192,128]{1,0:T(8,128)S(1)}, u32[]{:S(2)}, u32[]{:S(2)}) %collective-permute-start.4) | collective-permute-done | bytes 98336 | tf_op jit(solution)/shard_map/ppermute | solution.py:456
  32.7 2.2 %collective-permute-done.5.refs_3_.refs_21_ = f32[192,128]{1,0:T(8,128)S(1)} collective-permute-done((f32[192,128]{1,0:T(8,128)S(1)}, f32[192,128]{1,0:T(8,128)S(1)}, u32[]{:S(2)}, u32[]{:S(2)}) %collective-permute-start.5) | collective-permute-done | bytes 98336 | tf_op jit(solution)/shard_map/ppermute | solution.py:456
  35.6 2.3 %collective-permute-start.7 = (f32[132,2,128]{2,1,0:T(2,128)S(1)}, f32[132,2,128]{2,1,0:T(2,128)S(1)}, u32[]{:S(2)}, u32[]{:S(2)}) collective-permute-start(f32[132,2,128]{2,1,0:T(2,128)S(1)} %get-tuple-element.66), channel_id=1, source_target_pairs={{0,7},{1,2},{2,1},{3,4},{4,3},{5,6},{6,5},{7,0},{8,15},{9,10},{10,... | collective-permute-start | bytes 405512 | tf_op jit(solution)/shard_map/ppermute | solution.py:456
  38.0 3.4 %collective-permute-done.7.refs_23_ = f32[132,2,128]{2,1,0:T(2,128)S(1)} collective-permute-done((f32[132,2,128]{2,1,0:T(2,128)S(1)}, f32[132,2,128]{2,1,0:T(2,128)S(1)}, u32[]{:S(2)}, u32[]{:S(2)}) %collective-permute-start.7) | collective-permute-done | bytes 135200 | tf_op jit(solution)/shard_map/ppermute | solution.py:456
  41.4 6.0 %step_1.1 = (f32[3,16,16,128]{3,2,1,0:T(8,128)S(1)}, f32[3,8,8,256]{3,2,1,0:T(8,128)S(1)}, f32[8,128]{1,0:T(8,128)S(1)}, f32[192,128]{1,0:T(8,128)S(1)}, f32[192,128]{1,0:T(8,128)S(1)}) custom-call(s32[6]{0:T(128)S(1)} %stack.36.flags, f32[3,16,16,128]{3,2,1,0:T(8,128)S(1)} %get-tuple-element.56.refs_0_.refs_2_, ...), custom_call_target="tpu_custom_call" | custom-call | flops 4000000 | bytes 1048576 | tf_op jit(solution)/shard_map/step_1/pallas_call | solution.py:354
  50.1 2.0 %collective-permute-done.8.refs_2_.refs_20_ = f32[192,128]{1,0:T(8,128)S(1)} collective-permute-done((f32[192,128]{1,0:T(8,128)S(1)}, f32[192,128]{1,0:T(8,128)S(1)}, u32[]{:S(2)}, u32[]{:S(2)}) %collective-permute-start.8) | collective-permute-done | bytes 98336 | tf_op jit(solution)/shard_map/ppermute | solution.py:456
  52.1 4.0 %collective-permute-done.9.refs_3_.refs_21_ = f32[192,128]{1,0:T(8,128)S(1)} collective-permute-done((f32[192,128]{1,0:T(8,128)S(1)}, f32[192,128]{1,0:T(8,128)S(1)}, u32[]{:S(2)}, u32[]{:S(2)}) %collective-permute-start.9) | collective-permute-done | bytes 98336 | tf_op jit(solution)/shard_map/ppermute | solution.py:456
  57.5 2.4 %collective-permute-start.11 = (f32[132,2,128]{2,1,0:T(2,128)}, f32[132,2,128]{2,1,0:T(2,128)}, u32[]{:S(2)}, u32[]{:S(2)}) collective-permute-start(f32[132,2,128]{2,1,0:T(2,128)} %get-tuple-element.73), channel_id=1, source_target_pairs={{0,7},{1,2},{2,1},{3,4},{4,3},{5,6},{6,5},{7,0},{8,15},{9,10},{10,... | collective-permute-start | bytes 405512 | tf_op jit(solution)/shard_map/ppermute | solution.py:456
  59.9 3.6 %collective-permute-done.11.refs_23_ = f32[132,2,128]{2,1,0:T(2,128)} collective-permute-done((f32[132,2,128]{2,1,0:T(2,128)}, f32[132,2,128]{2,1,0:T(2,128)}, u32[]{:S(2)}, u32[]{:S(2)}) %collective-permute-start.11) | collective-permute-done | bytes 135200 | tf_op jit(solution)/shard_map/ppermute | solution.py:456
  65.3 7.1 %step_2.1 = (f32[3,16,16,128]{3,2,1,0:T(8,128)}, f32[3,8,8,256]{3,2,1,0:T(8,128)}, f32[8,128]{1,0:T(8,128)S(1)}) custom-call(s32[6]{0:T(128)S(1)} %stack.36.flags, f32[3,16,16,128]{3,2,1,0:T(8,128)S(1)} %get-tuple-element.67.refs_0_, f32[3,8,8,256]{3,2,1,0:T(8,128)S(1)} %get-tuple-element.68.refs_1_, ...), custom_call_target="tpu_custom_call" | custom-call | flops 4000000 | bytes 1048576 | tf_op jit(solution)/shard_map/step_2/pallas_call | solution.py:354
  73.6 2.3 %collective-permute-start.13 = (f32[8,128]{1,0:T(8,128)S(1)}, f32[8,128]{1,0:T(8,128)S(1)}, u32[]{:S(2)}, u32[]{:S(2)}) collective-permute-start(f32[8,128]{1,0:T(8,128)S(1)} %add_select_fusion.1), channel_id=1, source_target_pairs={{0,7},{1,2},{2,1},{3,4},{4,3},{5,6},{6,5},{7,0},{8,15},{9,10},{10,... | collective-permute-start | bytes 12296 | tf_op jit(solution)/shard_map/ppermute | solution.py:456
  77.9 3.0 %collective-permute-done.14 = f32[8,128]{1,0:T(8,128)S(1)} collective-permute-done((f32[8,128]{1,0:T(8,128)S(1)}, f32[8,128]{1,0:T(8,128)S(1)}, u32[]{:S(2)}, u32[]{:S(2)}) %collective-permute-start.14) | collective-permute-done | bytes 4128 | tf_op jit(solution)/shard_map/ppermute | solution.py:456
  82.4 2.3 %collective-permute-done.15 = f32[8,128]{1,0:T(8,128)S(1)} collective-permute-done((f32[8,128]{1,0:T(8,128)S(1)}, f32[8,128]{1,0:T(8,128)S(1)}, u32[]{:S(2)}, u32[]{:S(2)}) %collective-permute-start.15) | collective-permute-done | bytes 4128 | tf_op jit(solution)/shard_map/ppermute | solution.py:456
  84.8 5.3 %collective-permute-start.16 = (f32[8,128]{1,0:T(8,128)S(1)}, f32[8,128]{1,0:T(8,128)S(1)}, u32[]{:S(2)}, u32[]{:S(2)}) collective-permute-start(f32[8,128]{1,0:T(8,128)S(1)} %broadcast_add_fusion), channel_id=1, source_target_pairs={{0,24},{1,25},{2,26},{3,27},{4,28},{5,29},{6,30},{7,31},{8,16},{9,... | collective-permute-start | bytes 12296 | tf_op jit(solution)/shard_map/ppermute | solution.py:456
  91.8 3.6 %collective-permute-done.17 = f32[8,128]{1,0:T(8,128)S(1)} collective-permute-done((f32[8,128]{1,0:T(8,128)S(1)}, f32[8,128]{1,0:T(8,128)S(1)}, u32[]{:S(2)}, u32[]{:S(2)}) %collective-permute-start.17) | collective-permute-done | bytes 4128 | tf_op jit(solution)/shard_map/ppermute | solution.py:456
  95.4 5.6 %collective-permute-start.18 = (f32[8,128]{1,0:T(8,128)S(1)}, f32[8,128]{1,0:T(8,128)S(1)}, u32[]{:S(2)}, u32[]{:S(2)}) collective-permute-start(f32[8,128]{1,0:T(8,128)S(1)} %add_select_fusion), channel_id=1, source_target_pairs={{0,224},{1,225},{2,226},{3,227},{4,228},{5,229},{6,230},{7,231},{8... | collective-permute-start | bytes 12296 | tf_op jit(solution)/shard_map/ppermute | solution.py:456
  102.6 2.0 %collective-permute-start.19 = (f32[8,128]{1,0:T(8,128)S(1)}, f32[8,128]{1,0:T(8,128)S(1)}, u32[]{:S(2)}, u32[]{:S(2)}) collective-permute-start(f32[8,128]{1,0:T(8,128)S(1)} %add.50), channel_id=1, source_target_pairs={{0,96},{1,97},{2,98},{3,99},{4,100},{5,101},{6,102},{7,103},{8,104... | collective-permute-start | bytes 12296 | tf_op jit(solution)/shard_map/ppermute | solution.py:456
  104.6 3.4 %collective-permute-done.19 = f32[8,128]{1,0:T(8,128)S(1)} collective-permute-done((f32[8,128]{1,0:T(8,128)S(1)}, f32[8,128]{1,0:T(8,128)S(1)}, u32[]{:S(2)}, u32[]{:S(2)}) %collective-permute-start.19) | collective-permute-done | bytes 4128 | tf_op jit(solution)/shard_map/ppermute | solution.py:456
  (90 shorter events, 26.0 us)
Async XLA Ops:
  6.6 5.3 %collective-permute-start = (f32[256,128]{1,0:T(8,128)S(1)}, f32[256,128]{1,0:T(8,128)S(1)}, u32[]{:S(2)}, u32[]{:S(2)}) collective-permute-start(f32[256,128]{1,0:T(8,128)S(1)} %get-tuple-element.52), channel_id=1, source_target_pairs={{0,8},{1,9},{2,10},{3,11},{4,12},{5,13},{6,14},{7,15},{8,0},{9,1},... | collective-permute-start | bytes 393224 | tf_op jit(solution)/shard_map/ppermute | solution.py:456
  7.5 11.0 %copy-start.10 = (f32[8,8,256]{2,1,0:T(8,128)S(1)}, f32[8,8,256]{2,1,0:T(8,128)}, u32[]{:S(2)}) copy-start(f32[8,8,256]{2,1,0:T(8,128)} %refs_19_.1) | copy-start | bytes 196612
  7.5 11.0 %copy-start.19 = (f32[8,8,256]{2,1,0:T(8,128)S(1)}, f32[8,8,256]{2,1,0:T(8,128)}, u32[]{:S(2)}) copy-start(f32[8,8,256]{2,1,0:T(8,128)} %density.3) | copy-start | bytes 196612
  7.5 11.0 %copy-start.20 = (f32[8,8,256]{2,1,0:T(8,128)S(1)}, f32[8,8,256]{2,1,0:T(8,128)}, u32[]{:S(2)}) copy-start(f32[8,8,256]{2,1,0:T(8,128)} %lame.3) | copy-start | bytes 196612
  7.5 7.1 %collective-permute-start.1 = (f32[256,128]{1,0:T(8,128)S(1)}, f32[256,128]{1,0:T(8,128)S(1)}, u32[]{:S(2)}, u32[]{:S(2)}) collective-permute-start(f32[256,128]{1,0:T(8,128)S(1)} %get-tuple-element.53), channel_id=1, source_target_pairs={{0,248},{1,249},{2,250},{3,251},{4,252},{5,253},{6,254},{7,255},{8... | collective-permute-start | bytes 393224 | tf_op jit(solution)/shard_map/ppermute | solution.py:456
  14.6 7.1 %copy-start.11 = (f32[3,16,16,128]{3,2,1,0:T(8,128)S(1)}, f32[3,16,16,128]{3,2,1,0:T(8,128)}, u32[]{:S(2)}) copy-start(f32[3,16,16,128]{3,2,1,0:T(8,128)} %refs_2_.4) | copy-start | bytes 1179652
  15.3 3.6 %collective-permute-start.2 = (f32[164,2,128]{2,1,0:T(2,128)S(1)}, f32[164,2,128]{2,1,0:T(2,128)S(1)}, u32[]{:S(2)}, u32[]{:S(2)}) collective-permute-start(f32[164,2,128]{2,1,0:T(2,128)S(1)} %get-tuple-element.54), channel_id=1, source_target_pairs={{0,1},{1,0},{2,3},{3,2},{4,5},{5,4},{6,7},{7,6},{8,9},{9,8},{10,11... | collective-permute-start | bytes 503816 | tf_op jit(solution)/shard_map/ppermute | solution.py:456
  15.5 6.1 %collective-permute-start.3 = (f32[164,2,128]{2,1,0:T(2,128)S(1)}, f32[164,2,128]{2,1,0:T(2,128)S(1)}, u32[]{:S(2)}, u32[]{:S(2)}) collective-permute-start(f32[164,2,128]{2,1,0:T(2,128)S(1)} %get-tuple-element.55), channel_id=1, source_target_pairs={{0,7},{1,2},{2,1},{3,4},{4,3},{5,6},{6,5},{7,0},{8,15},{9,10},{10,... | collective-permute-start | bytes 503816 | tf_op jit(solution)/shard_map/ppermute | solution.py:456
  28.0 4.7 %collective-permute-start.4 = (f32[192,128]{1,0:T(8,128)S(1)}, f32[192,128]{1,0:T(8,128)S(1)}, u32[]{:S(2)}, u32[]{:S(2)}) collective-permute-start(f32[192,128]{1,0:T(8,128)S(1)} %get-tuple-element.63), channel_id=1, source_target_pairs={{0,8},{1,9},{2,10},{3,11},{4,12},{5,13},{6,14},{7,15},{8,0},{9,1},... | collective-permute-start | bytes 294920 | tf_op jit(solution)/shard_map/ppermute | solution.py:456
  28.1 6.8 %collective-permute-start.5 = (f32[192,128]{1,0:T(8,128)S(1)}, f32[192,128]{1,0:T(8,128)S(1)}, u32[]{:S(2)}, u32[]{:S(2)}) collective-permute-start(f32[192,128]{1,0:T(8,128)S(1)} %get-tuple-element.64), channel_id=1, source_target_pairs={{0,248},{1,249},{2,250},{3,251},{4,252},{5,253},{6,254},{7,255},{8... | collective-permute-start | bytes 294920 | tf_op jit(solution)/shard_map/ppermute | solution.py:456
  35.5 2.4 %collective-permute-start.6 = (f32[132,2,128]{2,1,0:T(2,128)S(1)}, f32[132,2,128]{2,1,0:T(2,128)S(1)}, u32[]{:S(2)}, u32[]{:S(2)}) collective-permute-start(f32[132,2,128]{2,1,0:T(2,128)S(1)} %get-tuple-element.65), channel_id=1, source_target_pairs={{0,1},{1,0},{2,3},{3,2},{4,5},{5,4},{6,7},{7,6},{8,9},{9,8},{10,11... | collective-permute-start | bytes 405512 | tf_op jit(solution)/shard_map/ppermute | solution.py:456
  35.6 5.7 %collective-permute-start.7 = (f32[132,2,128]{2,1,0:T(2,128)S(1)}, f32[132,2,128]{2,1,0:T(2,128)S(1)}, u32[]{:S(2)}, u32[]{:S(2)}) collective-permute-start(f32[132,2,128]{2,1,0:T(2,128)S(1)} %get-tuple-element.66), channel_id=1, source_target_pairs={{0,7},{1,2},{2,1},{3,4},{4,3},{5,6},{6,5},{7,0},{8,15},{9,10},{10,... | collective-permute-start | bytes 405512 | tf_op jit(solution)/shard_map/ppermute | solution.py:456
  47.4 4.7 %collective-permute-start.8 = (f32[192,128]{1,0:T(8,128)S(1)}, f32[192,128]{1,0:T(8,128)S(1)}, u32[]{:S(2)}, u32[]{:S(2)}) collective-permute-start(f32[192,128]{1,0:T(8,128)S(1)} %get-tuple-element.70), channel_id=1, source_target_pairs={{0,8},{1,9},{2,10},{3,11},{4,12},{5,13},{6,14},{7,15},{8,0},{9,1},... | collective-permute-start | bytes 294920 | tf_op jit(solution)/shard_map/ppermute | solution.py:456
  49.4 6.7 %collective-permute-start.9 = (f32[192,128]{1,0:T(8,128)S(1)}, f32[192,128]{1,0:T(8,128)S(1)}, u32[]{:S(2)}, u32[]{:S(2)}) collective-permute-start(f32[192,128]{1,0:T(8,128)S(1)} %get-tuple-element.71), channel_id=1, source_target_pairs={{0,248},{1,249},{2,250},{3,251},{4,252},{5,253},{6,254},{7,255},{8... | collective-permute-start | bytes 294920 | tf_op jit(solution)/shard_map/ppermute | solution.py:456
  57.4 2.4 %collective-permute-start.10 = (f32[132,2,128]{2,1,0:T(2,128)}, f32[132,2,128]{2,1,0:T(2,128)}, u32[]{:S(2)}, u32[]{:S(2)}) collective-permute-start(f32[132,2,128]{2,1,0:T(2,128)} %get-tuple-element.72), channel_id=1, source_target_pairs={{0,1},{1,0},{2,3},{3,2},{4,5},{5,4},{6,7},{7,6},{8,9},{9,8},{10,11... | collective-permute-start | bytes 405512 | tf_op jit(solution)/shard_map/ppermute | solution.py:456
  57.5 6.0 %collective-permute-start.11 = (f32[132,2,128]{2,1,0:T(2,128)}, f32[132,2,128]{2,1,0:T(2,128)}, u32[]{:S(2)}, u32[]{:S(2)}) collective-permute-start(f32[132,2,128]{2,1,0:T(2,128)} %get-tuple-element.73), channel_id=1, source_target_pairs={{0,7},{1,2},{2,1},{3,4},{4,3},{5,6},{6,5},{7,0},{8,15},{9,10},{10,... | collective-permute-start | bytes 405512 | tf_op jit(solution)/shard_map/ppermute | solution.py:456
  72.4 1.2 %collective-permute-start.12 = (f32[8,128]{1,0:T(8,128)S(1)}, f32[8,128]{1,0:T(8,128)S(1)}, u32[]{:S(2)}, u32[]{:S(2)}) collective-permute-start(f32[8,128]{1,0:T(8,128)S(1)} %get-tuple-element.76), channel_id=1, source_target_pairs={{0,1},{1,0},{2,3},{3,2},{4,5},{5,4},{6,7},{7,6},{8,9},{9,8},{10,11... | collective-permute-start | bytes 12296 | tf_op jit(solution)/shard_map/ppermute | solution.py:456
  73.6 4.2 %collective-permute-start.13 = (f32[8,128]{1,0:T(8,128)S(1)}, f32[8,128]{1,0:T(8,128)S(1)}, u32[]{:S(2)}, u32[]{:S(2)}) collective-permute-start(f32[8,128]{1,0:T(8,128)S(1)} %add_select_fusion.1), channel_id=1, source_target_pairs={{0,7},{1,2},{2,1},{3,4},{4,3},{5,6},{6,5},{7,0},{8,15},{9,10},{10,... | collective-permute-start | bytes 12296 | tf_op jit(solution)/shard_map/ppermute | solution.py:456
  77.9 3.0 %collective-permute-start.14 = (f32[8,128]{1,0:T(8,128)S(1)}, f32[8,128]{1,0:T(8,128)S(1)}, u32[]{:S(2)}, u32[]{:S(2)}) collective-permute-start(f32[8,128]{1,0:T(8,128)S(1)} %add.45), channel_id=1, source_target_pairs={{0,3},{1,6},{2,5},{3,0},{4,7},{5,2},{6,1},{7,4},{8,11},{9,14},{10,... | collective-permute-start | bytes 12296 | tf_op jit(solution)/shard_map/ppermute | solution.py:456
  81.1 3.6 %collective-permute-start.15 = (f32[8,128]{1,0:T(8,128)S(1)}, f32[8,128]{1,0:T(8,128)S(1)}, u32[]{:S(2)}, u32[]{:S(2)}) collective-permute-start(f32[8,128]{1,0:T(8,128)S(1)} %broadcast_in_dim.13), channel_id=1, source_target_pairs={{0,8},{1,9},{2,10},{3,11},{4,12},{5,13},{6,14},{7,15},{8,0},{9,1},... | collective-permute-start | bytes 12296 | tf_op jit(solution)/shard_map/ppermute | solution.py:456
  84.8 6.9 %collective-permute-start.16 = (f32[8,128]{1,0:T(8,128)S(1)}, f32[8,128]{1,0:T(8,128)S(1)}, u32[]{:S(2)}, u32[]{:S(2)}) collective-permute-start(f32[8,128]{1,0:T(8,128)S(1)} %broadcast_add_fusion), channel_id=1, source_target_pairs={{0,24},{1,25},{2,26},{3,27},{4,28},{5,29},{6,30},{7,31},{8,16},{9,... | collective-permute-start | bytes 12296 | tf_op jit(solution)/shard_map/ppermute | solution.py:456
  91.8 3.6 %collective-permute-start.17 = (f32[8,128]{1,0:T(8,128)S(1)}, f32[8,128]{1,0:T(8,128)S(1)}, u32[]{:S(2)}, u32[]{:S(2)}) collective-permute-start(f32[8,128]{1,0:T(8,128)S(1)} %fusion), channel_id=1, source_target_pairs={{0,32},{1,33},{2,34},{3,35},{4,36},{5,37},{6,38},{7,39},{8,40},{9,... | collective-permute-start | bytes 12296 | tf_op jit(solution)/shard_map/ppermute | solution.py:456
  95.4 7.2 %collective-permute-start.18 = (f32[8,128]{1,0:T(8,128)S(1)}, f32[8,128]{1,0:T(8,128)S(1)}, u32[]{:S(2)}, u32[]{:S(2)}) collective-permute-start(f32[8,128]{1,0:T(8,128)S(1)} %add_select_fusion), channel_id=1, source_target_pairs={{0,224},{1,225},{2,226},{3,227},{4,228},{5,229},{6,230},{7,231},{8... | collective-permute-start | bytes 12296 | tf_op jit(solution)/shard_map/ppermute | solution.py:456
  102.6 5.4 %collective-permute-start.19 = (f32[8,128]{1,0:T(8,128)S(1)}, f32[8,128]{1,0:T(8,128)S(1)}, u32[]{:S(2)}, u32[]{:S(2)}) collective-permute-start(f32[8,128]{1,0:T(8,128)S(1)} %add.50), channel_id=1, source_target_pairs={{0,96},{1,97},{2,98},{3,99},{4,100},{5,101},{6,102},{7,103},{8,104... | collective-permute-start | bytes 12296 | tf_op jit(solution)/shard_map/ppermute | solution.py:456
  (19 other events, 41.2 us)

commit v2 on v1

--- a/solution.py
+++ b/solution.py
@@ -42,7 +42,7 @@
     return slice(h * LANES, (h + 1) * LANES)
 
 
-def put_x(s, flags, outs, fine, coarse, mats):
+def put_x(s, flags, outs, fine, coarse):
     even = flags[EVEN_X] == 1
     for k, out in enumerate(outs):
         far = even if k == 0 else jnp.logical_not(even)
@@ -53,21 +53,37 @@
         for h in range(s.halves):
             base = s.x_coarse + h * 6 * s.cy
             out[base : base + 6 * s.cy, :] = strip[:, :, :, lanes_of(h)].reshape(6 * s.cy, LANES)
-        if mats is None:
-            continue
-        edge_f = jnp.where(far, s.fx - 1, 0)
-        edge_c = jnp.where(far, s.cx - 1, 0)
+
+
+def first_kernel(s, flags, fine, coarse, rig_f, met_f, rig_c, met_c, out_a, out_b, *scratch):
+    strip_f, strip_c, line_f, line_c, sems = scratch
+    copies = []
+
+    def fetch(source, target):
+        copies.append(pltpu.make_async_copy(source, target, sems.at[len(copies)]))
+        copies[-1].start()
+
+    even = flags[EVEN_X] == 1
+    for k in range(2):
+        far = even if k == 0 else jnp.logical_not(even)
+        fetch(fine.at[:, pl.ds(jnp.where(far, s.fx - 2, 0), 2)], strip_f.at[k])
+        fetch(coarse.at[:, pl.ds(jnp.where(far, s.cx - 2, 0), 2)], strip_c.at[k])
+        for m, (of_f, of_c) in enumerate(((rig_f, rig_c), (met_f, met_c))):
+            fetch(of_f.at[jnp.where(far, s.fx - 1, 0)], line_f.at[k, m])
+            fetch(of_c.at[jnp.where(far, s.cx - 1, 0)], line_c.at[k, m])
+    for copy in copies:
+        copy.wait()
+    for k, out in enumerate((out_a, out_b)):
+        out[0 : s.x_coarse, :] = strip_f[k].reshape(6 * s.fy, LANES)
         for m in range(2):
             base = s.x_fine_mats + m * s.fy
-            out[base : base + s.fy, :] = mats[m][edge_f]
-            line = mats[2 + m][edge_c]
-            for h in range(s.halves):
+            out[base : base + s.fy, :] = line_f[k, m]
+        for h in range(s.halves):
+            base = s.x_coarse + h * 6 * s.cy
+            out[base : base + 6 * s.cy, :] = strip_c[k, :, :, :, lanes_of(h)].reshape(6 * s.cy, LANES)
+            for m in range(2):
                 base = s.x_coarse_mats + (m * s.halves + h) * s.cy
-                out[base : base + s.cy, :] = line[:, lanes_of(h)]
-
-
-def first_kernel(s, flags, fine, coarse, rig_f, met_f, rig_c, met_c, out_a, out_b):
-    put_x(s, flags, (out_a, out_b), fine, coarse, (rig_f, met_f, rig_c, met_c))
+                out[base : base + s.cy, :] = line_c[k, m, :, lanes_of(h)]
 
 
 def sides(flags, even, has_low, has_high, a, b):
@@ -138,7 +154,7 @@
     return pltpu.roll(x, 1, x.ndim - 1)
 
 
-def own_kernel(density, lame, rigidity, metric, inverse, c1, c2, weight, above, below):
+def own_kernel(density, lame, rigidity, metric, inverse, c1, c2, weight, above, first):
     inv = 1.0 / metric[...]
     inverse[...] = inv
     over = 1.0 / density[...]
@@ -148,7 +164,7 @@
     v = rigidity[...] * inv
     lane = lax.broadcasted_iota(jnp.int32, v.shape, 2)
     above[...] = jnp.where(lane == v.shape[2] - 1, v, 0.5 * (v + up_one(v)))
-    below[...] = jnp.where(lane == 0, v, 0.5 * (v + down_one(v)))
+    first[...] = v[:, :, 0:LANES]
 
 
 def slope(f, up, down, lane):
@@ -175,8 +191,8 @@
 
 def fill_materials(s, flags, rigidity, metric, inverse, wide_ext, inv_ext, x_in, y_in, fine):
     x, y = (s.fx, s.fy) if fine else (s.cx, s.cy)
-    wide_ext[1 : 1 + x, 8 : 8 + y, :] = rigidity[...] * metric[...]
-    inv_ext[1 : 1 + x, 8 : 8 + y, :] = inverse[...]
+    wide_ext[1 : 1 + x, 1 : 1 + y, :] = rigidity[...] * metric[...]
+    inv_ext[1 : 1 + x, 1 : 1 + y, :] = inverse[...]
     for h in range(1 if fine else s.halves):
         at = lanes_of(h)
         got = []
@@ -188,8 +204,8 @@
             got.append((jnp.where(even, b, a), jnp.where(even, a, b)))
         for side, (flag, place) in enumerate(((HAS_XM, 0), (HAS_XP, x + 1))):
             rig, met = got[0][side], got[1][side]
-            wide_ext[place, 8 : 8 + y, at] = jnp.where(flags[flag] == 1, rig * met, 0.0)
-            inv_ext[place, 8 : 8 + y, at] = jnp.where(flags[flag] == 1, 1.0 / met, 0.0)
+            wide_ext[place, 1 : 1 + y, at] = jnp.where(flags[flag] == 1, rig * met, 0.0)
+            inv_ext[place, 1 : 1 + y, at] = jnp.where(flags[flag] == 1, 1.0 / met, 0.0)
         start = s.y_fine_mats if fine else s.y_coarse_mats + h * x
         rows = slice(start, start + x)
         got = []
@@ -197,7 +213,7 @@
             even = flags[EVEN_Y] == 1
             a, b = y_in[0][rows, m : m + 1, :], y_in[1][rows, m : m + 1, :]
             got.append((jnp.where(even, b, a), jnp.where(even, a, b)))
-        for side, (flag, place) in enumerate(((HAS_YM, 7), (HAS_YP, 8 + y))):
+        for side, (flag, place) in enumerate(((HAS_YM, 0), (HAS_YP, 1 + y))):
             rig, met = got[0][side], got[1][side]
             wide_ext[1 : 1 + x, place : place + 1, at] = jnp.where(flags[flag] == 1, rig * met, 0.0)
             inv_ext[1 : 1 + x, place : place + 1, at] = jnp.where(flags[flag] == 1, 1.0 / met, 0.0)
@@ -211,27 +227,27 @@
         along_x = ext[0, r + 2, 7 : 9 + y, :] - ext[0, r, 7 : 9 + y, :]
         along_y = ext[1, r + 1, 8 : 10 + y, :] - ext[1, r + 1, 6 : 8 + y, :]
         f = ext[2, r + 1, 7 : 9 + y, :]
-        inv = inv_ext[r, 7 : 9 + y, :]
+        inv = inv_ext[r, 0 : 2 + y, :]
         total = 0.5 * along_x + 0.5 * along_y + inv * slope(f, up_one(f), down_one(f), lane)
         div[r, 7 : 9 + y, :] = jnp.where(inv > 0.0, total, 0.0)
         return carry
 
-    lax.fori_loop(0, x + 2, row, 0)
+    lax.fori_loop(0, x + 2, row, 0, unroll=True)
 
 
 def update(x, y, ext, wide_ext, inv_ext, div, prev, coef, new, ghosts):
-    c1, c2, weight, above, below = coef
+    c1, c2, weight, above, vertical = coef
     z = ext.shape[-1]
     lane = lax.broadcasted_iota(jnp.int32, (y, z), 1)
-    mid, left, right = slice(8, 8 + y), slice(7, 7 + y), slice(9, 9 + y)
+    mid, left, right, own = slice(8, 8 + y), slice(7, 7 + y), slice(9, 9 + y), slice(1, 1 + y)
 
     def row(i, total):
-        wide = wide_ext[i + 1, mid, :]
-        w_xp = 0.5 * (wide + wide_ext[i + 2, mid, :])
-        w_xm = 0.5 * (wide_ext[i, mid, :] + wide)
-        w_yp = 0.5 * (wide + wide_ext[i + 1, right, :])
-        w_ym = 0.5 * (wide_ext[i + 1, left, :] + wide)
-        inv = inv_ext[i + 1, mid, :]
+        wide = wide_ext[i + 1, own, :]
+        w_xp = 0.5 * (wide + wide_ext[i + 2, own, :])
+        w_xm = 0.5 * (wide_ext[i, own, :] + wide)
+        w_yp = 0.5 * (wide + wide_ext[i + 1, 2 : 2 + y, :])
+        w_ym = 0.5 * (wide_ext[i + 1, 0:y, :] + wide)
+        inv = inv_ext[i + 1, own, :]
         f = div[i + 1, mid, :]
         gradient = (
             0.5 * (div[i + 2, mid, :] - div[i, mid, :]),
@@ -239,15 +255,16 @@
             inv * slope(f, up_one(f), down_one(f), lane),
         )
         top, bottom = ghosts(i)
-        k1, k2, dm, va, vb = c1[i], c2[i], weight[i], above[i], below[i]
+        k1, k2, dm, va = c1[i], c2[i], weight[i], above[i]
         inner = jnp.zeros((y, z), jnp.float32)
         for c in range(3):
             u = ext[c, i + 2, mid, :]
             up = jnp.where(lane == z - 1, bottom(c), up_one(u))
-            down = jnp.where(lane == 0, u if top is None else top(c), down_one(u))
             flux = w_xp * (ext[c, i + 3, mid, :] - u) - w_xm * (u - ext[c, i + 1, mid, :])
             flux += w_yp * (ext[c, i + 2, right, :] - u) - w_ym * (u - ext[c, i + 2, left, :])
-            flux += va * (up - u) - vb * (u - down)
+            over = va * (up - u)
+            entry = 0.0 if top is None else vertical[i, :, 0:1] * (u[:, 0:1] - top(c))
+            flux += over - jnp.where(lane == 0, entry, down_one(over))
             rate = flux * k1 + k2 * gradient[c]
             updated = 2.0 * u - prev[c, i] + STEP * rate
             change = updated - u
@@ -255,10 +272,10 @@
             new[c, i] = updated
         return total + dm * inner
 
-    return lax.fori_loop(0, x, row, jnp.zeros((y, z), jnp.float32))
-
-
-def step_kernel(s, step, flags, *refs):
+    return lax.fori_loop(0, x, row, jnp.zeros((y, z), jnp.float32), unroll=4)
+
+
+def step_kernel(s, step, cells, flags, *refs):
     refs = list(refs)
 
     def take(n):
@@ -307,7 +324,7 @@
     def fine_ghosts(i):
         half = i // 2
         near_x = jnp.where(i % 2 == 0, 0.75, 0.25)
-        off_x, off_y = offs[0, i], offs[1, i]
+        off_x, off_y = offs[i] // 4 - 1, offs[i] % 4 - 1
         total = jnp.zeros((s.fy, LANES), jnp.float32)
         weights = []
         for shift in (-1, 0, 1, 2):
@@ -328,8 +345,7 @@
     def coarse_ghosts(i):
         def top(c):
             both = pairs[c, i, pl.ds(0, s.cy, stride=2), :] + pairs[c, i, pl.ds(1, s.cy, stride=2), :]
-            column = pltpu.roll(0.25 * both, 1, 1)
-            return jnp.concatenate([column] * s.halves, axis=1)
+            return 0.25 * both[:, LANES - 1 :]
 
         return top, lambda c: jnp.zeros((s.cy, s.cz), jnp.float32)
 
@@ -339,24 +355,28 @@
     )
     place = lax.broadcasted_iota(jnp.int32, (8, LANES), 0)
     before = jnp.zeros((8, LANES), jnp.float32) if first else energy_in[...]
-    before = jnp.where(place == 2 * step, jnp.sum(sum_f), before)
-    energy[...] = jnp.where(place == 2 * step + 1, jnp.sum(sum_c), before)
+    before = jnp.where(place == step, jnp.sum(sum_f) / cells[0], before)
+    energy[...] = jnp.where(place == STEPS + step, jnp.sum(sum_c) / cells[1], before)
     if not final:
-        put_x(s, flags, x_out, new_f, new_c, None)
+        put_x(s, flags, x_out, new_f, new_c)
 
 
 VMEM = pl.BlockSpec(memory_space=pltpu.VMEM)
 SMEM = pl.BlockSpec(memory_space=pltpu.SMEM)
-
-
-def call(kernel, shapes, flops, *args, scratch=(), name=None, table=True):
+HBM = pl.BlockSpec(memory_space=pltpu.HBM)
+
+
+def call(kernel, shapes, flops, *args, scratch=(), name=None, specs=None, sems=0):
     shapes = [jax.ShapeDtypeStruct(shape, jnp.float32) for shape in shapes]
+    scratch = [pltpu.VMEM(shape, jnp.float32) for shape in scratch]
+    if sems:
+        scratch.append(pltpu.SemaphoreType.DMA((sems,)))
     return pl.pallas_call(
         kernel,
         out_shape=shapes,
-        in_specs=([SMEM] if table else []) + [VMEM] * (len(args) - table),
+        in_specs=specs or [SMEM] + [VMEM] * (len(args) - 1),
         out_specs=[VMEM] * len(shapes),
-        scratch_shapes=[pltpu.VMEM(shape, jnp.float32) for shape in scratch],
+        scratch_shapes=scratch,
         compiler_params=pltpu.CompilerParams(vmem_limit_bytes=VMEM_LIMIT),
         cost_estimate=pl.CostEstimate(flops=flops, bytes_accessed=1 << 20, transcendentals=0),
         name=name,
@@ -457,20 +477,35 @@
 
     def swap_both(pair, axes):
         second = swap(pair[1], axes, across)
-        return swap(pair[0], axes, beside), second
-
-    offs = jnp.broadcast_to(offsets[..., None], offsets.shape + (LANES,))
+        first = swap(pair[0], axes, beside)
+        return [pltpu.with_memory_space_constraint(x, pltpu.VMEM) for x in (first, second)]
+
+    offs = offsets[0] * 4 + offsets[1] + 5
+    offs = jnp.broadcast_to(offs[..., None], offs.shape + (LANES,))
     x_out = call(
         functools.partial(first_kernel, s),
         [(s.x_rows_mats, LANES)] * 2,
         1000,
         flags,
-        fine_disp,
-        coarse_disp,
-        fine_rigidity,
-        fine_metric,
-        coarse_rigidity,
-        coarse_metric,
+        *(
+            pltpu.with_memory_space_constraint(x, pltpu.HBM)
+            for x in (
+                fine_disp,
+                coarse_disp,
+                fine_rigidity,
+                fine_metric,
+                coarse_rigidity,
+                coarse_metric,
+            )
+        ),
+        scratch=[
+            (2, 3, 2, s.fy, s.fz),
+            (2, 3, 2, s.cy, s.cz),
+            (2, 2, s.fy, s.fz),
+            (2, 2, s.cy, s.cz),
+        ],
+        specs=[SMEM] + [HBM] * 6,
+        sems=12,
         name="first_strips",
     )
     own = []
@@ -481,30 +516,31 @@
         own.append(
             call(
                 own_kernel,
-                [metric.shape] * 6,
+                [metric.shape] * 5 + [metric.shape[:2] + (LANES,)],
                 2_000_000,
                 density,
                 lame,
                 rigidity,
                 metric,
                 name=f"own_{tag}",
-                table=False,
+                specs=[VMEM] * 4,
             )
         )
     inverse_f, *coef_f = own[0]
     inverse_c, *coef_c = own[1]
 
     fine, coarse = fine_disp, coarse_disp
-    fine_ext = (s.fx + 2, s.fy + 16, s.fz)
-    coarse_ext = (s.cx + 2, s.cy + 16, s.cz)
+    fine_ext = (s.fx + 2, s.fy + 2, s.fz)
+    coarse_ext = (s.cx + 2, s.cy + 2, s.cz)
     scratch = [
         (3, s.fe, s.fy + 16, s.fz),
         (3, s.ce, s.cy + 16, s.cz),
-        fine_ext,
-        coarse_ext,
+        (s.fx + 2, s.fy + 16, s.fz),
+        (s.cx + 2, s.cy + 16, s.cz),
         (s.ce, 2 * (s.cy + 4), LANES),
         (3, s.cx, s.fy, LANES),
     ]
+    cells = [count_x * count_y * s.fx * s.fy * s.fz, count_x * count_y * s.cx * s.cy * s.cz]
     energy = None
     for step in range(STEPS):
         first, final = step == 0, step == STEPS - 1
@@ -532,7 +568,7 @@
         if first:
             shapes += [fine_ext, fine_ext, coarse_ext, coarse_ext]
         outs = call(
-            functools.partial(step_kernel, s, step),
+            functools.partial(step_kernel, s, step, cells),
             shapes,
             4_000_000,
             flags,
@@ -556,8 +592,7 @@
         if first:
             ext_mats = outs[5:9]
     total = total_over_mesh(energy, swap)
-    cells = [count_x * count_y * s.fx * s.fy * s.fz, count_x * count_y * s.cx * s.cy * s.cz]
-    energy = total[: 2 * STEPS, 0].reshape(STEPS, 2) / jnp.array(cells, jnp.float32)
+    energy = total[: 2 * STEPS, 0].reshape(2, STEPS).T
     return fine, coarse, energy
 
 

time: 110 us -> 93.4 us (0.85)
  Pallas kernels: 22.9 us -> 14.5 us
  local copies, waits for them, and re-layouts: 8.71 us -> 0.98 us
    pallas_call x9, Pallas kernels: 22.9 us -> 14.5 us  [call(): pl.pallas_call(kernel, out_shape=shapes, in_specs=specs or [SMEM] + [VMEM...]
    unnamed x47 -> x26, local copies, waits for them, and re-layouts: 8.33 us -> 0.07 us
where the time goes in v2:
time: 93.4 us; the launch traced here: 93.2 us
  waiting for transfers between devices  43 us (46%)
  starting transfers between devices  33.4 us (36%)
  Pallas kernels  14.5 us (16%)
  local copies, waits for them, and re-layouts  0.98 us (1%)
    ppermute x20, waiting for transfers between devices, swap(): return lax.ppermute(value, ALL, device_pairs(mesh, axes, move))  43 us
    ppermute x20, starting transfers between devices, swap(): return lax.ppermute(value, ALL, device_pairs(mesh, axes, move))  33.4 us
    pallas_call x9, Pallas kernels, call(): pl.pallas_call(kernel, out_shape=shapes, in_specs=specs or [SMEM] + [VMEM...  14.5 us
  transfers between devices with their start and end apart: 20, of which 17 were waited for; matrix products, arithmetic and copies ran while one was open for 0% of the time, Pallas kernels for 0%

profile of v2, /device:TPU:6, one launch (start us, length us, event | category | flops | bytes accessed | tf_op | source)
XLA Modules:
  0.0 93.2 jit_solution(914181278669533396)
XLA Ops:
  3.4 2.5 %collective-permute-start.1 = (f32[256,128]{1,0:T(8,128)S(1)}, f32[256,128]{1,0:T(8,128)S(1)}, u32[]{:S(2)}, u32[]{:S(2)}) collective-permute-start(f32[256,128]{1,0:T(8,128)S(1)} %get-tuple-element.53), channel_id=1, source_target_pairs={{0,248},{1,249},{2,250},{3,251},{4,252},{5,253},{6,254},{7,255},{8... | collective-permute-start | bytes 393224 | tf_op jit(solution)/shard_map/ppermute | solution.py:476
  7.8 2.7 %collective-permute-done.1.refs_7_.refs_22_ = f32[256,128]{1,0:T(8,128)S(1)} collective-permute-done((f32[256,128]{1,0:T(8,128)S(1)}, f32[256,128]{1,0:T(8,128)S(1)}, u32[]{:S(2)}, u32[]{:S(2)}) %collective-permute-start.1) | collective-permute-done | bytes 131104 | tf_op jit(solution)/shard_map/ppermute | solution.py:476
  11.3 3.1 %collective-permute-start.3 = (f32[164,2,128]{2,1,0:T(2,128)S(1)}, f32[164,2,128]{2,1,0:T(2,128)S(1)}, u32[]{:S(2)}, u32[]{:S(2)}) collective-permute-start(f32[164,2,128]{2,1,0:T(2,128)S(1)} %get-tuple-element.55), channel_id=1, source_target_pairs={{0,7},{1,2},{2,1},{3,4},{4,3},{5,6},{6,5},{7,0},{8,15},{9,10},{10,... | collective-permute-start | bytes 503816 | tf_op jit(solution)/shard_map/ppermute | solution.py:476
  14.4 3.0 %collective-permute-done.3.refs_24_ = f32[164,2,128]{2,1,0:T(2,128)S(1)} collective-permute-done((f32[164,2,128]{2,1,0:T(2,128)S(1)}, f32[164,2,128]{2,1,0:T(2,128)S(1)}, u32[]{:S(2)}, u32[]{:S(2)}) %collective-permute-start.3) | collective-permute-done | bytes 167968 | tf_op jit(solution)/shard_map/ppermute | solution.py:476
  17.6 3.2 %step_0.1 = (f32[3,16,16,128]{3,2,1,0:T(8,128)S(1)}, f32[3,8,8,256]{3,2,1,0:T(8,128)S(1)}, f32[8,128]{1,0:T(8,128)S(1)}, f32[192,128]{1,0:T(8,128)S(1)}, f32[192...) custom-call(s32[6]{0:T(128)S(1)} %stack.36.flags, ...), custom_call_target="tpu_custom_call" | custom-call | flops 4000000 | bytes 1048576 | tf_op jit(solution)/shard_map/step_0/pallas_call | solution.py:374
  20.9 2.6 %collective-permute-start.5 = (f32[192,128]{1,0:T(8,128)S(1)}, f32[192,128]{1,0:T(8,128)S(1)}, u32[]{:S(2)}, u32[]{:S(2)}) collective-permute-start(f32[192,128]{1,0:T(8,128)S(1)} %get-tuple-element.64), channel_id=1, source_target_pairs={{0,248},{1,249},{2,250},{3,251},{4,252},{5,253},{6,254},{7,255},{8... | collective-permute-start | bytes 294920 | tf_op jit(solution)/shard_map/ppermute | solution.py:476
  23.5 2.0 %collective-permute-done.4.refs_2_.refs_20_ = f32[192,128]{1,0:T(8,128)S(1)} collective-permute-done((f32[192,128]{1,0:T(8,128)S(1)}, f32[192,128]{1,0:T(8,128)S(1)}, u32[]{:S(2)}, u32[]{:S(2)}) %collective-permute-start.4) | collective-permute-done | bytes 98336 | tf_op jit(solution)/shard_map/ppermute | solution.py:476
  25.5 2.2 %collective-permute-done.5.refs_3_.refs_21_ = f32[192,128]{1,0:T(8,128)S(1)} collective-permute-done((f32[192,128]{1,0:T(8,128)S(1)}, f32[192,128]{1,0:T(8,128)S(1)}, u32[]{:S(2)}, u32[]{:S(2)}) %collective-permute-start.5) | collective-permute-done | bytes 98336 | tf_op jit(solution)/shard_map/ppermute | solution.py:476
  28.5 2.3 %collective-permute-start.7 = (f32[132,2,128]{2,1,0:T(2,128)S(1)}, f32[132,2,128]{2,1,0:T(2,128)S(1)}, u32[]{:S(2)}, u32[]{:S(2)}) collective-permute-start(f32[132,2,128]{2,1,0:T(2,128)S(1)} %get-tuple-element.66), channel_id=1, source_target_pairs={{0,7},{1,2},{2,1},{3,4},{4,3},{5,6},{6,5},{7,0},{8,15},{9,10},{10,... | collective-permute-start | bytes 405512 | tf_op jit(solution)/shard_map/ppermute | solution.py:476
  30.8 3.4 %collective-permute-done.7.refs_23_ = f32[132,2,128]{2,1,0:T(2,128)S(1)} collective-permute-done((f32[132,2,128]{2,1,0:T(2,128)S(1)}, f32[132,2,128]{2,1,0:T(2,128)S(1)}, u32[]{:S(2)}, u32[]{:S(2)}) %collective-permute-start.7) | collective-permute-done | bytes 135200 | tf_op jit(solution)/shard_map/ppermute | solution.py:476
  34.2 3.1 %step_1.1 = (f32[3,16,16,128]{3,2,1,0:T(8,128)S(1)}, f32[3,8,8,256]{3,2,1,0:T(8,128)S(1)}, f32[8,128]{1,0:T(8,128)S(1)}, f32[192,128]{1,0:T(8,128)S(1)}, f32[192,128]{1,0:T(8,128)S(1)}) custom-call(s32[6]{0:T(128)S(1)} %stack.36.flags, f32[3,16,16,128]{3,2,1,0:T(8,128)S(1)} %get-tuple-element.56.refs_0_.refs_2_, ...), custom_call_target="tpu_custom_call" | custom-call | flops 4000000 | bytes 1048576 | tf_op jit(solution)/shard_map/step_1/pallas_call | solution.py:374
  40.0 2.0 %collective-permute-done.8.refs_2_.refs_20_ = f32[192,128]{1,0:T(8,128)S(1)} collective-permute-done((f32[192,128]{1,0:T(8,128)S(1)}, f32[192,128]{1,0:T(8,128)S(1)}, u32[]{:S(2)}, u32[]{:S(2)}) %collective-permute-start.8) | collective-permute-done | bytes 98336 | tf_op jit(solution)/shard_map/ppermute | solution.py:476
  42.0 4.0 %collective-permute-done.9.refs_3_.refs_21_ = f32[192,128]{1,0:T(8,128)S(1)} collective-permute-done((f32[192,128]{1,0:T(8,128)S(1)}, f32[192,128]{1,0:T(8,128)S(1)}, u32[]{:S(2)}, u32[]{:S(2)}) %collective-permute-start.9) | collective-permute-done | bytes 98336 | tf_op jit(solution)/shard_map/ppermute | solution.py:476
  47.3 2.4 %collective-permute-start.11 = (f32[132,2,128]{2,1,0:T(2,128)}, f32[132,2,128]{2,1,0:T(2,128)S(1)}, u32[]{:S(2)}, u32[]{:S(2)}) collective-permute-start(f32[132,2,128]{2,1,0:T(2,128)} %get-tuple-element.73), channel_id=1, source_target_pairs={{0,7},{1,2},{2,1},{3,4},{4,3},{5,6},{6,5},{7,0},{8,15},{9,10},{10,... | collective-permute-start | bytes 405512 | tf_op jit(solution)/shard_map/ppermute | solution.py:476
  49.7 3.5 %collective-permute-done.11.refs_23_ = f32[132,2,128]{2,1,0:T(2,128)S(1)} collective-permute-done((f32[132,2,128]{2,1,0:T(2,128)}, f32[132,2,128]{2,1,0:T(2,128)S(1)}, u32[]{:S(2)}, u32[]{:S(2)}) %collective-permute-start.11) | collective-permute-done | bytes 135200 | tf_op jit(solution)/shard_map/ppermute | solution.py:476
  53.2 3.7 %step_2.1 = (f32[3,16,16,128]{3,2,1,0:T(8,128)}, f32[3,8,8,256]{3,2,1,0:T(8,128)}, f32[8,128]{1,0:T(8,128)S(1)}) custom-call(s32[6]{0:T(128)S(1)} %stack.36.flags, f32[3,16,16,128]{3,2,1,0:T(8,128)S(1)} %get-tuple-element.67.refs_0_, f32[3,8,8,256]{3,2,1,0:T(8,128)S(1)} %get-tuple-element.68.refs_1_, ...), custom_call_target="tpu_custom_call" | custom-call | flops 4000000 | bytes 1048576 | tf_op jit(solution)/shard_map/step_2/pallas_call | solution.py:374
  58.0 2.4 %collective-permute-start.13 = (f32[8,128]{1,0:T(8,128)S(1)}, f32[8,128]{1,0:T(8,128)S(1)}, u32[]{:S(2)}, u32[]{:S(2)}) collective-permute-start(f32[8,128]{1,0:T(8,128)S(1)} %add_select_fusion.1), channel_id=1, source_target_pairs={{0,7},{1,2},{2,1},{3,4},{4,3},{5,6},{6,5},{7,0},{8,15},{9,10},{10,... | collective-permute-start | bytes 12296 | tf_op jit(solution)/shard_map/ppermute | solution.py:476
  62.3 3.0 %collective-permute-done.14 = f32[8,128]{1,0:T(8,128)S(1)} collective-permute-done((f32[8,128]{1,0:T(8,128)S(1)}, f32[8,128]{1,0:T(8,128)S(1)}, u32[]{:S(2)}, u32[]{:S(2)}) %collective-permute-start.14) | collective-permute-done | bytes 4128 | tf_op jit(solution)/shard_map/ppermute | solution.py:476
  66.9 2.3 %collective-permute-done.15 = f32[8,128]{1,0:T(8,128)S(1)} collective-permute-done((f32[8,128]{1,0:T(8,128)S(1)}, f32[8,128]{1,0:T(8,128)S(1)}, u32[]{:S(2)}, u32[]{:S(2)}) %collective-permute-start.15) | collective-permute-done | bytes 4128 | tf_op jit(solution)/shard_map/ppermute | solution.py:476
  69.2 5.3 %collective-permute-start.16 = (f32[8,128]{1,0:T(8,128)S(1)}, f32[8,128]{1,0:T(8,128)S(1)}, u32[]{:S(2)}, u32[]{:S(2)}) collective-permute-start(f32[8,128]{1,0:T(8,128)S(1)} %broadcast_add_fusion), channel_id=1, source_target_pairs={{0,24},{1,25},{2,26},{3,27},{4,28},{5,29},{6,30},{7,31},{8,16},{9,... | collective-permute-start | bytes 12296 | tf_op jit(solution)/shard_map/ppermute | solution.py:476
  76.2 3.6 %collective-permute-done.17 = f32[8,128]{1,0:T(8,128)S(1)} collective-permute-done((f32[8,128]{1,0:T(8,128)S(1)}, f32[8,128]{1,0:T(8,128)S(1)}, u32[]{:S(2)}, u32[]{:S(2)}) %collective-permute-start.17) | collective-permute-done | bytes 4128 | tf_op jit(solution)/shard_map/ppermute | solution.py:476
  79.8 5.6 %collective-permute-start.18 = (f32[8,128]{1,0:T(8,128)S(1)}, f32[8,128]{1,0:T(8,128)S(1)}, u32[]{:S(2)}, u32[]{:S(2)}) collective-permute-start(f32[8,128]{1,0:T(8,128)S(1)} %add_select_fusion), channel_id=1, source_target_pairs={{0,224},{1,225},{2,226},{3,227},{4,228},{5,229},{6,230},{7,231},{8... | collective-permute-start | bytes 12296 | tf_op jit(solution)/shard_map/ppermute | solution.py:476
  87.0 2.0 %collective-permute-start.19 = (f32[8,128]{1,0:T(8,128)S(1)}, f32[8,128]{1,0:T(8,128)S(1)}, u32[]{:S(2)}, u32[]{:S(2)}) collective-permute-start(f32[8,128]{1,0:T(8,128)S(1)} %add.75), channel_id=1, source_target_pairs={{0,96},{1,97},{2,98},{3,99},{4,100},{5,101},{6,102},{7,103},{8,104... | collective-permute-start | bytes 12296 | tf_op jit(solution)/shard_map/ppermute | solution.py:476
  89.0 3.4 %collective-permute-done.19 = f32[8,128]{1,0:T(8,128)S(1)} collective-permute-done((f32[8,128]{1,0:T(8,128)S(1)}, f32[8,128]{1,0:T(8,128)S(1)}, u32[]{:S(2)}, u32[]{:S(2)}) %collective-permute-start.19) | collective-permute-done | bytes 4128 | tf_op jit(solution)/shard_map/ppermute | solution.py:476
  (69 shorter events, 18.9 us)
Async XLA Ops:
  2.5 5.3 %collective-permute-start = (f32[256,128]{1,0:T(8,128)S(1)}, f32[256,128]{1,0:T(8,128)S(1)}, u32[]{:S(2)}, u32[]{:S(2)}) collective-permute-start(f32[256,128]{1,0:T(8,128)S(1)} %get-tuple-element.52), channel_id=1, source_target_pairs={{0,8},{1,9},{2,10},{3,11},{4,12},{5,13},{6,14},{7,15},{8,0},{9,1},... | collective-permute-start | bytes 393224 | tf_op jit(solution)/shard_map/ppermute | solution.py:476
  3.4 7.1 %copy-start = (f32[3,16,16,128]{3,2,1,0:T(8,128)S(1)}, f32[3,16,16,128]{3,2,1,0:T(8,128)}, u32[]{:S(2)}) copy-start(f32[3,16,16,128]{3,2,1,0:T(8,128)} %refs_2_.5) | copy-start | bytes 1179652
  3.4 7.1 %collective-permute-start.1 = (f32[256,128]{1,0:T(8,128)S(1)}, f32[256,128]{1,0:T(8,128)S(1)}, u32[]{:S(2)}, u32[]{:S(2)}) collective-permute-start(f32[256,128]{1,0:T(8,128)S(1)} %get-tuple-element.53), channel_id=1, source_target_pairs={{0,248},{1,249},{2,250},{3,251},{4,252},{5,253},{6,254},{7,255},{8... | collective-permute-start | bytes 393224 | tf_op jit(solution)/shard_map/ppermute | solution.py:476
  6.2 8.2 %copy-start.12 = (s32[2,16,16]{2,1,0:T(8,128)S(1)}, s32[2,16,16]{2,1,0:T(8,128)}, u32[]{:S(2)}) copy-start(s32[2,16,16]{2,1,0:T(8,128)} %param.25) | copy-start | bytes 6148
  10.5 7.1 %copy-start.6 = (f32[3,16,16,128]{3,2,1,0:T(8,128)S(1)}, f32[3,16,16,128]{3,2,1,0:T(8,128)}, u32[]{:S(2)}) copy-start(f32[3,16,16,128]{3,2,1,0:T(8,128)} %refs_2_.4) | copy-start | bytes 1179652
  10.5 7.1 %copy-start.7 = (f32[3,8,8,256]{3,2,1,0:T(8,128)S(1)}, f32[3,8,8,256]{3,2,1,0:T(8,128)}, u32[]{:S(2)}) copy-start(f32[3,8,8,256]{3,2,1,0:T(8,128)} %refs_3_.4) | copy-start | bytes 589828
  11.2 3.2 %collective-permute-start.2 = (f32[164,2,128]{2,1,0:T(2,128)S(1)}, f32[164,2,128]{2,1,0:T(2,128)S(1)}, u32[]{:S(2)}, u32[]{:S(2)}) collective-permute-start(f32[164,2,128]{2,1,0:T(2,128)S(1)} %get-tuple-element.54), channel_id=1, source_target_pairs={{0,1},{1,0},{2,3},{3,2},{4,5},{5,4},{6,7},{7,6},{8,9},{9,8},{10,11... | collective-permute-start | bytes 503816 | tf_op jit(solution)/shard_map/ppermute | solution.py:476
  11.3 6.2 %collective-permute-start.3 = (f32[164,2,128]{2,1,0:T(2,128)S(1)}, f32[164,2,128]{2,1,0:T(2,128)S(1)}, u32[]{:S(2)}, u32[]{:S(2)}) collective-permute-start(f32[164,2,128]{2,1,0:T(2,128)S(1)} %get-tuple-element.55), channel_id=1, source_target_pairs={{0,7},{1,2},{2,1},{3,4},{4,3},{5,6},{6,5},{7,0},{8,15},{9,10},{10,... | collective-permute-start | bytes 503816 | tf_op jit(solution)/shard_map/ppermute | solution.py:476
  20.8 4.7 %collective-permute-start.4 = (f32[192,128]{1,0:T(8,128)S(1)}, f32[192,128]{1,0:T(8,128)S(1)}, u32[]{:S(2)}, u32[]{:S(2)}) collective-permute-start(f32[192,128]{1,0:T(8,128)S(1)} %get-tuple-element.63), channel_id=1, source_target_pairs={{0,8},{1,9},{2,10},{3,11},{4,12},{5,13},{6,14},{7,15},{8,0},{9,1},... | collective-permute-start | bytes 294920 | tf_op jit(solution)/shard_map/ppermute | solution.py:476
  20.9 6.8 %collective-permute-start.5 = (f32[192,128]{1,0:T(8,128)S(1)}, f32[192,128]{1,0:T(8,128)S(1)}, u32[]{:S(2)}, u32[]{:S(2)}) collective-permute-start(f32[192,128]{1,0:T(8,128)S(1)} %get-tuple-element.64), channel_id=1, source_target_pairs={{0,248},{1,249},{2,250},{3,251},{4,252},{5,253},{6,254},{7,255},{8... | collective-permute-start | bytes 294920 | tf_op jit(solution)/shard_map/ppermute | solution.py:476
  28.4 2.4 %collective-permute-start.6 = (f32[132,2,128]{2,1,0:T(2,128)S(1)}, f32[132,2,128]{2,1,0:T(2,128)S(1)}, u32[]{:S(2)}, u32[]{:S(2)}) collective-permute-start(f32[132,2,128]{2,1,0:T(2,128)S(1)} %get-tuple-element.65), channel_id=1, source_target_pairs={{0,1},{1,0},{2,3},{3,2},{4,5},{5,4},{6,7},{7,6},{8,9},{9,8},{10,11... | collective-permute-start | bytes 405512 | tf_op jit(solution)/shard_map/ppermute | solution.py:476
  28.5 5.7 %collective-permute-start.7 = (f32[132,2,128]{2,1,0:T(2,128)S(1)}, f32[132,2,128]{2,1,0:T(2,128)S(1)}, u32[]{:S(2)}, u32[]{:S(2)}) collective-permute-start(f32[132,2,128]{2,1,0:T(2,128)S(1)} %get-tuple-element.66), channel_id=1, source_target_pairs={{0,7},{1,2},{2,1},{3,4},{4,3},{5,6},{6,5},{7,0},{8,15},{9,10},{10,... | collective-permute-start | bytes 405512 | tf_op jit(solution)/shard_map/ppermute | solution.py:476
  37.3 4.7 %collective-permute-start.8 = (f32[192,128]{1,0:T(8,128)S(1)}, f32[192,128]{1,0:T(8,128)S(1)}, u32[]{:S(2)}, u32[]{:S(2)}) collective-permute-start(f32[192,128]{1,0:T(8,128)S(1)} %get-tuple-element.70), channel_id=1, source_target_pairs={{0,8},{1,9},{2,10},{3,11},{4,12},{5,13},{6,14},{7,15},{8,0},{9,1},... | collective-permute-start | bytes 294920 | tf_op jit(solution)/shard_map/ppermute | solution.py:476
  39.2 6.7 %collective-permute-start.9 = (f32[192,128]{1,0:T(8,128)S(1)}, f32[192,128]{1,0:T(8,128)S(1)}, u32[]{:S(2)}, u32[]{:S(2)}) collective-permute-start(f32[192,128]{1,0:T(8,128)S(1)} %get-tuple-element.71), channel_id=1, source_target_pairs={{0,248},{1,249},{2,250},{3,251},{4,252},{5,253},{6,254},{7,255},{8... | collective-permute-start | bytes 294920 | tf_op jit(solution)/shard_map/ppermute | solution.py:476
  47.3 2.4 %collective-permute-start.10 = (f32[132,2,128]{2,1,0:T(2,128)}, f32[132,2,128]{2,1,0:T(2,128)S(1)}, u32[]{:S(2)}, u32[]{:S(2)}) collective-permute-start(f32[132,2,128]{2,1,0:T(2,128)} %get-tuple-element.72), channel_id=1, source_target_pairs={{0,1},{1,0},{2,3},{3,2},{4,5},{5,4},{6,7},{7,6},{8,9},{9,8},{10,11... | collective-permute-start | bytes 405512 | tf_op jit(solution)/shard_map/ppermute | solution.py:476
  47.3 5.9 %collective-permute-start.11 = (f32[132,2,128]{2,1,0:T(2,128)}, f32[132,2,128]{2,1,0:T(2,128)S(1)}, u32[]{:S(2)}, u32[]{:S(2)}) collective-permute-start(f32[132,2,128]{2,1,0:T(2,128)} %get-tuple-element.73), channel_id=1, source_target_pairs={{0,7},{1,2},{2,1},{3,4},{4,3},{5,6},{6,5},{7,0},{8,15},{9,10},{10,... | collective-permute-start | bytes 405512 | tf_op jit(solution)/shard_map/ppermute | solution.py:476
  56.9 1.2 %collective-permute-start.12 = (f32[8,128]{1,0:T(8,128)S(1)}, f32[8,128]{1,0:T(8,128)S(1)}, u32[]{:S(2)}, u32[]{:S(2)}) collective-permute-start(f32[8,128]{1,0:T(8,128)S(1)} %get-tuple-element.76), channel_id=1, source_target_pairs={{0,1},{1,0},{2,3},{3,2},{4,5},{5,4},{6,7},{7,6},{8,9},{9,8},{10,11... | collective-permute-start | bytes 12296 | tf_op jit(solution)/shard_map/ppermute | solution.py:476
  58.0 4.2 %collective-permute-start.13 = (f32[8,128]{1,0:T(8,128)S(1)}, f32[8,128]{1,0:T(8,128)S(1)}, u32[]{:S(2)}, u32[]{:S(2)}) collective-permute-start(f32[8,128]{1,0:T(8,128)S(1)} %add_select_fusion.1), channel_id=1, source_target_pairs={{0,7},{1,2},{2,1},{3,4},{4,3},{5,6},{6,5},{7,0},{8,15},{9,10},{10,... | collective-permute-start | bytes 12296 | tf_op jit(solution)/shard_map/ppermute | solution.py:476
  62.3 3.0 %collective-permute-start.14 = (f32[8,128]{1,0:T(8,128)S(1)}, f32[8,128]{1,0:T(8,128)S(1)}, u32[]{:S(2)}, u32[]{:S(2)}) collective-permute-start(f32[8,128]{1,0:T(8,128)S(1)} %add.70), channel_id=1, source_target_pairs={{0,3},{1,6},{2,5},{3,0},{4,7},{5,2},{6,1},{7,4},{8,11},{9,14},{10,... | collective-permute-start | bytes 12296 | tf_op jit(solution)/shard_map/ppermute | solution.py:476
  65.5 3.6 %collective-permute-start.15 = (f32[8,128]{1,0:T(8,128)S(1)}, f32[8,128]{1,0:T(8,128)S(1)}, u32[]{:S(2)}, u32[]{:S(2)}) collective-permute-start(f32[8,128]{1,0:T(8,128)S(1)} %broadcast_in_dim.13), channel_id=1, source_target_pairs={{0,8},{1,9},{2,10},{3,11},{4,12},{5,13},{6,14},{7,15},{8,0},{9,1},... | collective-permute-start | bytes 12296 | tf_op jit(solution)/shard_map/ppermute | solution.py:476
  69.2 6.9 %collective-permute-start.16 = (f32[8,128]{1,0:T(8,128)S(1)}, f32[8,128]{1,0:T(8,128)S(1)}, u32[]{:S(2)}, u32[]{:S(2)}) collective-permute-start(f32[8,128]{1,0:T(8,128)S(1)} %broadcast_add_fusion), channel_id=1, source_target_pairs={{0,24},{1,25},{2,26},{3,27},{4,28},{5,29},{6,30},{7,31},{8,16},{9,... | collective-permute-start | bytes 12296 | tf_op jit(solution)/shard_map/ppermute | solution.py:476
  76.2 3.6 %collective-permute-start.17 = (f32[8,128]{1,0:T(8,128)S(1)}, f32[8,128]{1,0:T(8,128)S(1)}, u32[]{:S(2)}, u32[]{:S(2)}) collective-permute-start(f32[8,128]{1,0:T(8,128)S(1)} %fusion), channel_id=1, source_target_pairs={{0,32},{1,33},{2,34},{3,35},{4,36},{5,37},{6,38},{7,39},{8,40},{9,... | collective-permute-start | bytes 12296 | tf_op jit(solution)/shard_map/ppermute | solution.py:476
  79.8 7.2 %collective-permute-start.18 = (f32[8,128]{1,0:T(8,128)S(1)}, f32[8,128]{1,0:T(8,128)S(1)}, u32[]{:S(2)}, u32[]{:S(2)}) collective-permute-start(f32[8,128]{1,0:T(8,128)S(1)} %add_select_fusion), channel_id=1, source_target_pairs={{0,224},{1,225},{2,226},{3,227},{4,228},{5,229},{6,230},{7,231},{8... | collective-permute-start | bytes 12296 | tf_op jit(solution)/shard_map/ppermute | solution.py:476
  87.0 5.4 %collective-permute-start.19 = (f32[8,128]{1,0:T(8,128)S(1)}, f32[8,128]{1,0:T(8,128)S(1)}, u32[]{:S(2)}, u32[]{:S(2)}) collective-permute-start(f32[8,128]{1,0:T(8,128)S(1)} %add.75), channel_id=1, source_target_pairs={{0,96},{1,97},{2,98},{3,99},{4,100},{5,101},{6,102},{7,103},{8,104... | collective-permute-start | bytes 12296 | tf_op jit(solution)/shard_map/ppermute | solution.py:476
  (9 other events, 43.1 us)

commit v3 on v2

--- a/solution.py
+++ b/solution.py
@@ -1,4 +1,5 @@
 import functools
+import math
 
 import jax
 import jax.numpy as jnp
@@ -383,62 +384,52 @@
     )(*args)
 
 
-def across(i, n):
-    return (i + 1) % n if i % 2 else (i - 1) % n
-
-
-def opposite(i, n):
-    return (i - 3) % n if i % 2 else (i + 3) % n
-
-
-def device_pairs(mesh, axes, move):
-    sizes = dict(mesh.shape)
-    names = list(sizes)
-    total = 1
-    for name in names:
-        total *= sizes[name]
-    count = 1
-    for name in axes:
-        count *= sizes[name]
+def swap_pairs(mesh, move):
+    sizes = list(mesh.shape.values())
     pairs = []
-    for source in range(total):
-        rest, at = source, {}
-        for name in reversed(names):
-            at[name] = rest % sizes[name]
-            rest //= sizes[name]
-        index = 0
-        for name in axes:
-            index = index * sizes[name] + at[name]
-        index = move(index, count)
-        for name in reversed(axes):
-            at[name] = index % sizes[name]
-            index //= sizes[name]
+    for source in range(math.prod(sizes)):
+        rest, at = source, []
+        for size in reversed(sizes):
+            at.insert(0, rest % size)
+            rest //= size
         target = 0
-        for name in names:
-            target = target * sizes[name] + at[name]
+        for index, size in zip(move(*at), sizes, strict=True):
+            target = target * size + index
         pairs.append((source, target))
     return pairs
 
 
-def beside(i, n):
-    return i ^ 1
-
-
-def total_over_mesh(value, swap):
-    lane = lax.broadcasted_iota(jnp.int32, (8, LANES), 1)
-
-    def ring_of_eight(value, axes):
-        value = value + swap(value, axes, beside)
-        pair = lax.axis_index(axes) // 2
-        slots = jnp.where(lane == pair, value, 0.0)
-        slots = slots + swap(slots, axes, across)
-        slots = slots + swap(slots, axes, opposite)
-        return jnp.broadcast_to(jnp.sum(slots[:, 0:4], axis=1, keepdims=True), (8, LANES))
-
-    value = ring_of_eight(value, GY)
-    value = value + swap(value, ("gx_1",), beside)
-    value = value + swap(value, ("gx_1",), across)
-    return ring_of_eight(value, ("gx_0",))
+def beside_x(z, x, y, core):
+    return z, x ^ 1, y, core
+
+
+def across_x(z, x, y, core):
+    place = 4 * z + x
+    if place in (0, 31):
+        return z, x, y, core ^ 1
+    place += 1 if place % 2 else -1
+    return place // 4, place % 4, y, core
+
+
+def beside_y(z, x, y, core):
+    return z, x, y, core ^ 1
+
+
+def across_y(z, x, y, core):
+    place = (2 * y + core + (1 if core else -1)) % 8
+    return z, x, place // 2, place % 2
+
+
+TOTAL = (
+    lambda z, x, y, core: (z, x, y, core ^ 1),
+    lambda z, x, y, core: (z, x, y ^ 1, core ^ 1),
+    lambda z, x, y, core: (z, x, y ^ 3, core ^ 1),
+    lambda z, x, y, core: (z, x ^ 1, y, core ^ 1),
+    lambda z, x, y, core: (z, x ^ 3, y, core ^ 1),
+    lambda z, x, y, core: (z ^ 1, x, y, core ^ 1),
+    lambda z, x, y, core: (z ^ 2, x, y, core ^ 1),
+    lambda z, x, y, core: (z ^ 7, x, y, core ^ 1),
+)
 
 
 def per_device(
@@ -472,12 +463,12 @@
         ]
     )
 
-    def swap(value, axes, move):
-        return lax.ppermute(value, ALL, device_pairs(mesh, axes, move))
-
-    def swap_both(pair, axes):
-        second = swap(pair[1], axes, across)
-        first = swap(pair[0], axes, beside)
+    def swap(value, move):
+        return lax.ppermute(value, ALL, swap_pairs(mesh, move))
+
+    def swap_both(pair, beside, across):
+        second = swap(pair[1], across)
+        first = swap(pair[0], beside)
         return [pltpu.with_memory_space_constraint(x, pltpu.VMEM) for x in (first, second)]
 
     offs = offsets[0] * 4 + offsets[1] + 5
@@ -545,7 +536,7 @@
     for step in range(STEPS):
         first, final = step == 0, step == STEPS - 1
         raw = [fine_rigidity, fine_metric, coarse_rigidity, coarse_metric] if first else []
-        x_in = swap_both(x_out, GX)
+        x_in = swap_both(x_out, beside_x, across_x)
         y_out = call(
             functools.partial(middle_kernel, s, first),
             [(s.y_rows_mats if first else s.y_rows, 2, LANES)] * 2,
@@ -557,7 +548,7 @@
             *x_in,
             name=f"corner_strips_{step}",
         )
-        y_in = swap_both(y_out, GY)
+        y_in = swap_both(y_out, beside_y, across_y)
         if first:
             extra = [fine_rigidity, fine_metric, inverse_f, coarse_rigidity, coarse_metric, inverse_c]
         else:
@@ -591,8 +582,9 @@
             x_out = outs[3:5]
         if first:
             ext_mats = outs[5:9]
-    total = total_over_mesh(energy, swap)
-    energy = total[: 2 * STEPS, 0].reshape(2, STEPS).T
+    for move in TOTAL:
+        energy = energy + swap(energy, move)
+    energy = energy[: 2 * STEPS, 0].reshape(2, STEPS).T
     return fine, coarse, energy
 
 

time: 93.4 us -> 88.8 us (0.951)
  the two profiles are of different devices: /device:TPU:6 before, /device:TPU:1 now
where the time goes in v3:
time: 88.8 us; the launch traced here: 88.4 us
  starting transfers between devices  42.6 us (48%)
  waiting for transfers between devices  29.9 us (34%)
  Pallas kernels  14 us (16%)
  local copies, waits for them, and re-layouts  1.04 us (1%)
    ppermute x20, starting transfers between devices, swap(): return lax.ppermute(value, ALL, swap_pairs(mesh, move))  42.6 us
    ppermute x20, waiting for transfers between devices, swap(): return lax.ppermute(value, ALL, swap_pairs(mesh, move))  29.9 us
    pallas_call x9, Pallas kernels, call(): pl.pallas_call(kernel, out_shape=shapes, in_specs=specs or [SMEM] + [VMEM...  14 us
  transfers between devices with their start and end apart: 20, of which 19 were waited for; matrix products, arithmetic and copies ran while one was open for 0% of the time, Pallas kernels for 0%

profile of v3, /device:TPU:1, one launch (start us, length us, event | category | flops | bytes accessed | tf_op | source)
XLA Modules:
  0.0 88.4 jit_solution(6129035361590925530)
XLA Ops:
  0.8 1.6 %first_strips.1 = (f32[256,128]{1,0:T(8,128)S(1)}, f32[256,128]{1,0:T(8,128)S(1)}) custom-call(s32[6]{0:T(128)S(1)} %stack.36.flags, f32[3,16,16,128]{3,2,1,0:T(8,128)} %refs_2_.5, f32[3,8,8,256]{3,2,1,0:T(8,128)} %refs_3_.5, f32[16,16,128]{2,1,0:T(8,128)} %refs_15_.1, f32[16,16,128]{2,1,0:T(8,128)} %refs_16_.1, f32[8,8,256]{2,1,0:T(8,128)} %refs_18_.1, ...), custom_call_target="tpu_custom_call" | custom-call | flops 1000 | bytes 1048576 | tf_op jit(solution)/shard_map/first_strips/pallas_call | solution.py:375
  2.5 2.1 %collective-permute-start = (f32[256,128]{1,0:T(8,128)S(1)}, f32[256,128]{1,0:T(8,128)S(1)}, u32[]{:S(2)}, u32[]{:S(2)}) collective-permute-start(f32[256,128]{1,0:T(8,128)S(1)} %get-tuple-element.52), channel_id=1, source_target_pairs={{0,8},{1,9},{2,10},{3,11},{4,12},{5,13},{6,14},{7,15},{8,0},{9,1},... | collective-permute-start | bytes 393224 | tf_op jit(solution)/shard_map/ppermute | solution.py:467
  4.6 1.3 %collective-permute-start.1 = (f32[256,128]{1,0:T(8,128)S(1)}, f32[256,128]{1,0:T(8,128)S(1)}, u32[]{:S(2)}, u32[]{:S(2)}) collective-permute-start(f32[256,128]{1,0:T(8,128)S(1)} %get-tuple-element.53), channel_id=1, source_target_pairs={{0,1},{1,0},{2,3},{3,2},{4,5},{5,4},{6,7},{7,6},{8,16},{9,17},{10,... | collective-permute-start | bytes 393224 | tf_op jit(solution)/shard_map/ppermute | solution.py:467
  7.7 3.9 %collective-permute-start.2 = (f32[164,2,128]{2,1,0:T(2,128)S(1)}, f32[164,2,128]{2,1,0:T(2,128)S(1)}, u32[]{:S(2)}, u32[]{:S(2)}) collective-permute-start(f32[164,2,128]{2,1,0:T(2,128)S(1)} %get-tuple-element.54), channel_id=1, source_target_pairs={{0,1},{1,0},{2,3},{3,2},{4,5},{5,4},{6,7},{7,6},{8,9},{9,8},{10,11... | collective-permute-start | bytes 503816 | tf_op jit(solution)/shard_map/ppermute | solution.py:467
  12.6 4.0 %collective-permute-done.3.refs_24_ = f32[164,2,128]{2,1,0:T(2,128)S(1)} collective-permute-done((f32[164,2,128]{2,1,0:T(2,128)S(1)}, f32[164,2,128]{2,1,0:T(2,128)S(1)}, u32[]{:S(2)}, u32[]{:S(2)}) %collective-permute-start.3) | collective-permute-done | bytes 167968 | tf_op jit(solution)/shard_map/ppermute | solution.py:467
  16.8 3.3 %step_0.1 = (f32[3,16,16,128]{3,2,1,0:T(8,128)S(1)}, f32[3,8,8,256]{3,2,1,0:T(8,128)S(1)}, f32[8,128]{1,0:T(8,128)S(1)}, f32[192,128]{1,0:T(8,128)S(1)}, f32[192...) custom-call(s32[6]{0:T(128)S(1)} %stack.36.flags, ...), custom_call_target="tpu_custom_call" | custom-call | flops 4000000 | bytes 1048576 | tf_op jit(solution)/shard_map/step_0/pallas_call | solution.py:375
  20.0 1.8 %collective-permute-start.4 = (f32[192,128]{1,0:T(8,128)S(1)}, f32[192,128]{1,0:T(8,128)S(1)}, u32[]{:S(2)}, u32[]{:S(2)}) collective-permute-start(f32[192,128]{1,0:T(8,128)S(1)} %get-tuple-element.63), channel_id=1, source_target_pairs={{0,8},{1,9},{2,10},{3,11},{4,12},{5,13},{6,14},{7,15},{8,0},{9,1},... | collective-permute-start | bytes 294920 | tf_op jit(solution)/shard_map/ppermute | solution.py:467
  21.9 1.3 %collective-permute-start.5 = (f32[192,128]{1,0:T(8,128)S(1)}, f32[192,128]{1,0:T(8,128)S(1)}, u32[]{:S(2)}, u32[]{:S(2)}) collective-permute-start(f32[192,128]{1,0:T(8,128)S(1)} %get-tuple-element.64), channel_id=1, source_target_pairs={{0,1},{1,0},{2,3},{3,2},{4,5},{5,4},{6,7},{7,6},{8,16},{9,17},{10,... | collective-permute-start | bytes 294920 | tf_op jit(solution)/shard_map/ppermute | solution.py:467
  24.8 1.8 %collective-permute-start.6 = (f32[132,2,128]{2,1,0:T(2,128)S(1)}, f32[132,2,128]{2,1,0:T(2,128)S(1)}, u32[]{:S(2)}, u32[]{:S(2)}) collective-permute-start(f32[132,2,128]{2,1,0:T(2,128)S(1)} %get-tuple-element.65), channel_id=1, source_target_pairs={{0,1},{1,0},{2,3},{3,2},{4,5},{5,4},{6,7},{7,6},{8,9},{9,8},{10,11... | collective-permute-start | bytes 405512 | tf_op jit(solution)/shard_map/ppermute | solution.py:467
  27.5 3.7 %collective-permute-done.7.refs_23_ = f32[132,2,128]{2,1,0:T(2,128)S(1)} collective-permute-done((f32[132,2,128]{2,1,0:T(2,128)S(1)}, f32[132,2,128]{2,1,0:T(2,128)S(1)}, u32[]{:S(2)}, u32[]{:S(2)}) %collective-permute-start.7) | collective-permute-done | bytes 135200 | tf_op jit(solution)/shard_map/ppermute | solution.py:467
  31.2 3.1 %step_1.1 = (f32[3,16,16,128]{3,2,1,0:T(8,128)S(1)}, f32[3,8,8,256]{3,2,1,0:T(8,128)S(1)}, f32[8,128]{1,0:T(8,128)S(1)}, f32[192,128]{1,0:T(8,128)S(1)}, f32[192,128]{1,0:T(8,128)S(1)}) custom-call(s32[6]{0:T(128)S(1)} %stack.36.flags, f32[3,16,16,128]{3,2,1,0:T(8,128)S(1)} %get-tuple-element.56.refs_0_.refs_2_, ...), custom_call_target="tpu_custom_call" | custom-call | flops 4000000 | bytes 1048576 | tf_op jit(solution)/shard_map/step_1/pallas_call | solution.py:375
  34.4 3.2 %collective-permute-start.8 = (f32[192,128]{1,0:T(8,128)S(1)}, f32[192,128]{1,0:T(8,128)S(1)}, u32[]{:S(2)}, u32[]{:S(2)}) collective-permute-start(f32[192,128]{1,0:T(8,128)S(1)} %get-tuple-element.70), channel_id=1, source_target_pairs={{0,8},{1,9},{2,10},{3,11},{4,12},{5,13},{6,14},{7,15},{8,0},{9,1},... | collective-permute-start | bytes 294920 | tf_op jit(solution)/shard_map/ppermute | solution.py:467
  37.6 1.3 %collective-permute-start.9 = (f32[192,128]{1,0:T(8,128)S(1)}, f32[192,128]{1,0:T(8,128)S(1)}, u32[]{:S(2)}, u32[]{:S(2)}) collective-permute-start(f32[192,128]{1,0:T(8,128)S(1)} %get-tuple-element.71), channel_id=1, source_target_pairs={{0,1},{1,0},{2,3},{3,2},{4,5},{5,4},{6,7},{7,6},{8,16},{9,17},{10,... | collective-permute-start | bytes 294920 | tf_op jit(solution)/shard_map/ppermute | solution.py:467
  40.5 1.7 %collective-permute-start.10 = (f32[132,2,128]{2,1,0:T(2,128)S(1)}, f32[132,2,128]{2,1,0:T(2,128)S(1)}, u32[]{:S(2)}, u32[]{:S(2)}) collective-permute-start(f32[132,2,128]{2,1,0:T(2,128)S(1)} %get-tuple-element.72), channel_id=1, source_target_pairs={{0,1},{1,0},{2,3},{3,2},{4,5},{5,4},{6,7},{7,6},{8,9},{9,8},{10,11... | collective-permute-start | bytes 405512 | tf_op jit(solution)/shard_map/ppermute | solution.py:467
  43.2 3.7 %collective-permute-done.11.refs_23_ = f32[132,2,128]{2,1,0:T(2,128)S(1)} collective-permute-done((f32[132,2,128]{2,1,0:T(2,128)S(1)}, f32[132,2,128]{2,1,0:T(2,128)S(1)}, u32[]{:S(2)}, u32[]{:S(2)}) %collective-permute-start.11) | collective-permute-done | bytes 135200 | tf_op jit(solution)/shard_map/ppermute | solution.py:467
  47.0 3.8 %step_2.1 = (f32[3,16,16,128]{3,2,1,0:T(8,128)}, f32[3,8,8,256]{3,2,1,0:T(8,128)}, f32[8,128]{1,0:T(8,128)S(1)}) custom-call(s32[6]{0:T(128)S(1)} %stack.36.flags, f32[3,16,16,128]{3,2,1,0:T(8,128)S(1)} %get-tuple-element.67.refs_0_, f32[3,8,8,256]{3,2,1,0:T(8,128)S(1)} %get-tuple-element.68.refs_1_, ...), custom_call_target="tpu_custom_call" | custom-call | flops 4000000 | bytes 1048576 | tf_op jit(solution)/shard_map/step_2/pallas_call | solution.py:375
  52.6 3.0 %collective-permute-done.13 = f32[8,128]{1,0:T(8,128)S(1)} collective-permute-done((f32[8,128]{1,0:T(8,128)S(1)}, f32[8,128]{1,0:T(8,128)S(1)}, u32[]{:S(2)}, u32[]{:S(2)}) %collective-permute-start.13) | collective-permute-done | bytes 4128 | tf_op jit(solution)/shard_map/ppermute | solution.py:467
  55.6 1.8 %collective-permute-start.14 = (f32[8,128]{1,0:T(8,128)S(1)}, f32[8,128]{1,0:T(8,128)S(1)}, u32[]{:S(2)}, u32[]{:S(2)}) collective-permute-start(f32[8,128]{1,0:T(8,128)S(1)} %add.67), channel_id=1, source_target_pairs={{0,7},{1,6},{2,5},{3,4},{4,3},{5,2},{6,1},{7,0},{8,15},{9,14},{10,... | collective-permute-start | bytes 12296 | tf_op jit(solution)/shard_map/ppermute | solution.py:467
  57.4 2.5 %collective-permute-done.14 = f32[8,128]{1,0:T(8,128)S(1)} collective-permute-done((f32[8,128]{1,0:T(8,128)S(1)}, f32[8,128]{1,0:T(8,128)S(1)}, u32[]{:S(2)}, u32[]{:S(2)}) %collective-permute-start.14) | collective-permute-done | bytes 4128 | tf_op jit(solution)/shard_map/ppermute | solution.py:467
  59.9 4.2 %collective-permute-start.15 = (f32[8,128]{1,0:T(8,128)S(1)}, f32[8,128]{1,0:T(8,128)S(1)}, u32[]{:S(2)}, u32[]{:S(2)}) collective-permute-start(f32[8,128]{1,0:T(8,128)S(1)} %add.68), channel_id=1, source_target_pairs={{0,9},{1,8},{2,11},{3,10},{4,13},{5,12},{6,15},{7,14},{8,1},{9,0},... | collective-permute-start | bytes 12296 | tf_op jit(solution)/shard_map/ppermute | solution.py:467
  65.4 4.6 %collective-permute-start.16 = (f32[8,128]{1,0:T(8,128)S(1)}, f32[8,128]{1,0:T(8,128)S(1)}, u32[]{:S(2)}, u32[]{:S(2)}) collective-permute-start(f32[8,128]{1,0:T(8,128)S(1)} %add.69), channel_id=1, source_target_pairs={{0,25},{1,24},{2,27},{3,26},{4,29},{5,28},{6,31},{7,30},{8,17},{9,... | collective-permute-start | bytes 12296 | tf_op jit(solution)/shard_map/ppermute | solution.py:467
  71.2 2.8 %collective-permute-start.17 = (f32[8,128]{1,0:T(8,128)S(1)}, f32[8,128]{1,0:T(8,128)S(1)}, u32[]{:S(2)}, u32[]{:S(2)}) collective-permute-start(f32[8,128]{1,0:T(8,128)S(1)} %add.70), channel_id=1, source_target_pairs={{0,33},{1,32},{2,35},{3,34},{4,37},{5,36},{6,39},{7,38},{8,41},{9,... | collective-permute-start | bytes 12296 | tf_op jit(solution)/shard_map/ppermute | solution.py:467
  75.3 5.8 %collective-permute-start.18 = (f32[8,128]{1,0:T(8,128)S(1)}, f32[8,128]{1,0:T(8,128)S(1)}, u32[]{:S(2)}, u32[]{:S(2)}) collective-permute-start(f32[8,128]{1,0:T(8,128)S(1)} %add.71), channel_id=1, source_target_pairs={{0,65},{1,64},{2,67},{3,66},{4,69},{5,68},{6,71},{7,70},{8,73},{9,... | collective-permute-start | bytes 12296 | tf_op jit(solution)/shard_map/ppermute | solution.py:467
  82.4 4.0 %collective-permute-start.19 = (f32[8,128]{1,0:T(8,128)S(1)}, f32[8,128]{1,0:T(8,128)S(1)}, u32[]{:S(2)}, u32[]{:S(2)}) collective-permute-start(f32[8,128]{1,0:T(8,128)S(1)} %add.72), channel_id=1, source_target_pairs={{0,225},{1,224},{2,227},{3,226},{4,229},{5,228},{6,231},{7,230},{8... | collective-permute-start | bytes 12296 | tf_op jit(solution)/shard_map/ppermute | solution.py:467
  (65 shorter events, 17.2 us)
Async XLA Ops:
  0.8 5.2 %copy-start.3 = (f32[16,16,128]{2,1,0:T(8,128)S(1)}, f32[16,16,128]{2,1,0:T(8,128)}, u32[]{:S(2)}) copy-start(f32[16,16,128]{2,1,0:T(8,128)} %refs_16_.1) | copy-start | bytes 393220
  2.5 4.5 %collective-permute-start = (f32[256,128]{1,0:T(8,128)S(1)}, f32[256,128]{1,0:T(8,128)S(1)}, u32[]{:S(2)}, u32[]{:S(2)}) collective-permute-start(f32[256,128]{1,0:T(8,128)S(1)} %get-tuple-element.52), channel_id=1, source_target_pairs={{0,8},{1,9},{2,10},{3,11},{4,12},{5,13},{6,14},{7,15},{8,0},{9,1},... | collective-permute-start | bytes 393224 | tf_op jit(solution)/shard_map/ppermute | solution.py:467
  4.6 2.4 %collective-permute-start.1 = (f32[256,128]{1,0:T(8,128)S(1)}, f32[256,128]{1,0:T(8,128)S(1)}, u32[]{:S(2)}, u32[]{:S(2)}) collective-permute-start(f32[256,128]{1,0:T(8,128)S(1)} %get-tuple-element.53), channel_id=1, source_target_pairs={{0,1},{1,0},{2,3},{3,2},{4,5},{5,4},{6,7},{7,6},{8,16},{9,17},{10,... | collective-permute-start | bytes 393224 | tf_op jit(solution)/shard_map/ppermute | solution.py:467
  6.2 5.4 %copy-start.12 = (s32[2,16,16]{2,1,0:T(8,128)S(1)}, s32[2,16,16]{2,1,0:T(8,128)}, u32[]{:S(2)}) copy-start(s32[2,16,16]{2,1,0:T(8,128)} %param.25) | copy-start | bytes 6148
  7.0 9.8 %copy-start.6 = (f32[3,16,16,128]{3,2,1,0:T(8,128)S(1)}, f32[3,16,16,128]{3,2,1,0:T(8,128)}, u32[]{:S(2)}) copy-start(f32[3,16,16,128]{3,2,1,0:T(8,128)} %refs_2_.4) | copy-start | bytes 1179652
  7.0 9.8 %copy-start.7 = (f32[3,8,8,256]{3,2,1,0:T(8,128)S(1)}, f32[3,8,8,256]{3,2,1,0:T(8,128)}, u32[]{:S(2)}) copy-start(f32[3,8,8,256]{3,2,1,0:T(8,128)} %refs_3_.4) | copy-start | bytes 589828
  7.7 4.9 %collective-permute-start.2 = (f32[164,2,128]{2,1,0:T(2,128)S(1)}, f32[164,2,128]{2,1,0:T(2,128)S(1)}, u32[]{:S(2)}, u32[]{:S(2)}) collective-permute-start(f32[164,2,128]{2,1,0:T(2,128)S(1)} %get-tuple-element.54), channel_id=1, source_target_pairs={{0,1},{1,0},{2,3},{3,2},{4,5},{5,4},{6,7},{7,6},{8,9},{9,8},{10,11... | collective-permute-start | bytes 503816 | tf_op jit(solution)/shard_map/ppermute | solution.py:467
  11.6 5.1 %collective-permute-start.3 = (f32[164,2,128]{2,1,0:T(2,128)S(1)}, f32[164,2,128]{2,1,0:T(2,128)S(1)}, u32[]{:S(2)}, u32[]{:S(2)}) collective-permute-start(f32[164,2,128]{2,1,0:T(2,128)S(1)} %get-tuple-element.55), channel_id=1, source_target_pairs={{0,7},{1,2},{2,1},{3,4},{4,3},{5,6},{6,5},{7,0},{8,15},{9,10},{10,... | collective-permute-start | bytes 503816 | tf_op jit(solution)/shard_map/ppermute | solution.py:467
  20.0 3.8 %collective-permute-start.4 = (f32[192,128]{1,0:T(8,128)S(1)}, f32[192,128]{1,0:T(8,128)S(1)}, u32[]{:S(2)}, u32[]{:S(2)}) collective-permute-start(f32[192,128]{1,0:T(8,128)S(1)} %get-tuple-element.63), channel_id=1, source_target_pairs={{0,8},{1,9},{2,10},{3,11},{4,12},{5,13},{6,14},{7,15},{8,0},{9,1},... | collective-permute-start | bytes 294920 | tf_op jit(solution)/shard_map/ppermute | solution.py:467
  21.9 2.2 %collective-permute-start.5 = (f32[192,128]{1,0:T(8,128)S(1)}, f32[192,128]{1,0:T(8,128)S(1)}, u32[]{:S(2)}, u32[]{:S(2)}) collective-permute-start(f32[192,128]{1,0:T(8,128)S(1)} %get-tuple-element.64), channel_id=1, source_target_pairs={{0,1},{1,0},{2,3},{3,2},{4,5},{5,4},{6,7},{7,6},{8,16},{9,17},{10,... | collective-permute-start | bytes 294920 | tf_op jit(solution)/shard_map/ppermute | solution.py:467
  24.8 2.7 %collective-permute-start.6 = (f32[132,2,128]{2,1,0:T(2,128)S(1)}, f32[132,2,128]{2,1,0:T(2,128)S(1)}, u32[]{:S(2)}, u32[]{:S(2)}) collective-permute-start(f32[132,2,128]{2,1,0:T(2,128)S(1)} %get-tuple-element.65), channel_id=1, source_target_pairs={{0,1},{1,0},{2,3},{3,2},{4,5},{5,4},{6,7},{7,6},{8,9},{9,8},{10,11... | collective-permute-start | bytes 405512 | tf_op jit(solution)/shard_map/ppermute | solution.py:467
  26.5 4.7 %collective-permute-start.7 = (f32[132,2,128]{2,1,0:T(2,128)S(1)}, f32[132,2,128]{2,1,0:T(2,128)S(1)}, u32[]{:S(2)}, u32[]{:S(2)}) collective-permute-start(f32[132,2,128]{2,1,0:T(2,128)S(1)} %get-tuple-element.66), channel_id=1, source_target_pairs={{0,7},{1,2},{2,1},{3,4},{4,3},{5,6},{6,5},{7,0},{8,15},{9,10},{10,... | collective-permute-start | bytes 405512 | tf_op jit(solution)/shard_map/ppermute | solution.py:467
  34.4 5.3 %collective-permute-start.8 = (f32[192,128]{1,0:T(8,128)S(1)}, f32[192,128]{1,0:T(8,128)S(1)}, u32[]{:S(2)}, u32[]{:S(2)}) collective-permute-start(f32[192,128]{1,0:T(8,128)S(1)} %get-tuple-element.70), channel_id=1, source_target_pairs={{0,8},{1,9},{2,10},{3,11},{4,12},{5,13},{6,14},{7,15},{8,0},{9,1},... | collective-permute-start | bytes 294920 | tf_op jit(solution)/shard_map/ppermute | solution.py:467
  37.6 2.2 %collective-permute-start.9 = (f32[192,128]{1,0:T(8,128)S(1)}, f32[192,128]{1,0:T(8,128)S(1)}, u32[]{:S(2)}, u32[]{:S(2)}) collective-permute-start(f32[192,128]{1,0:T(8,128)S(1)} %get-tuple-element.71), channel_id=1, source_target_pairs={{0,1},{1,0},{2,3},{3,2},{4,5},{5,4},{6,7},{7,6},{8,16},{9,17},{10,... | collective-permute-start | bytes 294920 | tf_op jit(solution)/shard_map/ppermute | solution.py:467
  40.5 2.7 %collective-permute-start.10 = (f32[132,2,128]{2,1,0:T(2,128)S(1)}, f32[132,2,128]{2,1,0:T(2,128)S(1)}, u32[]{:S(2)}, u32[]{:S(2)}) collective-permute-start(f32[132,2,128]{2,1,0:T(2,128)S(1)} %get-tuple-element.72), channel_id=1, source_target_pairs={{0,1},{1,0},{2,3},{3,2},{4,5},{5,4},{6,7},{7,6},{8,9},{9,8},{10,11... | collective-permute-start | bytes 405512 | tf_op jit(solution)/shard_map/ppermute | solution.py:467
  42.3 4.7 %collective-permute-start.11 = (f32[132,2,128]{2,1,0:T(2,128)S(1)}, f32[132,2,128]{2,1,0:T(2,128)S(1)}, u32[]{:S(2)}, u32[]{:S(2)}) collective-permute-start(f32[132,2,128]{2,1,0:T(2,128)S(1)} %get-tuple-element.73), channel_id=1, source_target_pairs={{0,7},{1,2},{2,1},{3,4},{4,3},{5,6},{6,5},{7,0},{8,15},{9,10},{10,... | collective-permute-start | bytes 405512 | tf_op jit(solution)/shard_map/ppermute | solution.py:467
  50.8 1.8 %collective-permute-start.12 = (f32[8,128]{1,0:T(8,128)S(1)}, f32[8,128]{1,0:T(8,128)S(1)}, u32[]{:S(2)}, u32[]{:S(2)}) collective-permute-start(f32[8,128]{1,0:T(8,128)S(1)} %get-tuple-element.76), channel_id=1, source_target_pairs={{0,1},{1,0},{2,3},{3,2},{4,5},{5,4},{6,7},{7,6},{8,9},{9,8},{10,11... | collective-permute-start | bytes 12296 | tf_op jit(solution)/shard_map/ppermute | solution.py:467
  52.6 3.0 %collective-permute-start.13 = (f32[8,128]{1,0:T(8,128)S(1)}, f32[8,128]{1,0:T(8,128)S(1)}, u32[]{:S(2)}, u32[]{:S(2)}) collective-permute-start(f32[8,128]{1,0:T(8,128)S(1)} %add.66), channel_id=1, source_target_pairs={{0,3},{1,2},{2,1},{3,0},{4,7},{5,6},{6,5},{7,4},{8,11},{9,10},{10,... | collective-permute-start | bytes 12296 | tf_op jit(solution)/shard_map/ppermute | solution.py:467
  55.6 4.2 %collective-permute-start.14 = (f32[8,128]{1,0:T(8,128)S(1)}, f32[8,128]{1,0:T(8,128)S(1)}, u32[]{:S(2)}, u32[]{:S(2)}) collective-permute-start(f32[8,128]{1,0:T(8,128)S(1)} %add.67), channel_id=1, source_target_pairs={{0,7},{1,6},{2,5},{3,4},{4,3},{5,2},{6,1},{7,0},{8,15},{9,14},{10,... | collective-permute-start | bytes 12296 | tf_op jit(solution)/shard_map/ppermute | solution.py:467
  59.9 5.5 %collective-permute-start.15 = (f32[8,128]{1,0:T(8,128)S(1)}, f32[8,128]{1,0:T(8,128)S(1)}, u32[]{:S(2)}, u32[]{:S(2)}) collective-permute-start(f32[8,128]{1,0:T(8,128)S(1)} %add.68), channel_id=1, source_target_pairs={{0,9},{1,8},{2,11},{3,10},{4,13},{5,12},{6,15},{7,14},{8,1},{9,0},... | collective-permute-start | bytes 12296 | tf_op jit(solution)/shard_map/ppermute | solution.py:467
  65.4 5.8 %collective-permute-start.16 = (f32[8,128]{1,0:T(8,128)S(1)}, f32[8,128]{1,0:T(8,128)S(1)}, u32[]{:S(2)}, u32[]{:S(2)}) collective-permute-start(f32[8,128]{1,0:T(8,128)S(1)} %add.69), channel_id=1, source_target_pairs={{0,25},{1,24},{2,27},{3,26},{4,29},{5,28},{6,31},{7,30},{8,17},{9,... | collective-permute-start | bytes 12296 | tf_op jit(solution)/shard_map/ppermute | solution.py:467
  71.2 4.1 %collective-permute-start.17 = (f32[8,128]{1,0:T(8,128)S(1)}, f32[8,128]{1,0:T(8,128)S(1)}, u32[]{:S(2)}, u32[]{:S(2)}) collective-permute-start(f32[8,128]{1,0:T(8,128)S(1)} %add.70), channel_id=1, source_target_pairs={{0,33},{1,32},{2,35},{3,34},{4,37},{5,36},{6,39},{7,38},{8,41},{9,... | collective-permute-start | bytes 12296 | tf_op jit(solution)/shard_map/ppermute | solution.py:467
  75.3 7.1 %collective-permute-start.18 = (f32[8,128]{1,0:T(8,128)S(1)}, f32[8,128]{1,0:T(8,128)S(1)}, u32[]{:S(2)}, u32[]{:S(2)}) collective-permute-start(f32[8,128]{1,0:T(8,128)S(1)} %add.71), channel_id=1, source_target_pairs={{0,65},{1,64},{2,67},{3,66},{4,69},{5,68},{6,71},{7,70},{8,73},{9,... | collective-permute-start | bytes 12296 | tf_op jit(solution)/shard_map/ppermute | solution.py:467
  82.4 5.3 %collective-permute-start.19 = (f32[8,128]{1,0:T(8,128)S(1)}, f32[8,128]{1,0:T(8,128)S(1)}, u32[]{:S(2)}, u32[]{:S(2)}) collective-permute-start(f32[8,128]{1,0:T(8,128)S(1)} %add.72), channel_id=1, source_target_pairs={{0,225},{1,224},{2,227},{3,226},{4,229},{5,228},{6,231},{7,230},{8... | collective-permute-start | bytes 12296 | tf_op jit(solution)/shard_map/ppermute | solution.py:467
  (9 other events, 35.5 us)

commit v4 on v3

--- a/solution.py
+++ b/solution.py
@@ -31,19 +31,28 @@
         self.x_fine_mats = self.x_rows
         self.x_coarse_mats = self.x_fine_mats + 2 * self.fy
         self.x_rows_mats = self.x_coarse_mats + 2 * self.halves * self.cy
+        self.x_fine_beta = self.x_rows
+        self.x_coarse_beta = self.x_fine_beta + 2 * self.fy
+        self.x_spread = self.x_coarse_beta + self.halves * 2 * self.cy
+        self.spread = self.cy + 8
+        self.x_rows_beta = self.x_spread + 2 * self.spread
         self.fe, self.ce = self.fx + 4, self.cx + 4
         self.y_coarse = 3 * self.fe
         self.y_rows = self.y_coarse + self.halves * 3 * self.ce
         self.y_fine_mats = self.y_rows
         self.y_coarse_mats = self.y_fine_mats + self.fx
         self.y_rows_mats = self.y_coarse_mats + self.halves * self.cx
+        self.y_fine_beta = self.y_rows
+        self.y_coarse_beta = self.y_fine_beta + self.fe
+        self.y_spread = self.y_coarse_beta + self.halves * self.ce
+        self.y_rows_beta = self.y_spread + self.cx
 
 
 def lanes_of(h):
     return slice(h * LANES, (h + 1) * LANES)
 
 
-def put_x(s, flags, outs, fine, coarse):
+def put_x(s, flags, outs, fine, coarse, betas=None, spread=None):
     even = flags[EVEN_X] == 1
     for k, out in enumerate(outs):
         far = even if k == 0 else jnp.logical_not(even)
@@ -54,6 +63,16 @@
         for h in range(s.halves):
             base = s.x_coarse + h * 6 * s.cy
             out[base : base + 6 * s.cy, :] = strip[:, :, :, lanes_of(h)].reshape(6 * s.cy, LANES)
+        if betas is None:
+            continue
+        strip = betas[0][pl.ds(start_f, 2), :, :]
+        out[s.x_fine_beta : s.x_coarse_beta, :] = strip.reshape(2 * s.fy, LANES)
+        strip = betas[1][pl.ds(start_c, 2), :, :]
+        for h in range(s.halves):
+            base = s.x_coarse_beta + h * 2 * s.cy
+            out[base : base + 2 * s.cy, :] = strip[:, :, lanes_of(h)].reshape(2 * s.cy, LANES)
+        start = jnp.where(far, s.cx + 2, 0)
+        out[s.x_spread : s.x_rows_beta, :] = spread[pl.ds(start, 2)].reshape(2 * s.spread, LANES)
 
 
 def first_kernel(s, flags, fine, coarse, rig_f, met_f, rig_c, met_c, out_a, out_b, *scratch):
@@ -95,56 +114,59 @@
     return low, high
 
 
-def middle_kernel(s, with_mats, flags, *refs):
-    if with_mats:
-        fine, coarse, rig_f, met_f, rig_c, met_c, in_a, in_b, out_a, out_b = refs
-    else:
-        fine, coarse, in_a, in_b, out_a, out_b = refs
+def middle_kernel(s, step, flags, *refs):
+    fine, coarse, *mats, in_a, in_b = refs[:-2] if step != 1 else refs[:-3]
+    out_a, out_b = refs[-2:] if step != 1 else refs[-3:-1]
     even = flags[EVEN_Y] == 1
 
     def put(index, low, high):
         out_a[index] = jnp.where(even, high, low)
         out_b[index] = jnp.where(even, low, high)
 
-    for c in range(3):
-        own = pl.ds(c * s.fe + 2, s.fx)
-        put(own, fine[c, :, 0:2, :], fine[c, :, s.fy - 2 : s.fy, :])
+    def field(own, x, y, x_base, y_base):
+        put(pl.ds(y_base + 2, x), own(slice(0, 2)), own(slice(y - 2, y)))
         for k in range(2):
-            base = (c * 2 + k) * s.fy
             pieces = []
-            for first in (0, s.fy - 2):
-                rows = slice(base + first, base + first + 2)
+            for first in (0, y - 2):
+                rows = slice(x_base + k * y + first, x_base + k * y + first + 2)
                 pieces.append(sides(flags, EVEN_X, HAS_XM, HAS_XP, in_a[rows, :], in_b[rows, :]))
             for side in range(2):
-                place = c * s.fe + (k if side == 0 else s.fx + 2 + k)
+                place = y_base + (k if side == 0 else x + 2 + k)
                 put(place, pieces[0][side], pieces[1][side])
+
+    for c in range(3):
+        field(lambda r: fine[c, :, r, :], s.fx, s.fy, c * 2 * s.fy, c * s.fe)
         for h in range(s.halves):
-            origin = s.y_coarse + (h * 3 + c) * s.ce
-            own = pl.ds(origin + 2, s.cx)
-            put(own, coarse[c, :, 0:2, lanes_of(h)], coarse[c, :, s.cy - 2 : s.cy, lanes_of(h)])
-            for k in range(2):
-                base = s.x_coarse + (h * 6 + c * 2 + k) * s.cy
-                pieces = []
-                for first in (0, s.cy - 2):
-                    rows = slice(base + first, base + first + 2)
-                    pieces.append(
-                        sides(flags, EVEN_X, HAS_XM, HAS_XP, in_a[rows, :], in_b[rows, :])
-                    )
-                for side in range(2):
-                    place = origin + (k if side == 0 else s.cx + 2 + k)
-                    put(place, pieces[0][side], pieces[1][side])
-    if not with_mats:
-        return
-    for m, (of_f, of_c) in enumerate(((rig_f, rig_c), (met_f, met_c))):
-        low, high = of_f[:, 0:1, :], of_f[:, s.fy - 1 : s.fy, :]
-        where = pl.ds(s.y_fine_mats, s.fx)
-        out_a[where, m : m + 1, :] = jnp.where(even, high, low)
-        out_b[where, m : m + 1, :] = jnp.where(even, low, high)
-        for h in range(s.halves):
-            low, high = of_c[:, 0:1, lanes_of(h)], of_c[:, s.cy - 1 : s.cy, lanes_of(h)]
-            where = pl.ds(s.y_coarse_mats + h * s.cx, s.cx)
+            at = lanes_of(h)
+            x_base, y_base = s.x_coarse + (h * 6 + c * 2) * s.cy, s.y_coarse + (h * 3 + c) * s.ce
+            field(lambda r: coarse[c, :, r, at], s.cx, s.cy, x_base, y_base)
+    if step == 0:
+        rig_f, met_f, rig_c, met_c = mats
+        for m, (of_f, of_c) in enumerate(((rig_f, rig_c), (met_f, met_c))):
+            low, high = of_f[:, 0:1, :], of_f[:, s.fy - 1 : s.fy, :]
+            where = pl.ds(s.y_fine_mats, s.fx)
             out_a[where, m : m + 1, :] = jnp.where(even, high, low)
             out_b[where, m : m + 1, :] = jnp.where(even, low, high)
+            for h in range(s.halves):
+                low, high = of_c[:, 0:1, lanes_of(h)], of_c[:, s.cy - 1 : s.cy, lanes_of(h)]
+                where = pl.ds(s.y_coarse_mats + h * s.cx, s.cx)
+                out_a[where, m : m + 1, :] = jnp.where(even, high, low)
+                out_b[where, m : m + 1, :] = jnp.where(even, low, high)
+    if step == 1:
+        beta_f, beta_c, spread = mats
+        field(lambda r: beta_f[:, r, :], s.fx, s.fy, s.x_fine_beta, s.y_fine_beta)
+        for h in range(s.halves):
+            at = lanes_of(h)
+            x_base, y_base = s.x_coarse_beta + h * 2 * s.cy, s.y_coarse_beta + h * s.ce
+            field(lambda r: beta_c[:, r, at], s.cx, s.cy, x_base, y_base)
+        total = refs[-1]
+        total[...] = spread[2 : 2 + s.cx]
+        for k in range(2):
+            rows = slice(s.x_spread + k * s.spread, s.x_spread + (k + 1) * s.spread)
+            low, high = sides(flags, EVEN_X, HAS_XM, HAS_XP, in_a[rows, :], in_b[rows, :])
+            total[k] += low
+            total[s.cx - 2 + k] += high
+        put(pl.ds(s.y_spread, s.cx), total[:, 0:2, :], total[:, s.cy + 2 : s.cy + 4, :])
 
 
 def up_one(x):
@@ -155,7 +177,7 @@
     return pltpu.roll(x, 1, x.ndim - 1)
 
 
-def own_kernel(density, lame, rigidity, metric, inverse, c1, c2, weight, above, first):
+def own_kernel(density, lame, rigidity, metric, inverse, c1, c2, weight, above, first, beta):
     inv = 1.0 / metric[...]
     inverse[...] = inv
     over = 1.0 / density[...]
@@ -166,11 +188,55 @@
     lane = lax.broadcasted_iota(jnp.int32, v.shape, 2)
     above[...] = jnp.where(lane == v.shape[2] - 1, v, 0.5 * (v + up_one(v)))
     first[...] = v[:, :, 0:LANES]
+    beta[...] = (lame[...] + rigidity[...]) * metric[...]
 
 
 def slope(f, up, down, lane):
     last = f.shape[-1] - 1
     return jnp.where(lane == 0, up - f, jnp.where(lane == last, f - down, 0.5 * (up - down)))
+
+
+def slope_transposed(q, lane):
+    last = q.shape[-1] - 1
+    half = jnp.where((lane == 0) | (lane == last), q, 0.5 * q)
+    down = jnp.where(lane == 0, -half, down_one(half))
+    return down - jnp.where(lane == last, -half, up_one(half))
+
+
+def fill_beta(s, flags, own, ext, x_in, y_in, fine):
+    x, y, e = (s.fx, s.fy, s.fe) if fine else (s.cx, s.cy, s.ce)
+    ext[2 : 2 + x, 8 : 8 + y, :] = own[...]
+    for h in range(1 if fine else s.halves):
+        at = lanes_of(h)
+        base = s.x_fine_beta if fine else s.x_coarse_beta + h * 2 * y
+        rows = slice(base, base + 2 * y)
+        low, high = sides(flags, EVEN_X, HAS_XM, HAS_XP, x_in[0][rows, :], x_in[1][rows, :])
+        ext[0:2, 8 : 8 + y, at] = low.reshape(2, y, LANES)
+        ext[x + 2 : x + 4, 8 : 8 + y, at] = high.reshape(2, y, LANES)
+        start = s.y_fine_beta if fine else s.y_coarse_beta + h * e
+        rows = slice(start, start + e)
+        low, high = sides(flags, EVEN_Y, HAS_YM, HAS_YP, y_in[0][rows], y_in[1][rows])
+        ext[:, 6:8, at] = low
+        ext[:, 8 + y : 10 + y, at] = high
+
+
+def fill_transposed(x, y, ext, beta, inv_ext, psi):
+    z = ext.shape[-1]
+    lane = lax.broadcasted_iota(jnp.int32, (y + 2, z), 1)
+    wide, low, high = slice(7, 9 + y), slice(6, 8 + y), slice(8, 10 + y)
+
+    def row(r, carry):
+        along_x = ext[0, r, wide, :] * beta[r, wide, :]
+        along_x -= ext[0, r + 2, wide, :] * beta[r + 2, wide, :]
+        along_y = ext[1, r + 1, low, :] * beta[r + 1, low, :]
+        along_y -= ext[1, r + 1, high, :] * beta[r + 1, high, :]
+        inv = inv_ext[r, 0 : 2 + y, :]
+        column = inv * beta[r + 1, wide, :] * ext[2, r + 1, wide, :]
+        total = 0.5 * along_x + 0.5 * along_y + slope_transposed(column, lane)
+        psi[r, wide, :] = jnp.where(inv > 0.0, total, 0.0)
+        return carry
+
+    lax.fori_loop(0, x + 2, row, 0, unroll=True)
 
 
 def fill_displacement(s, flags, own, ext, x_in, y_in, fine):
@@ -236,13 +302,13 @@
     lax.fori_loop(0, x + 2, row, 0, unroll=True)
 
 
-def update(x, y, ext, wide_ext, inv_ext, div, prev, coef, new, ghosts):
+def update(x, y, ext, wide_ext, inv_ext, div, prev, coef, new, ghosts, psi=None):
     c1, c2, weight, above, vertical = coef
     z = ext.shape[-1]
     lane = lax.broadcasted_iota(jnp.int32, (y, z), 1)
     mid, left, right, own = slice(8, 8 + y), slice(7, 7 + y), slice(9, 9 + y), slice(1, 1 + y)
 
-    def row(i, total):
+    def row(i, totals):
         wide = wide_ext[i + 1, own, :]
         w_xp = 0.5 * (wide + wide_ext[i + 2, own, :])
         w_xm = 0.5 * (wide_ext[i, own, :] + wide)
@@ -255,25 +321,44 @@
             0.5 * (div[i + 1, right, :] - div[i + 1, left, :]),
             inv * slope(f, up_one(f), down_one(f), lane),
         )
-        top, bottom = ghosts(i)
+        if psi is not None:
+            transposed = (
+                0.5 * (psi[i, mid, :] - psi[i + 2, mid, :]),
+                0.5 * (psi[i + 1, left, :] - psi[i + 1, right, :]),
+                slope_transposed(inv * psi[i + 1, mid, :], lane),
+            )
+        top, bottom, top_next = ghosts(i)
         k1, k2, dm, va = c1[i], c2[i], weight[i], above[i]
-        inner = jnp.zeros((y, z), jnp.float32)
+        first = vertical[i, :, 0:1]
+        inner, squares, cross = (jnp.zeros((y, z), jnp.float32) for _ in range(3))
         for c in range(3):
             u = ext[c, i + 2, mid, :]
-            up = jnp.where(lane == z - 1, bottom(c), up_one(u))
             flux = w_xp * (ext[c, i + 3, mid, :] - u) - w_xm * (u - ext[c, i + 1, mid, :])
             flux += w_yp * (ext[c, i + 2, right, :] - u) - w_ym * (u - ext[c, i + 2, left, :])
-            over = va * (up - u)
-            entry = 0.0 if top is None else vertical[i, :, 0:1] * (u[:, 0:1] - top(c))
+            over = va * (jnp.where(lane == z - 1, 0.0, up_one(u)) - u)
+            entry = 0.0 if top is None else first * u[:, 0:1]
             flux += over - jnp.where(lane == 0, entry, down_one(over))
-            rate = flux * k1 + k2 * gradient[c]
+            if top is None:
+                ghost = jnp.where(lane == z - 1, va * bottom(c), 0.0)
+            else:
+                ghost = jnp.where(lane == 0, first * top(c), 0.0)
+            rate = (flux + ghost) * k1 + k2 * gradient[c]
             updated = 2.0 * u - prev[c, i] + STEP * rate
             change = updated - u
             inner += change * change - STEP * updated * rate
             new[c, i] = updated
-        return total + dm * inner
-
-    return lax.fori_loop(0, x, row, jnp.zeros((y, z), jnp.float32), unroll=4)
+            if psi is not None:
+                squares += change * change
+                cross += updated * (flux + transposed[c])
+                if top is not None:
+                    cross += jnp.where(lane == 0, first * u[:, 0:1] * top_next(c), 0.0)
+        total = totals[0] + dm * inner
+        if psi is None:
+            return (total,)
+        return total, totals[1] + (dm * squares - STEP * cross)
+
+    start = (jnp.zeros((y, z), jnp.float32),) * (1 if psi is None else 2)
+    return lax.fori_loop(0, x, row, start, unroll=4)
 
 
 def step_kernel(s, step, cells, flags, *refs):
@@ -286,22 +371,26 @@
 
     fine, coarse, fine_prev, coarse_prev, offs = take(5)
     coef_f, coef_c = take(5), take(5)
-    first, final = step == 0, step == STEPS - 1
-    if first:
+    if step == 0:
         rig_f, met_f, inverse_f, rig_c, met_c, inverse_c = take(6)
     else:
-        wide_f, inv_f, wide_c, inv_c, energy_in = take(5)
+        wide_f, inv_f, wide_c, inv_c = take(4)
+    if step < 2:
+        beta_own = take(2)
+    if step == 1:
+        energy_in, spread_in = take(2)
     x_in, y_in = take(2), take(2)
-    new_f, new_c, energy = take(3)
-    if not final:
+    new_f, new_c = take(2)
+    if step < 2:
+        (energy,) = take(1)
         x_out = take(2)
-    if first:
-        wide_f, inv_f, wide_c, inv_c = take(4)
+    if step == 0:
+        wide_f, inv_f, wide_c, inv_c, spread_out = take(5)
     ext_f, ext_c, div_f, div_c, double, pairs = take(6)
 
     fill_displacement(s, flags, fine, ext_f, x_in, y_in, True)
     fill_displacement(s, flags, coarse, ext_c, x_in, y_in, False)
-    if first:
+    if step == 0:
         fill_materials(s, flags, rig_f, met_f, inverse_f, wide_f, inv_f, x_in, y_in, True)
         fill_materials(s, flags, rig_c, met_c, inverse_c, wide_c, inv_c, x_in, y_in, False)
 
@@ -318,48 +407,107 @@
 
     fill_divergence(s.fx, s.fy, ext_f, inv_f, div_f)
     fill_divergence(s.cx, s.cy, ext_c, inv_c, div_c)
+    psi_f = psi_c = None
+    if step == 1:
+        psi_f, psi_c, all_beta_f, all_beta_c, pairs_next, spread = take(6)
+        fill_beta(s, flags, beta_own[0], all_beta_f, x_in, y_in, True)
+        fill_beta(s, flags, beta_own[1], all_beta_c, x_in, y_in, False)
+        fill_transposed(s.fx, s.fy, ext_f, all_beta_f, inv_f, psi_f)
+        fill_transposed(s.cx, s.cy, ext_c, all_beta_c, inv_c, psi_c)
 
     odd_y = lax.broadcasted_iota(jnp.int32, (s.fy, LANES), 0) % 2
     near_y = jnp.where(odd_y == 0, 0.75, 0.25)
 
-    def fine_ghosts(i):
-        half = i // 2
+    def node_weights(i):
         near_x = jnp.where(i % 2 == 0, 0.75, 0.25)
         off_x, off_y = offs[i] // 4 - 1, offs[i] % 4 - 1
+        out = []
+        for off, near in ((off_x, near_x), (off_y, near_y)):
+            out.append(
+                [
+                    jnp.where(off == shift, near, 0.0)
+                    + jnp.where(off == shift - 1, 1.0 - near, 0.0)
+                    for shift in (-1, 0, 1, 2)
+                ]
+            )
+        return out
+
+    def fine_ghosts(i):
+        weights_x, weights_y = node_weights(i)
         total = jnp.zeros((s.fy, LANES), jnp.float32)
-        weights = []
-        for shift in (-1, 0, 1, 2):
-            weights.append(
-                jnp.where(off_y == shift, near_y, 0.0)
-                + jnp.where(off_y == shift - 1, 1.0 - near_y, 0.0)
-            )
-        for shift in (-1, 0, 1, 2):
-            weight_x = jnp.where(off_x == shift, near_x, 0.0) + jnp.where(
-                off_x == shift - 1, 1.0 - near_x, 0.0
-            )
+        for a in range(4):
             line = jnp.zeros((s.fy, LANES), jnp.float32)
-            for k in range(4):
-                line += weights[k] * double[half + 2 + shift, 2 * k + 2 : 2 * k + 2 + s.fy, :]
-            total += weight_x * line
-        return None, lambda c: pltpu.roll(total, LANES - 1 - c, 1)
+            for b in range(4):
+                line += weights_y[b] * double[i // 2 + 1 + a, 2 * b + 2 : 2 * b + 2 + s.fy, :]
+            total += weights_x[a] * line
+        return None, lambda c: pltpu.roll(total, LANES - 1 - c, 1), None
 
     def coarse_ghosts(i):
-        def top(c):
-            both = pairs[c, i, pl.ds(0, s.cy, stride=2), :] + pairs[c, i, pl.ds(1, s.cy, stride=2), :]
-            return 0.25 * both[:, LANES - 1 :]
-
-        return top, lambda c: jnp.zeros((s.cy, s.cz), jnp.float32)
-
-    sum_f = update(s.fx, s.fy, ext_f, wide_f, inv_f, div_f, fine_prev, coef_f, new_f, fine_ghosts)
-    sum_c = update(
-        s.cx, s.cy, ext_c, wide_c, inv_c, div_c, coarse_prev, coef_c, new_c, coarse_ghosts
+        def mean(of):
+            def top(c):
+                both = of[c, i, pl.ds(0, s.cy, stride=2), :] + of[c, i, pl.ds(1, s.cy, stride=2), :]
+                return 0.25 * both[:, LANES - 1 :]
+
+            return top
+
+        return mean(pairs), None, mean(pairs_next) if step == 1 else None
+
+    sums_f = update(
+        s.fx, s.fy, ext_f, wide_f, inv_f, div_f, fine_prev, coef_f, new_f, fine_ghosts, psi_f
     )
+    if step == 1:
+        for c in range(3):
+            for i in range(s.cx):
+                pairs_next[c, i] = new_f[c, 2 * i] + new_f[c, 2 * i + 1]
+    sums_c = update(
+        s.cx, s.cy, ext_c, wide_c, inv_c, div_c, coarse_prev, coef_c, new_c, coarse_ghosts, psi_c
+    )
+    if step == 2:
+        return
     place = lax.broadcasted_iota(jnp.int32, (8, LANES), 0)
-    before = jnp.zeros((8, LANES), jnp.float32) if first else energy_in[...]
-    before = jnp.where(place == step, jnp.sum(sum_f) / cells[0], before)
-    energy[...] = jnp.where(place == STEPS + step, jnp.sum(sum_c) / cells[1], before)
-    if not final:
+    table = jnp.zeros((8, LANES), jnp.float32) if step == 0 else energy_in[...]
+    table = jnp.where(place == step, jnp.sum(sums_f[0]) / cells[0], table)
+    table = jnp.where(place == STEPS + step, jnp.sum(sums_c[0]) / cells[1], table)
+    if step == 0:
+        line_lane = lax.broadcasted_iota(jnp.int32, (s.fy, LANES), 1)
+        double[...] = jnp.zeros(double.shape, jnp.float32)
+
+        def scatter(i, carry):
+            weights_x, weights_y = node_weights(i)
+            face = coef_f[3][i]
+            q = jnp.zeros((s.fy, LANES), jnp.float32)
+            for c in range(3):
+                q = jnp.where(line_lane == c, pltpu.roll(face * new_f[c, i], c + 1, 1), q)
+            for b in range(4):
+                part = weights_y[b] * q
+                for a in range(4):
+                    rows = slice(2 * b + 2, 2 * b + 2 + s.fy)
+                    double[i // 2 + 1 + a, rows, :] += weights_x[a] * part
+            return carry
+
+        lax.fori_loop(0, s.fx, scatter, 0, unroll=4)
+        rows = s.cy + 4
+        for i in range(s.ce):
+            evens = double[i, pl.ds(0, rows, stride=2), :]
+            spread_out[i, 0:rows, :] = evens + double[i, pl.ds(1, rows, stride=2), :]
+            spread_out[i, rows:, :] = jnp.zeros((s.spread - rows, LANES), jnp.float32)
+        put_x(s, flags, x_out, new_f, new_c, beta_own, spread_out)
+    if step == 1:
+        spread[...] = spread_in[:, 2 : 2 + s.cy, :]
+        rows = pl.ds(s.y_spread, s.cx)
+        low, high = sides(flags, EVEN_Y, HAS_YM, HAS_YP, y_in[0][rows], y_in[1][rows])
+        spread[:, 0:2, :] += low
+        spread[:, s.cy - 2 : s.cy, :] += high
+        joined = jnp.zeros((s.cy, LANES), jnp.float32)
+        for i in range(s.cx):
+            for c in range(3):
+                weights = spread[i] if c == 0 else pltpu.roll(spread[i], LANES - c, 1)
+                joined += new_c[c, i, :, 0:LANES] * weights
+        joined = jnp.sum(joined[:, 0:1])
+        table = jnp.where(place == 2, (jnp.sum(sums_f[1]) - STEP * joined) / cells[0], table)
+        table = jnp.where(place == STEPS + 2, jnp.sum(sums_c[1]) / cells[1], table)
         put_x(s, flags, x_out, new_f, new_c)
+    energy[...] = table
 
 
 VMEM = pl.BlockSpec(memory_space=pltpu.VMEM)
@@ -507,7 +655,7 @@
         own.append(
             call(
                 own_kernel,
-                [metric.shape] * 5 + [metric.shape[:2] + (LANES,)],
+                [metric.shape] * 5 + [metric.shape[:2] + (LANES,), metric.shape],
                 2_000_000,
                 density,
                 lame,
@@ -517,8 +665,8 @@
                 specs=[VMEM] * 4,
             )
         )
-    inverse_f, *coef_f = own[0]
-    inverse_c, *coef_c = own[1]
+    inverse_f, *coef_f, beta_f = own[0]
+    inverse_c, *coef_c, beta_c = own[1]
 
     fine, coarse = fine_disp, coarse_disp
     fine_ext = (s.fx + 2, s.fy + 2, s.fz)
@@ -532,32 +680,54 @@
         (3, s.cx, s.fy, LANES),
     ]
     cells = [count_x * count_y * s.fx * s.fy * s.fz, count_x * count_y * s.cx * s.cy * s.cz]
-    energy = None
+    spread = (s.ce, s.spread, LANES)
     for step in range(STEPS):
-        first, final = step == 0, step == STEPS - 1
-        raw = [fine_rigidity, fine_metric, coarse_rigidity, coarse_metric] if first else []
         x_in = swap_both(x_out, beside_x, across_x)
+        if step == 2:
+            for move in TOTAL[:2]:
+                energy = energy + swap(energy, move)
+            energy, *x_in = lax.optimization_barrier((energy, *x_in))
+            for move in TOTAL[2:-1]:
+                energy = energy + swap(energy, move)
+            other = swap(energy, TOTAL[-1])
+        shapes = [((s.y_rows_mats, s.y_rows_beta, s.y_rows)[step], 2, LANES)] * 2
+        if step == 0:
+            mats = [fine_rigidity, fine_metric, coarse_rigidity, coarse_metric]
+        if step == 1:
+            mats = [beta_f, beta_c, spread_own]
+            shapes.append((s.cx,) + spread[1:])
         y_out = call(
-            functools.partial(middle_kernel, s, first),
-            [(s.y_rows_mats if first else s.y_rows, 2, LANES)] * 2,
+            functools.partial(middle_kernel, s, step),
+            shapes,
             1000,
             flags,
             fine,
             coarse,
-            *raw,
+            *(mats if step < 2 else ()),
             *x_in,
             name=f"corner_strips_{step}",
         )
-        y_in = swap_both(y_out, beside_y, across_y)
-        if first:
+        y_in = swap_both(y_out[:2], beside_y, across_y)
+        shapes = [fine.shape, coarse.shape]
+        more_scratch = []
+        if step < 2:
+            shapes += [(8, LANES)] + [((s.x_rows_beta, s.x_rows)[step], LANES)] * 2
+        if step == 0:
             extra = [fine_rigidity, fine_metric, inverse_f, coarse_rigidity, coarse_metric, inverse_c]
+            extra += [beta_f, beta_c]
+            shapes += [fine_ext, fine_ext, coarse_ext, coarse_ext, spread]
         else:
-            extra = [*ext_mats, energy]
-        shapes = [fine.shape, coarse.shape, (8, LANES)]
-        if not final:
-            shapes += [(s.x_rows, LANES)] * 2
-        if first:
-            shapes += [fine_ext, fine_ext, coarse_ext, coarse_ext]
+            extra = list(ext_mats)
+        if step == 1:
+            extra += [beta_f, beta_c, energy, y_out[2]]
+            more_scratch = [
+                scratch[2],
+                scratch[3],
+                scratch[0][1:],
+                scratch[1][1:],
+                scratch[5],
+                (s.cx, s.cy, LANES),
+            ]
         outs = call(
             functools.partial(step_kernel, s, step, cells),
             shapes,
@@ -573,17 +743,17 @@
             *extra,
             *x_in,
             *y_in,
-            scratch=scratch,
+            scratch=scratch + more_scratch,
             name=f"step_{step}",
         )
         fine_prev, coarse_prev = fine, coarse
-        fine, coarse, energy = outs[:3]
-        if not final:
-            x_out = outs[3:5]
-        if first:
-            ext_mats = outs[5:9]
-    for move in TOTAL:
-        energy = energy + swap(energy, move)
+        fine, coarse = outs[:2]
+        if step < 2:
+            energy, x_out = outs[2], outs[3:5]
+        if step == 0:
+            *ext_mats, spread_own = outs[5:]
+    other, fine, coarse = lax.optimization_barrier((other, fine, coarse))
+    energy = energy + other
     energy = energy[: 2 * STEPS, 0].reshape(2, STEPS).T
     return fine, coarse, energy
 

time: 88.8 us -> 82.4 us (0.928)
  waiting for transfers between devices: 29.9 us -> 24.5 us
  starting transfers between devices: 42.6 us -> 40.4 us
  Pallas kernels: 14 us -> 15.3 us
    ppermute x20, waiting for transfers between devices: 29.9 us -> 24.5 us  [swap(): return lax.ppermute(value, ALL, swap_pairs(mesh, move))]
    ppermute x20, starting transfers between devices: 42.6 us -> 40.4 us  [swap(): return lax.ppermute(value, ALL, swap_pairs(mesh, move))]
    pallas_call x9, Pallas kernels: 14 us -> 15.3 us  [call(): pl.pallas_call(kernel, out_shape=shapes, in_specs=specs or [SMEM] + [VMEM...]
  transfers between devices with their start and end apart: 20 -> 20, of which waited for: 19 -> 13; matrix products, arithmetic and copies ran while one was open for 0% -> 0% of each run, Pallas kernels for 0% -> 5%
where the time goes in v4:
time: 82.4 us; the launch traced here: 82.2 us
  starting transfers between devices  40.4 us (49%)
  waiting for transfers between devices  24.5 us (30%)
  Pallas kernels  15.3 us (19%)
  local copies, waits for them, and re-layouts  1.05 us (1%)
  between operations  0.87 us (1%)
    ppermute x20, starting transfers between devices, swap(): return lax.ppermute(value, ALL, swap_pairs(mesh, move))  40.4 us
    ppermute x20, waiting for transfers between devices, swap(): return lax.ppermute(value, ALL, swap_pairs(mesh, move))  24.5 us
    pallas_call x9, Pallas kernels, call(): pl.pallas_call(kernel, out_shape=shapes, in_specs=specs or [SMEM] + [VMEM...  15.3 us
  transfers between devices with their start and end apart: 20, of which 13 were waited for; matrix products, arithmetic and copies ran while one was open for 0% of the time, Pallas kernels for 5%

profile of v4, /device:TPU:1, one launch (start us, length us, event | category | flops | bytes accessed | tf_op | source)
XLA Modules:
  0.0 82.2 jit_solution(12434216882359759905)
XLA Ops:
  0.8 1.6 %first_strips.1 = (f32[256,128]{1,0:T(8,128)S(1)}, f32[256,128]{1,0:T(8,128)S(1)}) custom-call(s32[6]{0:T(128)S(1)} %stack.36.flags, f32[3,16,16,128]{3,2,1,0:T(8,128)} %refs_2_.5, f32[3,8,8,256]{3,2,1,0:T(8,128)} %refs_3_.5, f32[16,16,128]{2,1,0:T(8,128)} %refs_15_.1, f32[16,16,128]{2,1,0:T(8,128)} %refs_16_.1, f32[8,8,256]{2,1,0:T(8,128)} %refs_18_.1, ...), custom_call_target="tpu_custom_call" | custom-call | flops 1000 | bytes 1048576 | tf_op jit(solution)/shard_map/first_strips/pallas_call | solution.py:523
  2.5 2.1 %collective-permute-start = (f32[256,128]{1,0:T(8,128)S(1)}, f32[256,128]{1,0:T(8,128)S(1)}, u32[]{:S(2)}, u32[]{:S(2)}) collective-permute-start(f32[256,128]{1,0:T(8,128)S(1)} %get-tuple-element.63), channel_id=1, source_target_pairs={{0,8},{1,9},{2,10},{3,11},{4,12},{5,13},{6,14},{7,15},{8,0},{9,1},... | collective-permute-start | bytes 393224 | tf_op jit(solution)/shard_map/ppermute | solution.py:615
  4.6 1.3 %collective-permute-start.1 = (f32[256,128]{1,0:T(8,128)S(1)}, f32[256,128]{1,0:T(8,128)S(1)}, u32[]{:S(2)}, u32[]{:S(2)}) collective-permute-start(f32[256,128]{1,0:T(8,128)S(1)} %get-tuple-element.64), channel_id=1, source_target_pairs={{0,1},{1,0},{2,3},{3,2},{4,5},{5,4},{6,7},{7,6},{8,16},{9,17},{10,... | collective-permute-start | bytes 393224 | tf_op jit(solution)/shard_map/ppermute | solution.py:615
  7.7 3.9 %collective-permute-start.2 = (f32[164,2,128]{2,1,0:T(2,128)S(1)}, f32[164,2,128]{2,1,0:T(2,128)S(1)}, u32[]{:S(2)}, u32[]{:S(2)}) collective-permute-start(f32[164,2,128]{2,1,0:T(2,128)S(1)} %get-tuple-element.65), channel_id=1, source_target_pairs={{0,1},{1,0},{2,3},{3,2},{4,5},{5,4},{6,7},{7,6},{8,9},{9,8},{10,11... | collective-permute-start | bytes 503816 | tf_op jit(solution)/shard_map/ppermute | solution.py:615
  12.6 4.0 %collective-permute-done.3.refs_26_ = f32[164,2,128]{2,1,0:T(2,128)S(1)} collective-permute-done((f32[164,2,128]{2,1,0:T(2,128)S(1)}, f32[164,2,128]{2,1,0:T(2,128)S(1)}, u32[]{:S(2)}, u32[]{:S(2)}) %collective-permute-start.3) | collective-permute-done | bytes 167968 | tf_op jit(solution)/shard_map/ppermute | solution.py:615
  16.8 4.0 %step_0.1 = (f32[3,16,16,128]{3,2,1,0:T(8,128)S(1)}, f32[3,8,8,256]{3,2,1,0:T(8,128)S(1)}, f32[8,128]{1,0:T(8,128)S(1)}, f32[288,128]{1,0:T(8,128)S(1)}, f32[288...) custom-call(s32[6]{0:T(128)S(1)} %stack.36.flags, ...), custom_call_target="tpu_custom_call" | custom-call | flops 4000000 | bytes 1048576 | tf_op jit(solution)/shard_map/step_0/pallas_call | solution.py:523
  20.7 1.8 %collective-permute-start.4 = (f32[288,128]{1,0:T(8,128)S(1)}, f32[288,128]{1,0:T(8,128)S(1)}, u32[]{:S(2)}, u32[]{:S(2)}) collective-permute-start(f32[288,128]{1,0:T(8,128)S(1)} %get-tuple-element.75), channel_id=1, source_target_pairs={{0,8},{1,9},{2,10},{3,11},{4,12},{5,13},{6,14},{7,15},{8,0},{9,1},... | collective-permute-start | bytes 442376 | tf_op jit(solution)/shard_map/ppermute | solution.py:615
  22.6 1.3 %collective-permute-start.5 = (f32[288,128]{1,0:T(8,128)S(1)}, f32[288,128]{1,0:T(8,128)S(1)}, u32[]{:S(2)}, u32[]{:S(2)}) collective-permute-start(f32[288,128]{1,0:T(8,128)S(1)} %get-tuple-element.76), channel_id=1, source_target_pairs={{0,1},{1,0},{2,3},{3,2},{4,5},{5,4},{6,7},{7,6},{8,16},{9,17},{10,... | collective-permute-start | bytes 442376 | tf_op jit(solution)/shard_map/ppermute | solution.py:615
  23.9 1.9 %collective-permute-done.4.refs_5_.refs_23_ = f32[288,128]{1,0:T(8,128)S(1)} collective-permute-done((f32[288,128]{1,0:T(8,128)S(1)}, f32[288,128]{1,0:T(8,128)S(1)}, u32[]{:S(2)}, u32[]{:S(2)}) %collective-permute-start.4) | collective-permute-done | bytes 147488 | tf_op jit(solution)/shard_map/ppermute | solution.py:615
  26.5 1.7 %collective-permute-start.6 = (f32[184,2,128]{2,1,0:T(2,128)S(1)}, f32[184,2,128]{2,1,0:T(2,128)S(1)}, u32[]{:S(2)}, u32[]{:S(2)}) collective-permute-start(f32[184,2,128]{2,1,0:T(2,128)S(1)} %get-tuple-element.78), channel_id=1, source_target_pairs={{0,1},{1,0},{2,3},{3,2},{4,5},{5,4},{6,7},{7,6},{8,9},{9,8},{10,11... | collective-permute-start | bytes 565256 | tf_op jit(solution)/shard_map/ppermute | solution.py:615
  29.2 4.2 %collective-permute-done.7.refs_26_ = f32[184,2,128]{2,1,0:T(2,128)S(1)} collective-permute-done((f32[184,2,128]{2,1,0:T(2,128)S(1)}, f32[184,2,128]{2,1,0:T(2,128)S(1)}, u32[]{:S(2)}, u32[]{:S(2)}) %collective-permute-start.7) | collective-permute-done | bytes 188448 | tf_op jit(solution)/shard_map/ppermute | solution.py:615
  33.5 3.9 %step_1.1 = (f32[3,16,16,128]{3,2,1,0:T(8,128)S(1)}, f32[3,8,8,256]{3,2,1,0:T(8,128)S(1)}, f32[8,128]{1,0:T(8,128)S(1)}, f32[192,128]{1,0:T(8,128)S(1)}, f32[192,128]{1,0:T(8,128)S(1)}) custom-call(s32[6]{0:T(128)S(1)} %stack.36.flags, f32[3,16,16,128]{3,2,1,0:T(8,128)S(1)} %get-tuple-element.67.refs_0_.refs_2_, ...), custom_call_target="tpu_custom_call" | custom-call | flops 4000000 | bytes 1048576 | tf_op jit(solution)/shard_map/step_1/pallas_call | solution.py:523
  37.4 2.9 %collective-permute-start.10 = (f32[192,128]{1,0:T(8,128)S(1)}, f32[192,128]{1,0:T(8,128)S(1)}, u32[]{:S(2)}, u32[]{:S(2)}) collective-permute-start(f32[192,128]{1,0:T(8,128)S(1)} %get-tuple-element.81), channel_id=1, source_target_pairs={{0,8},{1,9},{2,10},{3,11},{4,12},{5,13},{6,14},{7,15},{8,0},{9,1},... | collective-permute-start | bytes 294920 | tf_op jit(solution)/shard_map/ppermute | solution.py:615
  40.3 1.3 %collective-permute-start.11 = (f32[192,128]{1,0:T(8,128)S(1)}, f32[192,128]{1,0:T(8,128)S(1)}, u32[]{:S(2)}, u32[]{:S(2)}) collective-permute-start(f32[192,128]{1,0:T(8,128)S(1)} %get-tuple-element.82), channel_id=1, source_target_pairs={{0,1},{1,0},{2,3},{3,2},{4,5},{5,4},{6,7},{7,6},{8,16},{9,17},{10,... | collective-permute-start | bytes 294920 | tf_op jit(solution)/shard_map/ppermute | solution.py:615
  42.7 3.0 %collective-permute-done.9 = f32[8,128]{1,0:T(8,128)S(1)} collective-permute-done((f32[8,128]{1,0:T(8,128)S(1)}, f32[8,128]{1,0:T(8,128)S(1)}, u32[]{:S(2)}, u32[]{:S(2)}) %collective-permute-start.9) | collective-permute-done | bytes 4128 | tf_op jit(solution)/shard_map/ppermute | solution.py:615
  46.9 2.5 %collective-permute-start.12 = (f32[8,128]{1,0:T(8,128)S(1)}, f32[8,128]{1,0:T(8,128)S(1)}, u32[]{:S(2)}, u32[]{:S(2)}) collective-permute-start(f32[8,128]{1,0:T(8,128)S(1)} %add.67), channel_id=1, source_target_pairs={{0,7},{1,6},{2,5},{3,4},{4,3},{5,2},{6,1},{7,0},{8,15},{9,14},{10,... | collective-permute-start | bytes 12296 | tf_op jit(solution)/shard_map/ppermute | solution.py:615
  49.4 2.2 %collective-permute-done.12 = f32[8,128]{1,0:T(8,128)S(1)} collective-permute-done((f32[8,128]{1,0:T(8,128)S(1)}, f32[8,128]{1,0:T(8,128)S(1)}, u32[]{:S(2)}, u32[]{:S(2)}) %collective-permute-start.12) | collective-permute-done | bytes 4128 | tf_op jit(solution)/shard_map/ppermute | solution.py:615
  51.5 5.5 %collective-permute-start.13 = (f32[8,128]{1,0:T(8,128)S(1)}, f32[8,128]{1,0:T(8,128)S(1)}, u32[]{:S(2)}, u32[]{:S(2)}) collective-permute-start(f32[8,128]{1,0:T(8,128)S(1)} %add.68), channel_id=1, source_target_pairs={{0,9},{1,8},{2,11},{3,10},{4,13},{5,12},{6,15},{7,14},{8,1},{9,0},... | collective-permute-start | bytes 12296 | tf_op jit(solution)/shard_map/ppermute | solution.py:615
  58.3 3.2 %collective-permute-start.14 = (f32[8,128]{1,0:T(8,128)S(1)}, f32[8,128]{1,0:T(8,128)S(1)}, u32[]{:S(2)}, u32[]{:S(2)}) collective-permute-start(f32[8,128]{1,0:T(8,128)S(1)} %add.69), channel_id=1, source_target_pairs={{0,25},{1,24},{2,27},{3,26},{4,29},{5,28},{6,31},{7,30},{8,17},{9,... | collective-permute-start | bytes 12296 | tf_op jit(solution)/shard_map/ppermute | solution.py:615
  61.5 1.3 %collective-permute-done.14 = f32[8,128]{1,0:T(8,128)S(1)} collective-permute-done((f32[8,128]{1,0:T(8,128)S(1)}, f32[8,128]{1,0:T(8,128)S(1)}, u32[]{:S(2)}, u32[]{:S(2)}) %collective-permute-start.14) | collective-permute-done | bytes 4128 | tf_op jit(solution)/shard_map/ppermute | solution.py:615
  62.8 2.7 %collective-permute-start.15 = (f32[8,128]{1,0:T(8,128)S(1)}, f32[8,128]{1,0:T(8,128)S(1)}, u32[]{:S(2)}, u32[]{:S(2)}) collective-permute-start(f32[8,128]{1,0:T(8,128)S(1)} %add.70), channel_id=1, source_target_pairs={{0,33},{1,32},{2,35},{3,34},{4,37},{5,36},{6,39},{7,38},{8,41},{9,... | collective-permute-start | bytes 12296 | tf_op jit(solution)/shard_map/ppermute | solution.py:615
  66.8 5.9 %collective-permute-start.16 = (f32[8,128]{1,0:T(8,128)S(1)}, f32[8,128]{1,0:T(8,128)S(1)}, u32[]{:S(2)}, u32[]{:S(2)}) collective-permute-start(f32[8,128]{1,0:T(8,128)S(1)} %add.71), channel_id=1, source_target_pairs={{0,65},{1,64},{2,67},{3,66},{4,69},{5,68},{6,71},{7,70},{8,73},{9,... | collective-permute-start | bytes 12296 | tf_op jit(solution)/shard_map/ppermute | solution.py:615
  74.0 3.9 %collective-permute-start.17 = (f32[8,128]{1,0:T(8,128)S(1)}, f32[8,128]{1,0:T(8,128)S(1)}, u32[]{:S(2)}, u32[]{:S(2)}) collective-permute-start(f32[8,128]{1,0:T(8,128)S(1)} %add.72), channel_id=1, source_target_pairs={{0,225},{1,224},{2,227},{3,226},{4,229},{5,228},{6,231},{7,230},{8... | collective-permute-start | bytes 12296 | tf_op jit(solution)/shard_map/ppermute | solution.py:615
  77.9 3.5 %step_2.1 = (f32[3,16,16,128]{3,2,1,0:T(8,128)}, f32[3,8,8,256]{3,2,1,0:T(8,128)}) custom-call(s32[6]{0:T(128)S(1)} %stack.36.flags, f32[3,16,16,128]{3,2,1,0:T(8,128)S(1)} %get-tuple-element.84.refs_0_, f32[3,8,8,256]{3,2,1,0:T(8,128)S(1)} %get-tuple-element.85.refs_1_, f32[3,16,16,128]{3,2,1,0:T(8,128)S(1)} %get-tuple-element.67.refs_0_.refs_2_, ...), custom_call_target="tpu_custom_call" | custom-call | flops 4000000 | bytes 1048576 | tf_op jit(solution)/shard_map/step_2/pallas_call | solution.py:523
  (65 shorter events, 11.7 us)
Async XLA Ops:
  0.8 5.2 %copy-start.3 = (f32[16,16,128]{2,1,0:T(8,128)S(1)}, f32[16,16,128]{2,1,0:T(8,128)}, u32[]{:S(2)}) copy-start(f32[16,16,128]{2,1,0:T(8,128)} %refs_16_.1) | copy-start | bytes 393220
  2.5 4.5 %collective-permute-start = (f32[256,128]{1,0:T(8,128)S(1)}, f32[256,128]{1,0:T(8,128)S(1)}, u32[]{:S(2)}, u32[]{:S(2)}) collective-permute-start(f32[256,128]{1,0:T(8,128)S(1)} %get-tuple-element.63), channel_id=1, source_target_pairs={{0,8},{1,9},{2,10},{3,11},{4,12},{5,13},{6,14},{7,15},{8,0},{9,1},... | collective-permute-start | bytes 393224 | tf_op jit(solution)/shard_map/ppermute | solution.py:615
  4.6 2.4 %collective-permute-start.1 = (f32[256,128]{1,0:T(8,128)S(1)}, f32[256,128]{1,0:T(8,128)S(1)}, u32[]{:S(2)}, u32[]{:S(2)}) collective-permute-start(f32[256,128]{1,0:T(8,128)S(1)} %get-tuple-element.64), channel_id=1, source_target_pairs={{0,1},{1,0},{2,3},{3,2},{4,5},{5,4},{6,7},{7,6},{8,16},{9,17},{10,... | collective-permute-start | bytes 393224 | tf_op jit(solution)/shard_map/ppermute | solution.py:615
  6.2 5.4 %copy-start.12 = (s32[2,16,16]{2,1,0:T(8,128)S(1)}, s32[2,16,16]{2,1,0:T(8,128)}, u32[]{:S(2)}) copy-start(s32[2,16,16]{2,1,0:T(8,128)} %param.25) | copy-start | bytes 6148
  7.0 9.8 %copy-start.6 = (f32[3,16,16,128]{3,2,1,0:T(8,128)S(1)}, f32[3,16,16,128]{3,2,1,0:T(8,128)}, u32[]{:S(2)}) copy-start(f32[3,16,16,128]{3,2,1,0:T(8,128)} %refs_2_.4) | copy-start | bytes 1179652
  7.0 9.8 %copy-start.7 = (f32[3,8,8,256]{3,2,1,0:T(8,128)S(1)}, f32[3,8,8,256]{3,2,1,0:T(8,128)}, u32[]{:S(2)}) copy-start(f32[3,8,8,256]{3,2,1,0:T(8,128)} %refs_3_.4) | copy-start | bytes 589828
  7.7 4.9 %collective-permute-start.2 = (f32[164,2,128]{2,1,0:T(2,128)S(1)}, f32[164,2,128]{2,1,0:T(2,128)S(1)}, u32[]{:S(2)}, u32[]{:S(2)}) collective-permute-start(f32[164,2,128]{2,1,0:T(2,128)S(1)} %get-tuple-element.65), channel_id=1, source_target_pairs={{0,1},{1,0},{2,3},{3,2},{4,5},{5,4},{6,7},{7,6},{8,9},{9,8},{10,11... | collective-permute-start | bytes 503816 | tf_op jit(solution)/shard_map/ppermute | solution.py:615
  11.6 5.1 %collective-permute-start.3 = (f32[164,2,128]{2,1,0:T(2,128)S(1)}, f32[164,2,128]{2,1,0:T(2,128)S(1)}, u32[]{:S(2)}, u32[]{:S(2)}) collective-permute-start(f32[164,2,128]{2,1,0:T(2,128)S(1)} %get-tuple-element.66), channel_id=1, source_target_pairs={{0,7},{1,2},{2,1},{3,4},{4,3},{5,6},{6,5},{7,0},{8,15},{9,10},{10,... | collective-permute-start | bytes 503816 | tf_op jit(solution)/shard_map/ppermute | solution.py:615
  20.7 5.0 %collective-permute-start.4 = (f32[288,128]{1,0:T(8,128)S(1)}, f32[288,128]{1,0:T(8,128)S(1)}, u32[]{:S(2)}, u32[]{:S(2)}) collective-permute-start(f32[288,128]{1,0:T(8,128)S(1)} %get-tuple-element.75), channel_id=1, source_target_pairs={{0,8},{1,9},{2,10},{3,11},{4,12},{5,13},{6,14},{7,15},{8,0},{9,1},... | collective-permute-start | bytes 442376 | tf_op jit(solution)/shard_map/ppermute | solution.py:615
  22.6 3.2 %collective-permute-start.5 = (f32[288,128]{1,0:T(8,128)S(1)}, f32[288,128]{1,0:T(8,128)S(1)}, u32[]{:S(2)}, u32[]{:S(2)}) collective-permute-start(f32[288,128]{1,0:T(8,128)S(1)} %get-tuple-element.76), channel_id=1, source_target_pairs={{0,1},{1,0},{2,3},{3,2},{4,5},{5,4},{6,7},{7,6},{8,16},{9,17},{10,... | collective-permute-start | bytes 442376 | tf_op jit(solution)/shard_map/ppermute | solution.py:615
  26.5 2.7 %collective-permute-start.6 = (f32[184,2,128]{2,1,0:T(2,128)S(1)}, f32[184,2,128]{2,1,0:T(2,128)S(1)}, u32[]{:S(2)}, u32[]{:S(2)}) collective-permute-start(f32[184,2,128]{2,1,0:T(2,128)S(1)} %get-tuple-element.78), channel_id=1, source_target_pairs={{0,1},{1,0},{2,3},{3,2},{4,5},{5,4},{6,7},{7,6},{8,9},{9,8},{10,11... | collective-permute-start | bytes 565256 | tf_op jit(solution)/shard_map/ppermute | solution.py:615
  28.2 5.3 %collective-permute-start.7 = (f32[184,2,128]{2,1,0:T(2,128)S(1)}, f32[184,2,128]{2,1,0:T(2,128)S(1)}, u32[]{:S(2)}, u32[]{:S(2)}) collective-permute-start(f32[184,2,128]{2,1,0:T(2,128)S(1)} %get-tuple-element.79), channel_id=1, source_target_pairs={{0,7},{1,2},{2,1},{3,4},{4,3},{5,6},{6,5},{7,0},{8,15},{9,10},{10,... | collective-permute-start | bytes 565256 | tf_op jit(solution)/shard_map/ppermute | solution.py:615
  37.4 8.4 %collective-permute-start.10 = (f32[192,128]{1,0:T(8,128)S(1)}, f32[192,128]{1,0:T(8,128)S(1)}, u32[]{:S(2)}, u32[]{:S(2)}) collective-permute-start(f32[192,128]{1,0:T(8,128)S(1)} %get-tuple-element.81), channel_id=1, source_target_pairs={{0,8},{1,9},{2,10},{3,11},{4,12},{5,13},{6,14},{7,15},{8,0},{9,1},... | collective-permute-start | bytes 294920 | tf_op jit(solution)/shard_map/ppermute | solution.py:615
  40.3 5.5 %collective-permute-start.11 = (f32[192,128]{1,0:T(8,128)S(1)}, f32[192,128]{1,0:T(8,128)S(1)}, u32[]{:S(2)}, u32[]{:S(2)}) collective-permute-start(f32[192,128]{1,0:T(8,128)S(1)} %get-tuple-element.82), channel_id=1, source_target_pairs={{0,1},{1,0},{2,3},{3,2},{4,5},{5,4},{6,7},{7,6},{8,16},{9,17},{10,... | collective-permute-start | bytes 294920 | tf_op jit(solution)/shard_map/ppermute | solution.py:615
  41.6 1.2 %collective-permute-start.8 = (f32[8,128]{1,0:T(8,128)S(1)}, f32[8,128]{1,0:T(8,128)S(1)}, u32[]{:S(2)}, u32[]{:S(2)}) collective-permute-start(f32[8,128]{1,0:T(8,128)S(1)} %get-tuple-element.80), channel_id=1, source_target_pairs={{0,1},{1,0},{2,3},{3,2},{4,5},{5,4},{6,7},{7,6},{8,9},{9,8},{10,11... | collective-permute-start | bytes 12296 | tf_op jit(solution)/shard_map/ppermute | solution.py:615
  42.7 3.0 %collective-permute-start.9 = (f32[8,128]{1,0:T(8,128)S(1)}, f32[8,128]{1,0:T(8,128)S(1)}, u32[]{:S(2)}, u32[]{:S(2)}) collective-permute-start(f32[8,128]{1,0:T(8,128)S(1)} %add.66), channel_id=1, source_target_pairs={{0,3},{1,2},{2,1},{3,0},{4,7},{5,6},{6,5},{7,4},{8,11},{9,10},{10,... | collective-permute-start | bytes 12296 | tf_op jit(solution)/shard_map/ppermute | solution.py:615
  46.5 31.5 %collective-permute-start.18 = (f32[132,2,128]{2,1,0:T(2,128)S(1)}, f32[132,2,128]{2,1,0:T(2,128)S(1)}, u32[]{:S(2)}, u32[]{:S(2)}) collective-permute-start(f32[132,2,128]{2,1,0:T(2,128)S(1)} %get-tuple-element.88), channel_id=1, source_target_pairs={{0,1},{1,0},{2,3},{3,2},{4,5},{5,4},{6,7},{7,6},{8,9},{9,8},{10,11... | collective-permute-start | bytes 405512 | tf_op jit(solution)/shard_map/ppermute | solution.py:615
  46.7 31.2 %collective-permute-start.19 = (f32[132,2,128]{2,1,0:T(2,128)S(1)}, f32[132,2,128]{2,1,0:T(2,128)S(1)}, u32[]{:S(2)}, u32[]{:S(2)}) collective-permute-start(f32[132,2,128]{2,1,0:T(2,128)S(1)} %get-tuple-element.89), channel_id=1, source_target_pairs={{0,7},{1,2},{2,1},{3,4},{4,3},{5,6},{6,5},{7,0},{8,15},{9,10},{10,... | collective-permute-start | bytes 405512 | tf_op jit(solution)/shard_map/ppermute | solution.py:615
  46.9 4.6 %collective-permute-start.12 = (f32[8,128]{1,0:T(8,128)S(1)}, f32[8,128]{1,0:T(8,128)S(1)}, u32[]{:S(2)}, u32[]{:S(2)}) collective-permute-start(f32[8,128]{1,0:T(8,128)S(1)} %add.67), channel_id=1, source_target_pairs={{0,7},{1,6},{2,5},{3,4},{4,3},{5,2},{6,1},{7,0},{8,15},{9,14},{10,... | collective-permute-start | bytes 12296 | tf_op jit(solution)/shard_map/ppermute | solution.py:615
  51.5 6.8 %collective-permute-start.13 = (f32[8,128]{1,0:T(8,128)S(1)}, f32[8,128]{1,0:T(8,128)S(1)}, u32[]{:S(2)}, u32[]{:S(2)}) collective-permute-start(f32[8,128]{1,0:T(8,128)S(1)} %add.68), channel_id=1, source_target_pairs={{0,9},{1,8},{2,11},{3,10},{4,13},{5,12},{6,15},{7,14},{8,1},{9,0},... | collective-permute-start | bytes 12296 | tf_op jit(solution)/shard_map/ppermute | solution.py:615
  58.3 4.5 %collective-permute-start.14 = (f32[8,128]{1,0:T(8,128)S(1)}, f32[8,128]{1,0:T(8,128)S(1)}, u32[]{:S(2)}, u32[]{:S(2)}) collective-permute-start(f32[8,128]{1,0:T(8,128)S(1)} %add.69), channel_id=1, source_target_pairs={{0,25},{1,24},{2,27},{3,26},{4,29},{5,28},{6,31},{7,30},{8,17},{9,... | collective-permute-start | bytes 12296 | tf_op jit(solution)/shard_map/ppermute | solution.py:615
  62.8 4.0 %collective-permute-start.15 = (f32[8,128]{1,0:T(8,128)S(1)}, f32[8,128]{1,0:T(8,128)S(1)}, u32[]{:S(2)}, u32[]{:S(2)}) collective-permute-start(f32[8,128]{1,0:T(8,128)S(1)} %add.70), channel_id=1, source_target_pairs={{0,33},{1,32},{2,35},{3,34},{4,37},{5,36},{6,39},{7,38},{8,41},{9,... | collective-permute-start | bytes 12296 | tf_op jit(solution)/shard_map/ppermute | solution.py:615
  66.8 7.2 %collective-permute-start.16 = (f32[8,128]{1,0:T(8,128)S(1)}, f32[8,128]{1,0:T(8,128)S(1)}, u32[]{:S(2)}, u32[]{:S(2)}) collective-permute-start(f32[8,128]{1,0:T(8,128)S(1)} %add.71), channel_id=1, source_target_pairs={{0,65},{1,64},{2,67},{3,66},{4,69},{5,68},{6,71},{7,70},{8,73},{9,... | collective-permute-start | bytes 12296 | tf_op jit(solution)/shard_map/ppermute | solution.py:615
  74.0 7.4 %collective-permute-start.17 = (f32[8,128]{1,0:T(8,128)S(1)}, f32[8,128]{1,0:T(8,128)S(1)}, u32[]{:S(2)}, u32[]{:S(2)}) collective-permute-start(f32[8,128]{1,0:T(8,128)S(1)} %add.72), channel_id=1, source_target_pairs={{0,225},{1,224},{2,227},{3,226},{4,229},{5,228},{6,231},{7,230},{8... | collective-permute-start | bytes 12296 | tf_op jit(solution)/shard_map/ppermute | solution.py:615
  (9 other events, 35.6 us)

commit v5 on v4

--- a/solution.py
+++ b/solution.py
@@ -18,6 +18,12 @@
 VMEM_LIMIT = 20 * 1024 * 1024
 
 EVEN_X, HAS_XM, HAS_XP, EVEN_Y, HAS_YM, HAS_YP = range(6)
+
+
+def where_am_i():
+    x = 4 * lax.axis_index("gx_0") + lax.axis_index("gx_1")
+    y = 2 * lax.axis_index("gy_0") + lax.axis_index("gy_1")
+    return x % 2 == 0, x > 0, x < 31, y % 2 == 0, y > 0, y < 7
 
 
 class Sizes:
@@ -53,7 +59,7 @@
 
 
 def put_x(s, flags, outs, fine, coarse, betas=None, spread=None):
-    even = flags[EVEN_X] == 1
+    even = flags[EVEN_X]
     for k, out in enumerate(outs):
         far = even if k == 0 else jnp.logical_not(even)
         start_f = jnp.where(far, s.fx - 2, 0)
@@ -75,15 +81,16 @@
         out[s.x_spread : s.x_rows_beta, :] = spread[pl.ds(start, 2)].reshape(2 * s.spread, LANES)
 
 
-def first_kernel(s, flags, fine, coarse, rig_f, met_f, rig_c, met_c, out_a, out_b, *scratch):
+def first_kernel(s, fine, coarse, rig_f, met_f, rig_c, met_c, out_a, out_b, *scratch):
     strip_f, strip_c, line_f, line_c, sems = scratch
+    flags = where_am_i()
     copies = []
 
     def fetch(source, target):
         copies.append(pltpu.make_async_copy(source, target, sems.at[len(copies)]))
         copies[-1].start()
 
-    even = flags[EVEN_X] == 1
+    even = flags[EVEN_X]
     for k in range(2):
         far = even if k == 0 else jnp.logical_not(even)
         fetch(fine.at[:, pl.ds(jnp.where(far, s.fx - 2, 0), 2)], strip_f.at[k])
@@ -107,17 +114,18 @@
 
 
 def sides(flags, even, has_low, has_high, a, b):
-    low = jnp.where(flags[even] == 1, b, a)
-    high = jnp.where(flags[even] == 1, a, b)
-    low = jnp.where(flags[has_low] == 1, low, 0.0)
-    high = jnp.where(flags[has_high] == 1, high, 0.0)
+    low = jnp.where(flags[even], b, a)
+    high = jnp.where(flags[even], a, b)
+    low = jnp.where(flags[has_low], low, 0.0)
+    high = jnp.where(flags[has_high], high, 0.0)
     return low, high
 
 
-def middle_kernel(s, step, flags, *refs):
+def middle_kernel(s, step, *refs):
+    flags = where_am_i()
     fine, coarse, *mats, in_a, in_b = refs[:-2] if step != 1 else refs[:-3]
     out_a, out_b = refs[-2:] if step != 1 else refs[-3:-1]
-    even = flags[EVEN_Y] == 1
+    even = flags[EVEN_Y]
 
     def put(index, low, high):
         out_a[index] = jnp.where(even, high, low)
@@ -266,24 +274,24 @@
         for m in range(2):
             base = s.x_fine_mats + m * y if fine else s.x_coarse_mats + (m * s.halves + h) * y
             rows = slice(base, base + y)
-            even = flags[EVEN_X] == 1
+            even = flags[EVEN_X]
             a, b = x_in[0][rows, :], x_in[1][rows, :]
             got.append((jnp.where(even, b, a), jnp.where(even, a, b)))
         for side, (flag, place) in enumerate(((HAS_XM, 0), (HAS_XP, x + 1))):
             rig, met = got[0][side], got[1][side]
-            wide_ext[place, 1 : 1 + y, at] = jnp.where(flags[flag] == 1, rig * met, 0.0)
-            inv_ext[place, 1 : 1 + y, at] = jnp.where(flags[flag] == 1, 1.0 / met, 0.0)
+            wide_ext[place, 1 : 1 + y, at] = jnp.where(flags[flag], rig * met, 0.0)
+            inv_ext[place, 1 : 1 + y, at] = jnp.where(flags[flag], 1.0 / met, 0.0)
         start = s.y_fine_mats if fine else s.y_coarse_mats + h * x
         rows = slice(start, start + x)
         got = []
         for m in range(2):
-            even = flags[EVEN_Y] == 1
+            even = flags[EVEN_Y]
             a, b = y_in[0][rows, m : m + 1, :], y_in[1][rows, m : m + 1, :]
             got.append((jnp.where(even, b, a), jnp.where(even, a, b)))
         for side, (flag, place) in enumerate(((HAS_YM, 0), (HAS_YP, 1 + y))):
             rig, met = got[0][side], got[1][side]
-            wide_ext[1 : 1 + x, place : place + 1, at] = jnp.where(flags[flag] == 1, rig * met, 0.0)
-            inv_ext[1 : 1 + x, place : place + 1, at] = jnp.where(flags[flag] == 1, 1.0 / met, 0.0)
+            wide_ext[1 : 1 + x, place : place + 1, at] = jnp.where(flags[flag], rig * met, 0.0)
+            inv_ext[1 : 1 + x, place : place + 1, at] = jnp.where(flags[flag], 1.0 / met, 0.0)
 
 
 def fill_divergence(x, y, ext, inv_ext, div):
@@ -361,7 +369,8 @@
     return lax.fori_loop(0, x, row, start, unroll=4)
 
 
-def step_kernel(s, step, cells, flags, *refs):
+def step_kernel(s, step, cells, *refs):
+    flags = where_am_i()
     refs = list(refs)
 
     def take(n):
@@ -511,11 +520,10 @@
 
 
 VMEM = pl.BlockSpec(memory_space=pltpu.VMEM)
-SMEM = pl.BlockSpec(memory_space=pltpu.SMEM)
 HBM = pl.BlockSpec(memory_space=pltpu.HBM)
 
 
-def call(kernel, shapes, flops, *args, scratch=(), name=None, specs=None, sems=0):
+def call(kernel, shapes, flops, *args, scratch=(), spec=VMEM, sems=0):
     shapes = [jax.ShapeDtypeStruct(shape, jnp.float32) for shape in shapes]
     scratch = [pltpu.VMEM(shape, jnp.float32) for shape in scratch]
     if sems:
@@ -523,12 +531,11 @@
     return pl.pallas_call(
         kernel,
         out_shape=shapes,
-        in_specs=specs or [SMEM] + [VMEM] * (len(args) - 1),
+        in_specs=[spec] * len(args),
         out_specs=[VMEM] * len(shapes),
         scratch_shapes=scratch,
         compiler_params=pltpu.CompilerParams(vmem_limit_bytes=VMEM_LIMIT),
         cost_estimate=pl.CostEstimate(flops=flops, bytes_accessed=1 << 20, transcendentals=0),
-        name=name,
     )(*args)
 
 
@@ -599,17 +606,6 @@
     fine_shape, coarse_shape = fine_metric.shape, coarse_metric.shape
     s = Sizes(fine_shape, coarse_shape)
     count_x, count_y = lax.axis_size(GX), lax.axis_size(GY)
-    place_x, place_y = lax.axis_index(GX), lax.axis_index(GY)
-    flags = jnp.stack(
-        [
-            (place_x % 2 == 0).astype(jnp.int32),
-            (place_x > 0).astype(jnp.int32),
-            (place_x < count_x - 1).astype(jnp.int32),
-            (place_y % 2 == 0).astype(jnp.int32),
-            (place_y > 0).astype(jnp.int32),
-            (place_y < count_y - 1).astype(jnp.int32),
-        ]
-    )
 
     def swap(value, move):
         return lax.ppermute(value, ALL, swap_pairs(mesh, move))
@@ -625,7 +621,6 @@
         functools.partial(first_kernel, s),
         [(s.x_rows_mats, LANES)] * 2,
         1000,
-        flags,
         *(
             pltpu.with_memory_space_constraint(x, pltpu.HBM)
             for x in (
@@ -643,14 +638,13 @@
             (2, 2, s.fy, s.fz),
             (2, 2, s.cy, s.cz),
         ],
-        specs=[SMEM] + [HBM] * 6,
+        spec=HBM,
         sems=12,
-        name="first_strips",
     )
     own = []
-    for tag, density, lame, rigidity, metric in (
-        ("fine", fine_density, fine_lame, fine_rigidity, fine_metric),
-        ("coarse", coarse_density, coarse_lame, coarse_rigidity, coarse_metric),
+    for density, lame, rigidity, metric in (
+        (fine_density, fine_lame, fine_rigidity, fine_metric),
+        (coarse_density, coarse_lame, coarse_rigidity, coarse_metric),
     ):
         own.append(
             call(
@@ -661,8 +655,6 @@
                 lame,
                 rigidity,
                 metric,
-                name=f"own_{tag}",
-                specs=[VMEM] * 4,
             )
         )
     inverse_f, *coef_f, beta_f = own[0]
@@ -684,12 +676,10 @@
     for step in range(STEPS):
         x_in = swap_both(x_out, beside_x, across_x)
         if step == 2:
-            for move in TOTAL[:2]:
-                energy = energy + swap(energy, move)
-            energy, *x_in = lax.optimization_barrier((energy, *x_in))
-            for move in TOTAL[2:-1]:
-                energy = energy + swap(energy, move)
-            other = swap(energy, TOTAL[-1])
+            for k, move in enumerate(TOTAL):
+                other = swap(energy, move)
+                if k < len(TOTAL) - 1:
+                    energy = energy + other
         shapes = [((s.y_rows_mats, s.y_rows_beta, s.y_rows)[step], 2, LANES)] * 2
         if step == 0:
             mats = [fine_rigidity, fine_metric, coarse_rigidity, coarse_metric]
@@ -700,12 +690,10 @@
             functools.partial(middle_kernel, s, step),
             shapes,
             1000,
-            flags,
             fine,
             coarse,
             *(mats if step < 2 else ()),
             *x_in,
-            name=f"corner_strips_{step}",
         )
         y_in = swap_both(y_out[:2], beside_y, across_y)
         shapes = [fine.shape, coarse.shape]
@@ -732,7 +720,6 @@
             functools.partial(step_kernel, s, step, cells),
             shapes,
             4_000_000,
-            flags,
             fine,
             coarse,
             fine_prev,
@@ -744,7 +731,6 @@
             *x_in,
             *y_in,
             scratch=scratch + more_scratch,
-            name=f"step_{step}",
         )
         fine_prev, coarse_prev = fine, coarse
         fine, coarse = outs[:2]
@@ -762,10 +748,10 @@
     finer = Mesh(mesh.devices.reshape(8, 4, 4, 2), ALL)
     level, cell = P(None, GX, GY, None), P(GX, GY, None)
     in_specs = (level,) * 4 + (cell,) * 8 + (P(None, GX, GY),)
+
+    def body(*args):
+        return per_device(finer, *args)
+
     return jax.shard_map(
-        functools.partial(per_device, finer),
-        mesh=finer,
-        in_specs=in_specs,
-        out_specs=(level, level, P()),
-        check_vma=False,
+        body, mesh=finer, in_specs=in_specs, out_specs=(level, level, P()), check_vma=False
     )

time: 82.4 us -> 82.8 us (level)
  Pallas kernels: 15.3 us -> 11.7 us
  starting transfers between devices: 40.4 us -> 42.7 us
  waiting for transfers between devices: 24.5 us -> 26.5 us
    pallas_call x9, Pallas kernels: 15.3 us -> 11.7 us  [call(): pl.pallas_call(kernel, out_shape=shapes, in_specs=[spec] * len(args), out...]
    ppermute x20, starting transfers between devices: 40.4 us -> 42.7 us  [swap(): return lax.ppermute(value, ALL, swap_pairs(mesh, move))]
    ppermute x20, waiting for transfers between devices: 24.5 us -> 26.5 us  [swap(): return lax.ppermute(value, ALL, swap_pairs(mesh, move))]
  transfers between devices with their start and end apart: 20 -> 20, of which waited for: 13 -> 15; matrix products, arithmetic and copies ran while one was open for 0% -> 0% of each run, Pallas kernels for 5% -> 4%
where the time goes in v5:
time: 82.8 us; the launch traced here: 82.6 us
  starting transfers between devices  42.7 us (52%)
  waiting for transfers between devices  26.5 us (32%)
  Pallas kernels  11.7 us (14%)
  local copies, waits for them, and re-layouts  0.93 us (1%)
  between operations  0.85 us (1%)
    ppermute x20, starting transfers between devices, swap(): return lax.ppermute(value, ALL, swap_pairs(mesh, move))  42.7 us
    ppermute x20, waiting for transfers between devices, swap(): return lax.ppermute(value, ALL, swap_pairs(mesh, move))  26.5 us
    pallas_call x9, Pallas kernels, call(): pl.pallas_call(kernel, out_shape=shapes, in_specs=[spec] * len(args), out...  11.7 us
  transfers between devices with their start and end apart: 20, of which 15 were waited for; matrix products, arithmetic and copies ran while one was open for 0% of the time, Pallas kernels for 4%

profile of v5, /device:TPU:1, one launch (start us, length us, event | category | flops | bytes accessed | tf_op | source)
XLA Modules:
  0.0 82.6 jit_solution(10399830200993036013)
XLA Ops:
  1.9 2.1 %collective-permute-start = (f32[256,128]{1,0:T(8,128)S(1)}, f32[256,128]{1,0:T(8,128)S(1)}, u32[]{:S(2)}, u32[]{:S(2)}) collective-permute-start(f32[256,128]{1,0:T(8,128)S(1)} %get-tuple-element.60), channel_id=1, source_target_pairs={{0,8},{1,9},{2,10},{3,11},{4,12},{5,13},{6,14},{7,15},{8,0},{9,1},... | collective-permute-start | bytes 393224 | tf_op jit(solution)/shard_map/ppermute | solution.py:611
  4.0 1.3 %collective-permute-start.1 = (f32[256,128]{1,0:T(8,128)S(1)}, f32[256,128]{1,0:T(8,128)S(1)}, u32[]{:S(2)}, u32[]{:S(2)}) collective-permute-start(f32[256,128]{1,0:T(8,128)S(1)} %get-tuple-element.61), channel_id=1, source_target_pairs={{0,1},{1,0},{2,3},{3,2},{4,5},{5,4},{6,7},{7,6},{8,16},{9,17},{10,... | collective-permute-start | bytes 393224 | tf_op jit(solution)/shard_map/ppermute | solution.py:611
  6.6 3.9 %collective-permute-start.2 = (f32[164,2,128]{2,1,0:T(2,128)S(1)}, f32[164,2,128]{2,1,0:T(2,128)S(1)}, u32[]{:S(2)}, u32[]{:S(2)}) collective-permute-start(f32[164,2,128]{2,1,0:T(2,128)S(1)} %get-tuple-element.62), channel_id=1, source_target_pairs={{0,1},{1,0},{2,3},{3,2},{4,5},{5,4},{6,7},{7,6},{8,9},{9,8},{10,11... | collective-permute-start | bytes 503816 | tf_op jit(solution)/shard_map/ppermute | solution.py:611
  11.5 4.0 %collective-permute-done.3.refs_26_ = f32[164,2,128]{2,1,0:T(2,128)S(1)} collective-permute-done((f32[164,2,128]{2,1,0:T(2,128)S(1)}, f32[164,2,128]{2,1,0:T(2,128)S(1)}, u32[]{:S(2)}, u32[]{:S(2)}) %collective-permute-start.3) | collective-permute-done | bytes 167968 | tf_op jit(solution)/shard_map/ppermute | solution.py:611
  15.6 3.4 %shard_map.152 = (f32[3,16,16,128]{3,2,1,0:T(8,128)S(1)}, f32[3,8,8,256]{3,2,1,0:T(8,128)S(1)}, f32[8,128]{1,0:T(8,128)S(1)}, f32[288,128]{1,0:T(8,128)S(1)}, f3...) custom-call(f32[3,16,16,128]{3,2,1,0:T(8,128)S(1)} %copy-done, ...), custom_call_target="tpu_custom_call" | custom-call | flops 4000000 | bytes 1048576 | tf_op jit(solution)/shard_map/pallas_call | solution.py:531
  19.1 1.8 %collective-permute-start.4 = (f32[288,128]{1,0:T(8,128)S(1)}, f32[288,128]{1,0:T(8,128)S(1)}, u32[]{:S(2)}, u32[]{:S(2)}) collective-permute-start(f32[288,128]{1,0:T(8,128)S(1)} %get-tuple-element.72), channel_id=1, source_target_pairs={{0,8},{1,9},{2,10},{3,11},{4,12},{5,13},{6,14},{7,15},{8,0},{9,1},... | collective-permute-start | bytes 442376 | tf_op jit(solution)/shard_map/ppermute | solution.py:611
  20.9 1.3 %collective-permute-start.5 = (f32[288,128]{1,0:T(8,128)S(1)}, f32[288,128]{1,0:T(8,128)S(1)}, u32[]{:S(2)}, u32[]{:S(2)}) collective-permute-start(f32[288,128]{1,0:T(8,128)S(1)} %get-tuple-element.73), channel_id=1, source_target_pairs={{0,1},{1,0},{2,3},{3,2},{4,5},{5,4},{6,7},{7,6},{8,16},{9,17},{10,... | collective-permute-start | bytes 442376 | tf_op jit(solution)/shard_map/ppermute | solution.py:611
  22.2 1.9 %collective-permute-done.4.refs_5_.refs_23_ = f32[288,128]{1,0:T(8,128)S(1)} collective-permute-done((f32[288,128]{1,0:T(8,128)S(1)}, f32[288,128]{1,0:T(8,128)S(1)}, u32[]{:S(2)}, u32[]{:S(2)}) %collective-permute-start.4) | collective-permute-done | bytes 147488 | tf_op jit(solution)/shard_map/ppermute | solution.py:611
  24.3 1.7 %collective-permute-start.6 = (f32[184,2,128]{2,1,0:T(2,128)S(1)}, f32[184,2,128]{2,1,0:T(2,128)S(1)}, u32[]{:S(2)}, u32[]{:S(2)}) collective-permute-start(f32[184,2,128]{2,1,0:T(2,128)S(1)} %get-tuple-element.75), channel_id=1, source_target_pairs={{0,1},{1,0},{2,3},{3,2},{4,5},{5,4},{6,7},{7,6},{8,9},{9,8},{10,11... | collective-permute-start | bytes 565256 | tf_op jit(solution)/shard_map/ppermute | solution.py:611
  27.0 4.2 %collective-permute-done.7.refs_26_ = f32[184,2,128]{2,1,0:T(2,128)S(1)} collective-permute-done((f32[184,2,128]{2,1,0:T(2,128)S(1)}, f32[184,2,128]{2,1,0:T(2,128)S(1)}, u32[]{:S(2)}, u32[]{:S(2)}) %collective-permute-start.7) | collective-permute-done | bytes 188448 | tf_op jit(solution)/shard_map/ppermute | solution.py:611
  31.3 3.4 %shard_map.154 = (f32[3,16,16,128]{3,2,1,0:T(8,128)S(1)}, f32[3,8,8,256]{3,2,1,0:T(8,128)S(1)}, f32[8,128]{1,0:T(8,128)S(1)}, f32[192,128]{1,0:T(8,128)S(1)}, f32[192,128]{1,0:T(8,128)S(1)}) custom-call(f32[3,16,16,128]{3,2,1,0:T(8,128)S(1)} %get-tuple-element.64.refs_0_.refs_2_, f32[3,8,8,256]{3,2,1,0:T(8,128)S(1)} %get-tuple-element.65.refs_1_.refs_3_, ...), custom_call_target="tpu_custom_call" | custom-call | flops 4000000 | bytes 1048576 | tf_op jit(solution)/shard_map/pallas_call | solution.py:531
  34.7 2.9 %collective-permute-start.16 = (f32[192,128]{1,0:T(8,128)S(1)}, f32[192,128]{1,0:T(8,128)S(1)}, u32[]{:S(2)}, u32[]{:S(2)}) collective-permute-start(f32[192,128]{1,0:T(8,128)S(1)} %get-tuple-element.80), channel_id=1, source_target_pairs={{0,8},{1,9},{2,10},{3,11},{4,12},{5,13},{6,14},{7,15},{8,0},{9,1},... | collective-permute-start | bytes 294920 | tf_op jit(solution)/shard_map/ppermute | solution.py:611
  37.6 1.3 %collective-permute-start.17 = (f32[192,128]{1,0:T(8,128)S(1)}, f32[192,128]{1,0:T(8,128)S(1)}, u32[]{:S(2)}, u32[]{:S(2)}) collective-permute-start(f32[192,128]{1,0:T(8,128)S(1)} %get-tuple-element.81), channel_id=1, source_target_pairs={{0,1},{1,0},{2,3},{3,2},{4,5},{5,4},{6,7},{7,6},{8,16},{9,17},{10,... | collective-permute-start | bytes 294920 | tf_op jit(solution)/shard_map/ppermute | solution.py:611
  39.9 1.7 %collective-permute-start.18 = (f32[132,2,128]{2,1,0:T(2,128)S(1)}, f32[132,2,128]{2,1,0:T(2,128)S(1)}, u32[]{:S(2)}, u32[]{:S(2)}) collective-permute-start(f32[132,2,128]{2,1,0:T(2,128)S(1)} %get-tuple-element.82), channel_id=1, source_target_pairs={{0,1},{1,0},{2,3},{3,2},{4,5},{5,4},{6,7},{7,6},{8,9},{9,8},{10,11... | collective-permute-start | bytes 405512 | tf_op jit(solution)/shard_map/ppermute | solution.py:611
  42.2 1.8 %collective-permute-start.8 = (f32[8,128]{1,0:T(8,128)S(1)}, f32[8,128]{1,0:T(8,128)S(1)}, u32[]{:S(2)}, u32[]{:S(2)}) collective-permute-start(f32[8,128]{1,0:T(8,128)S(1)} %get-tuple-element.77), channel_id=1, source_target_pairs={{0,1},{1,0},{2,3},{3,2},{4,5},{5,4},{6,7},{7,6},{8,9},{9,8},{10,11... | collective-permute-start | bytes 12296 | tf_op jit(solution)/shard_map/ppermute | solution.py:611
  44.9 3.0 %collective-permute-done.9 = f32[8,128]{1,0:T(8,128)S(1)} collective-permute-done((f32[8,128]{1,0:T(8,128)S(1)}, f32[8,128]{1,0:T(8,128)S(1)}, u32[]{:S(2)}, u32[]{:S(2)}) %collective-permute-start.9) | collective-permute-done | bytes 4128 | tf_op jit(solution)/shard_map/ppermute | solution.py:611
  48.6 3.5 %collective-permute-done.10 = f32[8,128]{1,0:T(8,128)S(1)} collective-permute-done((f32[8,128]{1,0:T(8,128)S(1)}, f32[8,128]{1,0:T(8,128)S(1)}, u32[]{:S(2)}, u32[]{:S(2)}) %collective-permute-start.10) | collective-permute-done | bytes 4128 | tf_op jit(solution)/shard_map/ppermute | solution.py:611
  52.2 4.4 %collective-permute-start.11 = (f32[8,128]{1,0:T(8,128)S(1)}, f32[8,128]{1,0:T(8,128)S(1)}, u32[]{:S(2)}, u32[]{:S(2)}) collective-permute-start(f32[8,128]{1,0:T(8,128)S(1)} %add.51), channel_id=1, source_target_pairs={{0,9},{1,8},{2,11},{3,10},{4,13},{5,12},{6,15},{7,14},{8,1},{9,0},... | collective-permute-start | bytes 12296 | tf_op jit(solution)/shard_map/ppermute | solution.py:611
  57.9 4.6 %collective-permute-start.12 = (f32[8,128]{1,0:T(8,128)S(1)}, f32[8,128]{1,0:T(8,128)S(1)}, u32[]{:S(2)}, u32[]{:S(2)}) collective-permute-start(f32[8,128]{1,0:T(8,128)S(1)} %add.52), channel_id=1, source_target_pairs={{0,25},{1,24},{2,27},{3,26},{4,29},{5,28},{6,31},{7,30},{8,17},{9,... | collective-permute-start | bytes 12296 | tf_op jit(solution)/shard_map/ppermute | solution.py:611
  62.4 1.3 %collective-permute-done.12 = f32[8,128]{1,0:T(8,128)S(1)} collective-permute-done((f32[8,128]{1,0:T(8,128)S(1)}, f32[8,128]{1,0:T(8,128)S(1)}, u32[]{:S(2)}, u32[]{:S(2)}) %collective-permute-start.12) | collective-permute-done | bytes 4128 | tf_op jit(solution)/shard_map/ppermute | solution.py:611
  63.7 2.8 %collective-permute-start.13 = (f32[8,128]{1,0:T(8,128)S(1)}, f32[8,128]{1,0:T(8,128)S(1)}, u32[]{:S(2)}, u32[]{:S(2)}) collective-permute-start(f32[8,128]{1,0:T(8,128)S(1)} %add.53), channel_id=1, source_target_pairs={{0,33},{1,32},{2,35},{3,34},{4,37},{5,36},{6,39},{7,38},{8,41},{9,... | collective-permute-start | bytes 12296 | tf_op jit(solution)/shard_map/ppermute | solution.py:611
  67.8 5.8 %collective-permute-start.14 = (f32[8,128]{1,0:T(8,128)S(1)}, f32[8,128]{1,0:T(8,128)S(1)}, u32[]{:S(2)}, u32[]{:S(2)}) collective-permute-start(f32[8,128]{1,0:T(8,128)S(1)} %add.54), channel_id=1, source_target_pairs={{0,65},{1,64},{2,67},{3,66},{4,69},{5,68},{6,71},{7,70},{8,73},{9,... | collective-permute-start | bytes 12296 | tf_op jit(solution)/shard_map/ppermute | solution.py:611
  74.9 4.0 %collective-permute-start.15 = (f32[8,128]{1,0:T(8,128)S(1)}, f32[8,128]{1,0:T(8,128)S(1)}, u32[]{:S(2)}, u32[]{:S(2)}) collective-permute-start(f32[8,128]{1,0:T(8,128)S(1)} %add.55), channel_id=1, source_target_pairs={{0,225},{1,224},{2,227},{3,226},{4,229},{5,228},{6,231},{7,230},{8... | collective-permute-start | bytes 12296 | tf_op jit(solution)/shard_map/ppermute | solution.py:611
  78.9 3.0 %shard_map.156 = (f32[3,16,16,128]{3,2,1,0:T(8,128)}, f32[3,8,8,256]{3,2,1,0:T(8,128)}) custom-call(f32[3,16,16,128]{3,2,1,0:T(8,128)S(1)} %get-tuple-element.78.refs_0_, f32[3,8,8,256]{3,2,1,0:T(8,128)S(1)} %get-tuple-element.79.refs_1_, f32[3,16,16,128]{3,2,1,0:T(8,128)S(1)} %get-tuple-element.64.refs_0_.refs_2_, ...), custom_call_target="tpu_custom_call" | custom-call | flops 4000000 | bytes 1048576 | tf_op jit(solution)/shard_map/pallas_call | solution.py:531
  (63 shorter events, 12.6 us)
Async XLA Ops:
  0.7 4.8 %copy-start.3 = (f32[16,16,128]{2,1,0:T(8,128)S(1)}, f32[16,16,128]{2,1,0:T(8,128)}, u32[]{:S(2)}) copy-start(f32[16,16,128]{2,1,0:T(8,128)} %refs_16_.1) | copy-start | bytes 393220
  1.9 4.5 %collective-permute-start = (f32[256,128]{1,0:T(8,128)S(1)}, f32[256,128]{1,0:T(8,128)S(1)}, u32[]{:S(2)}, u32[]{:S(2)}) collective-permute-start(f32[256,128]{1,0:T(8,128)S(1)} %get-tuple-element.60), channel_id=1, source_target_pairs={{0,8},{1,9},{2,10},{3,11},{4,12},{5,13},{6,14},{7,15},{8,0},{9,1},... | collective-permute-start | bytes 393224 | tf_op jit(solution)/shard_map/ppermute | solution.py:611
  4.0 2.4 %collective-permute-start.1 = (f32[256,128]{1,0:T(8,128)S(1)}, f32[256,128]{1,0:T(8,128)S(1)}, u32[]{:S(2)}, u32[]{:S(2)}) collective-permute-start(f32[256,128]{1,0:T(8,128)S(1)} %get-tuple-element.61), channel_id=1, source_target_pairs={{0,1},{1,0},{2,3},{3,2},{4,5},{5,4},{6,7},{7,6},{8,16},{9,17},{10,... | collective-permute-start | bytes 393224 | tf_op jit(solution)/shard_map/ppermute | solution.py:611
  5.6 4.8 %copy-start.12 = (s32[2,16,16]{2,1,0:T(8,128)S(1)}, s32[2,16,16]{2,1,0:T(8,128)}, u32[]{:S(2)}) copy-start(s32[2,16,16]{2,1,0:T(8,128)} %param.25) | copy-start | bytes 6148
  6.4 9.2 %copy-start.6 = (f32[3,16,16,128]{3,2,1,0:T(8,128)S(1)}, f32[3,16,16,128]{3,2,1,0:T(8,128)}, u32[]{:S(2)}) copy-start(f32[3,16,16,128]{3,2,1,0:T(8,128)} %refs_2_.4) | copy-start | bytes 1179652
  6.4 9.2 %copy-start.7 = (f32[3,8,8,256]{3,2,1,0:T(8,128)S(1)}, f32[3,8,8,256]{3,2,1,0:T(8,128)}, u32[]{:S(2)}) copy-start(f32[3,8,8,256]{3,2,1,0:T(8,128)} %refs_3_.4) | copy-start | bytes 589828
  6.6 4.9 %collective-permute-start.2 = (f32[164,2,128]{2,1,0:T(2,128)S(1)}, f32[164,2,128]{2,1,0:T(2,128)S(1)}, u32[]{:S(2)}, u32[]{:S(2)}) collective-permute-start(f32[164,2,128]{2,1,0:T(2,128)S(1)} %get-tuple-element.62), channel_id=1, source_target_pairs={{0,1},{1,0},{2,3},{3,2},{4,5},{5,4},{6,7},{7,6},{8,9},{9,8},{10,11... | collective-permute-start | bytes 503816 | tf_op jit(solution)/shard_map/ppermute | solution.py:611
  10.4 5.1 %collective-permute-start.3 = (f32[164,2,128]{2,1,0:T(2,128)S(1)}, f32[164,2,128]{2,1,0:T(2,128)S(1)}, u32[]{:S(2)}, u32[]{:S(2)}) collective-permute-start(f32[164,2,128]{2,1,0:T(2,128)S(1)} %get-tuple-element.63), channel_id=1, source_target_pairs={{0,7},{1,2},{2,1},{3,4},{4,3},{5,6},{6,5},{7,0},{8,15},{9,10},{10,... | collective-permute-start | bytes 503816 | tf_op jit(solution)/shard_map/ppermute | solution.py:611
  19.1 5.0 %collective-permute-start.4 = (f32[288,128]{1,0:T(8,128)S(1)}, f32[288,128]{1,0:T(8,128)S(1)}, u32[]{:S(2)}, u32[]{:S(2)}) collective-permute-start(f32[288,128]{1,0:T(8,128)S(1)} %get-tuple-element.72), channel_id=1, source_target_pairs={{0,8},{1,9},{2,10},{3,11},{4,12},{5,13},{6,14},{7,15},{8,0},{9,1},... | collective-permute-start | bytes 442376 | tf_op jit(solution)/shard_map/ppermute | solution.py:611
  20.9 3.2 %collective-permute-start.5 = (f32[288,128]{1,0:T(8,128)S(1)}, f32[288,128]{1,0:T(8,128)S(1)}, u32[]{:S(2)}, u32[]{:S(2)}) collective-permute-start(f32[288,128]{1,0:T(8,128)S(1)} %get-tuple-element.73), channel_id=1, source_target_pairs={{0,1},{1,0},{2,3},{3,2},{4,5},{5,4},{6,7},{7,6},{8,16},{9,17},{10,... | collective-permute-start | bytes 442376 | tf_op jit(solution)/shard_map/ppermute | solution.py:611
  24.3 2.7 %collective-permute-start.6 = (f32[184,2,128]{2,1,0:T(2,128)S(1)}, f32[184,2,128]{2,1,0:T(2,128)S(1)}, u32[]{:S(2)}, u32[]{:S(2)}) collective-permute-start(f32[184,2,128]{2,1,0:T(2,128)S(1)} %get-tuple-element.75), channel_id=1, source_target_pairs={{0,1},{1,0},{2,3},{3,2},{4,5},{5,4},{6,7},{7,6},{8,9},{9,8},{10,11... | collective-permute-start | bytes 565256 | tf_op jit(solution)/shard_map/ppermute | solution.py:611
  26.0 5.3 %collective-permute-start.7 = (f32[184,2,128]{2,1,0:T(2,128)S(1)}, f32[184,2,128]{2,1,0:T(2,128)S(1)}, u32[]{:S(2)}, u32[]{:S(2)}) collective-permute-start(f32[184,2,128]{2,1,0:T(2,128)S(1)} %get-tuple-element.76), channel_id=1, source_target_pairs={{0,7},{1,2},{2,1},{3,4},{4,3},{5,6},{6,5},{7,0},{8,15},{9,10},{10,... | collective-permute-start | bytes 565256 | tf_op jit(solution)/shard_map/ppermute | solution.py:611
  34.7 4.9 %collective-permute-start.16 = (f32[192,128]{1,0:T(8,128)S(1)}, f32[192,128]{1,0:T(8,128)S(1)}, u32[]{:S(2)}, u32[]{:S(2)}) collective-permute-start(f32[192,128]{1,0:T(8,128)S(1)} %get-tuple-element.80), channel_id=1, source_target_pairs={{0,8},{1,9},{2,10},{3,11},{4,12},{5,13},{6,14},{7,15},{8,0},{9,1},... | collective-permute-start | bytes 294920 | tf_op jit(solution)/shard_map/ppermute | solution.py:611
  37.6 2.2 %collective-permute-start.17 = (f32[192,128]{1,0:T(8,128)S(1)}, f32[192,128]{1,0:T(8,128)S(1)}, u32[]{:S(2)}, u32[]{:S(2)}) collective-permute-start(f32[192,128]{1,0:T(8,128)S(1)} %get-tuple-element.81), channel_id=1, source_target_pairs={{0,1},{1,0},{2,3},{3,2},{4,5},{5,4},{6,7},{7,6},{8,16},{9,17},{10,... | collective-permute-start | bytes 294920 | tf_op jit(solution)/shard_map/ppermute | solution.py:611
  39.9 38.9 %collective-permute-start.18 = (f32[132,2,128]{2,1,0:T(2,128)S(1)}, f32[132,2,128]{2,1,0:T(2,128)S(1)}, u32[]{:S(2)}, u32[]{:S(2)}) collective-permute-start(f32[132,2,128]{2,1,0:T(2,128)S(1)} %get-tuple-element.82), channel_id=1, source_target_pairs={{0,1},{1,0},{2,3},{3,2},{4,5},{5,4},{6,7},{7,6},{8,9},{9,8},{10,11... | collective-permute-start | bytes 405512 | tf_op jit(solution)/shard_map/ppermute | solution.py:611
  41.7 37.2 %collective-permute-start.19 = (f32[132,2,128]{2,1,0:T(2,128)S(1)}, f32[132,2,128]{2,1,0:T(2,128)S(1)}, u32[]{:S(2)}, u32[]{:S(2)}) collective-permute-start(f32[132,2,128]{2,1,0:T(2,128)S(1)} %get-tuple-element.83), channel_id=1, source_target_pairs={{0,7},{1,2},{2,1},{3,4},{4,3},{5,6},{6,5},{7,0},{8,15},{9,10},{10,... | collective-permute-start | bytes 405512 | tf_op jit(solution)/shard_map/ppermute | solution.py:611
  42.2 2.6 %collective-permute-start.8 = (f32[8,128]{1,0:T(8,128)S(1)}, f32[8,128]{1,0:T(8,128)S(1)}, u32[]{:S(2)}, u32[]{:S(2)}) collective-permute-start(f32[8,128]{1,0:T(8,128)S(1)} %get-tuple-element.77), channel_id=1, source_target_pairs={{0,1},{1,0},{2,3},{3,2},{4,5},{5,4},{6,7},{7,6},{8,9},{9,8},{10,11... | collective-permute-start | bytes 12296 | tf_op jit(solution)/shard_map/ppermute | solution.py:611
  44.9 3.0 %collective-permute-start.9 = (f32[8,128]{1,0:T(8,128)S(1)}, f32[8,128]{1,0:T(8,128)S(1)}, u32[]{:S(2)}, u32[]{:S(2)}) collective-permute-start(f32[8,128]{1,0:T(8,128)S(1)} %add.49), channel_id=1, source_target_pairs={{0,3},{1,2},{2,1},{3,0},{4,7},{5,6},{6,5},{7,4},{8,11},{9,10},{10,... | collective-permute-start | bytes 12296 | tf_op jit(solution)/shard_map/ppermute | solution.py:611
  47.9 4.2 %collective-permute-start.10 = (f32[8,128]{1,0:T(8,128)S(1)}, f32[8,128]{1,0:T(8,128)S(1)}, u32[]{:S(2)}, u32[]{:S(2)}) collective-permute-start(f32[8,128]{1,0:T(8,128)S(1)} %add.50), channel_id=1, source_target_pairs={{0,7},{1,6},{2,5},{3,4},{4,3},{5,2},{6,1},{7,0},{8,15},{9,14},{10,... | collective-permute-start | bytes 12296 | tf_op jit(solution)/shard_map/ppermute | solution.py:611
  52.2 5.7 %collective-permute-start.11 = (f32[8,128]{1,0:T(8,128)S(1)}, f32[8,128]{1,0:T(8,128)S(1)}, u32[]{:S(2)}, u32[]{:S(2)}) collective-permute-start(f32[8,128]{1,0:T(8,128)S(1)} %add.51), channel_id=1, source_target_pairs={{0,9},{1,8},{2,11},{3,10},{4,13},{5,12},{6,15},{7,14},{8,1},{9,0},... | collective-permute-start | bytes 12296 | tf_op jit(solution)/shard_map/ppermute | solution.py:611
  57.9 5.8 %collective-permute-start.12 = (f32[8,128]{1,0:T(8,128)S(1)}, f32[8,128]{1,0:T(8,128)S(1)}, u32[]{:S(2)}, u32[]{:S(2)}) collective-permute-start(f32[8,128]{1,0:T(8,128)S(1)} %add.52), channel_id=1, source_target_pairs={{0,25},{1,24},{2,27},{3,26},{4,29},{5,28},{6,31},{7,30},{8,17},{9,... | collective-permute-start | bytes 12296 | tf_op jit(solution)/shard_map/ppermute | solution.py:611
  63.7 4.1 %collective-permute-start.13 = (f32[8,128]{1,0:T(8,128)S(1)}, f32[8,128]{1,0:T(8,128)S(1)}, u32[]{:S(2)}, u32[]{:S(2)}) collective-permute-start(f32[8,128]{1,0:T(8,128)S(1)} %add.53), channel_id=1, source_target_pairs={{0,33},{1,32},{2,35},{3,34},{4,37},{5,36},{6,39},{7,38},{8,41},{9,... | collective-permute-start | bytes 12296 | tf_op jit(solution)/shard_map/ppermute | solution.py:611
  67.8 7.1 %collective-permute-start.14 = (f32[8,128]{1,0:T(8,128)S(1)}, f32[8,128]{1,0:T(8,128)S(1)}, u32[]{:S(2)}, u32[]{:S(2)}) collective-permute-start(f32[8,128]{1,0:T(8,128)S(1)} %add.54), channel_id=1, source_target_pairs={{0,65},{1,64},{2,67},{3,66},{4,69},{5,68},{6,71},{7,70},{8,73},{9,... | collective-permute-start | bytes 12296 | tf_op jit(solution)/shard_map/ppermute | solution.py:611
  74.9 7.0 %collective-permute-start.15 = (f32[8,128]{1,0:T(8,128)S(1)}, f32[8,128]{1,0:T(8,128)S(1)}, u32[]{:S(2)}, u32[]{:S(2)}) collective-permute-start(f32[8,128]{1,0:T(8,128)S(1)} %add.55), channel_id=1, source_target_pairs={{0,225},{1,224},{2,227},{3,226},{4,229},{5,228},{6,231},{7,230},{8... | collective-permute-start | bytes 12296 | tf_op jit(solution)/shard_map/ppermute | solution.py:611
  (9 other events, 32.9 us)

commit v6 on v5

--- a/solution.py
+++ b/solution.py
@@ -395,7 +395,7 @@
         x_out = take(2)
     if step == 0:
         wide_f, inv_f, wide_c, inv_c, spread_out = take(5)
-    ext_f, ext_c, div_f, div_c, double, pairs = take(6)
+    ext_f, ext_c, div_f, div_c, double, moved, pairs = take(7)
 
     fill_displacement(s, flags, fine, ext_f, x_in, y_in, True)
     fill_displacement(s, flags, coarse, ext_c, x_in, y_in, False)
@@ -404,12 +404,16 @@
         fill_materials(s, flags, rig_c, met_c, inverse_c, wide_c, inv_c, x_in, y_in, False)
 
     lane = lax.broadcasted_iota(jnp.int32, (s.cy + 4, LANES), 1)
+    table = jnp.zeros((s.cy + 4, LANES), jnp.float32)
     for i in range(s.ce):
         e0, e1, e2 = (ext_c[c, i, 6 : 10 + s.cy, 0:LANES] for c in range(3))
         e1, e2 = pltpu.roll(e1, 1, 1), pltpu.roll(e2, 2, 1)
         plane = jnp.where(lane == 0, e0, jnp.where(lane == 1, e1, e2))
-        for j in range(s.cy + 4):
-            double[i, 2 * j : 2 * j + 2, :] = jnp.broadcast_to(plane[j : j + 1, :], (2, LANES))
+        for k in (2 * i, 2 * i + 1):
+            there = pltpu.roll(plane, 4 * k, 1) if k else plane
+            table = jnp.where(lane // 4 == k, there, table)
+    for j in range(s.cy + 4):
+        double[2 * j : 2 * j + 2, :] = jnp.broadcast_to(table[j : j + 1, :], (2, LANES))
     for c in range(3):
         for i in range(s.cx):
             pairs[c, i] = fine[c, 2 * i] + fine[c, 2 * i + 1]
@@ -424,32 +428,28 @@
         fill_transposed(s.fx, s.fy, ext_f, all_beta_f, inv_f, psi_f)
         fill_transposed(s.cx, s.cy, ext_c, all_beta_c, inv_c, psi_c)
 
-    odd_y = lax.broadcasted_iota(jnp.int32, (s.fy, LANES), 0) % 2
-    near_y = jnp.where(odd_y == 0, 0.75, 0.25)
-
-    def node_weights(i):
-        near_x = jnp.where(i % 2 == 0, 0.75, 0.25)
-        off_x, off_y = offs[i] // 4 - 1, offs[i] % 4 - 1
-        out = []
-        for off, near in ((off_x, near_x), (off_y, near_y)):
-            out.append(
-                [
-                    jnp.where(off == shift, near, 0.0)
-                    + jnp.where(off == shift - 1, 1.0 - near, 0.0)
-                    for shift in (-1, 0, 1, 2)
-                ]
-            )
-        return out
+    node = (s.fy, LANES)
+    node_lane = lax.broadcasted_iota(jnp.int32, node, 1)
+    near_x = jnp.where(node_lane // 4 % 2 == 0, 0.75, 0.25)
+    near_y = jnp.where(lax.broadcasted_iota(jnp.int32, node, 0) % 2 == 0, 0.75, 0.25)
+    code = offs[...]
+    weights_x, weights_y = (
+        [
+            jnp.where(off == shift, near, 0.0) + jnp.where(off == shift - 1, 1.0 - near, 0.0)
+            for shift in (-1, 0, 1, 2)
+        ]
+        for off, near in ((code // 4 - 1, near_x), (code % 4 - 1, near_y))
+    )
+    ghosts = jnp.zeros(node, jnp.float32)
+    for a in range(4):
+        moved[a] = pltpu.roll(double[...], LANES - 8 * (1 + a), 1)
+        line = jnp.zeros(node, jnp.float32)
+        for b in range(4):
+            line += weights_y[b] * moved[a, 2 * b + 2 : 2 * b + 2 + s.fy, :]
+        ghosts += weights_x[a] * line
 
     def fine_ghosts(i):
-        weights_x, weights_y = node_weights(i)
-        total = jnp.zeros((s.fy, LANES), jnp.float32)
-        for a in range(4):
-            line = jnp.zeros((s.fy, LANES), jnp.float32)
-            for b in range(4):
-                line += weights_y[b] * double[i // 2 + 1 + a, 2 * b + 2 : 2 * b + 2 + s.fy, :]
-            total += weights_x[a] * line
-        return None, lambda c: pltpu.roll(total, LANES - 1 - c, 1), None
+        return None, lambda c: pltpu.roll(ghosts, LANES - 1 - c - 4 * i, 1), None
 
     def coarse_ghosts(i):
         def mean(of):
@@ -478,27 +478,22 @@
     table = jnp.where(place == step, jnp.sum(sums_f[0]) / cells[0], table)
     table = jnp.where(place == STEPS + step, jnp.sum(sums_c[0]) / cells[1], table)
     if step == 0:
-        line_lane = lax.broadcasted_iota(jnp.int32, (s.fy, LANES), 1)
-        double[...] = jnp.zeros(double.shape, jnp.float32)
-
-        def scatter(i, carry):
-            weights_x, weights_y = node_weights(i)
-            face = coef_f[3][i]
-            q = jnp.zeros((s.fy, LANES), jnp.float32)
+        q = jnp.zeros(node, jnp.float32)
+        for i in range(s.fx):
             for c in range(3):
-                q = jnp.where(line_lane == c, pltpu.roll(face * new_f[c, i], c + 1, 1), q)
+                there = pltpu.roll(coef_f[3][i] * new_f[c, i], 4 * i + c + 1, 1)
+                q = jnp.where(node_lane == 4 * i + c, there, q)
+        moved[...] = jnp.zeros(moved.shape, jnp.float32)
+        for a in range(4):
+            part = weights_x[a] * q
             for b in range(4):
-                part = weights_y[b] * q
-                for a in range(4):
-                    rows = slice(2 * b + 2, 2 * b + 2 + s.fy)
-                    double[i // 2 + 1 + a, rows, :] += weights_x[a] * part
-            return carry
-
-        lax.fori_loop(0, s.fx, scatter, 0, unroll=4)
+                moved[a, 2 * b + 2 : 2 * b + 2 + s.fy, :] += weights_y[b] * part
+        double[...] = sum(pltpu.roll(moved[a], 8 * (1 + a), 1) for a in range(4))
         rows = s.cy + 4
+        both = double[pl.ds(0, rows, stride=2), :] + double[pl.ds(1, rows, stride=2), :]
         for i in range(s.ce):
-            evens = double[i, pl.ds(0, rows, stride=2), :]
-            spread_out[i, 0:rows, :] = evens + double[i, pl.ds(1, rows, stride=2), :]
+            there = pltpu.roll(both, LANES - 8 * i, 1) if i else both
+            spread_out[i, 0:rows, :] = there + pltpu.roll(there, LANES - 4, 1)
             spread_out[i, rows:, :] = jnp.zeros((s.spread - rows, LANES), jnp.float32)
         put_x(s, flags, x_out, new_f, new_c, beta_own, spread_out)
     if step == 1:
@@ -576,14 +571,14 @@
 
 
 TOTAL = (
+    lambda z, x, y, core: (z ^ 7, x, y, core),
     lambda z, x, y, core: (z, x, y, core ^ 1),
+    lambda z, x, y, core: (z ^ 2, x, y, core ^ 1),
     lambda z, x, y, core: (z, x, y ^ 1, core ^ 1),
+    lambda z, x, y, core: (z, x ^ 1, y, core ^ 1),
+    lambda z, x, y, core: (z ^ 1, x, y, core ^ 1),
+    lambda z, x, y, core: (z, x ^ 3, y, core ^ 1),
     lambda z, x, y, core: (z, x, y ^ 3, core ^ 1),
-    lambda z, x, y, core: (z, x ^ 1, y, core ^ 1),
-    lambda z, x, y, core: (z, x ^ 3, y, core ^ 1),
-    lambda z, x, y, core: (z ^ 1, x, y, core ^ 1),
-    lambda z, x, y, core: (z ^ 2, x, y, core ^ 1),
-    lambda z, x, y, core: (z ^ 7, x, y, core ^ 1),
 )
 
 
@@ -616,7 +611,7 @@
         return [pltpu.with_memory_space_constraint(x, pltpu.VMEM) for x in (first, second)]
 
     offs = offsets[0] * 4 + offsets[1] + 5
-    offs = jnp.broadcast_to(offs[..., None], offs.shape + (LANES,))
+    offs = jnp.pad(jnp.repeat(offs.T, 4, axis=1), ((0, 0), (0, LANES - 4 * s.fx)))
     x_out = call(
         functools.partial(first_kernel, s),
         [(s.x_rows_mats, LANES)] * 2,
@@ -668,7 +663,8 @@
         (3, s.ce, s.cy + 16, s.cz),
         (s.fx + 2, s.fy + 16, s.fz),
         (s.cx + 2, s.cy + 16, s.cz),
-        (s.ce, 2 * (s.cy + 4), LANES),
+        (2 * (s.cy + 4), LANES),
+        (4, 2 * (s.cy + 4), LANES),
         (3, s.cx, s.fy, LANES),
     ]
     cells = [count_x * count_y * s.fx * s.fy * s.fz, count_x * count_y * s.cx * s.cy * s.cz]
@@ -713,7 +709,7 @@
                 scratch[3],
                 scratch[0][1:],
                 scratch[1][1:],
-                scratch[5],
+                scratch[6],
                 (s.cx, s.cy, LANES),
             ]
         outs = call(

time: 82.8 us -> 80.7 us (0.975)
  starting transfers between devices: 42.7 us -> 40 us
    ppermute x20, starting transfers between devices: 42.7 us -> 40 us  [swap(): return lax.ppermute(value, ALL, swap_pairs(mesh, move))]
where the time goes in v6:
time: 80.7 us; the launch traced here: 80.5 us
  starting transfers between devices  40 us (50%)
  waiting for transfers between devices  27 us (33%)
  Pallas kernels  10.9 us (14%)
  local copies, waits for them, and re-layouts  1.65 us (2%)
  between operations  0.86 us (1%)
    ppermute x20, starting transfers between devices, swap(): return lax.ppermute(value, ALL, swap_pairs(mesh, move))  40 us
    ppermute x20, waiting for transfers between devices, swap(): return lax.ppermute(value, ALL, swap_pairs(mesh, move))  27 us
    pallas_call x9, Pallas kernels, call(): pl.pallas_call(kernel, out_shape=shapes, in_specs=[spec] * len(args), out...  10.9 us
  transfers between devices with their start and end apart: 20, of which 15 were waited for; matrix products, arithmetic and copies ran while one was open for 0% of the time, Pallas kernels for 4%

profile of v6, /device:TPU:1, one launch (start us, length us, event | category | flops | bytes accessed | tf_op | source)
XLA Modules:
  0.0 80.5 jit_solution(5297302383157553776)
XLA Ops:
  1.9 2.1 %collective-permute-start = (f32[256,128]{1,0:T(8,128)S(1)}, f32[256,128]{1,0:T(8,128)S(1)}, u32[]{:S(2)}, u32[]{:S(2)}) collective-permute-start(f32[256,128]{1,0:T(8,128)S(1)} %get-tuple-element.60), channel_id=1, source_target_pairs={{0,8},{1,9},{2,10},{3,11},{4,12},{5,13},{6,14},{7,15},{8,0},{9,1},... | collective-permute-start | bytes 393224 | tf_op jit(solution)/shard_map/ppermute | solution.py:606
  6.6 3.9 %collective-permute-start.2 = (f32[164,2,128]{2,1,0:T(2,128)S(1)}, f32[164,2,128]{2,1,0:T(2,128)S(1)}, u32[]{:S(2)}, u32[]{:S(2)}) collective-permute-start(f32[164,2,128]{2,1,0:T(2,128)S(1)} %get-tuple-element.62), channel_id=1, source_target_pairs={{0,1},{1,0},{2,3},{3,2},{4,5},{5,4},{6,7},{7,6},{8,9},{9,8},{10,11... | collective-permute-start | bytes 503816 | tf_op jit(solution)/shard_map/ppermute | solution.py:606
  11.6 4.0 %collective-permute-done.3.refs_26_ = f32[164,2,128]{2,1,0:T(2,128)S(1)} collective-permute-done((f32[164,2,128]{2,1,0:T(2,128)S(1)}, f32[164,2,128]{2,1,0:T(2,128)S(1)}, u32[]{:S(2)}, u32[]{:S(2)}) %collective-permute-start.3) | collective-permute-done | bytes 167968 | tf_op jit(solution)/shard_map/ppermute | solution.py:606
  15.5 2.8 %shard_map.152 = (f32[3,16,16,128]{3,2,1,0:T(8,128)S(1)}, f32[3,8,8,256]{3,2,1,0:T(8,128)S(1)}, f32[8,128]{1,0:T(8,128)S(1)}, f32[288,128]{1,0:T(8,128)S(1)}, f3...) custom-call(f32[3,16,16,128]{3,2,1,0:T(8,128)S(1)} %copy-done, ...), custom_call_target="tpu_custom_call" | custom-call | flops 4000000 | bytes 1048576 | tf_op jit(solution)/shard_map/pallas_call | solution.py:526
  18.4 1.8 %collective-permute-start.4 = (f32[288,128]{1,0:T(8,128)S(1)}, f32[288,128]{1,0:T(8,128)S(1)}, u32[]{:S(2)}, u32[]{:S(2)}) collective-permute-start(f32[288,128]{1,0:T(8,128)S(1)} %get-tuple-element.72), channel_id=1, source_target_pairs={{0,8},{1,9},{2,10},{3,11},{4,12},{5,13},{6,14},{7,15},{8,0},{9,1},... | collective-permute-start | bytes 442376 | tf_op jit(solution)/shard_map/ppermute | solution.py:606
  20.2 1.3 %collective-permute-start.5 = (f32[288,128]{1,0:T(8,128)S(1)}, f32[288,128]{1,0:T(8,128)S(1)}, u32[]{:S(2)}, u32[]{:S(2)}) collective-permute-start(f32[288,128]{1,0:T(8,128)S(1)} %get-tuple-element.73), channel_id=1, source_target_pairs={{0,1},{1,0},{2,3},{3,2},{4,5},{5,4},{6,7},{7,6},{8,16},{9,17},{10,... | collective-permute-start | bytes 442376 | tf_op jit(solution)/shard_map/ppermute | solution.py:606
  21.5 1.9 %collective-permute-done.4.refs_5_.refs_23_ = f32[288,128]{1,0:T(8,128)S(1)} collective-permute-done((f32[288,128]{1,0:T(8,128)S(1)}, f32[288,128]{1,0:T(8,128)S(1)}, u32[]{:S(2)}, u32[]{:S(2)}) %collective-permute-start.4) | collective-permute-done | bytes 147488 | tf_op jit(solution)/shard_map/ppermute | solution.py:606
  23.6 1.7 %collective-permute-start.6 = (f32[184,2,128]{2,1,0:T(2,128)S(1)}, f32[184,2,128]{2,1,0:T(2,128)S(1)}, u32[]{:S(2)}, u32[]{:S(2)}) collective-permute-start(f32[184,2,128]{2,1,0:T(2,128)S(1)} %get-tuple-element.75), channel_id=1, source_target_pairs={{0,1},{1,0},{2,3},{3,2},{4,5},{5,4},{6,7},{7,6},{8,9},{9,8},{10,11... | collective-permute-start | bytes 565256 | tf_op jit(solution)/shard_map/ppermute | solution.py:606
  26.3 4.2 %collective-permute-done.7.refs_26_ = f32[184,2,128]{2,1,0:T(2,128)S(1)} collective-permute-done((f32[184,2,128]{2,1,0:T(2,128)S(1)}, f32[184,2,128]{2,1,0:T(2,128)S(1)}, u32[]{:S(2)}, u32[]{:S(2)}) %collective-permute-start.7) | collective-permute-done | bytes 188448 | tf_op jit(solution)/shard_map/ppermute | solution.py:606
  30.6 3.3 %shard_map.154 = (f32[3,16,16,128]{3,2,1,0:T(8,128)S(1)}, f32[3,8,8,256]{3,2,1,0:T(8,128)S(1)}, f32[8,128]{1,0:T(8,128)S(1)}, f32[192,128]{1,0:T(8,128)S(1)}, f32[192,128]{1,0:T(8,128)S(1)}) custom-call(f32[3,16,16,128]{3,2,1,0:T(8,128)S(1)} %get-tuple-element.64.refs_0_.refs_2_, f32[3,8,8,256]{3,2,1,0:T(8,128)S(1)} %get-tuple-element.65.refs_1_.refs_3_, ...), custom_call_target="tpu_custom_call" | custom-call | flops 4000000 | bytes 1048576 | tf_op jit(solution)/shard_map/pallas_call | solution.py:526
  33.9 2.9 %collective-permute-start.16 = (f32[192,128]{1,0:T(8,128)S(1)}, f32[192,128]{1,0:T(8,128)S(1)}, u32[]{:S(2)}, u32[]{:S(2)}) collective-permute-start(f32[192,128]{1,0:T(8,128)S(1)} %get-tuple-element.80), channel_id=1, source_target_pairs={{0,8},{1,9},{2,10},{3,11},{4,12},{5,13},{6,14},{7,15},{8,0},{9,1},... | collective-permute-start | bytes 294920 | tf_op jit(solution)/shard_map/ppermute | solution.py:606
  36.8 1.3 %collective-permute-start.17 = (f32[192,128]{1,0:T(8,128)S(1)}, f32[192,128]{1,0:T(8,128)S(1)}, u32[]{:S(2)}, u32[]{:S(2)}) collective-permute-start(f32[192,128]{1,0:T(8,128)S(1)} %get-tuple-element.81), channel_id=1, source_target_pairs={{0,1},{1,0},{2,3},{3,2},{4,5},{5,4},{6,7},{7,6},{8,16},{9,17},{10,... | collective-permute-start | bytes 294920 | tf_op jit(solution)/shard_map/ppermute | solution.py:606
  39.2 1.7 %collective-permute-start.18 = (f32[132,2,128]{2,1,0:T(2,128)S(1)}, f32[132,2,128]{2,1,0:T(2,128)S(1)}, u32[]{:S(2)}, u32[]{:S(2)}) collective-permute-start(f32[132,2,128]{2,1,0:T(2,128)S(1)} %get-tuple-element.82), channel_id=1, source_target_pairs={{0,1},{1,0},{2,3},{3,2},{4,5},{5,4},{6,7},{7,6},{8,9},{9,8},{10,11... | collective-permute-start | bytes 405512 | tf_op jit(solution)/shard_map/ppermute | solution.py:606
  41.5 10.2 %collective-permute-start.8 = (f32[8,128]{1,0:T(8,128)S(1)}, f32[8,128]{1,0:T(8,128)S(1)}, u32[]{:S(2)}, u32[]{:S(2)}) collective-permute-start(f32[8,128]{1,0:T(8,128)S(1)} %get-tuple-element.77), channel_id=1, source_target_pairs={{0,224},{1,225},{2,226},{3,227},{4,228},{5,229},{6,230},{7,231},{8... | collective-permute-start | bytes 12296 | tf_op jit(solution)/shard_map/ppermute | solution.py:606
  52.7 3.2 %collective-permute-start.9 = (f32[8,128]{1,0:T(8,128)S(1)}, f32[8,128]{1,0:T(8,128)S(1)}, u32[]{:S(2)}, u32[]{:S(2)}) collective-permute-start(f32[8,128]{1,0:T(8,128)S(1)} %add.43), channel_id=1, source_target_pairs={{0,1},{1,0},{2,3},{3,2},{4,5},{5,4},{6,7},{7,6},{8,9},{9,8},{10,11... | collective-permute-start | bytes 12296 | tf_op jit(solution)/shard_map/ppermute | solution.py:606
  56.7 2.4 %collective-permute-start.10 = (f32[8,128]{1,0:T(8,128)S(1)}, f32[8,128]{1,0:T(8,128)S(1)}, u32[]{:S(2)}, u32[]{:S(2)}) collective-permute-start(f32[8,128]{1,0:T(8,128)S(1)} %add.44), channel_id=1, source_target_pairs={{0,65},{1,64},{2,67},{3,66},{4,69},{5,68},{6,71},{7,70},{8,73},{9,... | collective-permute-start | bytes 12296 | tf_op jit(solution)/shard_map/ppermute | solution.py:606
  59.1 1.5 %collective-permute-done.10 = f32[8,128]{1,0:T(8,128)S(1)} collective-permute-done((f32[8,128]{1,0:T(8,128)S(1)}, f32[8,128]{1,0:T(8,128)S(1)}, u32[]{:S(2)}, u32[]{:S(2)}) %collective-permute-start.10) | collective-permute-done | bytes 4128 | tf_op jit(solution)/shard_map/ppermute | solution.py:606
  60.7 3.0 %collective-permute-done.11 = f32[8,128]{1,0:T(8,128)S(1)} collective-permute-done((f32[8,128]{1,0:T(8,128)S(1)}, f32[8,128]{1,0:T(8,128)S(1)}, u32[]{:S(2)}, u32[]{:S(2)}) %collective-permute-start.11) | collective-permute-done | bytes 4128 | tf_op jit(solution)/shard_map/ppermute | solution.py:606
  63.7 3.0 %collective-permute-done.12 = f32[8,128]{1,0:T(8,128)S(1)} collective-permute-done((f32[8,128]{1,0:T(8,128)S(1)}, f32[8,128]{1,0:T(8,128)S(1)}, u32[]{:S(2)}, u32[]{:S(2)}) %collective-permute-start.12) | collective-permute-done | bytes 4128 | tf_op jit(solution)/shard_map/ppermute | solution.py:606
  66.7 3.2 %collective-permute-start.13 = (f32[8,128]{1,0:T(8,128)S(1)}, f32[8,128]{1,0:T(8,128)S(1)}, u32[]{:S(2)}, u32[]{:S(2)}) collective-permute-start(f32[8,128]{1,0:T(8,128)S(1)} %add.47), channel_id=1, source_target_pairs={{0,33},{1,32},{2,35},{3,34},{4,37},{5,36},{6,39},{7,38},{8,41},{9,... | collective-permute-start | bytes 12296 | tf_op jit(solution)/shard_map/ppermute | solution.py:606
  70.0 1.3 %collective-permute-done.13 = f32[8,128]{1,0:T(8,128)S(1)} collective-permute-done((f32[8,128]{1,0:T(8,128)S(1)}, f32[8,128]{1,0:T(8,128)S(1)}, u32[]{:S(2)}, u32[]{:S(2)}) %collective-permute-start.13) | collective-permute-done | bytes 4128 | tf_op jit(solution)/shard_map/ppermute | solution.py:606
  71.2 2.1 %collective-permute-start.14 = (f32[8,128]{1,0:T(8,128)S(1)}, f32[8,128]{1,0:T(8,128)S(1)}, u32[]{:S(2)}, u32[]{:S(2)}) collective-permute-start(f32[8,128]{1,0:T(8,128)S(1)} %add.48), channel_id=1, source_target_pairs={{0,25},{1,24},{2,27},{3,26},{4,29},{5,28},{6,31},{7,30},{8,17},{9,... | collective-permute-start | bytes 12296 | tf_op jit(solution)/shard_map/ppermute | solution.py:606
  73.4 2.1 %collective-permute-done.14 = f32[8,128]{1,0:T(8,128)S(1)} collective-permute-done((f32[8,128]{1,0:T(8,128)S(1)}, f32[8,128]{1,0:T(8,128)S(1)}, u32[]{:S(2)}, u32[]{:S(2)}) %collective-permute-start.14) | collective-permute-done | bytes 4128 | tf_op jit(solution)/shard_map/ppermute | solution.py:606
  75.7 3.0 %shard_map.156 = (f32[3,16,16,128]{3,2,1,0:T(8,128)}, f32[3,8,8,256]{3,2,1,0:T(8,128)}) custom-call(f32[3,16,16,128]{3,2,1,0:T(8,128)S(1)} %get-tuple-element.78.refs_0_, f32[3,8,8,256]{3,2,1,0:T(8,128)S(1)} %get-tuple-element.79.refs_1_, f32[3,16,16,128]{3,2,1,0:T(8,128)S(1)} %get-tuple-element.64.refs_0_.refs_2_, ...), custom_call_target="tpu_custom_call" | custom-call | flops 4000000 | bytes 1048576 | tf_op jit(solution)/shard_map/pallas_call | solution.py:526
  (65 shorter events, 11.6 us)
Async XLA Ops:
  0.6 5.7 %copy-start.5 = (f32[8,8,256]{2,1,0:T(8,128)S(1)}, f32[8,8,256]{2,1,0:T(8,128)}, u32[]{:S(2)}) copy-start(f32[8,8,256]{2,1,0:T(8,128)} %refs_19_.1) | copy-start | bytes 196612
  0.6 5.7 %copy-start.4 = (f32[8,8,256]{2,1,0:T(8,128)S(1)}, f32[8,8,256]{2,1,0:T(8,128)}, u32[]{:S(2)}) copy-start(f32[8,8,256]{2,1,0:T(8,128)} %refs_18_.1) | copy-start | bytes 196612
  0.7 5.7 %copy-start.3 = (f32[16,16,128]{2,1,0:T(8,128)S(1)}, f32[16,16,128]{2,1,0:T(8,128)}, u32[]{:S(2)}) copy-start(f32[16,16,128]{2,1,0:T(8,128)} %refs_16_.1) | copy-start | bytes 393220
  1.9 4.5 %collective-permute-start = (f32[256,128]{1,0:T(8,128)S(1)}, f32[256,128]{1,0:T(8,128)S(1)}, u32[]{:S(2)}, u32[]{:S(2)}) collective-permute-start(f32[256,128]{1,0:T(8,128)S(1)} %get-tuple-element.60), channel_id=1, source_target_pairs={{0,8},{1,9},{2,10},{3,11},{4,12},{5,13},{6,14},{7,15},{8,0},{9,1},... | collective-permute-start | bytes 393224 | tf_op jit(solution)/shard_map/ppermute | solution.py:606
  4.0 6.5 %copy-start.12 = (s32[2,16,16]{2,1,0:T(8,128)S(1)}, s32[2,16,16]{2,1,0:T(8,128)}, u32[]{:S(2)}) copy-start(s32[2,16,16]{2,1,0:T(8,128)} %param.25) | copy-start | bytes 6148
  4.0 2.4 %collective-permute-start.1 = (f32[256,128]{1,0:T(8,128)S(1)}, f32[256,128]{1,0:T(8,128)S(1)}, u32[]{:S(2)}, u32[]{:S(2)}) collective-permute-start(f32[256,128]{1,0:T(8,128)S(1)} %get-tuple-element.61), channel_id=1, source_target_pairs={{0,1},{1,0},{2,3},{3,2},{4,5},{5,4},{6,7},{7,6},{8,16},{9,17},{10,... | collective-permute-start | bytes 393224 | tf_op jit(solution)/shard_map/ppermute | solution.py:606
  6.6 5.0 %collective-permute-start.2 = (f32[164,2,128]{2,1,0:T(2,128)S(1)}, f32[164,2,128]{2,1,0:T(2,128)S(1)}, u32[]{:S(2)}, u32[]{:S(2)}) collective-permute-start(f32[164,2,128]{2,1,0:T(2,128)S(1)} %get-tuple-element.62), channel_id=1, source_target_pairs={{0,1},{1,0},{2,3},{3,2},{4,5},{5,4},{6,7},{7,6},{8,9},{9,8},{10,11... | collective-permute-start | bytes 503816 | tf_op jit(solution)/shard_map/ppermute | solution.py:606
  10.5 5.1 %collective-permute-start.3 = (f32[164,2,128]{2,1,0:T(2,128)S(1)}, f32[164,2,128]{2,1,0:T(2,128)S(1)}, u32[]{:S(2)}, u32[]{:S(2)}) collective-permute-start(f32[164,2,128]{2,1,0:T(2,128)S(1)} %get-tuple-element.63), channel_id=1, source_target_pairs={{0,7},{1,2},{2,1},{3,4},{4,3},{5,6},{6,5},{7,0},{8,15},{9,10},{10,... | collective-permute-start | bytes 503816 | tf_op jit(solution)/shard_map/ppermute | solution.py:606
  18.4 5.0 %collective-permute-start.4 = (f32[288,128]{1,0:T(8,128)S(1)}, f32[288,128]{1,0:T(8,128)S(1)}, u32[]{:S(2)}, u32[]{:S(2)}) collective-permute-start(f32[288,128]{1,0:T(8,128)S(1)} %get-tuple-element.72), channel_id=1, source_target_pairs={{0,8},{1,9},{2,10},{3,11},{4,12},{5,13},{6,14},{7,15},{8,0},{9,1},... | collective-permute-start | bytes 442376 | tf_op jit(solution)/shard_map/ppermute | solution.py:606
  20.2 3.2 %collective-permute-start.5 = (f32[288,128]{1,0:T(8,128)S(1)}, f32[288,128]{1,0:T(8,128)S(1)}, u32[]{:S(2)}, u32[]{:S(2)}) collective-permute-start(f32[288,128]{1,0:T(8,128)S(1)} %get-tuple-element.73), channel_id=1, source_target_pairs={{0,1},{1,0},{2,3},{3,2},{4,5},{5,4},{6,7},{7,6},{8,16},{9,17},{10,... | collective-permute-start | bytes 442376 | tf_op jit(solution)/shard_map/ppermute | solution.py:606
  23.6 2.7 %collective-permute-start.6 = (f32[184,2,128]{2,1,0:T(2,128)S(1)}, f32[184,2,128]{2,1,0:T(2,128)S(1)}, u32[]{:S(2)}, u32[]{:S(2)}) collective-permute-start(f32[184,2,128]{2,1,0:T(2,128)S(1)} %get-tuple-element.75), channel_id=1, source_target_pairs={{0,1},{1,0},{2,3},{3,2},{4,5},{5,4},{6,7},{7,6},{8,9},{9,8},{10,11... | collective-permute-start | bytes 565256 | tf_op jit(solution)/shard_map/ppermute | solution.py:606
  25.3 5.3 %collective-permute-start.7 = (f32[184,2,128]{2,1,0:T(2,128)S(1)}, f32[184,2,128]{2,1,0:T(2,128)S(1)}, u32[]{:S(2)}, u32[]{:S(2)}) collective-permute-start(f32[184,2,128]{2,1,0:T(2,128)S(1)} %get-tuple-element.76), channel_id=1, source_target_pairs={{0,7},{1,2},{2,1},{3,4},{4,3},{5,6},{6,5},{7,0},{8,15},{9,10},{10,... | collective-permute-start | bytes 565256 | tf_op jit(solution)/shard_map/ppermute | solution.py:606
  33.9 4.9 %collective-permute-start.16 = (f32[192,128]{1,0:T(8,128)S(1)}, f32[192,128]{1,0:T(8,128)S(1)}, u32[]{:S(2)}, u32[]{:S(2)}) collective-permute-start(f32[192,128]{1,0:T(8,128)S(1)} %get-tuple-element.80), channel_id=1, source_target_pairs={{0,8},{1,9},{2,10},{3,11},{4,12},{5,13},{6,14},{7,15},{8,0},{9,1},... | collective-permute-start | bytes 294920 | tf_op jit(solution)/shard_map/ppermute | solution.py:606
  36.8 2.2 %collective-permute-start.17 = (f32[192,128]{1,0:T(8,128)S(1)}, f32[192,128]{1,0:T(8,128)S(1)}, u32[]{:S(2)}, u32[]{:S(2)}) collective-permute-start(f32[192,128]{1,0:T(8,128)S(1)} %get-tuple-element.81), channel_id=1, source_target_pairs={{0,1},{1,0},{2,3},{3,2},{4,5},{5,4},{6,7},{7,6},{8,16},{9,17},{10,... | collective-permute-start | bytes 294920 | tf_op jit(solution)/shard_map/ppermute | solution.py:606
  39.2 36.5 %collective-permute-start.18 = (f32[132,2,128]{2,1,0:T(2,128)S(1)}, f32[132,2,128]{2,1,0:T(2,128)S(1)}, u32[]{:S(2)}, u32[]{:S(2)}) collective-permute-start(f32[132,2,128]{2,1,0:T(2,128)S(1)} %get-tuple-element.82), channel_id=1, source_target_pairs={{0,1},{1,0},{2,3},{3,2},{4,5},{5,4},{6,7},{7,6},{8,9},{9,8},{10,11... | collective-permute-start | bytes 405512 | tf_op jit(solution)/shard_map/ppermute | solution.py:606
  40.9 34.8 %collective-permute-start.19 = (f32[132,2,128]{2,1,0:T(2,128)S(1)}, f32[132,2,128]{2,1,0:T(2,128)S(1)}, u32[]{:S(2)}, u32[]{:S(2)}) collective-permute-start(f32[132,2,128]{2,1,0:T(2,128)S(1)} %get-tuple-element.83), channel_id=1, source_target_pairs={{0,7},{1,2},{2,1},{3,4},{4,3},{5,6},{6,5},{7,0},{8,15},{9,10},{10,... | collective-permute-start | bytes 405512 | tf_op jit(solution)/shard_map/ppermute | solution.py:606
  41.5 11.2 %collective-permute-start.8 = (f32[8,128]{1,0:T(8,128)S(1)}, f32[8,128]{1,0:T(8,128)S(1)}, u32[]{:S(2)}, u32[]{:S(2)}) collective-permute-start(f32[8,128]{1,0:T(8,128)S(1)} %get-tuple-element.77), channel_id=1, source_target_pairs={{0,224},{1,225},{2,226},{3,227},{4,228},{5,229},{6,230},{7,231},{8... | collective-permute-start | bytes 12296 | tf_op jit(solution)/shard_map/ppermute | solution.py:606
  52.7 4.0 %collective-permute-start.9 = (f32[8,128]{1,0:T(8,128)S(1)}, f32[8,128]{1,0:T(8,128)S(1)}, u32[]{:S(2)}, u32[]{:S(2)}) collective-permute-start(f32[8,128]{1,0:T(8,128)S(1)} %add.43), channel_id=1, source_target_pairs={{0,1},{1,0},{2,3},{3,2},{4,5},{5,4},{6,7},{7,6},{8,9},{9,8},{10,11... | collective-permute-start | bytes 12296 | tf_op jit(solution)/shard_map/ppermute | solution.py:606
  56.7 3.9 %collective-permute-start.10 = (f32[8,128]{1,0:T(8,128)S(1)}, f32[8,128]{1,0:T(8,128)S(1)}, u32[]{:S(2)}, u32[]{:S(2)}) collective-permute-start(f32[8,128]{1,0:T(8,128)S(1)} %add.44), channel_id=1, source_target_pairs={{0,65},{1,64},{2,67},{3,66},{4,69},{5,68},{6,71},{7,70},{8,73},{9,... | collective-permute-start | bytes 12296 | tf_op jit(solution)/shard_map/ppermute | solution.py:606
  60.7 3.0 %collective-permute-start.11 = (f32[8,128]{1,0:T(8,128)S(1)}, f32[8,128]{1,0:T(8,128)S(1)}, u32[]{:S(2)}, u32[]{:S(2)}) collective-permute-start(f32[8,128]{1,0:T(8,128)S(1)} %add.45), channel_id=1, source_target_pairs={{0,3},{1,2},{2,1},{3,0},{4,7},{5,6},{6,5},{7,4},{8,11},{9,10},{10,... | collective-permute-start | bytes 12296 | tf_op jit(solution)/shard_map/ppermute | solution.py:606
  63.7 3.0 %collective-permute-start.12 = (f32[8,128]{1,0:T(8,128)S(1)}, f32[8,128]{1,0:T(8,128)S(1)}, u32[]{:S(2)}, u32[]{:S(2)}) collective-permute-start(f32[8,128]{1,0:T(8,128)S(1)} %add.46), channel_id=1, source_target_pairs={{0,9},{1,8},{2,11},{3,10},{4,13},{5,12},{6,15},{7,14},{8,1},{9,0},... | collective-permute-start | bytes 12296 | tf_op jit(solution)/shard_map/ppermute | solution.py:606
  66.7 4.5 %collective-permute-start.13 = (f32[8,128]{1,0:T(8,128)S(1)}, f32[8,128]{1,0:T(8,128)S(1)}, u32[]{:S(2)}, u32[]{:S(2)}) collective-permute-start(f32[8,128]{1,0:T(8,128)S(1)} %add.47), channel_id=1, source_target_pairs={{0,33},{1,32},{2,35},{3,34},{4,37},{5,36},{6,39},{7,38},{8,41},{9,... | collective-permute-start | bytes 12296 | tf_op jit(solution)/shard_map/ppermute | solution.py:606
  71.2 4.2 %collective-permute-start.14 = (f32[8,128]{1,0:T(8,128)S(1)}, f32[8,128]{1,0:T(8,128)S(1)}, u32[]{:S(2)}, u32[]{:S(2)}) collective-permute-start(f32[8,128]{1,0:T(8,128)S(1)} %add.48), channel_id=1, source_target_pairs={{0,25},{1,24},{2,27},{3,26},{4,29},{5,28},{6,31},{7,30},{8,17},{9,... | collective-permute-start | bytes 12296 | tf_op jit(solution)/shard_map/ppermute | solution.py:606
  75.5 4.2 %collective-permute-start.15 = (f32[8,128]{1,0:T(8,128)S(1)}, f32[8,128]{1,0:T(8,128)S(1)}, u32[]{:S(2)}, u32[]{:S(2)}) collective-permute-start(f32[8,128]{1,0:T(8,128)S(1)} %add.49), channel_id=1, source_target_pairs={{0,7},{1,6},{2,5},{3,4},{4,3},{5,2},{6,1},{7,0},{8,15},{9,14},{10,... | collective-permute-start | bytes 12296 | tf_op jit(solution)/shard_map/ppermute | solution.py:606
  (9 other events, 36.2 us)

commit v7 on v6

--- a/solution.py
+++ b/solution.py
@@ -31,9 +31,9 @@
         self.fx, self.fy, self.fz = fine
         self.cx, self.cy, self.cz = coarse
         self.halves = self.cz // LANES
-        self.x_fine = 0
-        self.x_coarse = 6 * self.fy
-        self.x_rows = self.x_coarse + self.halves * 6 * self.cy
+        self.x_coarse = 4 * self.fy
+        self.x_plane = self.x_coarse + self.halves * 4 * self.cy
+        self.x_rows = self.x_plane + self.cy
         self.x_fine_mats = self.x_rows
         self.x_coarse_mats = self.x_fine_mats + 2 * self.fy
         self.x_rows_mats = self.x_coarse_mats + 2 * self.halves * self.cy
@@ -43,8 +43,9 @@
         self.spread = self.cy + 8
         self.x_rows_beta = self.x_spread + 2 * self.spread
         self.fe, self.ce = self.fx + 4, self.cx + 4
-        self.y_coarse = 3 * self.fe
-        self.y_rows = self.y_coarse + self.halves * 3 * self.ce
+        self.y_coarse = 2 * self.fe
+        self.y_plane = self.y_coarse + self.halves * 2 * self.ce
+        self.y_rows = self.y_plane + self.ce
         self.y_fine_mats = self.y_rows
         self.y_coarse_mats = self.y_fine_mats + self.fx
         self.y_rows_mats = self.y_coarse_mats + self.halves * self.cx
@@ -58,17 +59,27 @@
     return slice(h * LANES, (h + 1) * LANES)
 
 
+def put_strips(s, out, far, fine, coarse, at_f, at_c):
+    near, second = jnp.where(far, 1, 0), jnp.where(far, 0, 1)
+    for n, (c, row) in enumerate(((0, 0), (0, 1), (1, near), (2, near))):
+        out[n * s.fy : (n + 1) * s.fy, :] = fine[c, at_f + row]
+        line = coarse[c, at_c + row]
+        for h in range(s.halves):
+            base = s.x_coarse + (h * 4 + n) * s.cy
+            out[base : base + s.cy, :] = line[:, lanes_of(h)]
+    along_y, along_z = (coarse[c, at_c + second][:, 0:LANES] for c in (1, 2))
+    lane = lax.broadcasted_iota(jnp.int32, along_y.shape, 1)
+    plane = jnp.where(lane == 1, pltpu.roll(along_y, 1, 1), pltpu.roll(along_z, 2, 1))
+    out[s.x_plane : s.x_plane + s.cy, :] = plane
+
+
 def put_x(s, flags, outs, fine, coarse, betas=None, spread=None):
     even = flags[EVEN_X]
     for k, out in enumerate(outs):
         far = even if k == 0 else jnp.logical_not(even)
         start_f = jnp.where(far, s.fx - 2, 0)
         start_c = jnp.where(far, s.cx - 2, 0)
-        out[0 : s.x_coarse, :] = fine[:, pl.ds(start_f, 2), :, :].reshape(6 * s.fy, LANES)
-        strip = coarse[:, pl.ds(start_c, 2), :, :]
-        for h in range(s.halves):
-            base = s.x_coarse + h * 6 * s.cy
-            out[base : base + 6 * s.cy, :] = strip[:, :, :, lanes_of(h)].reshape(6 * s.cy, LANES)
+        put_strips(s, out, far, fine, coarse, start_f, start_c)
         if betas is None:
             continue
         strip = betas[0][pl.ds(start_f, 2), :, :]
@@ -101,14 +112,12 @@
     for copy in copies:
         copy.wait()
     for k, out in enumerate((out_a, out_b)):
-        out[0 : s.x_coarse, :] = strip_f[k].reshape(6 * s.fy, LANES)
+        far = even if k == 0 else jnp.logical_not(even)
+        put_strips(s, out, far, strip_f.at[k], strip_c.at[k], 0, 0)
         for m in range(2):
             base = s.x_fine_mats + m * s.fy
             out[base : base + s.fy, :] = line_f[k, m]
-        for h in range(s.halves):
-            base = s.x_coarse + h * 6 * s.cy
-            out[base : base + 6 * s.cy, :] = strip_c[k, :, :, :, lanes_of(h)].reshape(6 * s.cy, LANES)
-            for m in range(2):
+            for h in range(s.halves):
                 base = s.x_coarse_mats + (m * s.halves + h) * s.cy
                 out[base : base + s.cy, :] = line_c[k, m, :, lanes_of(h)]
 
@@ -131,23 +140,56 @@
         out_a[index] = jnp.where(even, high, low)
         out_b[index] = jnp.where(even, low, high)
 
+    def put_one(index, m, low, high):
+        out_a[index, m : m + 1, :] = jnp.where(even, high, low)
+        out_b[index, m : m + 1, :] = jnp.where(even, low, high)
+
+    def came(first, count):
+        rows = slice(first, first + count)
+        return sides(flags, EVEN_X, HAS_XM, HAS_XP, in_a[rows, :], in_b[rows, :])
+
+    def level(own, x, y, x_base, y_base, y_size, plane):
+        both, single = y_base, y_base + y_size
+        here = pl.ds(both + 2, x)
+        put(here, own(1, slice(0, 2)), own(1, slice(y - 2, y)))
+        for m, c in enumerate((0, 2)):
+            here = pl.ds(single + 2, x)
+            put_one(here, m, own(c, slice(0, 1)), own(c, slice(y - 1, y)))
+            if plane:
+                here = pl.ds(s.y_plane + 2, x)
+                put_one(here, m, own(c, slice(1, 2)), own(c, slice(y - 2, y - 1)))
+        for side in range(2):
+            for k in range(2):
+                place = k if side == 0 else x + 2 + k
+                near = k == 1 - side
+
+                def row(c, first, count):
+                    if c == 0:
+                        return came(x_base + k * y + first, count)[side]
+                    if near:
+                        return came(x_base + (1 + c) * y + first, count)[side]
+                    return pltpu.roll(came(s.x_plane + first, count)[side], LANES - c, 1)
+
+                if near or plane:
+                    put(both + place, row(1, 0, 2), row(1, y - 2, 2))
+                for m, c in enumerate((0, 2)):
+                    if c == 0 or near or plane:
+                        put_one(single + place, m, row(c, 0, 1), row(c, y - 1, 1))
+                    if plane:
+                        put_one(s.y_plane + place, m, row(c, 1, 1), row(c, y - 2, 1))
+
     def field(own, x, y, x_base, y_base):
         put(pl.ds(y_base + 2, x), own(slice(0, 2)), own(slice(y - 2, y)))
         for k in range(2):
-            pieces = []
-            for first in (0, y - 2):
-                rows = slice(x_base + k * y + first, x_base + k * y + first + 2)
-                pieces.append(sides(flags, EVEN_X, HAS_XM, HAS_XP, in_a[rows, :], in_b[rows, :]))
+            low, high = came(x_base + k * y, 2), came(x_base + (k + 1) * y - 2, 2)
             for side in range(2):
-                place = y_base + (k if side == 0 else x + 2 + k)
-                put(place, pieces[0][side], pieces[1][side])
-
-    for c in range(3):
-        field(lambda r: fine[c, :, r, :], s.fx, s.fy, c * 2 * s.fy, c * s.fe)
-        for h in range(s.halves):
-            at = lanes_of(h)
-            x_base, y_base = s.x_coarse + (h * 6 + c * 2) * s.cy, s.y_coarse + (h * 3 + c) * s.ce
-            field(lambda r: coarse[c, :, r, at], s.cx, s.cy, x_base, y_base)
+                put(y_base + (k if side == 0 else x + 2 + k), low[side], high[side])
+
+    level(lambda c, r: fine[c, :, r, :], s.fx, s.fy, 0, 0, s.fe, False)
+    for h in range(s.halves):
+        at = lanes_of(h)
+        x_base, y_base = s.x_coarse + h * 4 * s.cy, s.y_coarse + h * 2 * s.ce
+        level(lambda c, r: coarse[c, :, r, at], s.cx, s.cy, x_base, y_base, s.ce, h == 0)
     if step == 0:
         rig_f, met_f, rig_c, met_c = mats
         for m, (of_f, of_c) in enumerate(((rig_f, rig_c), (met_f, met_c))):
@@ -247,21 +289,45 @@
     lax.fori_loop(0, x + 2, row, 0, unroll=True)
 
 
-def fill_displacement(s, flags, own, ext, x_in, y_in, fine):
+def fill_displacement(s, flags, own, ext, x_in, y_in, fine, halves=None):
     x, y, e = (s.fx, s.fy, s.fe) if fine else (s.cx, s.cy, s.ce)
-    ext[:, 2 : 2 + x, 8 : 8 + y, :] = own[...]
-    for h in range(1 if fine else s.halves):
-        base = s.x_fine if fine else s.x_coarse + h * 6 * y
-        rows = slice(base, base + 6 * y)
-        low, high = sides(flags, EVEN_X, HAS_XM, HAS_XP, x_in[0][rows, :], x_in[1][rows, :])
-        ext[:, 0:2, 8 : 8 + y, lanes_of(h)] = low.reshape(3, 2, y, LANES)
-        ext[:, x + 2 : x + 4, 8 : 8 + y, lanes_of(h)] = high.reshape(3, 2, y, LANES)
-        for c in range(3):
-            start = c * e if fine else s.y_coarse + (h * 3 + c) * e
-            rows = slice(start, start + e)
-            low, high = sides(flags, EVEN_Y, HAS_YM, HAS_YP, y_in[0][rows], y_in[1][rows])
-            ext[c, :, 6:8, lanes_of(h)] = low
-            ext[c, :, 8 + y : 10 + y, lanes_of(h)] = high
+    halves = 1 if fine else halves or s.halves
+    ext[:, 2 : 2 + x, 8 : 8 + y, :] = own[:, :, :, 0 : halves * LANES]
+    mid = slice(8, 8 + y)
+
+    def from_x(first, rows):
+        rows = slice(first, first + rows)
+        return sides(flags, EVEN_X, HAS_XM, HAS_XP, x_in[0][rows, :], x_in[1][rows, :])
+
+    def from_y(first):
+        rows = slice(first, first + e)
+        return sides(flags, EVEN_Y, HAS_YM, HAS_YP, y_in[0][rows], y_in[1][rows])
+
+    for h in range(halves):
+        at = lanes_of(h)
+        base = 0 if fine else s.x_coarse + h * 4 * y
+        low, high = from_x(base, 2 * y)
+        ext[0, 0:2, mid, at] = low.reshape(2, y, LANES)
+        ext[0, x + 2 : x + 4, mid, at] = high.reshape(2, y, LANES)
+        for c in (1, 2):
+            ext[c, 1, mid, at], ext[c, x + 2, mid, at] = from_x(base + (1 + c) * y, y)
+        start = 0 if fine else s.y_coarse + h * 2 * e
+        ext[1, :, 6:8, at], ext[1, :, 8 + y : 10 + y, at] = from_y(start)
+        low, high = from_y(start + e)
+        for m, c in enumerate((0, 2)):
+            ext[c, :, 7:8, at] = low[:, m : m + 1, :]
+            ext[c, :, 8 + y : 9 + y, at] = high[:, m : m + 1, :]
+    if fine:
+        return
+    at = lanes_of(0)
+    low, high = from_x(s.x_plane, y)
+    for c in (1, 2):
+        ext[c, 0, mid, at] = pltpu.roll(low, LANES - c, 1)
+        ext[c, x + 3, mid, at] = pltpu.roll(high, LANES - c, 1)
+    low, high = from_y(s.y_plane)
+    for m, c in enumerate((0, 2)):
+        ext[c, :, 6:7, at] = low[:, m : m + 1, :]
+        ext[c, :, 9 + y : 10 + y, at] = high[:, m : m + 1, :]
 
 
 def fill_materials(s, flags, rigidity, metric, inverse, wide_ext, inv_ext, x_in, y_in, fine):
@@ -369,40 +435,7 @@
     return lax.fori_loop(0, x, row, start, unroll=4)
 
 
-def step_kernel(s, step, cells, *refs):
-    flags = where_am_i()
-    refs = list(refs)
-
-    def take(n):
-        out = refs[:n]
-        del refs[:n]
-        return out
-
-    fine, coarse, fine_prev, coarse_prev, offs = take(5)
-    coef_f, coef_c = take(5), take(5)
-    if step == 0:
-        rig_f, met_f, inverse_f, rig_c, met_c, inverse_c = take(6)
-    else:
-        wide_f, inv_f, wide_c, inv_c = take(4)
-    if step < 2:
-        beta_own = take(2)
-    if step == 1:
-        energy_in, spread_in = take(2)
-    x_in, y_in = take(2), take(2)
-    new_f, new_c = take(2)
-    if step < 2:
-        (energy,) = take(1)
-        x_out = take(2)
-    if step == 0:
-        wide_f, inv_f, wide_c, inv_c, spread_out = take(5)
-    ext_f, ext_c, div_f, div_c, double, moved, pairs = take(7)
-
-    fill_displacement(s, flags, fine, ext_f, x_in, y_in, True)
-    fill_displacement(s, flags, coarse, ext_c, x_in, y_in, False)
-    if step == 0:
-        fill_materials(s, flags, rig_f, met_f, inverse_f, wide_f, inv_f, x_in, y_in, True)
-        fill_materials(s, flags, rig_c, met_c, inverse_c, wide_c, inv_c, x_in, y_in, False)
-
+def double_plane(s, ext_c, double):
     lane = lax.broadcasted_iota(jnp.int32, (s.cy + 4, LANES), 1)
     table = jnp.zeros((s.cy + 4, LANES), jnp.float32)
     for i in range(s.ce):
@@ -414,20 +447,15 @@
             table = jnp.where(lane // 4 == k, there, table)
     for j in range(s.cy + 4):
         double[2 * j : 2 * j + 2, :] = jnp.broadcast_to(table[j : j + 1, :], (2, LANES))
+
+
+def add_pairs(s, fine, pairs):
     for c in range(3):
         for i in range(s.cx):
             pairs[c, i] = fine[c, 2 * i] + fine[c, 2 * i + 1]
 
-    fill_divergence(s.fx, s.fy, ext_f, inv_f, div_f)
-    fill_divergence(s.cx, s.cy, ext_c, inv_c, div_c)
-    psi_f = psi_c = None
-    if step == 1:
-        psi_f, psi_c, all_beta_f, all_beta_c, pairs_next, spread = take(6)
-        fill_beta(s, flags, beta_own[0], all_beta_f, x_in, y_in, True)
-        fill_beta(s, flags, beta_own[1], all_beta_c, x_in, y_in, False)
-        fill_transposed(s.fx, s.fy, ext_f, all_beta_f, inv_f, psi_f)
-        fill_transposed(s.cx, s.cy, ext_c, all_beta_c, inv_c, psi_c)
-
+
+def node_weights(s, offs):
     node = (s.fy, LANES)
     node_lane = lax.broadcasted_iota(jnp.int32, node, 1)
     near_x = jnp.where(node_lane // 4 % 2 == 0, 0.75, 0.25)
@@ -440,6 +468,12 @@
         ]
         for off, near in ((code // 4 - 1, near_x), (code % 4 - 1, near_y))
     )
+    return weights_x, weights_y
+
+
+def bottom_ghosts(s, weights, double, moved):
+    weights_x, weights_y = weights
+    node = (s.fy, LANES)
     ghosts = jnp.zeros(node, jnp.float32)
     for a in range(4):
         moved[a] = pltpu.roll(double[...], LANES - 8 * (1 + a), 1)
@@ -447,37 +481,82 @@
         for b in range(4):
             line += weights_y[b] * moved[a, 2 * b + 2 : 2 * b + 2 + s.fy, :]
         ghosts += weights_x[a] * line
-
-    def fine_ghosts(i):
-        return None, lambda c: pltpu.roll(ghosts, LANES - 1 - c - 4 * i, 1), None
-
-    def coarse_ghosts(i):
-        def mean(of):
-            def top(c):
-                both = of[c, i, pl.ds(0, s.cy, stride=2), :] + of[c, i, pl.ds(1, s.cy, stride=2), :]
-                return 0.25 * both[:, LANES - 1 :]
-
-            return top
-
-        return mean(pairs), None, mean(pairs_next) if step == 1 else None
-
+    return lambda i: (None, lambda c: pltpu.roll(ghosts, LANES - 1 - c - 4 * i, 1), None)
+
+
+def top_ghosts(s, pairs, pairs_next=None):
+    def mean(of, i):
+        def top(c):
+            both = of[c, i, pl.ds(0, s.cy, stride=2), :] + of[c, i, pl.ds(1, s.cy, stride=2), :]
+            return 0.25 * both[:, LANES - 1 :]
+
+        return top
+
+    return lambda i: (mean(pairs, i), None, mean(pairs_next, i) if pairs_next is not None else None)
+
+
+def step_kernel(s, step, cells, *refs):
+    flags = where_am_i()
+    refs = list(refs)
+
+    def take(n):
+        out = refs[:n]
+        del refs[:n]
+        return out
+
+    fine, coarse, fine_prev, coarse_prev, offs = take(5)
+    coef_f, coef_c = take(5), take(5)
+    if step == 0:
+        rig_f, met_f, inverse_f, rig_c, met_c, inverse_c = take(6)
+    else:
+        wide_f, inv_f, wide_c, inv_c = take(4)
+    beta_own = take(2)
+    if step == 1:
+        energy_in, spread_in = take(2)
+    x_in, y_in = take(2), take(2)
+    new_f, new_c, energy = take(3)
+    x_out = take(2)
+    if step == 0:
+        wide_f, inv_f, wide_c, inv_c, spread_out = take(5)
+    ext_f, ext_c, div_f, div_c, double, moved, pairs = take(7)
+
+    fill_displacement(s, flags, fine, ext_f, x_in, y_in, True)
+    fill_displacement(s, flags, coarse, ext_c, x_in, y_in, False)
+    if step == 0:
+        fill_materials(s, flags, rig_f, met_f, inverse_f, wide_f, inv_f, x_in, y_in, True)
+        fill_materials(s, flags, rig_c, met_c, inverse_c, wide_c, inv_c, x_in, y_in, False)
+
+    double_plane(s, ext_c, double)
+    add_pairs(s, fine, pairs)
+    fill_divergence(s.fx, s.fy, ext_f, inv_f, div_f)
+    fill_divergence(s.cx, s.cy, ext_c, inv_c, div_c)
+    psi_f = psi_c = None
+    if step == 1:
+        psi_f, psi_c, all_beta_f, all_beta_c, pairs_next, spread = take(6)
+        fill_beta(s, flags, beta_own[0], all_beta_f, x_in, y_in, True)
+        fill_beta(s, flags, beta_own[1], all_beta_c, x_in, y_in, False)
+        fill_transposed(s.fx, s.fy, ext_f, all_beta_f, inv_f, psi_f)
+        fill_transposed(s.cx, s.cy, ext_c, all_beta_c, inv_c, psi_c)
+
+    weights = node_weights(s, offs)
+    fine_ghosts = bottom_ghosts(s, weights, double, moved)
+    coarse_ghosts = top_ghosts(s, pairs, pairs_next if step == 1 else None)
     sums_f = update(
         s.fx, s.fy, ext_f, wide_f, inv_f, div_f, fine_prev, coef_f, new_f, fine_ghosts, psi_f
     )
     if step == 1:
-        for c in range(3):
-            for i in range(s.cx):
-                pairs_next[c, i] = new_f[c, 2 * i] + new_f[c, 2 * i + 1]
+        add_pairs(s, new_f, pairs_next)
     sums_c = update(
         s.cx, s.cy, ext_c, wide_c, inv_c, div_c, coarse_prev, coef_c, new_c, coarse_ghosts, psi_c
     )
-    if step == 2:
-        return
     place = lax.broadcasted_iota(jnp.int32, (8, LANES), 0)
     table = jnp.zeros((8, LANES), jnp.float32) if step == 0 else energy_in[...]
     table = jnp.where(place == step, jnp.sum(sums_f[0]) / cells[0], table)
     table = jnp.where(place == STEPS + step, jnp.sum(sums_c[0]) / cells[1], table)
     if step == 0:
+        weights_x, weights_y = weights
+        node = (s.fy, LANES)
+        node_lane = lax.broadcasted_iota(jnp.int32, node, 1)
         q = jnp.zeros(node, jnp.float32)
         for i in range(s.fx):
             for c in range(3):
@@ -512,6 +591,27 @@
         table = jnp.where(place == STEPS + 2, jnp.sum(sums_c[1]) / cells[1], table)
         put_x(s, flags, x_out, new_f, new_c)
     energy[...] = table
+
+
+def final_fine_kernel(s, fine, coarse, prev, offs, *refs):
+    coef, (wide, inv, xa, xb, ya, yb, new) = refs[:5], refs[5:12]
+    ext_f, ext_c, div, double, moved = refs[12:]
+    flags = where_am_i()
+    fill_displacement(s, flags, fine, ext_f, (xa, xb), (ya, yb), True)
+    fill_displacement(s, flags, coarse, ext_c, (xa, xb), (ya, yb), False, 1)
+    double_plane(s, ext_c, double)
+    fill_divergence(s.fx, s.fy, ext_f, inv, div)
+    ghosts = bottom_ghosts(s, node_weights(s, offs), double, moved)
+    update(s.fx, s.fy, ext_f, wide, inv, div, prev, coef, new, ghosts)
+
+
+def final_coarse_kernel(s, fine, coarse, prev, *refs):
+    coef, (wide, inv, xa, xb, ya, yb, new) = refs[:5], refs[5:12]
+    ext, div, pairs = refs[12:]
+    fill_displacement(s, where_am_i(), coarse, ext, (xa, xb), (ya, yb), False)
+    add_pairs(s, fine, pairs)
+    fill_divergence(s.cx, s.cy, ext, inv, div)
+    update(s.cx, s.cy, ext, wide, inv, div, prev, coef, new, top_ghosts(s, pairs))
 
 
 VMEM = pl.BlockSpec(memory_space=pltpu.VMEM)
@@ -692,10 +792,41 @@
             *x_in,
         )
         y_in = swap_both(y_out[:2], beside_y, across_y)
-        shapes = [fine.shape, coarse.shape]
+        if step == 2:
+            wide_f, inv_f, wide_c, inv_c = ext_mats
+            (fine_final,) = call(
+                functools.partial(final_fine_kernel, s),
+                [fine.shape],
+                2_000_000,
+                fine,
+                coarse,
+                fine_prev,
+                offs,
+                *coef_f,
+                wide_f,
+                inv_f,
+                *x_in,
+                *y_in,
+                scratch=[scratch[0], scratch[1][:3] + (LANES,), scratch[2], *scratch[4:6]],
+            )
+            (coarse_final,) = call(
+                functools.partial(final_coarse_kernel, s),
+                [coarse.shape],
+                2_000_000,
+                fine,
+                coarse,
+                coarse_prev,
+                *coef_c,
+                wide_c,
+                inv_c,
+                *x_in,
+                *y_in,
+                scratch=[scratch[1], scratch[3], scratch[6]],
+            )
+            break
+        shapes = [fine.shape, coarse.shape, (8, LANES)]
+        shapes += [((s.x_rows_beta, s.x_rows)[step], LANES)] * 2
         more_scratch = []
-        if step < 2:
-            shapes += [(8, LANES)] + [((s.x_rows_beta, s.x_rows)[step], LANES)] * 2
         if step == 0:
             extra = [fine_rigidity, fine_metric, inverse_f, coarse_rigidity, coarse_metric, inverse_c]
             extra += [beta_f, beta_c]
@@ -729,12 +860,11 @@
             scratch=scratch + more_scratch,
         )
         fine_prev, coarse_prev = fine, coarse
-        fine, coarse = outs[:2]
-        if step < 2:
-            energy, x_out = outs[2], outs[3:5]
+        fine, coarse, energy = outs[:3]
+        x_out = outs[3:5]
         if step == 0:
             *ext_mats, spread_own = outs[5:]
-    other, fine, coarse = lax.optimization_barrier((other, fine, coarse))
+    other, fine, coarse = lax.optimization_barrier((other, fine_final, coarse_final))
     energy = energy + other
     energy = energy[: 2 * STEPS, 0].reshape(2, STEPS).T
     return fine, coarse, energy

time: 80.7 us -> 78.5 us (0.973)
  waiting for transfers between devices: 27 us -> 24.8 us
  Pallas kernels: 10.9 us -> 11.8 us
    ppermute x20, waiting for transfers between devices: 27 us -> 24.8 us  [swap(): return lax.ppermute(value, ALL, swap_pairs(mesh, move))]
    pallas_call x9 -> x10, Pallas kernels: 10.9 us -> 11.8 us  [call(): pl.pallas_call(kernel, out_shape=shapes, in_specs=[spec] * len(args), out...]
  transfers between devices with their start and end apart: 20 -> 20, of which waited for: 15 -> 16; matrix products, arithmetic and copies ran while one was open for 0% -> 0% of each run, Pallas kernels for 4% -> 5%
where the time goes in v7:
time: 78.5 us; the launch traced here: 78.4 us
  starting transfers between devices  39.3 us (50%)
  waiting for transfers between devices  24.8 us (32%)
  Pallas kernels  11.8 us (15%)
  local copies, waits for them, and re-layouts  1.65 us (2%)
  between operations  0.84 us (1%)
    ppermute x20, starting transfers between devices, swap(): return lax.ppermute(value, ALL, swap_pairs(mesh, move))  39.3 us
    ppermute x20, waiting for transfers between devices, swap(): return lax.ppermute(value, ALL, swap_pairs(mesh, move))  24.8 us
    pallas_call x10, Pallas kernels, call(): pl.pallas_call(kernel, out_shape=shapes, in_specs=[spec] * len(args), out...  11.8 us
  transfers between devices with their start and end apart: 20, of which 16 were waited for; matrix products, arithmetic and copies ran while one was open for 0% of the time, Pallas kernels for 5%

profile of v7, /device:TPU:1, one launch (start us, length us, event | category | flops | bytes accessed | tf_op | source)
XLA Modules:
  0.0 78.4 jit_solution(5197218854640729122)
XLA Ops:
  1.9 2.1 %collective-permute-start = (f32[200,128]{1,0:T(8,128)S(1)}, f32[200,128]{1,0:T(8,128)S(1)}, u32[]{:S(2)}, u32[]{:S(2)}) collective-permute-start(f32[200,128]{1,0:T(8,128)S(1)} %get-tuple-element.58), channel_id=1, source_target_pairs={{0,8},{1,9},{2,10},{3,11},{4,12},{5,13},{6,14},{7,15},{8,0},{9,1},... | collective-permute-start | bytes 307208 | tf_op jit(solution)/shard_map/ppermute | solution.py:706
  6.5 3.7 %collective-permute-start.2 = (f32[132,2,128]{2,1,0:T(2,128)S(1)}, f32[132,2,128]{2,1,0:T(2,128)S(1)}, u32[]{:S(2)}, u32[]{:S(2)}) collective-permute-start(f32[132,2,128]{2,1,0:T(2,128)S(1)} %get-tuple-element.60), channel_id=1, source_target_pairs={{0,1},{1,0},{2,3},{3,2},{4,5},{5,4},{6,7},{7,6},{8,9},{9,8},{10,11... | collective-permute-start | bytes 405512 | tf_op jit(solution)/shard_map/ppermute | solution.py:706
  11.4 3.6 %collective-permute-done.3.refs_26_ = f32[132,2,128]{2,1,0:T(2,128)S(1)} collective-permute-done((f32[132,2,128]{2,1,0:T(2,128)S(1)}, f32[132,2,128]{2,1,0:T(2,128)S(1)}, u32[]{:S(2)}, u32[]{:S(2)}) %collective-permute-start.3) | collective-permute-done | bytes 135200 | tf_op jit(solution)/shard_map/ppermute | solution.py:706
  15.0 2.8 %shard_map.152 = (f32[3,16,16,128]{3,2,1,0:T(8,128)S(1)}, f32[3,8,8,256]{3,2,1,0:T(8,128)S(1)}, f32[8,128]{1,0:T(8,128)S(1)}, f32[232,128]{1,0:T(8,128)S(1)}, f3...) custom-call(f32[3,16,16,128]{3,2,1,0:T(8,128)S(1)} %copy-done, ...), custom_call_target="tpu_custom_call" | custom-call | flops 4000000 | bytes 1048576 | tf_op jit(solution)/shard_map/pallas_call | solution.py:626
  17.8 1.8 %collective-permute-start.4 = (f32[232,128]{1,0:T(8,128)S(1)}, f32[232,128]{1,0:T(8,128)S(1)}, u32[]{:S(2)}, u32[]{:S(2)}) collective-permute-start(f32[232,128]{1,0:T(8,128)S(1)} %get-tuple-element.70), channel_id=1, source_target_pairs={{0,8},{1,9},{2,10},{3,11},{4,12},{5,13},{6,14},{7,15},{8,0},{9,1},... | collective-permute-start | bytes 356360 | tf_op jit(solution)/shard_map/ppermute | solution.py:706
  19.6 1.3 %collective-permute-start.5 = (f32[232,128]{1,0:T(8,128)S(1)}, f32[232,128]{1,0:T(8,128)S(1)}, u32[]{:S(2)}, u32[]{:S(2)}) collective-permute-start(f32[232,128]{1,0:T(8,128)S(1)} %get-tuple-element.71), channel_id=1, source_target_pairs={{0,1},{1,0},{2,3},{3,2},{4,5},{5,4},{6,7},{7,6},{8,16},{9,17},{10,... | collective-permute-start | bytes 356360 | tf_op jit(solution)/shard_map/ppermute | solution.py:706
  20.9 1.3 %collective-permute-done.4.refs_5_.refs_23_ = f32[232,128]{1,0:T(8,128)S(1)} collective-permute-done((f32[232,128]{1,0:T(8,128)S(1)}, f32[232,128]{1,0:T(8,128)S(1)}, u32[]{:S(2)}, u32[]{:S(2)}) %collective-permute-start.4) | collective-permute-done | bytes 118816 | tf_op jit(solution)/shard_map/ppermute | solution.py:706
  22.4 1.7 %collective-permute-start.6 = (f32[152,2,128]{2,1,0:T(2,128)S(1)}, f32[152,2,128]{2,1,0:T(2,128)S(1)}, u32[]{:S(2)}, u32[]{:S(2)}) collective-permute-start(f32[152,2,128]{2,1,0:T(2,128)S(1)} %get-tuple-element.73), channel_id=1, source_target_pairs={{0,1},{1,0},{2,3},{3,2},{4,5},{5,4},{6,7},{7,6},{8,9},{9,8},{10,11... | collective-permute-start | bytes 466952 | tf_op jit(solution)/shard_map/ppermute | solution.py:706
  25.1 3.9 %collective-permute-done.7.refs_26_ = f32[152,2,128]{2,1,0:T(2,128)S(1)} collective-permute-done((f32[152,2,128]{2,1,0:T(2,128)S(1)}, f32[152,2,128]{2,1,0:T(2,128)S(1)}, u32[]{:S(2)}, u32[]{:S(2)}) %collective-permute-start.7) | collective-permute-done | bytes 155680 | tf_op jit(solution)/shard_map/ppermute | solution.py:706
  29.0 3.3 %shard_map.154 = (f32[3,16,16,128]{3,2,1,0:T(8,128)S(1)}, f32[3,8,8,256]{3,2,1,0:T(8,128)S(1)}, f32[8,128]{1,0:T(8,128)S(1)}, f32[136,128]{1,0:T(8,128)S(1)}, f32[136,128]{1,0:T(8,128)S(1)}) custom-call(f32[3,16,16,128]{3,2,1,0:T(8,128)S(1)} %get-tuple-element.62.refs_0_.prev, f32[3,8,8,256]{3,2,1,0:T(8,128)S(1)} %get-tuple-element.63.refs_1_.prev, ...), custom_call_target="tpu_custom_call" | custom-call | flops 4000000 | bytes 1048576 | tf_op jit(solution)/shard_map/pallas_call | solution.py:626
  32.3 3.2 %collective-permute-start.16 = (f32[136,128]{1,0:T(8,128)S(1)}, f32[136,128]{1,0:T(8,128)S(1)}, u32[]{:S(2)}, u32[]{:S(2)}) collective-permute-start(f32[136,128]{1,0:T(8,128)S(1)} %get-tuple-element.78), channel_id=1, source_target_pairs={{0,8},{1,9},{2,10},{3,11},{4,12},{5,13},{6,14},{7,15},{8,0},{9,1},... | collective-permute-start | bytes 208904 | tf_op jit(solution)/shard_map/ppermute | solution.py:706
  35.5 1.3 %collective-permute-start.17 = (f32[136,128]{1,0:T(8,128)S(1)}, f32[136,128]{1,0:T(8,128)S(1)}, u32[]{:S(2)}, u32[]{:S(2)}) collective-permute-start(f32[136,128]{1,0:T(8,128)S(1)} %get-tuple-element.79), channel_id=1, source_target_pairs={{0,1},{1,0},{2,3},{3,2},{4,5},{5,4},{6,7},{7,6},{8,16},{9,17},{10,... | collective-permute-start | bytes 208904 | tf_op jit(solution)/shard_map/ppermute | solution.py:706
  37.9 1.5 %collective-permute-start.18 = (f32[100,2,128]{2,1,0:T(2,128)S(1)}, f32[100,2,128]{2,1,0:T(2,128)S(1)}, u32[]{:S(2)}, u32[]{:S(2)}) collective-permute-start(f32[100,2,128]{2,1,0:T(2,128)S(1)} %get-tuple-element.80), channel_id=1, source_target_pairs={{0,1},{1,0},{2,3},{3,2},{4,5},{5,4},{6,7},{7,6},{8,9},{9,8},{10,11... | collective-permute-start | bytes 307208 | tf_op jit(solution)/shard_map/ppermute | solution.py:706
  39.4 10.5 %collective-permute-start.8 = (f32[8,128]{1,0:T(8,128)S(1)}, f32[8,128]{1,0:T(8,128)S(1)}, u32[]{:S(2)}, u32[]{:S(2)}) collective-permute-start(f32[8,128]{1,0:T(8,128)S(1)} %get-tuple-element.75), channel_id=1, source_target_pairs={{0,224},{1,225},{2,226},{3,227},{4,228},{5,229},{6,230},{7,231},{8... | collective-permute-start | bytes 12296 | tf_op jit(solution)/shard_map/ppermute | solution.py:706
  50.9 2.9 %collective-permute-start.9 = (f32[8,128]{1,0:T(8,128)S(1)}, f32[8,128]{1,0:T(8,128)S(1)}, u32[]{:S(2)}, u32[]{:S(2)}) collective-permute-start(f32[8,128]{1,0:T(8,128)S(1)} %add.43), channel_id=1, source_target_pairs={{0,1},{1,0},{2,3},{3,2},{4,5},{5,4},{6,7},{7,6},{8,9},{9,8},{10,11... | collective-permute-start | bytes 12296 | tf_op jit(solution)/shard_map/ppermute | solution.py:706
  54.6 2.4 %collective-permute-start.10 = (f32[8,128]{1,0:T(8,128)S(1)}, f32[8,128]{1,0:T(8,128)S(1)}, u32[]{:S(2)}, u32[]{:S(2)}) collective-permute-start(f32[8,128]{1,0:T(8,128)S(1)} %add.44), channel_id=1, source_target_pairs={{0,65},{1,64},{2,67},{3,66},{4,69},{5,68},{6,71},{7,70},{8,73},{9,... | collective-permute-start | bytes 12296 | tf_op jit(solution)/shard_map/ppermute | solution.py:706
  57.0 1.5 %collective-permute-done.10 = f32[8,128]{1,0:T(8,128)S(1)} collective-permute-done((f32[8,128]{1,0:T(8,128)S(1)}, f32[8,128]{1,0:T(8,128)S(1)}, u32[]{:S(2)}, u32[]{:S(2)}) %collective-permute-start.10) | collective-permute-done | bytes 4128 | tf_op jit(solution)/shard_map/ppermute | solution.py:706
  58.6 3.0 %collective-permute-done.11 = f32[8,128]{1,0:T(8,128)S(1)} collective-permute-done((f32[8,128]{1,0:T(8,128)S(1)}, f32[8,128]{1,0:T(8,128)S(1)}, u32[]{:S(2)}, u32[]{:S(2)}) %collective-permute-start.11) | collective-permute-done | bytes 4128 | tf_op jit(solution)/shard_map/ppermute | solution.py:706
  61.6 3.0 %collective-permute-done.12 = f32[8,128]{1,0:T(8,128)S(1)} collective-permute-done((f32[8,128]{1,0:T(8,128)S(1)}, f32[8,128]{1,0:T(8,128)S(1)}, u32[]{:S(2)}, u32[]{:S(2)}) %collective-permute-start.12) | collective-permute-done | bytes 4128 | tf_op jit(solution)/shard_map/ppermute | solution.py:706
  64.6 3.2 %collective-permute-start.13 = (f32[8,128]{1,0:T(8,128)S(1)}, f32[8,128]{1,0:T(8,128)S(1)}, u32[]{:S(2)}, u32[]{:S(2)}) collective-permute-start(f32[8,128]{1,0:T(8,128)S(1)} %add.47), channel_id=1, source_target_pairs={{0,33},{1,32},{2,35},{3,34},{4,37},{5,36},{6,39},{7,38},{8,41},{9,... | collective-permute-start | bytes 12296 | tf_op jit(solution)/shard_map/ppermute | solution.py:706
  69.1 2.1 %collective-permute-start.14 = (f32[8,128]{1,0:T(8,128)S(1)}, f32[8,128]{1,0:T(8,128)S(1)}, u32[]{:S(2)}, u32[]{:S(2)}) collective-permute-start(f32[8,128]{1,0:T(8,128)S(1)} %add.48), channel_id=1, source_target_pairs={{0,25},{1,24},{2,27},{3,26},{4,29},{5,28},{6,31},{7,30},{8,17},{9,... | collective-permute-start | bytes 12296 | tf_op jit(solution)/shard_map/ppermute | solution.py:706
  71.3 2.1 %collective-permute-done.14 = f32[8,128]{1,0:T(8,128)S(1)} collective-permute-done((f32[8,128]{1,0:T(8,128)S(1)}, f32[8,128]{1,0:T(8,128)S(1)}, u32[]{:S(2)}, u32[]{:S(2)}) %collective-permute-start.14) | collective-permute-done | bytes 4128 | tf_op jit(solution)/shard_map/ppermute | solution.py:706
  73.6 2.0 %shard_map.156 = f32[3,16,16,128]{3,2,1,0:T(8,128)} custom-call(f32[3,16,16,128]{3,2,1,0:T(8,128)S(1)} %get-tuple-element.76.refs_0_.fine, f32[3,8,8,256]{3,2,1,0:T(8,128)S(1)} %get-tuple-element.77.refs_1_.coarse, f32[3,16,16,128]{3,2,1,0:T(8,128)S(1)} %get-tuple-element.62.refs_0_.prev, s32[16,128]{1,0:T(8,128)S(1)} %pad.4.refs_4_.offs, ...), custom_call_target="tpu_custom_call" | custom-call | flops 2000000 | bytes 1048576 | tf_op jit(solution)/shard_map/pallas_call | solution.py:626
  75.6 1.6 %shard_map.157 = f32[3,8,8,256]{3,2,1,0:T(8,128)} custom-call(f32[3,16,16,128]{3,2,1,0:T(8,128)S(1)} %get-tuple-element.76.refs_0_.fine, f32[3,8,8,256]{3,2,1,0:T(8,128)S(1)} %get-tuple-element.77.refs_1_.coarse, f32[3,8,8,256]{3,2,1,0:T(8,128)S(1)} %get-tuple-element.63.refs_1_.prev, f32[8,8,256]{2,1,0:T(8,128)S(1)} %get-tuple-element.49.refs_10_.refs_0_, ...), custom_call_target="tpu_custom_call" | custom-call | flops 2000000 | bytes 1048576 | tf_op jit(solution)/shard_map/pallas_call | solution.py:626
  (66 shorter events, 11.6 us)
Async XLA Ops:
  0.6 5.7 %copy-start.5 = (f32[8,8,256]{2,1,0:T(8,128)S(1)}, f32[8,8,256]{2,1,0:T(8,128)}, u32[]{:S(2)}) copy-start(f32[8,8,256]{2,1,0:T(8,128)} %refs_19_.1) | copy-start | bytes 196612
  0.6 5.6 %copy-start.4 = (f32[8,8,256]{2,1,0:T(8,128)S(1)}, f32[8,8,256]{2,1,0:T(8,128)}, u32[]{:S(2)}) copy-start(f32[8,8,256]{2,1,0:T(8,128)} %refs_18_.1) | copy-start | bytes 196612
  0.7 5.6 %copy-start.3 = (f32[16,16,128]{2,1,0:T(8,128)S(1)}, f32[16,16,128]{2,1,0:T(8,128)}, u32[]{:S(2)}) copy-start(f32[16,16,128]{2,1,0:T(8,128)} %refs_16_.1) | copy-start | bytes 393220
  1.9 4.2 %collective-permute-start = (f32[200,128]{1,0:T(8,128)S(1)}, f32[200,128]{1,0:T(8,128)S(1)}, u32[]{:S(2)}, u32[]{:S(2)}) collective-permute-start(f32[200,128]{1,0:T(8,128)S(1)} %get-tuple-element.58), channel_id=1, source_target_pairs={{0,8},{1,9},{2,10},{3,11},{4,12},{5,13},{6,14},{7,15},{8,0},{9,1},... | collective-permute-start | bytes 307208 | tf_op jit(solution)/shard_map/ppermute | solution.py:706
  4.0 6.2 %copy-start.12 = (s32[2,16,16]{2,1,0:T(8,128)S(1)}, s32[2,16,16]{2,1,0:T(8,128)}, u32[]{:S(2)}) copy-start(s32[2,16,16]{2,1,0:T(8,128)} %param.25) | copy-start | bytes 6148
  4.0 2.2 %collective-permute-start.1 = (f32[200,128]{1,0:T(8,128)S(1)}, f32[200,128]{1,0:T(8,128)S(1)}, u32[]{:S(2)}, u32[]{:S(2)}) collective-permute-start(f32[200,128]{1,0:T(8,128)S(1)} %get-tuple-element.59), channel_id=1, source_target_pairs={{0,1},{1,0},{2,3},{3,2},{4,5},{5,4},{6,7},{7,6},{8,16},{9,17},{10,... | collective-permute-start | bytes 307208 | tf_op jit(solution)/shard_map/ppermute | solution.py:706
  6.5 4.8 %collective-permute-start.2 = (f32[132,2,128]{2,1,0:T(2,128)S(1)}, f32[132,2,128]{2,1,0:T(2,128)S(1)}, u32[]{:S(2)}, u32[]{:S(2)}) collective-permute-start(f32[132,2,128]{2,1,0:T(2,128)S(1)} %get-tuple-element.60), channel_id=1, source_target_pairs={{0,1},{1,0},{2,3},{3,2},{4,5},{5,4},{6,7},{7,6},{8,9},{9,8},{10,11... | collective-permute-start | bytes 405512 | tf_op jit(solution)/shard_map/ppermute | solution.py:706
  10.2 4.7 %collective-permute-start.3 = (f32[132,2,128]{2,1,0:T(2,128)S(1)}, f32[132,2,128]{2,1,0:T(2,128)S(1)}, u32[]{:S(2)}, u32[]{:S(2)}) collective-permute-start(f32[132,2,128]{2,1,0:T(2,128)S(1)} %get-tuple-element.61), channel_id=1, source_target_pairs={{0,7},{1,2},{2,1},{3,4},{4,3},{5,6},{6,5},{7,0},{8,15},{9,10},{10,... | collective-permute-start | bytes 405512 | tf_op jit(solution)/shard_map/ppermute | solution.py:706
  17.8 4.4 %collective-permute-start.4 = (f32[232,128]{1,0:T(8,128)S(1)}, f32[232,128]{1,0:T(8,128)S(1)}, u32[]{:S(2)}, u32[]{:S(2)}) collective-permute-start(f32[232,128]{1,0:T(8,128)S(1)} %get-tuple-element.70), channel_id=1, source_target_pairs={{0,8},{1,9},{2,10},{3,11},{4,12},{5,13},{6,14},{7,15},{8,0},{9,1},... | collective-permute-start | bytes 356360 | tf_op jit(solution)/shard_map/ppermute | solution.py:706
  19.6 2.6 %collective-permute-start.5 = (f32[232,128]{1,0:T(8,128)S(1)}, f32[232,128]{1,0:T(8,128)S(1)}, u32[]{:S(2)}, u32[]{:S(2)}) collective-permute-start(f32[232,128]{1,0:T(8,128)S(1)} %get-tuple-element.71), channel_id=1, source_target_pairs={{0,1},{1,0},{2,3},{3,2},{4,5},{5,4},{6,7},{7,6},{8,16},{9,17},{10,... | collective-permute-start | bytes 356360 | tf_op jit(solution)/shard_map/ppermute | solution.py:706
  22.4 2.7 %collective-permute-start.6 = (f32[152,2,128]{2,1,0:T(2,128)S(1)}, f32[152,2,128]{2,1,0:T(2,128)S(1)}, u32[]{:S(2)}, u32[]{:S(2)}) collective-permute-start(f32[152,2,128]{2,1,0:T(2,128)S(1)} %get-tuple-element.73), channel_id=1, source_target_pairs={{0,1},{1,0},{2,3},{3,2},{4,5},{5,4},{6,7},{7,6},{8,9},{9,8},{10,11... | collective-permute-start | bytes 466952 | tf_op jit(solution)/shard_map/ppermute | solution.py:706
  24.1 5.0 %collective-permute-start.7 = (f32[152,2,128]{2,1,0:T(2,128)S(1)}, f32[152,2,128]{2,1,0:T(2,128)S(1)}, u32[]{:S(2)}, u32[]{:S(2)}) collective-permute-start(f32[152,2,128]{2,1,0:T(2,128)S(1)} %get-tuple-element.74), channel_id=1, source_target_pairs={{0,7},{1,2},{2,1},{3,4},{4,3},{5,6},{6,5},{7,0},{8,15},{9,10},{10,... | collective-permute-start | bytes 466952 | tf_op jit(solution)/shard_map/ppermute | solution.py:706
  32.3 4.9 %collective-permute-start.16 = (f32[136,128]{1,0:T(8,128)S(1)}, f32[136,128]{1,0:T(8,128)S(1)}, u32[]{:S(2)}, u32[]{:S(2)}) collective-permute-start(f32[136,128]{1,0:T(8,128)S(1)} %get-tuple-element.78), channel_id=1, source_target_pairs={{0,8},{1,9},{2,10},{3,11},{4,12},{5,13},{6,14},{7,15},{8,0},{9,1},... | collective-permute-start | bytes 208904 | tf_op jit(solution)/shard_map/ppermute | solution.py:706
  35.5 2.2 %collective-permute-start.17 = (f32[136,128]{1,0:T(8,128)S(1)}, f32[136,128]{1,0:T(8,128)S(1)}, u32[]{:S(2)}, u32[]{:S(2)}) collective-permute-start(f32[136,128]{1,0:T(8,128)S(1)} %get-tuple-element.79), channel_id=1, source_target_pairs={{0,1},{1,0},{2,3},{3,2},{4,5},{5,4},{6,7},{7,6},{8,16},{9,17},{10,... | collective-permute-start | bytes 208904 | tf_op jit(solution)/shard_map/ppermute | solution.py:706
  37.9 35.7 %collective-permute-start.18 = (f32[100,2,128]{2,1,0:T(2,128)S(1)}, f32[100,2,128]{2,1,0:T(2,128)S(1)}, u32[]{:S(2)}, u32[]{:S(2)}) collective-permute-start(f32[100,2,128]{2,1,0:T(2,128)S(1)} %get-tuple-element.80), channel_id=1, source_target_pairs={{0,1},{1,0},{2,3},{3,2},{4,5},{5,4},{6,7},{7,6},{8,9},{9,8},{10,11... | collective-permute-start | bytes 307208 | tf_op jit(solution)/shard_map/ppermute | solution.py:706
  39.4 34.2 %collective-permute-start.19 = (f32[100,2,128]{2,1,0:T(2,128)S(1)}, f32[100,2,128]{2,1,0:T(2,128)S(1)}, u32[]{:S(2)}, u32[]{:S(2)}) collective-permute-start(f32[100,2,128]{2,1,0:T(2,128)S(1)} %get-tuple-element.81), channel_id=1, source_target_pairs={{0,7},{1,2},{2,1},{3,4},{4,3},{5,6},{6,5},{7,0},{8,15},{9,10},{10,... | collective-permute-start | bytes 307208 | tf_op jit(solution)/shard_map/ppermute | solution.py:706
  39.4 11.5 %collective-permute-start.8 = (f32[8,128]{1,0:T(8,128)S(1)}, f32[8,128]{1,0:T(8,128)S(1)}, u32[]{:S(2)}, u32[]{:S(2)}) collective-permute-start(f32[8,128]{1,0:T(8,128)S(1)} %get-tuple-element.75), channel_id=1, source_target_pairs={{0,224},{1,225},{2,226},{3,227},{4,228},{5,229},{6,230},{7,231},{8... | collective-permute-start | bytes 12296 | tf_op jit(solution)/shard_map/ppermute | solution.py:706
  50.9 3.7 %collective-permute-start.9 = (f32[8,128]{1,0:T(8,128)S(1)}, f32[8,128]{1,0:T(8,128)S(1)}, u32[]{:S(2)}, u32[]{:S(2)}) collective-permute-start(f32[8,128]{1,0:T(8,128)S(1)} %add.43), channel_id=1, source_target_pairs={{0,1},{1,0},{2,3},{3,2},{4,5},{5,4},{6,7},{7,6},{8,9},{9,8},{10,11... | collective-permute-start | bytes 12296 | tf_op jit(solution)/shard_map/ppermute | solution.py:706
  54.6 3.9 %collective-permute-start.10 = (f32[8,128]{1,0:T(8,128)S(1)}, f32[8,128]{1,0:T(8,128)S(1)}, u32[]{:S(2)}, u32[]{:S(2)}) collective-permute-start(f32[8,128]{1,0:T(8,128)S(1)} %add.44), channel_id=1, source_target_pairs={{0,65},{1,64},{2,67},{3,66},{4,69},{5,68},{6,71},{7,70},{8,73},{9,... | collective-permute-start | bytes 12296 | tf_op jit(solution)/shard_map/ppermute | solution.py:706
  58.5 3.0 %collective-permute-start.11 = (f32[8,128]{1,0:T(8,128)S(1)}, f32[8,128]{1,0:T(8,128)S(1)}, u32[]{:S(2)}, u32[]{:S(2)}) collective-permute-start(f32[8,128]{1,0:T(8,128)S(1)} %add.45), channel_id=1, source_target_pairs={{0,3},{1,2},{2,1},{3,0},{4,7},{5,6},{6,5},{7,4},{8,11},{9,10},{10,... | collective-permute-start | bytes 12296 | tf_op jit(solution)/shard_map/ppermute | solution.py:706
  61.6 3.0 %collective-permute-start.12 = (f32[8,128]{1,0:T(8,128)S(1)}, f32[8,128]{1,0:T(8,128)S(1)}, u32[]{:S(2)}, u32[]{:S(2)}) collective-permute-start(f32[8,128]{1,0:T(8,128)S(1)} %add.46), channel_id=1, source_target_pairs={{0,9},{1,8},{2,11},{3,10},{4,13},{5,12},{6,15},{7,14},{8,1},{9,0},... | collective-permute-start | bytes 12296 | tf_op jit(solution)/shard_map/ppermute | solution.py:706
  64.6 4.5 %collective-permute-start.13 = (f32[8,128]{1,0:T(8,128)S(1)}, f32[8,128]{1,0:T(8,128)S(1)}, u32[]{:S(2)}, u32[]{:S(2)}) collective-permute-start(f32[8,128]{1,0:T(8,128)S(1)} %add.47), channel_id=1, source_target_pairs={{0,33},{1,32},{2,35},{3,34},{4,37},{5,36},{6,39},{7,38},{8,41},{9,... | collective-permute-start | bytes 12296 | tf_op jit(solution)/shard_map/ppermute | solution.py:706
  69.1 4.2 %collective-permute-start.14 = (f32[8,128]{1,0:T(8,128)S(1)}, f32[8,128]{1,0:T(8,128)S(1)}, u32[]{:S(2)}, u32[]{:S(2)}) collective-permute-start(f32[8,128]{1,0:T(8,128)S(1)} %add.48), channel_id=1, source_target_pairs={{0,25},{1,24},{2,27},{3,26},{4,29},{5,28},{6,31},{7,30},{8,17},{9,... | collective-permute-start | bytes 12296 | tf_op jit(solution)/shard_map/ppermute | solution.py:706
  73.4 4.2 %collective-permute-start.15 = (f32[8,128]{1,0:T(8,128)S(1)}, f32[8,128]{1,0:T(8,128)S(1)}, u32[]{:S(2)}, u32[]{:S(2)}) collective-permute-start(f32[8,128]{1,0:T(8,128)S(1)} %add.49), channel_id=1, source_target_pairs={{0,7},{1,6},{2,5},{3,4},{4,3},{5,2},{6,1},{7,0},{8,15},{9,14},{10,... | collective-permute-start | bytes 12296 | tf_op jit(solution)/shard_map/ppermute | solution.py:706
  (9 other events, 35.0 us)

commit v8 on v7

--- a/solution.py
+++ b/solution.py
@@ -227,30 +227,34 @@
     return pltpu.roll(x, 1, x.ndim - 1)
 
 
+def edge_factor(shape, first, last):
+    lane = first + lax.broadcasted_iota(jnp.int32, shape, len(shape) - 1)
+    return jnp.where((lane == 0) | (lane == last), 2.0, 1.0)
+
+
 def own_kernel(density, lame, rigidity, metric, inverse, c1, c2, weight, above, first, beta):
     inv = 1.0 / metric[...]
-    inverse[...] = inv
+    last = inv.shape[2] - 1
+    inverse[...] = inv * edge_factor(inv.shape, 0, last)
     over = 1.0 / density[...]
-    c1[...] = inv * over
-    c2[...] = (lame[...] + rigidity[...]) * over
+    c1[...] = (0.5 * STEP) * (inv * over)
+    c2[...] = (0.25 * STEP) * ((lame[...] + rigidity[...]) * over)
     weight[...] = density[...] * metric[...]
     v = rigidity[...] * inv
     lane = lax.broadcasted_iota(jnp.int32, v.shape, 2)
-    above[...] = jnp.where(lane == v.shape[2] - 1, v, 0.5 * (v + up_one(v)))
-    first[...] = v[:, :, 0:LANES]
-    beta[...] = (lame[...] + rigidity[...]) * metric[...]
-
-
-def slope(f, up, down, lane):
-    last = f.shape[-1] - 1
-    return jnp.where(lane == 0, up - f, jnp.where(lane == last, f - down, 0.5 * (up - down)))
-
-
-def slope_transposed(q, lane):
-    last = q.shape[-1] - 1
-    half = jnp.where((lane == 0) | (lane == last), q, 0.5 * q)
-    down = jnp.where(lane == 0, -half, down_one(half))
-    return down - jnp.where(lane == last, -half, up_one(half))
+    above[...] = v + jnp.where(lane == last, v, up_one(v))
+    first[...] = 2.0 * v[:, :, 0:LANES]
+    beta[...] = 0.5 * ((lame[...] + rigidity[...]) * metric[...])
+
+
+def difference(f, lane):
+    up = jnp.where(lane == f.shape[-1] - 1, f, up_one(f))
+    return up - jnp.where(lane == 0, f, down_one(f))
+
+
+def difference_transposed(q, lane):
+    down = jnp.where(lane == 0, -q, down_one(q))
+    return down - jnp.where(lane == q.shape[-1] - 1, -q, up_one(q))
 
 
 def fill_beta(s, flags, own, ext, x_in, y_in, fine):
@@ -282,7 +286,7 @@
         along_y -= ext[1, r + 1, high, :] * beta[r + 1, high, :]
         inv = inv_ext[r, 0 : 2 + y, :]
         column = inv * beta[r + 1, wide, :] * ext[2, r + 1, wide, :]
-        total = 0.5 * along_x + 0.5 * along_y + slope_transposed(column, lane)
+        total = along_x + along_y + difference_transposed(column, lane)
         psi[r, wide, :] = jnp.where(inv > 0.0, total, 0.0)
         return carry
 
@@ -332,10 +336,12 @@
 
 def fill_materials(s, flags, rigidity, metric, inverse, wide_ext, inv_ext, x_in, y_in, fine):
     x, y = (s.fx, s.fy) if fine else (s.cx, s.cy)
+    own_z = metric.shape[2]
     wide_ext[1 : 1 + x, 1 : 1 + y, :] = rigidity[...] * metric[...]
     inv_ext[1 : 1 + x, 1 : 1 + y, :] = inverse[...]
     for h in range(1 if fine else s.halves):
         at = lanes_of(h)
+        edge = edge_factor((y, LANES), h * LANES, own_z - 1)
         got = []
         for m in range(2):
             base = s.x_fine_mats + m * y if fine else s.x_coarse_mats + (m * s.halves + h) * y
@@ -346,7 +352,7 @@
         for side, (flag, place) in enumerate(((HAS_XM, 0), (HAS_XP, x + 1))):
             rig, met = got[0][side], got[1][side]
             wide_ext[place, 1 : 1 + y, at] = jnp.where(flags[flag], rig * met, 0.0)
-            inv_ext[place, 1 : 1 + y, at] = jnp.where(flags[flag], 1.0 / met, 0.0)
+            inv_ext[place, 1 : 1 + y, at] = jnp.where(flags[flag], edge / met, 0.0)
         start = s.y_fine_mats if fine else s.y_coarse_mats + h * x
         rows = slice(start, start + x)
         got = []
@@ -357,7 +363,7 @@
         for side, (flag, place) in enumerate(((HAS_YM, 0), (HAS_YP, 1 + y))):
             rig, met = got[0][side], got[1][side]
             wide_ext[1 : 1 + x, place : place + 1, at] = jnp.where(flags[flag], rig * met, 0.0)
-            inv_ext[1 : 1 + x, place : place + 1, at] = jnp.where(flags[flag], 1.0 / met, 0.0)
+            inv_ext[1 : 1 + x, place : place + 1, at] = jnp.where(flags[flag], edge[None, 0:1] / met, 0.0)
 
 
 def fill_divergence(x, y, ext, inv_ext, div):
@@ -369,7 +375,7 @@
         along_y = ext[1, r + 1, 8 : 10 + y, :] - ext[1, r + 1, 6 : 8 + y, :]
         f = ext[2, r + 1, 7 : 9 + y, :]
         inv = inv_ext[r, 0 : 2 + y, :]
-        total = 0.5 * along_x + 0.5 * along_y + inv * slope(f, up_one(f), down_one(f), lane)
+        total = along_x + along_y + inv * difference(f, lane)
         div[r, 7 : 9 + y, :] = jnp.where(inv > 0.0, total, 0.0)
         return carry
 
@@ -384,22 +390,21 @@
 
     def row(i, totals):
         wide = wide_ext[i + 1, own, :]
-        w_xp = 0.5 * (wide + wide_ext[i + 2, own, :])
-        w_xm = 0.5 * (wide_ext[i, own, :] + wide)
-        w_yp = 0.5 * (wide + wide_ext[i + 1, 2 : 2 + y, :])
-        w_ym = 0.5 * (wide_ext[i + 1, 0:y, :] + wide)
+        w_xp = wide + wide_ext[i + 2, own, :]
+        w_xm = wide_ext[i, own, :] + wide
+        w_yp = wide + wide_ext[i + 1, 2 : 2 + y, :]
+        w_ym = wide_ext[i + 1, 0:y, :] + wide
         inv = inv_ext[i + 1, own, :]
-        f = div[i + 1, mid, :]
         gradient = (
-            0.5 * (div[i + 2, mid, :] - div[i, mid, :]),
-            0.5 * (div[i + 1, right, :] - div[i + 1, left, :]),
-            inv * slope(f, up_one(f), down_one(f), lane),
+            div[i + 2, mid, :] - div[i, mid, :],
+            div[i + 1, right, :] - div[i + 1, left, :],
+            inv * difference(div[i + 1, mid, :], lane),
         )
         if psi is not None:
             transposed = (
-                0.5 * (psi[i, mid, :] - psi[i + 2, mid, :]),
-                0.5 * (psi[i + 1, left, :] - psi[i + 1, right, :]),
-                slope_transposed(inv * psi[i + 1, mid, :], lane),
+                psi[i, mid, :] - psi[i + 2, mid, :],
+                psi[i + 1, left, :] - psi[i + 1, right, :],
+                difference_transposed(inv * psi[i + 1, mid, :], lane),
             )
         top, bottom, top_next = ghosts(i)
         k1, k2, dm, va = c1[i], c2[i], weight[i], above[i]
@@ -409,17 +414,26 @@
             u = ext[c, i + 2, mid, :]
             flux = w_xp * (ext[c, i + 3, mid, :] - u) - w_xm * (u - ext[c, i + 1, mid, :])
             flux += w_yp * (ext[c, i + 2, right, :] - u) - w_ym * (u - ext[c, i + 2, left, :])
-            over = va * (jnp.where(lane == z - 1, 0.0, up_one(u)) - u)
-            entry = 0.0 if top is None else first * u[:, 0:1]
+            below = entry = 0.0
+            if psi is None:
+                below = 0.0 if bottom is None else bottom(c)
+                entry = 0.0 if top is None else first * (u[:, 0:1] - top(c))
+            elif top is not None:
+                entry = first * u[:, 0:1]
+            over = va * (jnp.where(lane == z - 1, below, up_one(u)) - u)
             flux += over - jnp.where(lane == 0, entry, down_one(over))
-            if top is None:
-                ghost = jnp.where(lane == z - 1, va * bottom(c), 0.0)
-            else:
-                ghost = jnp.where(lane == 0, first * top(c), 0.0)
-            rate = (flux + ghost) * k1 + k2 * gradient[c]
-            updated = 2.0 * u - prev[c, i] + STEP * rate
-            change = updated - u
-            inner += change * change - STEP * updated * rate
+            whole = flux
+            if psi is not None:
+                if top is None:
+                    whole = flux + jnp.where(lane == z - 1, va * bottom(c), 0.0)
+                else:
+                    whole = flux + jnp.where(lane == 0, first * top(c), 0.0)
+            push = whole * k1 + k2 * gradient[c]
+            before = prev[c, i]
+            change = u - before
+            inner += change * change - before * push
+            change += push
+            updated = u + change
             new[c, i] = updated
             if psi is not None:
                 squares += change * change
@@ -429,7 +443,7 @@
         total = totals[0] + dm * inner
         if psi is None:
             return (total,)
-        return total, totals[1] + (dm * squares - STEP * cross)
+        return total, totals[1] + (dm * squares - (0.5 * STEP) * cross)
 
     start = (jnp.zeros((y, z), jnp.float32),) * (1 if psi is None else 2)
     return lax.fori_loop(0, x, row, start, unroll=4)
@@ -587,7 +601,7 @@
                 weights = spread[i] if c == 0 else pltpu.roll(spread[i], LANES - c, 1)
                 joined += new_c[c, i, :, 0:LANES] * weights
         joined = jnp.sum(joined[:, 0:1])
-        table = jnp.where(place == 2, (jnp.sum(sums_f[1]) - STEP * joined) / cells[0], table)
+        table = jnp.where(place == 2, (jnp.sum(sums_f[1]) - (0.5 * STEP) * joined) / cells[0], table)
         table = jnp.where(place == STEPS + 2, jnp.sum(sums_c[1]) / cells[1], table)
         put_x(s, flags, x_out, new_f, new_c)
     energy[...] = table

time: 78.5 us -> 78.2 us (level)
  no operation moved by 1% of the time
where the time goes in v8:
time: 78.2 us; the launch traced here: 78 us
  starting transfers between devices  39.3 us (50%)
  waiting for transfers between devices  24.9 us (32%)
  Pallas kernels  11.3 us (14%)
  local copies, waits for them, and re-layouts  1.64 us (2%)
  between operations  0.84 us (1%)
    ppermute x20, starting transfers between devices, swap(): return lax.ppermute(value, ALL, swap_pairs(mesh, move))  39.3 us
    ppermute x20, waiting for transfers between devices, swap(): return lax.ppermute(value, ALL, swap_pairs(mesh, move))  24.9 us
    pallas_call x10, Pallas kernels, call(): pl.pallas_call(kernel, out_shape=shapes, in_specs=[spec] * len(args), out...  11.3 us
  transfers between devices with their start and end apart: 20, of which 16 were waited for; matrix products, arithmetic and copies ran while one was open for 0% of the time, Pallas kernels for 5%

profile of v8, /device:TPU:1, one launch (start us, length us, event | category | flops | bytes accessed | tf_op | source)
XLA Modules:
  0.0 78.0 jit_solution(17676076627664140092)
XLA Ops:
  1.9 2.1 %collective-permute-start = (f32[200,128]{1,0:T(8,128)S(1)}, f32[200,128]{1,0:T(8,128)S(1)}, u32[]{:S(2)}, u32[]{:S(2)}) collective-permute-start(f32[200,128]{1,0:T(8,128)S(1)} %get-tuple-element.58), channel_id=1, source_target_pairs={{0,8},{1,9},{2,10},{3,11},{4,12},{5,13},{6,14},{7,15},{8,0},{9,1},... | collective-permute-start | bytes 307208 | tf_op jit(solution)/shard_map/ppermute | solution.py:720
  6.5 3.7 %collective-permute-start.2 = (f32[132,2,128]{2,1,0:T(2,128)S(1)}, f32[132,2,128]{2,1,0:T(2,128)S(1)}, u32[]{:S(2)}, u32[]{:S(2)}) collective-permute-start(f32[132,2,128]{2,1,0:T(2,128)S(1)} %get-tuple-element.60), channel_id=1, source_target_pairs={{0,1},{1,0},{2,3},{3,2},{4,5},{5,4},{6,7},{7,6},{8,9},{9,8},{10,11... | collective-permute-start | bytes 405512 | tf_op jit(solution)/shard_map/ppermute | solution.py:720
  11.4 3.6 %collective-permute-done.3.refs_26_ = f32[132,2,128]{2,1,0:T(2,128)S(1)} collective-permute-done((f32[132,2,128]{2,1,0:T(2,128)S(1)}, f32[132,2,128]{2,1,0:T(2,128)S(1)}, u32[]{:S(2)}, u32[]{:S(2)}) %collective-permute-start.3) | collective-permute-done | bytes 135200 | tf_op jit(solution)/shard_map/ppermute | solution.py:720
  15.0 2.6 %shard_map.152 = (f32[3,16,16,128]{3,2,1,0:T(8,128)S(1)}, f32[3,8,8,256]{3,2,1,0:T(8,128)S(1)}, f32[8,128]{1,0:T(8,128)S(1)}, f32[232,128]{1,0:T(8,128)S(1)}, f3...) custom-call(f32[3,16,16,128]{3,2,1,0:T(8,128)S(1)} %copy-done, ...), custom_call_target="tpu_custom_call" | custom-call | flops 4000000 | bytes 1048576 | tf_op jit(solution)/shard_map/pallas_call | solution.py:640
  17.6 1.8 %collective-permute-start.4 = (f32[232,128]{1,0:T(8,128)S(1)}, f32[232,128]{1,0:T(8,128)S(1)}, u32[]{:S(2)}, u32[]{:S(2)}) collective-permute-start(f32[232,128]{1,0:T(8,128)S(1)} %get-tuple-element.70), channel_id=1, source_target_pairs={{0,8},{1,9},{2,10},{3,11},{4,12},{5,13},{6,14},{7,15},{8,0},{9,1},... | collective-permute-start | bytes 356360 | tf_op jit(solution)/shard_map/ppermute | solution.py:720
  19.4 1.3 %collective-permute-start.5 = (f32[232,128]{1,0:T(8,128)S(1)}, f32[232,128]{1,0:T(8,128)S(1)}, u32[]{:S(2)}, u32[]{:S(2)}) collective-permute-start(f32[232,128]{1,0:T(8,128)S(1)} %get-tuple-element.71), channel_id=1, source_target_pairs={{0,1},{1,0},{2,3},{3,2},{4,5},{5,4},{6,7},{7,6},{8,16},{9,17},{10,... | collective-permute-start | bytes 356360 | tf_op jit(solution)/shard_map/ppermute | solution.py:720
  20.7 1.3 %collective-permute-done.4.refs_5_.refs_23_ = f32[232,128]{1,0:T(8,128)S(1)} collective-permute-done((f32[232,128]{1,0:T(8,128)S(1)}, f32[232,128]{1,0:T(8,128)S(1)}, u32[]{:S(2)}, u32[]{:S(2)}) %collective-permute-start.4) | collective-permute-done | bytes 118816 | tf_op jit(solution)/shard_map/ppermute | solution.py:720
  22.2 1.7 %collective-permute-start.6 = (f32[152,2,128]{2,1,0:T(2,128)S(1)}, f32[152,2,128]{2,1,0:T(2,128)S(1)}, u32[]{:S(2)}, u32[]{:S(2)}) collective-permute-start(f32[152,2,128]{2,1,0:T(2,128)S(1)} %get-tuple-element.73), channel_id=1, source_target_pairs={{0,1},{1,0},{2,3},{3,2},{4,5},{5,4},{6,7},{7,6},{8,9},{9,8},{10,11... | collective-permute-start | bytes 466952 | tf_op jit(solution)/shard_map/ppermute | solution.py:720
  24.9 3.9 %collective-permute-done.7.refs_26_ = f32[152,2,128]{2,1,0:T(2,128)S(1)} collective-permute-done((f32[152,2,128]{2,1,0:T(2,128)S(1)}, f32[152,2,128]{2,1,0:T(2,128)S(1)}, u32[]{:S(2)}, u32[]{:S(2)}) %collective-permute-start.7) | collective-permute-done | bytes 155680 | tf_op jit(solution)/shard_map/ppermute | solution.py:720
  28.9 3.1 %shard_map.154 = (f32[3,16,16,128]{3,2,1,0:T(8,128)S(1)}, f32[3,8,8,256]{3,2,1,0:T(8,128)S(1)}, f32[8,128]{1,0:T(8,128)S(1)}, f32[136,128]{1,0:T(8,128)S(1)}, f32[136,128]{1,0:T(8,128)S(1)}) custom-call(f32[3,16,16,128]{3,2,1,0:T(8,128)S(1)} %get-tuple-element.62.refs_0_.prev, f32[3,8,8,256]{3,2,1,0:T(8,128)S(1)} %get-tuple-element.63.refs_1_.prev, ...), custom_call_target="tpu_custom_call" | custom-call | flops 4000000 | bytes 1048576 | tf_op jit(solution)/shard_map/pallas_call | solution.py:640
  31.9 3.2 %collective-permute-start.16 = (f32[136,128]{1,0:T(8,128)S(1)}, f32[136,128]{1,0:T(8,128)S(1)}, u32[]{:S(2)}, u32[]{:S(2)}) collective-permute-start(f32[136,128]{1,0:T(8,128)S(1)} %get-tuple-element.78), channel_id=1, source_target_pairs={{0,8},{1,9},{2,10},{3,11},{4,12},{5,13},{6,14},{7,15},{8,0},{9,1},... | collective-permute-start | bytes 208904 | tf_op jit(solution)/shard_map/ppermute | solution.py:720
  35.1 1.3 %collective-permute-start.17 = (f32[136,128]{1,0:T(8,128)S(1)}, f32[136,128]{1,0:T(8,128)S(1)}, u32[]{:S(2)}, u32[]{:S(2)}) collective-permute-start(f32[136,128]{1,0:T(8,128)S(1)} %get-tuple-element.79), channel_id=1, source_target_pairs={{0,1},{1,0},{2,3},{3,2},{4,5},{5,4},{6,7},{7,6},{8,16},{9,17},{10,... | collective-permute-start | bytes 208904 | tf_op jit(solution)/shard_map/ppermute | solution.py:720
  37.5 1.5 %collective-permute-start.18 = (f32[100,2,128]{2,1,0:T(2,128)S(1)}, f32[100,2,128]{2,1,0:T(2,128)S(1)}, u32[]{:S(2)}, u32[]{:S(2)}) collective-permute-start(f32[100,2,128]{2,1,0:T(2,128)S(1)} %get-tuple-element.80), channel_id=1, source_target_pairs={{0,1},{1,0},{2,3},{3,2},{4,5},{5,4},{6,7},{7,6},{8,9},{9,8},{10,11... | collective-permute-start | bytes 307208 | tf_op jit(solution)/shard_map/ppermute | solution.py:720
  39.0 10.5 %collective-permute-start.8 = (f32[8,128]{1,0:T(8,128)S(1)}, f32[8,128]{1,0:T(8,128)S(1)}, u32[]{:S(2)}, u32[]{:S(2)}) collective-permute-start(f32[8,128]{1,0:T(8,128)S(1)} %get-tuple-element.75), channel_id=1, source_target_pairs={{0,224},{1,225},{2,226},{3,227},{4,228},{5,229},{6,230},{7,231},{8... | collective-permute-start | bytes 12296 | tf_op jit(solution)/shard_map/ppermute | solution.py:720
  50.5 2.9 %collective-permute-start.9 = (f32[8,128]{1,0:T(8,128)S(1)}, f32[8,128]{1,0:T(8,128)S(1)}, u32[]{:S(2)}, u32[]{:S(2)}) collective-permute-start(f32[8,128]{1,0:T(8,128)S(1)} %add.43), channel_id=1, source_target_pairs={{0,1},{1,0},{2,3},{3,2},{4,5},{5,4},{6,7},{7,6},{8,9},{9,8},{10,11... | collective-permute-start | bytes 12296 | tf_op jit(solution)/shard_map/ppermute | solution.py:720
  54.2 2.4 %collective-permute-start.10 = (f32[8,128]{1,0:T(8,128)S(1)}, f32[8,128]{1,0:T(8,128)S(1)}, u32[]{:S(2)}, u32[]{:S(2)}) collective-permute-start(f32[8,128]{1,0:T(8,128)S(1)} %add.44), channel_id=1, source_target_pairs={{0,65},{1,64},{2,67},{3,66},{4,69},{5,68},{6,71},{7,70},{8,73},{9,... | collective-permute-start | bytes 12296 | tf_op jit(solution)/shard_map/ppermute | solution.py:720
  56.6 1.5 %collective-permute-done.10 = f32[8,128]{1,0:T(8,128)S(1)} collective-permute-done((f32[8,128]{1,0:T(8,128)S(1)}, f32[8,128]{1,0:T(8,128)S(1)}, u32[]{:S(2)}, u32[]{:S(2)}) %collective-permute-start.10) | collective-permute-done | bytes 4128 | tf_op jit(solution)/shard_map/ppermute | solution.py:720
  58.2 3.0 %collective-permute-done.11 = f32[8,128]{1,0:T(8,128)S(1)} collective-permute-done((f32[8,128]{1,0:T(8,128)S(1)}, f32[8,128]{1,0:T(8,128)S(1)}, u32[]{:S(2)}, u32[]{:S(2)}) %collective-permute-start.11) | collective-permute-done | bytes 4128 | tf_op jit(solution)/shard_map/ppermute | solution.py:720
  61.2 3.0 %collective-permute-done.12 = f32[8,128]{1,0:T(8,128)S(1)} collective-permute-done((f32[8,128]{1,0:T(8,128)S(1)}, f32[8,128]{1,0:T(8,128)S(1)}, u32[]{:S(2)}, u32[]{:S(2)}) %collective-permute-start.12) | collective-permute-done | bytes 4128 | tf_op jit(solution)/shard_map/ppermute | solution.py:720
  64.2 3.2 %collective-permute-start.13 = (f32[8,128]{1,0:T(8,128)S(1)}, f32[8,128]{1,0:T(8,128)S(1)}, u32[]{:S(2)}, u32[]{:S(2)}) collective-permute-start(f32[8,128]{1,0:T(8,128)S(1)} %add.47), channel_id=1, source_target_pairs={{0,33},{1,32},{2,35},{3,34},{4,37},{5,36},{6,39},{7,38},{8,41},{9,... | collective-permute-start | bytes 12296 | tf_op jit(solution)/shard_map/ppermute | solution.py:720
  68.7 2.1 %collective-permute-start.14 = (f32[8,128]{1,0:T(8,128)S(1)}, f32[8,128]{1,0:T(8,128)S(1)}, u32[]{:S(2)}, u32[]{:S(2)}) collective-permute-start(f32[8,128]{1,0:T(8,128)S(1)} %add.48), channel_id=1, source_target_pairs={{0,25},{1,24},{2,27},{3,26},{4,29},{5,28},{6,31},{7,30},{8,17},{9,... | collective-permute-start | bytes 12296 | tf_op jit(solution)/shard_map/ppermute | solution.py:720
  70.9 2.1 %collective-permute-done.14 = f32[8,128]{1,0:T(8,128)S(1)} collective-permute-done((f32[8,128]{1,0:T(8,128)S(1)}, f32[8,128]{1,0:T(8,128)S(1)}, u32[]{:S(2)}, u32[]{:S(2)}) %collective-permute-start.14) | collective-permute-done | bytes 4128 | tf_op jit(solution)/shard_map/ppermute | solution.py:720
  73.2 2.0 %shard_map.156 = f32[3,16,16,128]{3,2,1,0:T(8,128)} custom-call(f32[3,16,16,128]{3,2,1,0:T(8,128)S(1)} %get-tuple-element.76.refs_0_.fine, f32[3,8,8,256]{3,2,1,0:T(8,128)S(1)} %get-tuple-element.77.refs_1_.coarse, f32[3,16,16,128]{3,2,1,0:T(8,128)S(1)} %get-tuple-element.62.refs_0_.prev, s32[16,128]{1,0:T(8,128)S(1)} %pad.4.refs_4_.offs, ...), custom_call_target="tpu_custom_call" | custom-call | flops 2000000 | bytes 1048576 | tf_op jit(solution)/shard_map/pallas_call | solution.py:640
  75.2 1.5 %shard_map.157 = f32[3,8,8,256]{3,2,1,0:T(8,128)} custom-call(f32[3,16,16,128]{3,2,1,0:T(8,128)S(1)} %get-tuple-element.76.refs_0_.fine, f32[3,8,8,256]{3,2,1,0:T(8,128)S(1)} %get-tuple-element.77.refs_1_.coarse, f32[3,8,8,256]{3,2,1,0:T(8,128)S(1)} %get-tuple-element.63.refs_1_.prev, f32[8,8,256]{2,1,0:T(8,128)S(1)} %get-tuple-element.49.refs_10_.refs_0_, ...), custom_call_target="tpu_custom_call" | custom-call | flops 2000000 | bytes 1048576 | tf_op jit(solution)/shard_map/pallas_call | solution.py:640
  (66 shorter events, 11.7 us)
Async XLA Ops:
  0.6 5.7 %copy-start.5 = (f32[8,8,256]{2,1,0:T(8,128)S(1)}, f32[8,8,256]{2,1,0:T(8,128)}, u32[]{:S(2)}) copy-start(f32[8,8,256]{2,1,0:T(8,128)} %refs_19_.1) | copy-start | bytes 196612
  0.6 5.6 %copy-start.4 = (f32[8,8,256]{2,1,0:T(8,128)S(1)}, f32[8,8,256]{2,1,0:T(8,128)}, u32[]{:S(2)}) copy-start(f32[8,8,256]{2,1,0:T(8,128)} %refs_18_.1) | copy-start | bytes 196612
  0.7 5.6 %copy-start.3 = (f32[16,16,128]{2,1,0:T(8,128)S(1)}, f32[16,16,128]{2,1,0:T(8,128)}, u32[]{:S(2)}) copy-start(f32[16,16,128]{2,1,0:T(8,128)} %refs_16_.1) | copy-start | bytes 393220
  1.9 4.2 %collective-permute-start = (f32[200,128]{1,0:T(8,128)S(1)}, f32[200,128]{1,0:T(8,128)S(1)}, u32[]{:S(2)}, u32[]{:S(2)}) collective-permute-start(f32[200,128]{1,0:T(8,128)S(1)} %get-tuple-element.58), channel_id=1, source_target_pairs={{0,8},{1,9},{2,10},{3,11},{4,12},{5,13},{6,14},{7,15},{8,0},{9,1},... | collective-permute-start | bytes 307208 | tf_op jit(solution)/shard_map/ppermute | solution.py:720
  4.0 6.2 %copy-start.12 = (s32[2,16,16]{2,1,0:T(8,128)S(1)}, s32[2,16,16]{2,1,0:T(8,128)}, u32[]{:S(2)}) copy-start(s32[2,16,16]{2,1,0:T(8,128)} %param.25) | copy-start | bytes 6148
  4.0 2.2 %collective-permute-start.1 = (f32[200,128]{1,0:T(8,128)S(1)}, f32[200,128]{1,0:T(8,128)S(1)}, u32[]{:S(2)}, u32[]{:S(2)}) collective-permute-start(f32[200,128]{1,0:T(8,128)S(1)} %get-tuple-element.59), channel_id=1, source_target_pairs={{0,1},{1,0},{2,3},{3,2},{4,5},{5,4},{6,7},{7,6},{8,16},{9,17},{10,... | collective-permute-start | bytes 307208 | tf_op jit(solution)/shard_map/ppermute | solution.py:720
  6.5 4.8 %collective-permute-start.2 = (f32[132,2,128]{2,1,0:T(2,128)S(1)}, f32[132,2,128]{2,1,0:T(2,128)S(1)}, u32[]{:S(2)}, u32[]{:S(2)}) collective-permute-start(f32[132,2,128]{2,1,0:T(2,128)S(1)} %get-tuple-element.60), channel_id=1, source_target_pairs={{0,1},{1,0},{2,3},{3,2},{4,5},{5,4},{6,7},{7,6},{8,9},{9,8},{10,11... | collective-permute-start | bytes 405512 | tf_op jit(solution)/shard_map/ppermute | solution.py:720
  10.2 4.7 %collective-permute-start.3 = (f32[132,2,128]{2,1,0:T(2,128)S(1)}, f32[132,2,128]{2,1,0:T(2,128)S(1)}, u32[]{:S(2)}, u32[]{:S(2)}) collective-permute-start(f32[132,2,128]{2,1,0:T(2,128)S(1)} %get-tuple-element.61), channel_id=1, source_target_pairs={{0,7},{1,2},{2,1},{3,4},{4,3},{5,6},{6,5},{7,0},{8,15},{9,10},{10,... | collective-permute-start | bytes 405512 | tf_op jit(solution)/shard_map/ppermute | solution.py:720
  17.6 4.4 %collective-permute-start.4 = (f32[232,128]{1,0:T(8,128)S(1)}, f32[232,128]{1,0:T(8,128)S(1)}, u32[]{:S(2)}, u32[]{:S(2)}) collective-permute-start(f32[232,128]{1,0:T(8,128)S(1)} %get-tuple-element.70), channel_id=1, source_target_pairs={{0,8},{1,9},{2,10},{3,11},{4,12},{5,13},{6,14},{7,15},{8,0},{9,1},... | collective-permute-start | bytes 356360 | tf_op jit(solution)/shard_map/ppermute | solution.py:720
  19.4 2.6 %collective-permute-start.5 = (f32[232,128]{1,0:T(8,128)S(1)}, f32[232,128]{1,0:T(8,128)S(1)}, u32[]{:S(2)}, u32[]{:S(2)}) collective-permute-start(f32[232,128]{1,0:T(8,128)S(1)} %get-tuple-element.71), channel_id=1, source_target_pairs={{0,1},{1,0},{2,3},{3,2},{4,5},{5,4},{6,7},{7,6},{8,16},{9,17},{10,... | collective-permute-start | bytes 356360 | tf_op jit(solution)/shard_map/ppermute | solution.py:720
  22.2 2.7 %collective-permute-start.6 = (f32[152,2,128]{2,1,0:T(2,128)S(1)}, f32[152,2,128]{2,1,0:T(2,128)S(1)}, u32[]{:S(2)}, u32[]{:S(2)}) collective-permute-start(f32[152,2,128]{2,1,0:T(2,128)S(1)} %get-tuple-element.73), channel_id=1, source_target_pairs={{0,1},{1,0},{2,3},{3,2},{4,5},{5,4},{6,7},{7,6},{8,9},{9,8},{10,11... | collective-permute-start | bytes 466952 | tf_op jit(solution)/shard_map/ppermute | solution.py:720
  23.9 5.0 %collective-permute-start.7 = (f32[152,2,128]{2,1,0:T(2,128)S(1)}, f32[152,2,128]{2,1,0:T(2,128)S(1)}, u32[]{:S(2)}, u32[]{:S(2)}) collective-permute-start(f32[152,2,128]{2,1,0:T(2,128)S(1)} %get-tuple-element.74), channel_id=1, source_target_pairs={{0,7},{1,2},{2,1},{3,4},{4,3},{5,6},{6,5},{7,0},{8,15},{9,10},{10,... | collective-permute-start | bytes 466952 | tf_op jit(solution)/shard_map/ppermute | solution.py:720
  31.9 4.9 %collective-permute-start.16 = (f32[136,128]{1,0:T(8,128)S(1)}, f32[136,128]{1,0:T(8,128)S(1)}, u32[]{:S(2)}, u32[]{:S(2)}) collective-permute-start(f32[136,128]{1,0:T(8,128)S(1)} %get-tuple-element.78), channel_id=1, source_target_pairs={{0,8},{1,9},{2,10},{3,11},{4,12},{5,13},{6,14},{7,15},{8,0},{9,1},... | collective-permute-start | bytes 208904 | tf_op jit(solution)/shard_map/ppermute | solution.py:720
  35.1 2.2 %collective-permute-start.17 = (f32[136,128]{1,0:T(8,128)S(1)}, f32[136,128]{1,0:T(8,128)S(1)}, u32[]{:S(2)}, u32[]{:S(2)}) collective-permute-start(f32[136,128]{1,0:T(8,128)S(1)} %get-tuple-element.79), channel_id=1, source_target_pairs={{0,1},{1,0},{2,3},{3,2},{4,5},{5,4},{6,7},{7,6},{8,16},{9,17},{10,... | collective-permute-start | bytes 208904 | tf_op jit(solution)/shard_map/ppermute | solution.py:720
  37.5 35.7 %collective-permute-start.18 = (f32[100,2,128]{2,1,0:T(2,128)S(1)}, f32[100,2,128]{2,1,0:T(2,128)S(1)}, u32[]{:S(2)}, u32[]{:S(2)}) collective-permute-start(f32[100,2,128]{2,1,0:T(2,128)S(1)} %get-tuple-element.80), channel_id=1, source_target_pairs={{0,1},{1,0},{2,3},{3,2},{4,5},{5,4},{6,7},{7,6},{8,9},{9,8},{10,11... | collective-permute-start | bytes 307208 | tf_op jit(solution)/shard_map/ppermute | solution.py:720
  39.0 34.2 %collective-permute-start.19 = (f32[100,2,128]{2,1,0:T(2,128)S(1)}, f32[100,2,128]{2,1,0:T(2,128)S(1)}, u32[]{:S(2)}, u32[]{:S(2)}) collective-permute-start(f32[100,2,128]{2,1,0:T(2,128)S(1)} %get-tuple-element.81), channel_id=1, source_target_pairs={{0,7},{1,2},{2,1},{3,4},{4,3},{5,6},{6,5},{7,0},{8,15},{9,10},{10,... | collective-permute-start | bytes 307208 | tf_op jit(solution)/shard_map/ppermute | solution.py:720
  39.0 11.5 %collective-permute-start.8 = (f32[8,128]{1,0:T(8,128)S(1)}, f32[8,128]{1,0:T(8,128)S(1)}, u32[]{:S(2)}, u32[]{:S(2)}) collective-permute-start(f32[8,128]{1,0:T(8,128)S(1)} %get-tuple-element.75), channel_id=1, source_target_pairs={{0,224},{1,225},{2,226},{3,227},{4,228},{5,229},{6,230},{7,231},{8... | collective-permute-start | bytes 12296 | tf_op jit(solution)/shard_map/ppermute | solution.py:720
  50.5 3.7 %collective-permute-start.9 = (f32[8,128]{1,0:T(8,128)S(1)}, f32[8,128]{1,0:T(8,128)S(1)}, u32[]{:S(2)}, u32[]{:S(2)}) collective-permute-start(f32[8,128]{1,0:T(8,128)S(1)} %add.43), channel_id=1, source_target_pairs={{0,1},{1,0},{2,3},{3,2},{4,5},{5,4},{6,7},{7,6},{8,9},{9,8},{10,11... | collective-permute-start | bytes 12296 | tf_op jit(solution)/shard_map/ppermute | solution.py:720
  54.2 3.9 %collective-permute-start.10 = (f32[8,128]{1,0:T(8,128)S(1)}, f32[8,128]{1,0:T(8,128)S(1)}, u32[]{:S(2)}, u32[]{:S(2)}) collective-permute-start(f32[8,128]{1,0:T(8,128)S(1)} %add.44), channel_id=1, source_target_pairs={{0,65},{1,64},{2,67},{3,66},{4,69},{5,68},{6,71},{7,70},{8,73},{9,... | collective-permute-start | bytes 12296 | tf_op jit(solution)/shard_map/ppermute | solution.py:720
  58.2 3.0 %collective-permute-start.11 = (f32[8,128]{1,0:T(8,128)S(1)}, f32[8,128]{1,0:T(8,128)S(1)}, u32[]{:S(2)}, u32[]{:S(2)}) collective-permute-start(f32[8,128]{1,0:T(8,128)S(1)} %add.45), channel_id=1, source_target_pairs={{0,3},{1,2},{2,1},{3,0},{4,7},{5,6},{6,5},{7,4},{8,11},{9,10},{10,... | collective-permute-start | bytes 12296 | tf_op jit(solution)/shard_map/ppermute | solution.py:720
  61.2 3.0 %collective-permute-start.12 = (f32[8,128]{1,0:T(8,128)S(1)}, f32[8,128]{1,0:T(8,128)S(1)}, u32[]{:S(2)}, u32[]{:S(2)}) collective-permute-start(f32[8,128]{1,0:T(8,128)S(1)} %add.46), channel_id=1, source_target_pairs={{0,9},{1,8},{2,11},{3,10},{4,13},{5,12},{6,15},{7,14},{8,1},{9,0},... | collective-permute-start | bytes 12296 | tf_op jit(solution)/shard_map/ppermute | solution.py:720
  64.2 4.5 %collective-permute-start.13 = (f32[8,128]{1,0:T(8,128)S(1)}, f32[8,128]{1,0:T(8,128)S(1)}, u32[]{:S(2)}, u32[]{:S(2)}) collective-permute-start(f32[8,128]{1,0:T(8,128)S(1)} %add.47), channel_id=1, source_target_pairs={{0,33},{1,32},{2,35},{3,34},{4,37},{5,36},{6,39},{7,38},{8,41},{9,... | collective-permute-start | bytes 12296 | tf_op jit(solution)/shard_map/ppermute | solution.py:720
  68.7 4.2 %collective-permute-start.14 = (f32[8,128]{1,0:T(8,128)S(1)}, f32[8,128]{1,0:T(8,128)S(1)}, u32[]{:S(2)}, u32[]{:S(2)}) collective-permute-start(f32[8,128]{1,0:T(8,128)S(1)} %add.48), channel_id=1, source_target_pairs={{0,25},{1,24},{2,27},{3,26},{4,29},{5,28},{6,31},{7,30},{8,17},{9,... | collective-permute-start | bytes 12296 | tf_op jit(solution)/shard_map/ppermute | solution.py:720
  73.0 4.2 %collective-permute-start.15 = (f32[8,128]{1,0:T(8,128)S(1)}, f32[8,128]{1,0:T(8,128)S(1)}, u32[]{:S(2)}, u32[]{:S(2)}) collective-permute-start(f32[8,128]{1,0:T(8,128)S(1)} %add.49), channel_id=1, source_target_pairs={{0,7},{1,6},{2,5},{3,4},{4,3},{5,2},{6,1},{7,0},{8,15},{9,14},{10,... | collective-permute-start | bytes 12296 | tf_op jit(solution)/shard_map/ppermute | solution.py:720
  (9 other events, 35.0 us)

commit v9 on v8

--- a/solution.py
+++ b/solution.py
@@ -51,8 +51,13 @@
         self.y_rows_mats = self.y_coarse_mats + self.halves * self.cx
         self.y_fine_beta = self.y_rows
         self.y_coarse_beta = self.y_fine_beta + self.fe
-        self.y_spread = self.y_coarse_beta + self.halves * self.ce
-        self.y_rows_beta = self.y_spread + self.cx
+        self.y_rows_beta = self.y_coarse_beta + self.halves * self.ce
+        self.f_coarse = 2
+        self.f_plane = self.f_coarse + 2 * self.halves
+        self.f_beta = self.f_plane + 1
+        self.corner_rows = 4 * self.f_beta
+        self.corner_spread = 4 * (self.f_beta + 1 + self.halves)
+        self.corner_rows_beta = self.corner_spread + self.cx
 
 
 def lanes_of(h):
@@ -130,11 +135,19 @@
     return low, high
 
 
-def middle_kernel(s, step, *refs):
+def y_kernel(s, step, part, *refs):
     flags = where_am_i()
-    fine, coarse, *mats, in_a, in_b = refs[:-2] if step != 1 else refs[:-3]
-    out_a, out_b = refs[-2:] if step != 1 else refs[-3:-1]
+    refs = list(refs)
     even = flags[EVEN_Y]
+    has_own, has_corners = part != "corners", part != "own"
+    if has_own:
+        fine, coarse = refs[:2]
+        mats = refs[2:-2] if part == "own" else []
+    if has_corners:
+        total = refs.pop() if step == 1 else None
+        in_a, in_b = refs[-4:-2]
+        spread = refs[0]
+    out_a, out_b = refs[-2:]
 
     def put(index, low, high):
         out_a[index] = jnp.where(even, high, low)
@@ -148,75 +161,81 @@
         rows = slice(first, first + count)
         return sides(flags, EVEN_X, HAS_XM, HAS_XP, in_a[rows, :], in_b[rows, :])
 
-    def level(own, x, y, x_base, y_base, y_size, plane):
+    def corner(base, field, x, side, k):
+        return 4 * field + 2 * side + k if part == "corners" else base + side * (x + 2) + k
+
+    def level(own, x, y, x_base, y_base, y_size, field, plane):
         both, single = y_base, y_base + y_size
-        here = pl.ds(both + 2, x)
-        put(here, own(1, slice(0, 2)), own(1, slice(y - 2, y)))
-        for m, c in enumerate((0, 2)):
-            here = pl.ds(single + 2, x)
-            put_one(here, m, own(c, slice(0, 1)), own(c, slice(y - 1, y)))
-            if plane:
-                here = pl.ds(s.y_plane + 2, x)
-                put_one(here, m, own(c, slice(1, 2)), own(c, slice(y - 2, y - 1)))
-        for side in range(2):
-            for k in range(2):
-                place = k if side == 0 else x + 2 + k
-                near = k == 1 - side
-
-                def row(c, first, count):
-                    if c == 0:
-                        return came(x_base + k * y + first, count)[side]
-                    if near:
-                        return came(x_base + (1 + c) * y + first, count)[side]
-                    return pltpu.roll(came(s.x_plane + first, count)[side], LANES - c, 1)
-
-                if near or plane:
-                    put(both + place, row(1, 0, 2), row(1, y - 2, 2))
-                for m, c in enumerate((0, 2)):
-                    if c == 0 or near or plane:
-                        put_one(single + place, m, row(c, 0, 1), row(c, y - 1, 1))
-                    if plane:
-                        put_one(s.y_plane + place, m, row(c, 1, 1), row(c, y - 2, 1))
-
-    def field(own, x, y, x_base, y_base):
-        put(pl.ds(y_base + 2, x), own(slice(0, 2)), own(slice(y - 2, y)))
-        for k in range(2):
+        if has_own:
+            put(pl.ds(both + 2, x), own(1, slice(0, 2)), own(1, slice(y - 2, y)))
+            for m, c in enumerate((0, 2)):
+                here = pl.ds(single + 2, x)
+                put_one(here, m, own(c, slice(0, 1)), own(c, slice(y - 1, y)))
+                if plane:
+                    here = pl.ds(s.y_plane + 2, x)
+                    put_one(here, m, own(c, slice(1, 2)), own(c, slice(y - 2, y - 1)))
+        for side, k in ((0, 0), (0, 1), (1, 0), (1, 1)) if has_corners else ():
+            near = k == 1 - side
+
+            def row(c, first, count):
+                if c == 0:
+                    return came(x_base + k * y + first, count)[side]
+                if near:
+                    return came(x_base + (1 + c) * y + first, count)[side]
+                return pltpu.roll(came(s.x_plane + first, count)[side], LANES - c, 1)
+
+            if near or plane:
+                put(corner(both, field, x, side, k), row(1, 0, 2), row(1, y - 2, 2))
+            for m, c in enumerate((0, 2)):
+                if c == 0 or near or plane:
+                    here = corner(single, field + 1, x, side, k)
+                    put_one(here, m, row(c, 0, 1), row(c, y - 1, 1))
+                if plane:
+                    here = corner(s.y_plane, s.f_plane, x, side, k)
+                    put_one(here, m, row(c, 1, 1), row(c, y - 2, 1))
+
+    def two_deep(own, x, y, x_base, y_base, field):
+        if has_own:
+            put(pl.ds(y_base + 2, x), own(slice(0, 2)), own(slice(y - 2, y)))
+        for k in range(2) if has_corners else ():
             low, high = came(x_base + k * y, 2), came(x_base + (k + 1) * y - 2, 2)
             for side in range(2):
-                put(y_base + (k if side == 0 else x + 2 + k), low[side], high[side])
-
-    level(lambda c, r: fine[c, :, r, :], s.fx, s.fy, 0, 0, s.fe, False)
+                put(corner(y_base, field, x, side, k), low[side], high[side])
+
+    level(lambda c, r: fine[c, :, r, :], s.fx, s.fy, 0, 0, s.fe, 0, False)
     for h in range(s.halves):
+        x_base, y_base = s.x_coarse + h * 4 * s.cy, s.y_coarse + h * 2 * s.ce
+        field = s.f_coarse + 2 * h
         at = lanes_of(h)
-        x_base, y_base = s.x_coarse + h * 4 * s.cy, s.y_coarse + h * 2 * s.ce
-        level(lambda c, r: coarse[c, :, r, at], s.cx, s.cy, x_base, y_base, s.ce, h == 0)
-    if step == 0:
+        level(
+            lambda c, r: coarse[c, :, r, at], s.cx, s.cy, x_base, y_base, s.ce, field, h == 0
+        )
+    if step == 0 and has_own:
         rig_f, met_f, rig_c, met_c = mats
         for m, (of_f, of_c) in enumerate(((rig_f, rig_c), (met_f, met_c))):
-            low, high = of_f[:, 0:1, :], of_f[:, s.fy - 1 : s.fy, :]
-            where = pl.ds(s.y_fine_mats, s.fx)
-            out_a[where, m : m + 1, :] = jnp.where(even, high, low)
-            out_b[where, m : m + 1, :] = jnp.where(even, low, high)
+            here = pl.ds(s.y_fine_mats, s.fx)
+            put_one(here, m, of_f[:, 0:1, :], of_f[:, s.fy - 1 : s.fy, :])
             for h in range(s.halves):
+                here = pl.ds(s.y_coarse_mats + h * s.cx, s.cx)
                 low, high = of_c[:, 0:1, lanes_of(h)], of_c[:, s.cy - 1 : s.cy, lanes_of(h)]
-                where = pl.ds(s.y_coarse_mats + h * s.cx, s.cx)
-                out_a[where, m : m + 1, :] = jnp.where(even, high, low)
-                out_b[where, m : m + 1, :] = jnp.where(even, low, high)
+                put_one(here, m, low, high)
     if step == 1:
-        beta_f, beta_c, spread = mats
-        field(lambda r: beta_f[:, r, :], s.fx, s.fy, s.x_fine_beta, s.y_fine_beta)
+        beta_f, beta_c = mats if has_own else (None, None)
+        x_base, y_base = s.x_fine_beta, s.y_fine_beta
+        two_deep(lambda r: beta_f[:, r, :], s.fx, s.fy, x_base, y_base, s.f_beta)
         for h in range(s.halves):
             at = lanes_of(h)
             x_base, y_base = s.x_coarse_beta + h * 2 * s.cy, s.y_coarse_beta + h * s.ce
-            field(lambda r: beta_c[:, r, at], s.cx, s.cy, x_base, y_base)
-        total = refs[-1]
+            field = s.f_beta + 1 + h
+            two_deep(lambda r: beta_c[:, r, at], s.cx, s.cy, x_base, y_base, field)
+    if step == 1 and has_corners:
         total[...] = spread[2 : 2 + s.cx]
         for k in range(2):
-            rows = slice(s.x_spread + k * s.spread, s.x_spread + (k + 1) * s.spread)
-            low, high = sides(flags, EVEN_X, HAS_XM, HAS_XP, in_a[rows, :], in_b[rows, :])
+            low, high = came(s.x_spread + k * s.spread, s.spread)
             total[k] += low
             total[s.cx - 2 + k] += high
-        put(pl.ds(s.y_spread, s.cx), total[:, 0:2, :], total[:, s.cy + 2 : s.cy + 4, :])
+        here = pl.ds(s.corner_spread, s.cx)
+        put(here, total[:, 0:2, :], total[:, s.cy + 2 : s.cy + 4, :])
 
 
 def up_one(x):
@@ -257,6 +276,22 @@
     return down - jnp.where(lane == q.shape[-1] - 1, -q, up_one(q))
 
 
+def y_pieces(flags, y_in, start, x, field):
+    def taken(a, b):
+        return sides(flags, EVEN_Y, HAS_YM, HAS_YP, a, b)
+
+    if len(y_in) == 2:
+        rows = slice(start, start + x + 4)
+        return [(slice(0, x + 4), *taken(y_in[0][rows], y_in[1][rows]))]
+    rows = slice(start + 2, start + 2 + x)
+    out = [(slice(2, 2 + x), *taken(y_in[0][rows], y_in[1][rows]))]
+    for side in range(2):
+        rows = slice(4 * field + 2 * side, 4 * field + 2 * side + 2)
+        at = slice(side * (x + 2), side * (x + 2) + 2)
+        out.append((at, *taken(y_in[2][rows], y_in[3][rows])))
+    return out
+
+
 def fill_beta(s, flags, own, ext, x_in, y_in, fine):
     x, y, e = (s.fx, s.fy, s.fe) if fine else (s.cx, s.cy, s.ce)
     ext[2 : 2 + x, 8 : 8 + y, :] = own[...]
@@ -268,10 +303,10 @@
         ext[0:2, 8 : 8 + y, at] = low.reshape(2, y, LANES)
         ext[x + 2 : x + 4, 8 : 8 + y, at] = high.reshape(2, y, LANES)
         start = s.y_fine_beta if fine else s.y_coarse_beta + h * e
-        rows = slice(start, start + e)
-        low, high = sides(flags, EVEN_Y, HAS_YM, HAS_YP, y_in[0][rows], y_in[1][rows])
-        ext[:, 6:8, at] = low
-        ext[:, 8 + y : 10 + y, at] = high
+        field = s.f_beta if fine else s.f_beta + 1 + h
+        for i, low, high in y_pieces(flags, y_in, start, x, field):
+            ext[i, 6:8, at] = low
+            ext[i, 8 + y : 10 + y, at] = high
 
 
 def fill_transposed(x, y, ext, beta, inv_ext, psi):
@@ -303,10 +338,6 @@
         rows = slice(first, first + rows)
         return sides(flags, EVEN_X, HAS_XM, HAS_XP, x_in[0][rows, :], x_in[1][rows, :])
 
-    def from_y(first):
-        rows = slice(first, first + e)
-        return sides(flags, EVEN_Y, HAS_YM, HAS_YP, y_in[0][rows], y_in[1][rows])
-
     for h in range(halves):
         at = lanes_of(h)
         base = 0 if fine else s.x_coarse + h * 4 * y
@@ -316,11 +347,14 @@
         for c in (1, 2):
             ext[c, 1, mid, at], ext[c, x + 2, mid, at] = from_x(base + (1 + c) * y, y)
         start = 0 if fine else s.y_coarse + h * 2 * e
-        ext[1, :, 6:8, at], ext[1, :, 8 + y : 10 + y, at] = from_y(start)
-        low, high = from_y(start + e)
-        for m, c in enumerate((0, 2)):
-            ext[c, :, 7:8, at] = low[:, m : m + 1, :]
-            ext[c, :, 8 + y : 9 + y, at] = high[:, m : m + 1, :]
+        field = 0 if fine else s.f_coarse + 2 * h
+        for i, low, high in y_pieces(flags, y_in, start, x, field):
+            ext[1, i, 6:8, at] = low
+            ext[1, i, 8 + y : 10 + y, at] = high
+        for i, low, high in y_pieces(flags, y_in, start + e, x, field + 1):
+            for m, c in enumerate((0, 2)):
+                ext[c, i, 7:8, at] = low[:, m : m + 1, :]
+                ext[c, i, 8 + y : 9 + y, at] = high[:, m : m + 1, :]
     if fine:
         return
     at = lanes_of(0)
@@ -328,10 +362,10 @@
     for c in (1, 2):
         ext[c, 0, mid, at] = pltpu.roll(low, LANES - c, 1)
         ext[c, x + 3, mid, at] = pltpu.roll(high, LANES - c, 1)
-    low, high = from_y(s.y_plane)
-    for m, c in enumerate((0, 2)):
-        ext[c, :, 6:7, at] = low[:, m : m + 1, :]
-        ext[c, :, 9 + y : 10 + y, at] = high[:, m : m + 1, :]
+    for i, low, high in y_pieces(flags, y_in, s.y_plane, x, s.f_plane):
+        for m, c in enumerate((0, 2)):
+            ext[c, i, 6:7, at] = low[:, m : m + 1, :]
+            ext[c, i, 9 + y : 10 + y, at] = high[:, m : m + 1, :]
 
 
 def fill_materials(s, flags, rigidity, metric, inverse, wide_ext, inv_ext, x_in, y_in, fine):
@@ -527,7 +561,7 @@
     beta_own = take(2)
     if step == 1:
         energy_in, spread_in = take(2)
-    x_in, y_in = take(2), take(2)
+    x_in, y_in = take(2), take(4)
     new_f, new_c, energy = take(3)
     x_out = take(2)
     if step == 0:
@@ -591,8 +625,8 @@
         put_x(s, flags, x_out, new_f, new_c, beta_own, spread_out)
     if step == 1:
         spread[...] = spread_in[:, 2 : 2 + s.cy, :]
-        rows = pl.ds(s.y_spread, s.cx)
-        low, high = sides(flags, EVEN_Y, HAS_YM, HAS_YP, y_in[0][rows], y_in[1][rows])
+        rows = pl.ds(s.corner_spread, s.cx)
+        low, high = sides(flags, EVEN_Y, HAS_YM, HAS_YP, y_in[2][rows], y_in[3][rows])
         spread[:, 0:2, :] += low
         spread[:, s.cy - 2 : s.cy, :] += high
         joined = jnp.zeros((s.cy, LANES), jnp.float32)
@@ -790,22 +824,27 @@
                 other = swap(energy, move)
                 if k < len(TOTAL) - 1:
                     energy = energy + other
-        shapes = [((s.y_rows_mats, s.y_rows_beta, s.y_rows)[step], 2, LANES)] * 2
-        if step == 0:
-            mats = [fine_rigidity, fine_metric, coarse_rigidity, coarse_metric]
-        if step == 1:
-            mats = [beta_f, beta_c, spread_own]
-            shapes.append((s.cx,) + spread[1:])
-        y_out = call(
-            functools.partial(middle_kernel, s, step),
-            shapes,
-            1000,
-            fine,
-            coarse,
-            *(mats if step < 2 else ()),
-            *x_in,
-        )
-        y_in = swap_both(y_out[:2], beside_y, across_y)
+
+        def y_strips(part, shapes, *args):
+            kernel = functools.partial(y_kernel, s, step, part)
+            return call(kernel, shapes, 500_000, *args)
+
+        pairs = [(s.y_rows_mats, s.y_rows_beta, s.y_rows)[step], 2, LANES]
+        if step == 2:
+            y_out = y_strips("all", [tuple(pairs)] * 2, fine, coarse, *x_in)
+            y_in = swap_both(y_out, beside_y, across_y)
+        else:
+            if step == 0:
+                mats = [fine_rigidity, fine_metric, coarse_rigidity, coarse_metric]
+                more, shapes = [], [(s.corner_rows, 2, LANES)] * 2
+            else:
+                mats = [beta_f, beta_c]
+                more, shapes = [spread_own], [(s.corner_rows_beta, 2, LANES)] * 2
+                shapes.append((s.cx,) + spread[1:])
+            y_out = y_strips("own", [tuple(pairs)] * 2, fine, coarse, *mats)
+            y_in = swap_both(y_out, beside_y, across_y)
+            y_out = y_strips("corners", shapes, *more, *x_in)
+            y_in += swap_both(y_out[:2], beside_y, across_y)
         if step == 2:
             wide_f, inv_f, wide_c, inv_c = ext_mats
             (fine_final,) = call(

time: 78.2 us -> 75.9 us (0.971)
  waiting for transfers between devices: 24.9 us -> 19.8 us
  starting transfers between devices: 39.3 us -> 41.9 us
    ppermute x20 -> x24, waiting for transfers between devices: 24.9 us -> 19.8 us  [swap(): return lax.ppermute(value, ALL, swap_pairs(mesh, move))]
    ppermute x20 -> x24, starting transfers between devices: 39.3 us -> 41.9 us  [swap(): return lax.ppermute(value, ALL, swap_pairs(mesh, move))]
    pallas_call x10 -> x12, Pallas kernels: 11.3 us -> 11.4 us  [call(): pl.pallas_call(kernel, out_shape=shapes, in_specs=[spec] * len(args), out...]
  transfers between devices with their start and end apart: 20 -> 24, of which waited for: 16 -> 15; matrix products, arithmetic and copies ran while one was open for 0% -> 0% of each run, Pallas kernels for 5% -> 6%
where the time goes in v9:
time: 75.9 us; the launch traced here: 75.7 us
  starting transfers between devices  41.9 us (55%)
  waiting for transfers between devices  19.8 us (26%)
  Pallas kernels  11.4 us (15%)
  local copies, waits for them, and re-layouts  1.64 us (2%)
  between operations  0.88 us (1%)
    ppermute x24, starting transfers between devices, swap(): return lax.ppermute(value, ALL, swap_pairs(mesh, move))  41.9 us
    ppermute x24, waiting for transfers between devices, swap(): return lax.ppermute(value, ALL, swap_pairs(mesh, move))  19.8 us
    pallas_call x12, Pallas kernels, call(): pl.pallas_call(kernel, out_shape=shapes, in_specs=[spec] * len(args), out...  11.4 us
  transfers between devices with their start and end apart: 24, of which 15 were waited for; matrix products, arithmetic and copies ran while one was open for 0% of the time, Pallas kernels for 6%

profile of v9, /device:TPU:1, one launch (start us, length us, event | category | flops | bytes accessed | tf_op | source)
XLA Modules:
  0.0 75.7 jit_solution(17782329951502375010)
XLA Ops:
  1.9 2.1 %collective-permute-start = (f32[200,128]{1,0:T(8,128)S(1)}, f32[200,128]{1,0:T(8,128)S(1)}, u32[]{:S(2)}, u32[]{:S(2)}) collective-permute-start(f32[200,128]{1,0:T(8,128)S(1)} %get-tuple-element.62), channel_id=1, source_target_pairs={{0,8},{1,9},{2,10},{3,11},{4,12},{5,13},{6,14},{7,15},{8,0},{9,1},... | collective-permute-start | bytes 307208 | tf_op jit(solution)/shard_map/ppermute | solution.py:754
  7.1 3.0 %collective-permute-start.4 = (f32[28,2,128]{2,1,0:T(2,128)S(1)}, f32[28,2,128]{2,1,0:T(2,128)S(1)}, u32[]{:S(2)}, u32[]{:S(2)}) collective-permute-start(f32[28,2,128]{2,1,0:T(2,128)S(1)} %get-tuple-element.66), channel_id=1, source_target_pairs={{0,1},{1,0},{2,3},{3,2},{4,5},{5,4},{6,7},{7,6},{8,9},{9,8},{10,11... | collective-permute-start | bytes 86024 | tf_op jit(solution)/shard_map/ppermute | solution.py:754
  11.2 2.2 %collective-permute-done.5.refs_28_ = f32[28,2,128]{2,1,0:T(2,128)S(1)} collective-permute-done((f32[28,2,128]{2,1,0:T(2,128)S(1)}, f32[28,2,128]{2,1,0:T(2,128)S(1)}, u32[]{:S(2)}, u32[]{:S(2)}) %collective-permute-start.5) | collective-permute-done | bytes 28704 | tf_op jit(solution)/shard_map/ppermute | solution.py:754
  13.4 2.6 %shard_map.153 = (f32[3,16,16,128]{3,2,1,0:T(8,128)S(1)}, f32[3,8,8,256]{3,2,1,0:T(8,128)S(1)}, f32[8,128]{1,0:T(8,128)S(1)}, f32[232,128]{1,0:T(8,128)S(1)}, f3...) custom-call(f32[3,16,16,128]{3,2,1,0:T(8,128)S(1)} %copy-done, ...), custom_call_target="tpu_custom_call" | custom-call | flops 4000000 | bytes 1048576 | tf_op jit(solution)/shard_map/pallas_call | solution.py:674
  16.1 1.8 %collective-permute-start.6 = (f32[232,128]{1,0:T(8,128)S(1)}, f32[232,128]{1,0:T(8,128)S(1)}, u32[]{:S(2)}, u32[]{:S(2)}) collective-permute-start(f32[232,128]{1,0:T(8,128)S(1)} %get-tuple-element.76), channel_id=1, source_target_pairs={{0,8},{1,9},{2,10},{3,11},{4,12},{5,13},{6,14},{7,15},{8,0},{9,1},... | collective-permute-start | bytes 356360 | tf_op jit(solution)/shard_map/ppermute | solution.py:754
  17.9 1.6 %collective-permute-start.7 = (f32[232,128]{1,0:T(8,128)S(1)}, f32[232,128]{1,0:T(8,128)S(1)}, u32[]{:S(2)}, u32[]{:S(2)}) collective-permute-start(f32[232,128]{1,0:T(8,128)S(1)} %get-tuple-element.77), channel_id=1, source_target_pairs={{0,1},{1,0},{2,3},{3,2},{4,5},{5,4},{6,7},{7,6},{8,16},{9,17},{10,... | collective-permute-start | bytes 356360 | tf_op jit(solution)/shard_map/ppermute | solution.py:754
  20.6 1.9 %collective-permute-start.10 = (f32[48,2,128]{2,1,0:T(2,128)S(1)}, f32[48,2,128]{2,1,0:T(2,128)S(1)}, u32[]{:S(2)}, u32[]{:S(2)}) collective-permute-start(f32[48,2,128]{2,1,0:T(2,128)S(1)} %get-tuple-element.81), channel_id=1, source_target_pairs={{0,1},{1,0},{2,3},{3,2},{4,5},{5,4},{6,7},{7,6},{8,9},{9,8},{10,11... | collective-permute-start | bytes 147464 | tf_op jit(solution)/shard_map/ppermute | solution.py:754
  22.5 2.1 %collective-permute-done.9.refs_26_ = f32[144,2,128]{2,1,0:T(2,128)S(1)} collective-permute-done((f32[144,2,128]{2,1,0:T(2,128)S(1)}, f32[144,2,128]{2,1,0:T(2,128)S(1)}, u32[]{:S(2)}, u32[]{:S(2)}) %collective-permute-start.9) | collective-permute-done | bytes 147488 | tf_op jit(solution)/shard_map/ppermute | solution.py:754
  24.7 1.4 %collective-permute-done.11.refs_28_ = f32[48,2,128]{2,1,0:T(2,128)S(1)} collective-permute-done((f32[48,2,128]{2,1,0:T(2,128)S(1)}, f32[48,2,128]{2,1,0:T(2,128)S(1)}, u32[]{:S(2)}, u32[]{:S(2)}) %collective-permute-start.11) | collective-permute-done | bytes 49184 | tf_op jit(solution)/shard_map/ppermute | solution.py:754
  26.0 3.1 %shard_map.156 = (f32[3,16,16,128]{3,2,1,0:T(8,128)S(1)}, f32[3,8,8,256]{3,2,1,0:T(8,128)S(1)}, f32[8,128]{1,0:T(8,128)S(1)}, f32[136,128]{1,0:T(8,128)S(1)}, f32[136,128]{1,0:T(8,128)S(1)}) custom-call(f32[3,16,16,128]{3,2,1,0:T(8,128)S(1)} %get-tuple-element.68.refs_0_.prev, f32[3,8,8,256]{3,2,1,0:T(8,128)S(1)} %get-tuple-element.69.refs_1_.prev, ...), custom_call_target="tpu_custom_call" | custom-call | flops 4000000 | bytes 1048576 | tf_op jit(solution)/shard_map/pallas_call | solution.py:674
  29.1 3.6 %collective-permute-start.20 = (f32[136,128]{1,0:T(8,128)S(1)}, f32[136,128]{1,0:T(8,128)S(1)}, u32[]{:S(2)}, u32[]{:S(2)}) collective-permute-start(f32[136,128]{1,0:T(8,128)S(1)} %get-tuple-element.86), channel_id=1, source_target_pairs={{0,8},{1,9},{2,10},{3,11},{4,12},{5,13},{6,14},{7,15},{8,0},{9,1},... | collective-permute-start | bytes 208904 | tf_op jit(solution)/shard_map/ppermute | solution.py:754
  32.7 1.6 %collective-permute-start.21 = (f32[136,128]{1,0:T(8,128)S(1)}, f32[136,128]{1,0:T(8,128)S(1)}, u32[]{:S(2)}, u32[]{:S(2)}) collective-permute-start(f32[136,128]{1,0:T(8,128)S(1)} %get-tuple-element.87), channel_id=1, source_target_pairs={{0,1},{1,0},{2,3},{3,2},{4,5},{5,4},{6,7},{7,6},{8,16},{9,17},{10,... | collective-permute-start | bytes 208904 | tf_op jit(solution)/shard_map/ppermute | solution.py:754
  35.4 1.7 %collective-permute-start.22 = (f32[100,2,128]{2,1,0:T(2,128)S(1)}, f32[100,2,128]{2,1,0:T(2,128)S(1)}, u32[]{:S(2)}, u32[]{:S(2)}) collective-permute-start(f32[100,2,128]{2,1,0:T(2,128)S(1)} %get-tuple-element.88), channel_id=1, source_target_pairs={{0,1},{1,0},{2,3},{3,2},{4,5},{5,4},{6,7},{7,6},{8,9},{9,8},{10,11... | collective-permute-start | bytes 307208 | tf_op jit(solution)/shard_map/ppermute | solution.py:754
  37.1 10.5 %collective-permute-start.12 = (f32[8,128]{1,0:T(8,128)S(1)}, f32[8,128]{1,0:T(8,128)S(1)}, u32[]{:S(2)}, u32[]{:S(2)}) collective-permute-start(f32[8,128]{1,0:T(8,128)S(1)} %get-tuple-element.83), channel_id=1, source_target_pairs={{0,224},{1,225},{2,226},{3,227},{4,228},{5,229},{6,230},{7,231},{8... | collective-permute-start | bytes 12296 | tf_op jit(solution)/shard_map/ppermute | solution.py:754
  48.6 2.6 %collective-permute-start.13 = (f32[8,128]{1,0:T(8,128)S(1)}, f32[8,128]{1,0:T(8,128)S(1)}, u32[]{:S(2)}, u32[]{:S(2)}) collective-permute-start(f32[8,128]{1,0:T(8,128)S(1)} %add.43), channel_id=1, source_target_pairs={{0,1},{1,0},{2,3},{3,2},{4,5},{5,4},{6,7},{7,6},{8,9},{9,8},{10,11... | collective-permute-start | bytes 12296 | tf_op jit(solution)/shard_map/ppermute | solution.py:754
  52.0 2.4 %collective-permute-start.14 = (f32[8,128]{1,0:T(8,128)S(1)}, f32[8,128]{1,0:T(8,128)S(1)}, u32[]{:S(2)}, u32[]{:S(2)}) collective-permute-start(f32[8,128]{1,0:T(8,128)S(1)} %add.44), channel_id=1, source_target_pairs={{0,65},{1,64},{2,67},{3,66},{4,69},{5,68},{6,71},{7,70},{8,73},{9,... | collective-permute-start | bytes 12296 | tf_op jit(solution)/shard_map/ppermute | solution.py:754
  54.4 1.5 %collective-permute-done.14 = f32[8,128]{1,0:T(8,128)S(1)} collective-permute-done((f32[8,128]{1,0:T(8,128)S(1)}, f32[8,128]{1,0:T(8,128)S(1)}, u32[]{:S(2)}, u32[]{:S(2)}) %collective-permute-start.14) | collective-permute-done | bytes 4128 | tf_op jit(solution)/shard_map/ppermute | solution.py:754
  56.3 2.7 %collective-permute-done.15 = f32[8,128]{1,0:T(8,128)S(1)} collective-permute-done((f32[8,128]{1,0:T(8,128)S(1)}, f32[8,128]{1,0:T(8,128)S(1)}, u32[]{:S(2)}, u32[]{:S(2)}) %collective-permute-start.15) | collective-permute-done | bytes 4128 | tf_op jit(solution)/shard_map/ppermute | solution.py:754
  59.0 3.0 %collective-permute-done.16 = f32[8,128]{1,0:T(8,128)S(1)} collective-permute-done((f32[8,128]{1,0:T(8,128)S(1)}, f32[8,128]{1,0:T(8,128)S(1)}, u32[]{:S(2)}, u32[]{:S(2)}) %collective-permute-start.16) | collective-permute-done | bytes 4128 | tf_op jit(solution)/shard_map/ppermute | solution.py:754
  62.0 3.2 %collective-permute-start.17 = (f32[8,128]{1,0:T(8,128)S(1)}, f32[8,128]{1,0:T(8,128)S(1)}, u32[]{:S(2)}, u32[]{:S(2)}) collective-permute-start(f32[8,128]{1,0:T(8,128)S(1)} %add.47), channel_id=1, source_target_pairs={{0,33},{1,32},{2,35},{3,34},{4,37},{5,36},{6,39},{7,38},{8,41},{9,... | collective-permute-start | bytes 12296 | tf_op jit(solution)/shard_map/ppermute | solution.py:754
  66.5 2.1 %collective-permute-start.18 = (f32[8,128]{1,0:T(8,128)S(1)}, f32[8,128]{1,0:T(8,128)S(1)}, u32[]{:S(2)}, u32[]{:S(2)}) collective-permute-start(f32[8,128]{1,0:T(8,128)S(1)} %add.48), channel_id=1, source_target_pairs={{0,25},{1,24},{2,27},{3,26},{4,29},{5,28},{6,31},{7,30},{8,17},{9,... | collective-permute-start | bytes 12296 | tf_op jit(solution)/shard_map/ppermute | solution.py:754
  68.6 2.1 %collective-permute-done.18 = f32[8,128]{1,0:T(8,128)S(1)} collective-permute-done((f32[8,128]{1,0:T(8,128)S(1)}, f32[8,128]{1,0:T(8,128)S(1)}, u32[]{:S(2)}, u32[]{:S(2)}) %collective-permute-start.18) | collective-permute-done | bytes 4128 | tf_op jit(solution)/shard_map/ppermute | solution.py:754
  71.2 2.0 %shard_map.158 = f32[3,16,16,128]{3,2,1,0:T(8,128)} custom-call(f32[3,16,16,128]{3,2,1,0:T(8,128)S(1)} %get-tuple-element.84.refs_0_.fine, f32[3,8,8,256]{3,2,1,0:T(8,128)S(1)} %get-tuple-element.85.refs_1_.coarse, f32[3,16,16,128]{3,2,1,0:T(8,128)S(1)} %get-tuple-element.68.refs_0_.prev, s32[16,128]{1,0:T(8,128)S(1)} %pad.4.refs_4_.offs, ...), custom_call_target="tpu_custom_call" | custom-call | flops 2000000 | bytes 1048576 | tf_op jit(solution)/shard_map/pallas_call | solution.py:674
  73.3 1.5 %shard_map.159 = f32[3,8,8,256]{3,2,1,0:T(8,128)} custom-call(f32[3,16,16,128]{3,2,1,0:T(8,128)S(1)} %get-tuple-element.84.refs_0_.fine, f32[3,8,8,256]{3,2,1,0:T(8,128)S(1)} %get-tuple-element.85.refs_1_.coarse, f32[3,8,8,256]{3,2,1,0:T(8,128)S(1)} %get-tuple-element.69.refs_1_.prev, f32[8,8,256]{2,1,0:T(8,128)S(1)} %get-tuple-element.53.refs_10_.refs_0_, ...), custom_call_target="tpu_custom_call" | custom-call | flops 2000000 | bytes 1048576 | tf_op jit(solution)/shard_map/pallas_call | solution.py:674
  (76 shorter events, 12.5 us)
Async XLA Ops:
  1.9 5.0 %collective-permute-start = (f32[200,128]{1,0:T(8,128)S(1)}, f32[200,128]{1,0:T(8,128)S(1)}, u32[]{:S(2)}, u32[]{:S(2)}) collective-permute-start(f32[200,128]{1,0:T(8,128)S(1)} %get-tuple-element.62), channel_id=1, source_target_pairs={{0,8},{1,9},{2,10},{3,11},{4,12},{5,13},{6,14},{7,15},{8,0},{9,1},... | collective-permute-start | bytes 307208 | tf_op jit(solution)/shard_map/ppermute | solution.py:754
  4.0 2.9 %collective-permute-start.1 = (f32[200,128]{1,0:T(8,128)S(1)}, f32[200,128]{1,0:T(8,128)S(1)}, u32[]{:S(2)}, u32[]{:S(2)}) collective-permute-start(f32[200,128]{1,0:T(8,128)S(1)} %get-tuple-element.63), channel_id=1, source_target_pairs={{0,1},{1,0},{2,3},{3,2},{4,5},{5,4},{6,7},{7,6},{8,16},{9,17},{10,... | collective-permute-start | bytes 307208 | tf_op jit(solution)/shard_map/ppermute | solution.py:754
  5.5 7.9 %collective-permute-start.2 = (f32[132,2,128]{2,1,0:T(2,128)S(1)}, f32[132,2,128]{2,1,0:T(2,128)S(1)}, u32[]{:S(2)}, u32[]{:S(2)}) collective-permute-start(f32[132,2,128]{2,1,0:T(2,128)S(1)} %get-tuple-element.64), channel_id=1, source_target_pairs={{0,1},{1,0},{2,3},{3,2},{4,5},{5,4},{6,7},{7,6},{8,9},{9,8},{10,11... | collective-permute-start | bytes 405512 | tf_op jit(solution)/shard_map/ppermute | solution.py:754
  5.6 7.8 %collective-permute-start.3 = (f32[132,2,128]{2,1,0:T(2,128)S(1)}, f32[132,2,128]{2,1,0:T(2,128)S(1)}, u32[]{:S(2)}, u32[]{:S(2)}) collective-permute-start(f32[132,2,128]{2,1,0:T(2,128)S(1)} %get-tuple-element.65), channel_id=1, source_target_pairs={{0,7},{1,2},{2,1},{3,4},{4,3},{5,6},{6,5},{7,0},{8,15},{9,10},{10,... | collective-permute-start | bytes 405512 | tf_op jit(solution)/shard_map/ppermute | solution.py:754
  7.1 4.1 %collective-permute-start.4 = (f32[28,2,128]{2,1,0:T(2,128)S(1)}, f32[28,2,128]{2,1,0:T(2,128)S(1)}, u32[]{:S(2)}, u32[]{:S(2)}) collective-permute-start(f32[28,2,128]{2,1,0:T(2,128)S(1)} %get-tuple-element.66), channel_id=1, source_target_pairs={{0,1},{1,0},{2,3},{3,2},{4,5},{5,4},{6,7},{7,6},{8,9},{9,8},{10,11... | collective-permute-start | bytes 86024 | tf_op jit(solution)/shard_map/ppermute | solution.py:754
  10.1 3.3 %collective-permute-start.5 = (f32[28,2,128]{2,1,0:T(2,128)S(1)}, f32[28,2,128]{2,1,0:T(2,128)S(1)}, u32[]{:S(2)}, u32[]{:S(2)}) collective-permute-start(f32[28,2,128]{2,1,0:T(2,128)S(1)} %get-tuple-element.67), channel_id=1, source_target_pairs={{0,7},{1,2},{2,1},{3,4},{4,3},{5,6},{6,5},{7,0},{8,15},{9,10},{10,... | collective-permute-start | bytes 86024 | tf_op jit(solution)/shard_map/ppermute | solution.py:754
  16.1 4.1 %collective-permute-start.6 = (f32[232,128]{1,0:T(8,128)S(1)}, f32[232,128]{1,0:T(8,128)S(1)}, u32[]{:S(2)}, u32[]{:S(2)}) collective-permute-start(f32[232,128]{1,0:T(8,128)S(1)} %get-tuple-element.76), channel_id=1, source_target_pairs={{0,8},{1,9},{2,10},{3,11},{4,12},{5,13},{6,14},{7,15},{8,0},{9,1},... | collective-permute-start | bytes 356360 | tf_op jit(solution)/shard_map/ppermute | solution.py:754
  17.9 2.6 %collective-permute-start.7 = (f32[232,128]{1,0:T(8,128)S(1)}, f32[232,128]{1,0:T(8,128)S(1)}, u32[]{:S(2)}, u32[]{:S(2)}) collective-permute-start(f32[232,128]{1,0:T(8,128)S(1)} %get-tuple-element.77), channel_id=1, source_target_pairs={{0,1},{1,0},{2,3},{3,2},{4,5},{5,4},{6,7},{7,6},{8,16},{9,17},{10,... | collective-permute-start | bytes 356360 | tf_op jit(solution)/shard_map/ppermute | solution.py:754
  19.6 2.9 %collective-permute-start.8 = (f32[144,2,128]{2,1,0:T(2,128)S(1)}, f32[144,2,128]{2,1,0:T(2,128)S(1)}, u32[]{:S(2)}, u32[]{:S(2)}) collective-permute-start(f32[144,2,128]{2,1,0:T(2,128)S(1)} %get-tuple-element.79), channel_id=1, source_target_pairs={{0,1},{1,0},{2,3},{3,2},{4,5},{5,4},{6,7},{7,6},{8,9},{9,8},{10,11... | collective-permute-start | bytes 442376 | tf_op jit(solution)/shard_map/ppermute | solution.py:754
  19.7 5.0 %collective-permute-start.9 = (f32[144,2,128]{2,1,0:T(2,128)S(1)}, f32[144,2,128]{2,1,0:T(2,128)S(1)}, u32[]{:S(2)}, u32[]{:S(2)}) collective-permute-start(f32[144,2,128]{2,1,0:T(2,128)S(1)} %get-tuple-element.80), channel_id=1, source_target_pairs={{0,7},{1,2},{2,1},{3,4},{4,3},{5,6},{6,5},{7,0},{8,15},{9,10},{10,... | collective-permute-start | bytes 442376 | tf_op jit(solution)/shard_map/ppermute | solution.py:754
  20.6 4.1 %collective-permute-start.10 = (f32[48,2,128]{2,1,0:T(2,128)S(1)}, f32[48,2,128]{2,1,0:T(2,128)S(1)}, u32[]{:S(2)}, u32[]{:S(2)}) collective-permute-start(f32[48,2,128]{2,1,0:T(2,128)S(1)} %get-tuple-element.81), channel_id=1, source_target_pairs={{0,1},{1,0},{2,3},{3,2},{4,5},{5,4},{6,7},{7,6},{8,9},{9,8},{10,11... | collective-permute-start | bytes 147464 | tf_op jit(solution)/shard_map/ppermute | solution.py:754
  22.5 3.5 %collective-permute-start.11 = (f32[48,2,128]{2,1,0:T(2,128)S(1)}, f32[48,2,128]{2,1,0:T(2,128)S(1)}, u32[]{:S(2)}, u32[]{:S(2)}) collective-permute-start(f32[48,2,128]{2,1,0:T(2,128)S(1)} %get-tuple-element.82), channel_id=1, source_target_pairs={{0,7},{1,2},{2,1},{3,4},{4,3},{5,6},{6,5},{7,0},{8,15},{9,10},{10,... | collective-permute-start | bytes 147464 | tf_op jit(solution)/shard_map/ppermute | solution.py:754
  29.1 5.3 %collective-permute-start.20 = (f32[136,128]{1,0:T(8,128)S(1)}, f32[136,128]{1,0:T(8,128)S(1)}, u32[]{:S(2)}, u32[]{:S(2)}) collective-permute-start(f32[136,128]{1,0:T(8,128)S(1)} %get-tuple-element.86), channel_id=1, source_target_pairs={{0,8},{1,9},{2,10},{3,11},{4,12},{5,13},{6,14},{7,15},{8,0},{9,1},... | collective-permute-start | bytes 208904 | tf_op jit(solution)/shard_map/ppermute | solution.py:754
  32.7 2.5 %collective-permute-start.21 = (f32[136,128]{1,0:T(8,128)S(1)}, f32[136,128]{1,0:T(8,128)S(1)}, u32[]{:S(2)}, u32[]{:S(2)}) collective-permute-start(f32[136,128]{1,0:T(8,128)S(1)} %get-tuple-element.87), channel_id=1, source_target_pairs={{0,1},{1,0},{2,3},{3,2},{4,5},{5,4},{6,7},{7,6},{8,16},{9,17},{10,... | collective-permute-start | bytes 208904 | tf_op jit(solution)/shard_map/ppermute | solution.py:754
  35.4 35.8 %collective-permute-start.22 = (f32[100,2,128]{2,1,0:T(2,128)S(1)}, f32[100,2,128]{2,1,0:T(2,128)S(1)}, u32[]{:S(2)}, u32[]{:S(2)}) collective-permute-start(f32[100,2,128]{2,1,0:T(2,128)S(1)} %get-tuple-element.88), channel_id=1, source_target_pairs={{0,1},{1,0},{2,3},{3,2},{4,5},{5,4},{6,7},{7,6},{8,9},{9,8},{10,11... | collective-permute-start | bytes 307208 | tf_op jit(solution)/shard_map/ppermute | solution.py:754
  37.1 34.2 %collective-permute-start.23 = (f32[100,2,128]{2,1,0:T(2,128)S(1)}, f32[100,2,128]{2,1,0:T(2,128)S(1)}, u32[]{:S(2)}, u32[]{:S(2)}) collective-permute-start(f32[100,2,128]{2,1,0:T(2,128)S(1)} %get-tuple-element.89), channel_id=1, source_target_pairs={{0,7},{1,2},{2,1},{3,4},{4,3},{5,6},{6,5},{7,0},{8,15},{9,10},{10,... | collective-permute-start | bytes 307208 | tf_op jit(solution)/shard_map/ppermute | solution.py:754
  37.1 11.5 %collective-permute-start.12 = (f32[8,128]{1,0:T(8,128)S(1)}, f32[8,128]{1,0:T(8,128)S(1)}, u32[]{:S(2)}, u32[]{:S(2)}) collective-permute-start(f32[8,128]{1,0:T(8,128)S(1)} %get-tuple-element.83), channel_id=1, source_target_pairs={{0,224},{1,225},{2,226},{3,227},{4,228},{5,229},{6,230},{7,231},{8... | collective-permute-start | bytes 12296 | tf_op jit(solution)/shard_map/ppermute | solution.py:754
  48.6 3.4 %collective-permute-start.13 = (f32[8,128]{1,0:T(8,128)S(1)}, f32[8,128]{1,0:T(8,128)S(1)}, u32[]{:S(2)}, u32[]{:S(2)}) collective-permute-start(f32[8,128]{1,0:T(8,128)S(1)} %add.43), channel_id=1, source_target_pairs={{0,1},{1,0},{2,3},{3,2},{4,5},{5,4},{6,7},{7,6},{8,9},{9,8},{10,11... | collective-permute-start | bytes 12296 | tf_op jit(solution)/shard_map/ppermute | solution.py:754
  52.0 3.9 %collective-permute-start.14 = (f32[8,128]{1,0:T(8,128)S(1)}, f32[8,128]{1,0:T(8,128)S(1)}, u32[]{:S(2)}, u32[]{:S(2)}) collective-permute-start(f32[8,128]{1,0:T(8,128)S(1)} %add.44), channel_id=1, source_target_pairs={{0,65},{1,64},{2,67},{3,66},{4,69},{5,68},{6,71},{7,70},{8,73},{9,... | collective-permute-start | bytes 12296 | tf_op jit(solution)/shard_map/ppermute | solution.py:754
  55.9 3.0 %collective-permute-start.15 = (f32[8,128]{1,0:T(8,128)S(1)}, f32[8,128]{1,0:T(8,128)S(1)}, u32[]{:S(2)}, u32[]{:S(2)}) collective-permute-start(f32[8,128]{1,0:T(8,128)S(1)} %add.45), channel_id=1, source_target_pairs={{0,3},{1,2},{2,1},{3,0},{4,7},{5,6},{6,5},{7,4},{8,11},{9,10},{10,... | collective-permute-start | bytes 12296 | tf_op jit(solution)/shard_map/ppermute | solution.py:754
  59.0 3.0 %collective-permute-start.16 = (f32[8,128]{1,0:T(8,128)S(1)}, f32[8,128]{1,0:T(8,128)S(1)}, u32[]{:S(2)}, u32[]{:S(2)}) collective-permute-start(f32[8,128]{1,0:T(8,128)S(1)} %add.46), channel_id=1, source_target_pairs={{0,9},{1,8},{2,11},{3,10},{4,13},{5,12},{6,15},{7,14},{8,1},{9,0},... | collective-permute-start | bytes 12296 | tf_op jit(solution)/shard_map/ppermute | solution.py:754
  62.0 4.5 %collective-permute-start.17 = (f32[8,128]{1,0:T(8,128)S(1)}, f32[8,128]{1,0:T(8,128)S(1)}, u32[]{:S(2)}, u32[]{:S(2)}) collective-permute-start(f32[8,128]{1,0:T(8,128)S(1)} %add.47), channel_id=1, source_target_pairs={{0,33},{1,32},{2,35},{3,34},{4,37},{5,36},{6,39},{7,38},{8,41},{9,... | collective-permute-start | bytes 12296 | tf_op jit(solution)/shard_map/ppermute | solution.py:754
  66.5 4.2 %collective-permute-start.18 = (f32[8,128]{1,0:T(8,128)S(1)}, f32[8,128]{1,0:T(8,128)S(1)}, u32[]{:S(2)}, u32[]{:S(2)}) collective-permute-start(f32[8,128]{1,0:T(8,128)S(1)} %add.48), channel_id=1, source_target_pairs={{0,25},{1,24},{2,27},{3,26},{4,29},{5,28},{6,31},{7,30},{8,17},{9,... | collective-permute-start | bytes 12296 | tf_op jit(solution)/shard_map/ppermute | solution.py:754
  70.7 4.2 %collective-permute-start.19 = (f32[8,128]{1,0:T(8,128)S(1)}, f32[8,128]{1,0:T(8,128)S(1)}, u32[]{:S(2)}, u32[]{:S(2)}) collective-permute-start(f32[8,128]{1,0:T(8,128)S(1)} %add.49), channel_id=1, source_target_pairs={{0,7},{1,6},{2,5},{3,4},{4,3},{5,2},{6,1},{7,0},{8,15},{9,14},{10,... | collective-permute-start | bytes 12296 | tf_op jit(solution)/shard_map/ppermute | solution.py:754
  (13 other events, 46.2 us)

commit v10 on v9

--- a/solution.py
+++ b/solution.py
@@ -285,7 +285,7 @@
         return [(slice(0, x + 4), *taken(y_in[0][rows], y_in[1][rows]))]
     rows = slice(start + 2, start + 2 + x)
     out = [(slice(2, 2 + x), *taken(y_in[0][rows], y_in[1][rows]))]
-    for side in range(2):
+    for side in range(2 if y_in[2] is not None else 0):
         rows = slice(4 * field + 2 * side, 4 * field + 2 * side + 2)
         at = slice(side * (x + 2), side * (x + 2) + 2)
         out.append((at, *taken(y_in[2][rows], y_in[3][rows])))
@@ -309,12 +309,12 @@
             ext[i, 8 + y : 10 + y, at] = high
 
 
-def fill_transposed(x, y, ext, beta, inv_ext, psi):
+def fill_transposed(y, ext, beta, inv_ext, psi, rows):
     z = ext.shape[-1]
     lane = lax.broadcasted_iota(jnp.int32, (y + 2, z), 1)
     wide, low, high = slice(7, 9 + y), slice(6, 8 + y), slice(8, 10 + y)
 
-    def row(r, carry):
+    for r in rows:
         along_x = ext[0, r, wide, :] * beta[r, wide, :]
         along_x -= ext[0, r + 2, wide, :] * beta[r + 2, wide, :]
         along_y = ext[1, r + 1, low, :] * beta[r + 1, low, :]
@@ -323,9 +323,6 @@
         column = inv * beta[r + 1, wide, :] * ext[2, r + 1, wide, :]
         total = along_x + along_y + difference_transposed(column, lane)
         psi[r, wide, :] = jnp.where(inv > 0.0, total, 0.0)
-        return carry
-
-    lax.fori_loop(0, x + 2, row, 0, unroll=True)
 
 
 def fill_displacement(s, flags, own, ext, x_in, y_in, fine, halves=None):
@@ -400,23 +397,20 @@
             inv_ext[1 : 1 + x, place : place + 1, at] = jnp.where(flags[flag], edge[None, 0:1] / met, 0.0)
 
 
-def fill_divergence(x, y, ext, inv_ext, div):
+def fill_divergence(x, y, ext, inv_ext, div, rows=None):
     z = ext.shape[-1]
     lane = lax.broadcasted_iota(jnp.int32, (y + 2, z), 1)
 
-    def row(r, carry):
+    for r in rows or range(x + 2):
         along_x = ext[0, r + 2, 7 : 9 + y, :] - ext[0, r, 7 : 9 + y, :]
         along_y = ext[1, r + 1, 8 : 10 + y, :] - ext[1, r + 1, 6 : 8 + y, :]
         f = ext[2, r + 1, 7 : 9 + y, :]
         inv = inv_ext[r, 0 : 2 + y, :]
         total = along_x + along_y + inv * difference(f, lane)
         div[r, 7 : 9 + y, :] = jnp.where(inv > 0.0, total, 0.0)
-        return carry
-
-    lax.fori_loop(0, x + 2, row, 0, unroll=True)
-
-
-def update(x, y, ext, wide_ext, inv_ext, div, prev, coef, new, ghosts, psi=None):
+
+
+def update(x, y, ext, wide_ext, inv_ext, div, prev, coef, new, ghosts, psi=None, rows=None):
     c1, c2, weight, above, vertical = coef
     z = ext.shape[-1]
     lane = lax.broadcasted_iota(jnp.int32, (y, z), 1)
@@ -480,7 +474,8 @@
         return total, totals[1] + (dm * squares - (0.5 * STEP) * cross)
 
     start = (jnp.zeros((y, z), jnp.float32),) * (1 if psi is None else 2)
-    return lax.fori_loop(0, x, row, start, unroll=4)
+    count, index, unroll = rows or (x, lambda k: k, 4)
+    return lax.fori_loop(0, count, lambda k, t: row(index(k), t), start, unroll=unroll)
 
 
 def double_plane(s, ext_c, double):
@@ -543,7 +538,13 @@
     return lambda i: (mean(pairs, i), None, mean(pairs_next, i) if pairs_next is not None else None)
 
 
-def step_kernel(s, step, cells, *refs):
+INNER_F, OUTER_F = (10, lambda k: k + 2, 5), (6, lambda k: jnp.where(k < 2, k, k + 10), 3)
+INNER_C, OUTER_C = (4, lambda k: k + 1, 4), (4, lambda k: jnp.where(k < 1, k, k + 4), 4)
+INNER_DIV_F, OUTER_DIV_F = tuple(range(2, 14)), (0, 1, 2, 3, *range(12, 18))
+INNER_DIV_C, OUTER_DIV_C = tuple(range(1, 7)), (0, 1, 2, *range(5, 10))
+
+
+def step_kernel(s, step, inner, cells, *refs):
     flags = where_am_i()
     refs = list(refs)
 
@@ -554,54 +555,68 @@
 
     fine, coarse, fine_prev, coarse_prev, offs = take(5)
     coef_f, coef_c = take(5), take(5)
-    if step == 0:
+    makes_mats = inner and step == 0
+    if makes_mats:
         rig_f, met_f, inverse_f, rig_c, met_c, inverse_c = take(6)
     else:
         wide_f, inv_f, wide_c, inv_c = take(4)
     beta_own = take(2)
-    if step == 1:
-        energy_in, spread_in = take(2)
-    x_in, y_in = take(2), take(4)
+    table_in = take(1)[0] if step == 1 or not inner else None
+    if not inner:
+        done_f, done_c = take(2)
+    if step == 1 and not inner:
+        (spread_in,) = take(1)
+    x_in = take(2)
+    y_in = take(2) + [None, None] if inner else take(4)
     new_f, new_c, energy = take(3)
-    x_out = take(2)
-    if step == 0:
-        wide_f, inv_f, wide_c, inv_c, spread_out = take(5)
+    if not inner:
+        x_out = take(2)
+    if makes_mats:
+        wide_f, inv_f, wide_c, inv_c = take(4)
+    if step == 0 and not inner:
+        (spread_out,) = take(1)
     ext_f, ext_c, div_f, div_c, double, moved, pairs = take(7)
 
     fill_displacement(s, flags, fine, ext_f, x_in, y_in, True)
     fill_displacement(s, flags, coarse, ext_c, x_in, y_in, False)
-    if step == 0:
+    if makes_mats:
         fill_materials(s, flags, rig_f, met_f, inverse_f, wide_f, inv_f, x_in, y_in, True)
         fill_materials(s, flags, rig_c, met_c, inverse_c, wide_c, inv_c, x_in, y_in, False)
-
     double_plane(s, ext_c, double)
     add_pairs(s, fine, pairs)
-    fill_divergence(s.fx, s.fy, ext_f, inv_f, div_f)
-    fill_divergence(s.cx, s.cy, ext_c, inv_c, div_c)
-    psi_f = psi_c = None
+    rows_f, rows_c = (INNER_F, INNER_C) if inner else (OUTER_F, OUTER_C)
+    lines_f, lines_c = (INNER_DIV_F, INNER_DIV_C) if inner else (OUTER_DIV_F, OUTER_DIV_C)
+    fill_divergence(s.fx, s.fy, ext_f, inv_f, div_f, lines_f)
+    fill_divergence(s.cx, s.cy, ext_c, inv_c, div_c, lines_c)
+    psi_f = psi_c = pairs_next = None
     if step == 1:
         psi_f, psi_c, all_beta_f, all_beta_c, pairs_next, spread = take(6)
         fill_beta(s, flags, beta_own[0], all_beta_f, x_in, y_in, True)
         fill_beta(s, flags, beta_own[1], all_beta_c, x_in, y_in, False)
-        fill_transposed(s.fx, s.fy, ext_f, all_beta_f, inv_f, psi_f)
-        fill_transposed(s.cx, s.cy, ext_c, all_beta_c, inv_c, psi_c)
+        fill_transposed(s.fy, ext_f, all_beta_f, inv_f, psi_f, lines_f)
+        fill_transposed(s.cy, ext_c, all_beta_c, inv_c, psi_c, lines_c)
+    if not inner:
+        new_f[:, 2:12] = done_f[:, 2:12]
+        new_c[:, 1:5] = done_c[:, 1:5]
 
     weights = node_weights(s, offs)
-    fine_ghosts = bottom_ghosts(s, weights, double, moved)
-    coarse_ghosts = top_ghosts(s, pairs, pairs_next if step == 1 else None)
+    ghosts_f = bottom_ghosts(s, weights, double, moved)
+    ghosts_c = top_ghosts(s, pairs, pairs_next)
     sums_f = update(
-        s.fx, s.fy, ext_f, wide_f, inv_f, div_f, fine_prev, coef_f, new_f, fine_ghosts, psi_f
+        s.fx, s.fy, ext_f, wide_f, inv_f, div_f, fine_prev, coef_f, new_f, ghosts_f, psi_f, rows_f
     )
     if step == 1:
         add_pairs(s, new_f, pairs_next)
     sums_c = update(
-        s.cx, s.cy, ext_c, wide_c, inv_c, div_c, coarse_prev, coef_c, new_c, coarse_ghosts, psi_c
+        s.cx, s.cy, ext_c, wide_c, inv_c, div_c, coarse_prev, coef_c, new_c, ghosts_c, psi_c, rows_c
     )
     place = lax.broadcasted_iota(jnp.int32, (8, LANES), 0)
-    table = jnp.zeros((8, LANES), jnp.float32) if step == 0 else energy_in[...]
-    table = jnp.where(place == step, jnp.sum(sums_f[0]) / cells[0], table)
-    table = jnp.where(place == STEPS + step, jnp.sum(sums_c[0]) / cells[1], table)
-    if step == 0:
+    table = jnp.zeros((8, LANES), jnp.float32) if table_in is None else table_in[...]
+    adds = [(step, jnp.sum(sums_f[0]) / cells[0]), (STEPS + step, jnp.sum(sums_c[0]) / cells[1])]
+    if step == 1:
+        adds.append((2, jnp.sum(sums_f[1]) / cells[0]))
+        adds.append((STEPS + 2, jnp.sum(sums_c[1]) / cells[1]))
+    if step == 0 and not inner:
         weights_x, weights_y = weights
         node = (s.fy, LANES)
         node_lane = lax.broadcasted_iota(jnp.int32, node, 1)
@@ -623,7 +638,7 @@
             spread_out[i, 0:rows, :] = there + pltpu.roll(there, LANES - 4, 1)
             spread_out[i, rows:, :] = jnp.zeros((s.spread - rows, LANES), jnp.float32)
         put_x(s, flags, x_out, new_f, new_c, beta_own, spread_out)
-    if step == 1:
+    if step == 1 and not inner:
         spread[...] = spread_in[:, 2 : 2 + s.cy, :]
         rows = pl.ds(s.corner_spread, s.cx)
         low, high = sides(flags, EVEN_Y, HAS_YM, HAS_YP, y_in[2][rows], y_in[3][rows])
@@ -632,12 +647,12 @@
         joined = jnp.zeros((s.cy, LANES), jnp.float32)
         for i in range(s.cx):
             for c in range(3):
-                weights = spread[i] if c == 0 else pltpu.roll(spread[i], LANES - c, 1)
-                joined += new_c[c, i, :, 0:LANES] * weights
-        joined = jnp.sum(joined[:, 0:1])
-        table = jnp.where(place == 2, (jnp.sum(sums_f[1]) - (0.5 * STEP) * joined) / cells[0], table)
-        table = jnp.where(place == STEPS + 2, jnp.sum(sums_c[1]) / cells[1], table)
+                line = spread[i] if c == 0 else pltpu.roll(spread[i], LANES - c, 1)
+                joined += new_c[c, i, :, 0:LANES] * line
+        adds.append((2, (-0.5 * STEP) * jnp.sum(joined[:, 0:1]) / cells[0]))
         put_x(s, flags, x_out, new_f, new_c)
+    for row, value in adds:
+        table = table + jnp.where(place == row, value, 0.0)
     energy[...] = table
 
 
@@ -877,46 +892,49 @@
                 scratch=[scratch[1], scratch[3], scratch[6]],
             )
             break
-        shapes = [fine.shape, coarse.shape, (8, LANES)]
-        shapes += [((s.x_rows_beta, s.x_rows)[step], LANES)] * 2
-        more_scratch = []
+
+        def part_of_step(inner, shapes, *args):
+            return call(
+                functools.partial(step_kernel, s, step, inner, cells),
+                [fine.shape, coarse.shape, (8, LANES)] + shapes,
+                2_000_000,
+                fine,
+                coarse,
+                fine_prev,
+                coarse_prev,
+                offs,
+                *coef_f,
+                *coef_c,
+                *args,
+                scratch=scratch + (more_scratch if step == 1 else []),
+            )
+
+        more_scratch = [
+            scratch[2],
+            scratch[3],
+            scratch[0][1:],
+            scratch[1][1:],
+            scratch[6],
+            (s.cx, s.cy, LANES),
+        ]
+        betas = [beta_f, beta_c]
         if step == 0:
-            extra = [fine_rigidity, fine_metric, inverse_f, coarse_rigidity, coarse_metric, inverse_c]
-            extra += [beta_f, beta_c]
-            shapes += [fine_ext, fine_ext, coarse_ext, coarse_ext, spread]
+            raw = [fine_rigidity, fine_metric, inverse_f, coarse_rigidity, coarse_metric, inverse_c]
+            shapes = [fine_ext, fine_ext, coarse_ext, coarse_ext]
+            *done, energy, w_f, i_f, w_c, i_c = part_of_step(
+                True, shapes, *raw, *betas, *x_in, *y_in[:2]
+            )
+            ext_mats = [w_f, i_f, w_c, i_c]
+            shapes, added = [(s.x_rows_beta, LANES)] * 2 + [spread], []
         else:
-            extra = list(ext_mats)
-        if step == 1:
-            extra += [beta_f, beta_c, energy, y_out[2]]
-            more_scratch = [
-                scratch[2],
-                scratch[3],
-                scratch[0][1:],
-                scratch[1][1:],
-                scratch[6],
-                (s.cx, s.cy, LANES),
-            ]
-        outs = call(
-            functools.partial(step_kernel, s, step, cells),
-            shapes,
-            4_000_000,
-            fine,
-            coarse,
-            fine_prev,
-            coarse_prev,
-            offs,
-            *coef_f,
-            *coef_c,
-            *extra,
-            *x_in,
-            *y_in,
-            scratch=scratch + more_scratch,
-        )
+            *done, energy = part_of_step(True, [], *ext_mats, *betas, energy, *x_in, *y_in[:2])
+            shapes, added = [(s.x_rows, LANES)] * 2, [y_out[2]]
+        outs = part_of_step(False, shapes, *ext_mats, *betas, energy, *done, *added, *x_in, *y_in)
         fine_prev, coarse_prev = fine, coarse
         fine, coarse, energy = outs[:3]
         x_out = outs[3:5]
         if step == 0:
-            *ext_mats, spread_own = outs[5:]
+            spread_own = outs[5]
     other, fine, coarse = lax.optimization_barrier((other, fine_final, coarse_final))
     energy = energy + other
     energy = energy[: 2 * STEPS, 0].reshape(2, STEPS).T

time: 75.9 us -> 74.9 us (0.987)
  waiting for transfers between devices: 19.8 us -> 14 us
  starting transfers between devices: 41.9 us -> 45 us
  Pallas kernels: 11.4 us -> 12.4 us
  local copies, waits for them, and re-layouts: 1.64 us -> 2.44 us
    ppermute x24, waiting for transfers between devices: 19.8 us -> 14 us  [swap(): return lax.ppermute(value, ALL, swap_pairs(mesh, move))]
    ppermute x24, starting transfers between devices: 41.9 us -> 45 us  [swap(): return lax.ppermute(value, ALL, swap_pairs(mesh, move))]
    pallas_call x12 -> x14, Pallas kernels: 11.4 us -> 12.4 us  [call(): pl.pallas_call(kernel, out_shape=shapes, in_specs=[spec] * len(args), out...]
    unnamed x26, local copies, waits for them, and re-layouts: 0.8 us -> 1.6 us
  transfers between devices with their start and end apart: 24 -> 24, of which waited for: 15 -> 11; matrix products, arithmetic and copies ran while one was open for 0% -> 0% of each run, Pallas kernels for 6% -> 10%
where the time goes in v10:
time: 74.9 us; the launch traced here: 74.7 us
  starting transfers between devices  45 us (60%)
  waiting for transfers between devices  14 us (19%)
  Pallas kernels  12.4 us (17%)
  local copies, waits for them, and re-layouts  2.44 us (3%)
  between operations  0.9 us (1%)
    ppermute x24, starting transfers between devices, swap(): return lax.ppermute(value, ALL, swap_pairs(mesh, move))  45 us
    ppermute x24, waiting for transfers between devices, swap(): return lax.ppermute(value, ALL, swap_pairs(mesh, move))  14 us
    pallas_call x14, Pallas kernels, call(): pl.pallas_call(kernel, out_shape=shapes, in_specs=[spec] * len(args), out...  12.4 us
    unnamed x26, local copies, waits for them, and re-layouts  1.6 us
  transfers between devices with their start and end apart: 24, of which 11 were waited for; matrix products, arithmetic and copies ran while one was open for 0% of the time, Pallas kernels for 10%

profile of v10, /device:TPU:1, one launch (start us, length us, event | category | flops | bytes accessed | tf_op | source)
XLA Modules:
  0.0 74.7 jit_solution(17771132855690498936)
XLA Ops:
  1.9 2.1 %collective-permute-start = (f32[200,128]{1,0:T(8,128)S(1)}, f32[200,128]{1,0:T(8,128)S(1)}, u32[]{:S(2)}, u32[]{:S(2)}) collective-permute-start(f32[200,128]{1,0:T(8,128)S(1)} %get-tuple-element.68), channel_id=1, source_target_pairs={{0,8},{1,9},{2,10},{3,11},{4,12},{5,13},{6,14},{7,15},{8,0},{9,1},... | collective-permute-start | bytes 307208 | tf_op jit(solution)/shard_map/ppermute | solution.py:769
  7.1 3.0 %collective-permute-start.4 = (f32[28,2,128]{2,1,0:T(2,128)S(1)}, f32[28,2,128]{2,1,0:T(2,128)S(1)}, u32[]{:S(2)}, u32[]{:S(2)}) collective-permute-start(f32[28,2,128]{2,1,0:T(2,128)S(1)} %get-tuple-element.79), channel_id=1, source_target_pairs={{0,1},{1,0},{2,3},{3,2},{4,5},{5,4},{6,7},{7,6},{8,9},{9,8},{10,11... | collective-permute-start | bytes 86024 | tf_op jit(solution)/shard_map/ppermute | solution.py:769
  12.0 1.5 %shard_map.152 = (f32[3,16,16,128]{3,2,1,0:T(8,128)S(1)}, f32[3,8,8,256]{3,2,1,0:T(8,128)S(1)}, f32[8,128]{1,0:T(8,128)S(1)}, f32[18,18,128]{2,1,0:T(8,128)S(1)}...) custom-call(f32[3,16,16,128]{3,2,1,0:T(8,128)S(1)} %copy-done, ...), custom_call_target="tpu_custom_call" | custom-call | flops 2000000 | bytes 1048576 | tf_op jit(solution)/shard_map/pallas_call | solution.py:689
  13.5 1.6 %shard_map.154 = (f32[3,16,16,128]{3,2,1,0:T(8,128)S(1)}, f32[3,8,8,256]{3,2,1,0:T(8,128)S(1)}, f32[8,128]{1,0:T(8,128)S(1)}, f32[232,128]{1,0:T(8,128)S(1)}, f3...) custom-call(f32[3,16,16,128]{3,2,1,0:T(8,128)S(1)} %copy-done, f32[3,8,8,256]{3,2,1,0:T(8,128)S(1)} %copy-done.1, ...), custom_call_target="tpu_custom_call" | custom-call | flops 2000000 | bytes 1048576 | tf_op jit(solution)/shard_map/pallas_call | solution.py:689
  15.1 1.8 %collective-permute-start.6 = (f32[232,128]{1,0:T(8,128)S(1)}, f32[232,128]{1,0:T(8,128)S(1)}, u32[]{:S(2)}, u32[]{:S(2)}) collective-permute-start(f32[232,128]{1,0:T(8,128)S(1)} %get-tuple-element.84), channel_id=1, source_target_pairs={{0,8},{1,9},{2,10},{3,11},{4,12},{5,13},{6,14},{7,15},{8,0},{9,1},... | collective-permute-start | bytes 356360 | tf_op jit(solution)/shard_map/ppermute | solution.py:769
  17.0 1.8 %collective-permute-start.7 = (f32[232,128]{1,0:T(8,128)S(1)}, f32[232,128]{1,0:T(8,128)S(1)}, u32[]{:S(2)}, u32[]{:S(2)}) collective-permute-start(f32[232,128]{1,0:T(8,128)S(1)} %get-tuple-element.85), channel_id=1, source_target_pairs={{0,1},{1,0},{2,3},{3,2},{4,5},{5,4},{6,7},{7,6},{8,16},{9,17},{10,... | collective-permute-start | bytes 356360 | tf_op jit(solution)/shard_map/ppermute | solution.py:769
  19.9 1.9 %collective-permute-start.10 = (f32[48,2,128]{2,1,0:T(2,128)S(1)}, f32[48,2,128]{2,1,0:T(2,128)S(1)}, u32[]{:S(2)}, u32[]{:S(2)}) collective-permute-start(f32[48,2,128]{2,1,0:T(2,128)S(1)} %get-tuple-element.93), channel_id=1, source_target_pairs={{0,1},{1,0},{2,3},{3,2},{4,5},{5,4},{6,7},{7,6},{8,9},{9,8},{10,11... | collective-permute-start | bytes 147464 | tf_op jit(solution)/shard_map/ppermute | solution.py:769
  22.5 1.4 %collective-permute-done.9.refs_25_.refs_28_ = f32[144,2,128]{2,1,0:T(2,128)S(1)} collective-permute-done((f32[144,2,128]{2,1,0:T(2,128)S(1)}, f32[144,2,128]{2,1,0:T(2,128)S(1)}, u32[]{:S(2)}, u32[]{:S(2)}) %collective-permute-start.9) | collective-permute-done | bytes 147488 | tf_op jit(solution)/shard_map/ppermute | solution.py:769
  23.9 1.8 %shard_map.156 = (f32[3,16,16,128]{3,2,1,0:T(8,128)S(1)}, f32[3,8,8,256]{3,2,1,0:T(8,128)S(1)}, f32[8,128]{1,0:T(8,128)S(1)}) custom-call(f32[3,16,16,128]{3,2,1,0:T(8,128)S(1)} %get-tuple-element.81.refs_0_.prev, f32[3,8,8,256]{3,2,1,0:T(8,128)S(1)} %get-tuple-element.82.refs_1_.prev, f32[3,16,16,128]{3,2,1,0:T(8,128)S(1)} %copy-done, ...), custom_call_target="tpu_custom_call" | custom-call | flops 2000000 | bytes 1048576 | tf_op jit(solution)/shard_map/pallas_call | solution.py:689
  25.8 1.8 %shard_map.158 = (f32[3,16,16,128]{3,2,1,0:T(8,128)S(1)}, f32[3,8,8,256]{3,2,1,0:T(8,128)S(1)}, f32[8,128]{1,0:T(8,128)S(1)}, f32[136,128]{1,0:T(8,128)S(1)}, f32[136,128]{1,0:T(8,128)S(1)}) custom-call(f32[3,16,16,128]{3,2,1,0:T(8,128)S(1)} %get-tuple-element.81.refs_0_.prev, f32[3,8,8,256]{3,2,1,0:T(8,128)S(1)} %get-tuple-element.82.refs_1_.prev, ...), custom_call_target="tpu_custom_call" | custom-call | flops 2000000 | bytes 1048576 | tf_op jit(solution)/shard_map/pallas_call | solution.py:689
  27.6 4.7 %collective-permute-start.20 = (f32[136,128]{1,0:T(8,128)S(1)}, f32[136,128]{1,0:T(8,128)S(1)}, u32[]{:S(2)}, u32[]{:S(2)}) collective-permute-start(f32[136,128]{1,0:T(8,128)S(1)} %get-tuple-element.98), channel_id=1, source_target_pairs={{0,8},{1,9},{2,10},{3,11},{4,12},{5,13},{6,14},{7,15},{8,0},{9,1},... | collective-permute-start | bytes 208904 | tf_op jit(solution)/shard_map/ppermute | solution.py:769
  32.3 1.4 %collective-permute-start.21 = (f32[136,128]{1,0:T(8,128)S(1)}, f32[136,128]{1,0:T(8,128)S(1)}, u32[]{:S(2)}, u32[]{:S(2)}) collective-permute-start(f32[136,128]{1,0:T(8,128)S(1)} %get-tuple-element.99), channel_id=1, source_target_pairs={{0,1},{1,0},{2,3},{3,2},{4,5},{5,4},{6,7},{7,6},{8,16},{9,17},{10,... | collective-permute-start | bytes 208904 | tf_op jit(solution)/shard_map/ppermute | solution.py:769
  34.8 1.5 %collective-permute-start.22 = (f32[100,2,128]{2,1,0:T(2,128)S(1)}, f32[100,2,128]{2,1,0:T(2,128)S(1)}, u32[]{:S(2)}, u32[]{:S(2)}) collective-permute-start(f32[100,2,128]{2,1,0:T(2,128)S(1)} %get-tuple-element.100), channel_id=1, source_target_pairs={{0,1},{1,0},{2,3},{3,2},{4,5},{5,4},{6,7},{7,6},{8,9},{9,8},{10,11... | collective-permute-start | bytes 307208 | tf_op jit(solution)/shard_map/ppermute | solution.py:769
  36.3 10.5 %collective-permute-start.12 = (f32[8,128]{1,0:T(8,128)S(1)}, f32[8,128]{1,0:T(8,128)S(1)}, u32[]{:S(2)}, u32[]{:S(2)}) collective-permute-start(f32[8,128]{1,0:T(8,128)S(1)} %get-tuple-element.95), channel_id=1, source_target_pairs={{0,224},{1,225},{2,226},{3,227},{4,228},{5,229},{6,230},{7,231},{8... | collective-permute-start | bytes 12296 | tf_op jit(solution)/shard_map/ppermute | solution.py:769
  47.8 1.8 %collective-permute-start.13 = (f32[8,128]{1,0:T(8,128)S(1)}, f32[8,128]{1,0:T(8,128)S(1)}, u32[]{:S(2)}, u32[]{:S(2)}) collective-permute-start(f32[8,128]{1,0:T(8,128)S(1)} %add.43), channel_id=1, source_target_pairs={{0,1},{1,0},{2,3},{3,2},{4,5},{5,4},{6,7},{7,6},{8,9},{9,8},{10,11... | collective-permute-start | bytes 12296 | tf_op jit(solution)/shard_map/ppermute | solution.py:769
  50.4 2.4 %collective-permute-start.14 = (f32[8,128]{1,0:T(8,128)S(1)}, f32[8,128]{1,0:T(8,128)S(1)}, u32[]{:S(2)}, u32[]{:S(2)}) collective-permute-start(f32[8,128]{1,0:T(8,128)S(1)} %add.44), channel_id=1, source_target_pairs={{0,65},{1,64},{2,67},{3,66},{4,69},{5,68},{6,71},{7,70},{8,73},{9,... | collective-permute-start | bytes 12296 | tf_op jit(solution)/shard_map/ppermute | solution.py:769
  52.8 1.5 %collective-permute-done.14 = f32[8,128]{1,0:T(8,128)S(1)} collective-permute-done((f32[8,128]{1,0:T(8,128)S(1)}, f32[8,128]{1,0:T(8,128)S(1)}, u32[]{:S(2)}, u32[]{:S(2)}) %collective-permute-start.14) | collective-permute-done | bytes 4128 | tf_op jit(solution)/shard_map/ppermute | solution.py:769
  55.5 1.9 %collective-permute-done.15 = f32[8,128]{1,0:T(8,128)S(1)} collective-permute-done((f32[8,128]{1,0:T(8,128)S(1)}, f32[8,128]{1,0:T(8,128)S(1)}, u32[]{:S(2)}, u32[]{:S(2)}) %collective-permute-start.15) | collective-permute-done | bytes 4128 | tf_op jit(solution)/shard_map/ppermute | solution.py:769
  57.4 3.0 %collective-permute-done.16 = f32[8,128]{1,0:T(8,128)S(1)} collective-permute-done((f32[8,128]{1,0:T(8,128)S(1)}, f32[8,128]{1,0:T(8,128)S(1)}, u32[]{:S(2)}, u32[]{:S(2)}) %collective-permute-start.16) | collective-permute-done | bytes 4128 | tf_op jit(solution)/shard_map/ppermute | solution.py:769
  60.4 3.2 %collective-permute-start.17 = (f32[8,128]{1,0:T(8,128)S(1)}, f32[8,128]{1,0:T(8,128)S(1)}, u32[]{:S(2)}, u32[]{:S(2)}) collective-permute-start(f32[8,128]{1,0:T(8,128)S(1)} %add.47), channel_id=1, source_target_pairs={{0,33},{1,32},{2,35},{3,34},{4,37},{5,36},{6,39},{7,38},{8,41},{9,... | collective-permute-start | bytes 12296 | tf_op jit(solution)/shard_map/ppermute | solution.py:769
  64.9 2.1 %collective-permute-start.18 = (f32[8,128]{1,0:T(8,128)S(1)}, f32[8,128]{1,0:T(8,128)S(1)}, u32[]{:S(2)}, u32[]{:S(2)}) collective-permute-start(f32[8,128]{1,0:T(8,128)S(1)} %add.48), channel_id=1, source_target_pairs={{0,25},{1,24},{2,27},{3,26},{4,29},{5,28},{6,31},{7,30},{8,17},{9,... | collective-permute-start | bytes 12296 | tf_op jit(solution)/shard_map/ppermute | solution.py:769
  67.0 2.1 %collective-permute-done.18 = f32[8,128]{1,0:T(8,128)S(1)} collective-permute-done((f32[8,128]{1,0:T(8,128)S(1)}, f32[8,128]{1,0:T(8,128)S(1)}, u32[]{:S(2)}, u32[]{:S(2)}) %collective-permute-start.18) | collective-permute-done | bytes 4128 | tf_op jit(solution)/shard_map/ppermute | solution.py:769
  70.4 2.0 %shard_map.160 = f32[3,16,16,128]{3,2,1,0:T(8,128)} custom-call(f32[3,16,16,128]{3,2,1,0:T(8,128)S(1)} %get-tuple-element.96.refs_0_.fine, f32[3,8,8,256]{3,2,1,0:T(8,128)S(1)} %get-tuple-element.97.refs_1_.coarse, f32[3,16,16,128]{3,2,1,0:T(8,128)S(1)} %get-tuple-element.81.refs_0_.prev, s32[16,128]{1,0:T(8,128)S(1)} %pad.4.refs_4_.offs, ...), custom_call_target="tpu_custom_call" | custom-call | flops 2000000 | bytes 1048576 | tf_op jit(solution)/shard_map/pallas_call | solution.py:689
  72.4 1.5 %shard_map.161 = f32[3,8,8,256]{3,2,1,0:T(8,128)} custom-call(f32[3,16,16,128]{3,2,1,0:T(8,128)S(1)} %get-tuple-element.96.refs_0_.fine, f32[3,8,8,256]{3,2,1,0:T(8,128)S(1)} %get-tuple-element.97.refs_1_.coarse, f32[3,8,8,256]{3,2,1,0:T(8,128)S(1)} %get-tuple-element.82.refs_1_.prev, f32[8,8,256]{2,1,0:T(8,128)S(1)} %get-tuple-element.59.refs_10_.refs_0_, ...), custom_call_target="tpu_custom_call" | custom-call | flops 2000000 | bytes 1048576 | tf_op jit(solution)/shard_map/pallas_call | solution.py:689
  (78 shorter events, 15.4 us)
Async XLA Ops:
  1.9 5.0 %collective-permute-start = (f32[200,128]{1,0:T(8,128)S(1)}, f32[200,128]{1,0:T(8,128)S(1)}, u32[]{:S(2)}, u32[]{:S(2)}) collective-permute-start(f32[200,128]{1,0:T(8,128)S(1)} %get-tuple-element.68), channel_id=1, source_target_pairs={{0,8},{1,9},{2,10},{3,11},{4,12},{5,13},{6,14},{7,15},{8,0},{9,1},... | collective-permute-start | bytes 307208 | tf_op jit(solution)/shard_map/ppermute | solution.py:769
  4.0 2.9 %collective-permute-start.1 = (f32[200,128]{1,0:T(8,128)S(1)}, f32[200,128]{1,0:T(8,128)S(1)}, u32[]{:S(2)}, u32[]{:S(2)}) collective-permute-start(f32[200,128]{1,0:T(8,128)S(1)} %get-tuple-element.69), channel_id=1, source_target_pairs={{0,1},{1,0},{2,3},{3,2},{4,5},{5,4},{6,7},{7,6},{8,16},{9,17},{10,... | collective-permute-start | bytes 307208 | tf_op jit(solution)/shard_map/ppermute | solution.py:769
  5.4 5.7 %collective-permute-start.2 = (f32[132,2,128]{2,1,0:T(2,128)S(1)}, f32[132,2,128]{2,1,0:T(2,128)S(1)}, u32[]{:S(2)}, u32[]{:S(2)}) collective-permute-start(f32[132,2,128]{2,1,0:T(2,128)S(1)} %get-tuple-element.70), channel_id=1, source_target_pairs={{0,1},{1,0},{2,3},{3,2},{4,5},{5,4},{6,7},{7,6},{8,9},{9,8},{10,11... | collective-permute-start | bytes 405512 | tf_op jit(solution)/shard_map/ppermute | solution.py:769
  5.6 5.6 %collective-permute-start.3 = (f32[132,2,128]{2,1,0:T(2,128)S(1)}, f32[132,2,128]{2,1,0:T(2,128)S(1)}, u32[]{:S(2)}, u32[]{:S(2)}) collective-permute-start(f32[132,2,128]{2,1,0:T(2,128)S(1)} %get-tuple-element.71), channel_id=1, source_target_pairs={{0,7},{1,2},{2,1},{3,4},{4,3},{5,6},{6,5},{7,0},{8,15},{9,10},{10,... | collective-permute-start | bytes 405512 | tf_op jit(solution)/shard_map/ppermute | solution.py:769
  7.1 6.4 %collective-permute-start.4 = (f32[28,2,128]{2,1,0:T(2,128)S(1)}, f32[28,2,128]{2,1,0:T(2,128)S(1)}, u32[]{:S(2)}, u32[]{:S(2)}) collective-permute-start(f32[28,2,128]{2,1,0:T(2,128)S(1)} %get-tuple-element.79), channel_id=1, source_target_pairs={{0,1},{1,0},{2,3},{3,2},{4,5},{5,4},{6,7},{7,6},{8,9},{9,8},{10,11... | collective-permute-start | bytes 86024 | tf_op jit(solution)/shard_map/ppermute | solution.py:769
  10.0 3.4 %collective-permute-start.5 = (f32[28,2,128]{2,1,0:T(2,128)S(1)}, f32[28,2,128]{2,1,0:T(2,128)S(1)}, u32[]{:S(2)}, u32[]{:S(2)}) collective-permute-start(f32[28,2,128]{2,1,0:T(2,128)S(1)} %get-tuple-element.80), channel_id=1, source_target_pairs={{0,7},{1,2},{2,1},{3,4},{4,3},{5,6},{6,5},{7,0},{8,15},{9,10},{10,... | collective-permute-start | bytes 86024 | tf_op jit(solution)/shard_map/ppermute | solution.py:769
  15.1 4.6 %collective-permute-start.6 = (f32[232,128]{1,0:T(8,128)S(1)}, f32[232,128]{1,0:T(8,128)S(1)}, u32[]{:S(2)}, u32[]{:S(2)}) collective-permute-start(f32[232,128]{1,0:T(8,128)S(1)} %get-tuple-element.84), channel_id=1, source_target_pairs={{0,8},{1,9},{2,10},{3,11},{4,12},{5,13},{6,14},{7,15},{8,0},{9,1},... | collective-permute-start | bytes 356360 | tf_op jit(solution)/shard_map/ppermute | solution.py:769
  17.0 2.8 %collective-permute-start.7 = (f32[232,128]{1,0:T(8,128)S(1)}, f32[232,128]{1,0:T(8,128)S(1)}, u32[]{:S(2)}, u32[]{:S(2)}) collective-permute-start(f32[232,128]{1,0:T(8,128)S(1)} %get-tuple-element.85), channel_id=1, source_target_pairs={{0,1},{1,0},{2,3},{3,2},{4,5},{5,4},{6,7},{7,6},{8,16},{9,17},{10,... | collective-permute-start | bytes 356360 | tf_op jit(solution)/shard_map/ppermute | solution.py:769
  18.9 3.6 %collective-permute-start.8 = (f32[144,2,128]{2,1,0:T(2,128)S(1)}, f32[144,2,128]{2,1,0:T(2,128)S(1)}, u32[]{:S(2)}, u32[]{:S(2)}) collective-permute-start(f32[144,2,128]{2,1,0:T(2,128)S(1)} %get-tuple-element.86), channel_id=1, source_target_pairs={{0,1},{1,0},{2,3},{3,2},{4,5},{5,4},{6,7},{7,6},{8,9},{9,8},{10,11... | collective-permute-start | bytes 442376 | tf_op jit(solution)/shard_map/ppermute | solution.py:769
  19.0 5.0 %collective-permute-start.9 = (f32[144,2,128]{2,1,0:T(2,128)S(1)}, f32[144,2,128]{2,1,0:T(2,128)S(1)}, u32[]{:S(2)}, u32[]{:S(2)}) collective-permute-start(f32[144,2,128]{2,1,0:T(2,128)S(1)} %get-tuple-element.87), channel_id=1, source_target_pairs={{0,7},{1,2},{2,1},{3,4},{4,3},{5,6},{6,5},{7,0},{8,15},{9,10},{10,... | collective-permute-start | bytes 442376 | tf_op jit(solution)/shard_map/ppermute | solution.py:769
  19.9 5.9 %collective-permute-start.10 = (f32[48,2,128]{2,1,0:T(2,128)S(1)}, f32[48,2,128]{2,1,0:T(2,128)S(1)}, u32[]{:S(2)}, u32[]{:S(2)}) collective-permute-start(f32[48,2,128]{2,1,0:T(2,128)S(1)} %get-tuple-element.93), channel_id=1, source_target_pairs={{0,1},{1,0},{2,3},{3,2},{4,5},{5,4},{6,7},{7,6},{8,9},{9,8},{10,11... | collective-permute-start | bytes 147464 | tf_op jit(solution)/shard_map/ppermute | solution.py:769
  21.8 3.9 %collective-permute-start.11 = (f32[48,2,128]{2,1,0:T(2,128)S(1)}, f32[48,2,128]{2,1,0:T(2,128)S(1)}, u32[]{:S(2)}, u32[]{:S(2)}) collective-permute-start(f32[48,2,128]{2,1,0:T(2,128)S(1)} %get-tuple-element.94), channel_id=1, source_target_pairs={{0,7},{1,2},{2,1},{3,4},{4,3},{5,6},{6,5},{7,0},{8,15},{9,10},{10,... | collective-permute-start | bytes 147464 | tf_op jit(solution)/shard_map/ppermute | solution.py:769
  27.6 6.4 %collective-permute-start.20 = (f32[136,128]{1,0:T(8,128)S(1)}, f32[136,128]{1,0:T(8,128)S(1)}, u32[]{:S(2)}, u32[]{:S(2)}) collective-permute-start(f32[136,128]{1,0:T(8,128)S(1)} %get-tuple-element.98), channel_id=1, source_target_pairs={{0,8},{1,9},{2,10},{3,11},{4,12},{5,13},{6,14},{7,15},{8,0},{9,1},... | collective-permute-start | bytes 208904 | tf_op jit(solution)/shard_map/ppermute | solution.py:769
  32.3 2.3 %collective-permute-start.21 = (f32[136,128]{1,0:T(8,128)S(1)}, f32[136,128]{1,0:T(8,128)S(1)}, u32[]{:S(2)}, u32[]{:S(2)}) collective-permute-start(f32[136,128]{1,0:T(8,128)S(1)} %get-tuple-element.99), channel_id=1, source_target_pairs={{0,1},{1,0},{2,3},{3,2},{4,5},{5,4},{6,7},{7,6},{8,16},{9,17},{10,... | collective-permute-start | bytes 208904 | tf_op jit(solution)/shard_map/ppermute | solution.py:769
  34.8 35.6 %collective-permute-start.22 = (f32[100,2,128]{2,1,0:T(2,128)S(1)}, f32[100,2,128]{2,1,0:T(2,128)S(1)}, u32[]{:S(2)}, u32[]{:S(2)}) collective-permute-start(f32[100,2,128]{2,1,0:T(2,128)S(1)} %get-tuple-element.100), channel_id=1, source_target_pairs={{0,1},{1,0},{2,3},{3,2},{4,5},{5,4},{6,7},{7,6},{8,9},{9,8},{10,11... | collective-permute-start | bytes 307208 | tf_op jit(solution)/shard_map/ppermute | solution.py:769
  36.3 34.2 %collective-permute-start.23 = (f32[100,2,128]{2,1,0:T(2,128)S(1)}, f32[100,2,128]{2,1,0:T(2,128)S(1)}, u32[]{:S(2)}, u32[]{:S(2)}) collective-permute-start(f32[100,2,128]{2,1,0:T(2,128)S(1)} %get-tuple-element.101), channel_id=1, source_target_pairs={{0,7},{1,2},{2,1},{3,4},{4,3},{5,6},{6,5},{7,0},{8,15},{9,10},{10,... | collective-permute-start | bytes 307208 | tf_op jit(solution)/shard_map/ppermute | solution.py:769
  36.3 11.5 %collective-permute-start.12 = (f32[8,128]{1,0:T(8,128)S(1)}, f32[8,128]{1,0:T(8,128)S(1)}, u32[]{:S(2)}, u32[]{:S(2)}) collective-permute-start(f32[8,128]{1,0:T(8,128)S(1)} %get-tuple-element.95), channel_id=1, source_target_pairs={{0,224},{1,225},{2,226},{3,227},{4,228},{5,229},{6,230},{7,231},{8... | collective-permute-start | bytes 12296 | tf_op jit(solution)/shard_map/ppermute | solution.py:769
  47.8 2.6 %collective-permute-start.13 = (f32[8,128]{1,0:T(8,128)S(1)}, f32[8,128]{1,0:T(8,128)S(1)}, u32[]{:S(2)}, u32[]{:S(2)}) collective-permute-start(f32[8,128]{1,0:T(8,128)S(1)} %add.43), channel_id=1, source_target_pairs={{0,1},{1,0},{2,3},{3,2},{4,5},{5,4},{6,7},{7,6},{8,9},{9,8},{10,11... | collective-permute-start | bytes 12296 | tf_op jit(solution)/shard_map/ppermute | solution.py:769
  50.4 3.9 %collective-permute-start.14 = (f32[8,128]{1,0:T(8,128)S(1)}, f32[8,128]{1,0:T(8,128)S(1)}, u32[]{:S(2)}, u32[]{:S(2)}) collective-permute-start(f32[8,128]{1,0:T(8,128)S(1)} %add.44), channel_id=1, source_target_pairs={{0,65},{1,64},{2,67},{3,66},{4,69},{5,68},{6,71},{7,70},{8,73},{9,... | collective-permute-start | bytes 12296 | tf_op jit(solution)/shard_map/ppermute | solution.py:769
  54.3 3.0 %collective-permute-start.15 = (f32[8,128]{1,0:T(8,128)S(1)}, f32[8,128]{1,0:T(8,128)S(1)}, u32[]{:S(2)}, u32[]{:S(2)}) collective-permute-start(f32[8,128]{1,0:T(8,128)S(1)} %add.45), channel_id=1, source_target_pairs={{0,3},{1,2},{2,1},{3,0},{4,7},{5,6},{6,5},{7,4},{8,11},{9,10},{10,... | collective-permute-start | bytes 12296 | tf_op jit(solution)/shard_map/ppermute | solution.py:769
  57.4 3.0 %collective-permute-start.16 = (f32[8,128]{1,0:T(8,128)S(1)}, f32[8,128]{1,0:T(8,128)S(1)}, u32[]{:S(2)}, u32[]{:S(2)}) collective-permute-start(f32[8,128]{1,0:T(8,128)S(1)} %add.46), channel_id=1, source_target_pairs={{0,9},{1,8},{2,11},{3,10},{4,13},{5,12},{6,15},{7,14},{8,1},{9,0},... | collective-permute-start | bytes 12296 | tf_op jit(solution)/shard_map/ppermute | solution.py:769
  60.4 4.5 %collective-permute-start.17 = (f32[8,128]{1,0:T(8,128)S(1)}, f32[8,128]{1,0:T(8,128)S(1)}, u32[]{:S(2)}, u32[]{:S(2)}) collective-permute-start(f32[8,128]{1,0:T(8,128)S(1)} %add.47), channel_id=1, source_target_pairs={{0,33},{1,32},{2,35},{3,34},{4,37},{5,36},{6,39},{7,38},{8,41},{9,... | collective-permute-start | bytes 12296 | tf_op jit(solution)/shard_map/ppermute | solution.py:769
  64.9 4.2 %collective-permute-start.18 = (f32[8,128]{1,0:T(8,128)S(1)}, f32[8,128]{1,0:T(8,128)S(1)}, u32[]{:S(2)}, u32[]{:S(2)}) collective-permute-start(f32[8,128]{1,0:T(8,128)S(1)} %add.48), channel_id=1, source_target_pairs={{0,25},{1,24},{2,27},{3,26},{4,29},{5,28},{6,31},{7,30},{8,17},{9,... | collective-permute-start | bytes 12296 | tf_op jit(solution)/shard_map/ppermute | solution.py:769
  69.2 4.8 %collective-permute-start.19 = (f32[8,128]{1,0:T(8,128)S(1)}, f32[8,128]{1,0:T(8,128)S(1)}, u32[]{:S(2)}, u32[]{:S(2)}) collective-permute-start(f32[8,128]{1,0:T(8,128)S(1)} %add.49), channel_id=1, source_target_pairs={{0,7},{1,6},{2,5},{3,4},{4,3},{5,2},{6,1},{7,0},{8,15},{9,14},{10,... | collective-permute-start | bytes 12296 | tf_op jit(solution)/shard_map/ppermute | solution.py:769
  (13 other events, 42.4 us)

commit v11 on v10

--- a/solution.py
+++ b/solution.py
@@ -539,9 +539,9 @@
 
 
 INNER_F, OUTER_F = (10, lambda k: k + 2, 5), (6, lambda k: jnp.where(k < 2, k, k + 10), 3)
-INNER_C, OUTER_C = (4, lambda k: k + 1, 4), (4, lambda k: jnp.where(k < 1, k, k + 4), 4)
+INNER_C, OUTER_C = (5, lambda k: k + 1, 5), (3, lambda k: jnp.where(k < 1, k, k + 5), 3)
 INNER_DIV_F, OUTER_DIV_F = tuple(range(2, 14)), (0, 1, 2, 3, *range(12, 18))
-INNER_DIV_C, OUTER_DIV_C = tuple(range(1, 7)), (0, 1, 2, *range(5, 10))
+INNER_DIV_C, OUTER_DIV_C = tuple(range(1, 8)), (0, 1, 2, *range(6, 10))
 
 
 def step_kernel(s, step, inner, cells, *refs):
@@ -597,7 +597,7 @@
         fill_transposed(s.cy, ext_c, all_beta_c, inv_c, psi_c, lines_c)
     if not inner:
         new_f[:, 2:12] = done_f[:, 2:12]
-        new_c[:, 1:5] = done_c[:, 1:5]
+        new_c[:, 1:6] = done_c[:, 1:6]
 
     weights = node_weights(s, offs)
     ghosts_f = bottom_ghosts(s, weights, double, moved)

time: 74.9 us -> 74.7 us (level)
  no operation moved by 1% of the time
where the time goes in v11:
time: 74.7 us; the launch traced here: 74.5 us
  starting transfers between devices  44.9 us (60%)
  waiting for transfers between devices  14 us (19%)
  Pallas kernels  12.3 us (16%)
  local copies, waits for them, and re-layouts  2.44 us (3%)
  between operations  0.9 us (1%)
    ppermute x24, starting transfers between devices, swap(): return lax.ppermute(value, ALL, swap_pairs(mesh, move))  44.9 us
    ppermute x24, waiting for transfers between devices, swap(): return lax.ppermute(value, ALL, swap_pairs(mesh, move))  14 us
    pallas_call x14, Pallas kernels, call(): pl.pallas_call(kernel, out_shape=shapes, in_specs=[spec] * len(args), out...  12.3 us
    unnamed x26, local copies, waits for them, and re-layouts  1.6 us
  transfers between devices with their start and end apart: 24, of which 11 were waited for; matrix products, arithmetic and copies ran while one was open for 0% of the time, Pallas kernels for 10%

profile of v11, /device:TPU:1, one launch (start us, length us, event | category | flops | bytes accessed | tf_op | source)
XLA Modules:
  0.0 74.5 jit_solution(2398463037385322606)
XLA Ops:
  1.9 2.1 %collective-permute-start = (f32[200,128]{1,0:T(8,128)S(1)}, f32[200,128]{1,0:T(8,128)S(1)}, u32[]{:S(2)}, u32[]{:S(2)}) collective-permute-start(f32[200,128]{1,0:T(8,128)S(1)} %get-tuple-element.68), channel_id=1, source_target_pairs={{0,8},{1,9},{2,10},{3,11},{4,12},{5,13},{6,14},{7,15},{8,0},{9,1},... | collective-permute-start | bytes 307208 | tf_op jit(solution)/shard_map/ppermute | solution.py:769
  5.6 1.3 %collective-permute-start.3 = (f32[132,2,128]{2,1,0:T(2,128)S(1)}, f32[132,2,128]{2,1,0:T(2,128)S(1)}, u32[]{:S(2)}, u32[]{:S(2)}) collective-permute-start(f32[132,2,128]{2,1,0:T(2,128)S(1)} %get-tuple-element.71), channel_id=1, source_target_pairs={{0,7},{1,2},{2,1},{3,4},{4,3},{5,6},{6,5},{7,0},{8,15},{9,10},{10,... | collective-permute-start | bytes 405512 | tf_op jit(solution)/shard_map/ppermute | solution.py:769
  7.1 3.0 %collective-permute-start.4 = (f32[28,2,128]{2,1,0:T(2,128)S(1)}, f32[28,2,128]{2,1,0:T(2,128)S(1)}, u32[]{:S(2)}, u32[]{:S(2)}) collective-permute-start(f32[28,2,128]{2,1,0:T(2,128)S(1)} %get-tuple-element.79), channel_id=1, source_target_pairs={{0,1},{1,0},{2,3},{3,2},{4,5},{5,4},{6,7},{7,6},{8,9},{9,8},{10,11... | collective-permute-start | bytes 86024 | tf_op jit(solution)/shard_map/ppermute | solution.py:769
  12.0 1.5 %shard_map.152 = (f32[3,16,16,128]{3,2,1,0:T(8,128)S(1)}, f32[3,8,8,256]{3,2,1,0:T(8,128)S(1)}, f32[8,128]{1,0:T(8,128)S(1)}, f32[18,18,128]{2,1,0:T(8,128)S(1)}...) custom-call(f32[3,16,16,128]{3,2,1,0:T(8,128)S(1)} %copy-done, ...), custom_call_target="tpu_custom_call" | custom-call | flops 2000000 | bytes 1048576 | tf_op jit(solution)/shard_map/pallas_call | solution.py:689
  13.6 1.5 %shard_map.154 = (f32[3,16,16,128]{3,2,1,0:T(8,128)S(1)}, f32[3,8,8,256]{3,2,1,0:T(8,128)S(1)}, f32[8,128]{1,0:T(8,128)S(1)}, f32[232,128]{1,0:T(8,128)S(1)}, f3...) custom-call(f32[3,16,16,128]{3,2,1,0:T(8,128)S(1)} %copy-done, f32[3,8,8,256]{3,2,1,0:T(8,128)S(1)} %copy-done.1, ...), custom_call_target="tpu_custom_call" | custom-call | flops 2000000 | bytes 1048576 | tf_op jit(solution)/shard_map/pallas_call | solution.py:689
  15.1 1.8 %collective-permute-start.6 = (f32[232,128]{1,0:T(8,128)S(1)}, f32[232,128]{1,0:T(8,128)S(1)}, u32[]{:S(2)}, u32[]{:S(2)}) collective-permute-start(f32[232,128]{1,0:T(8,128)S(1)} %get-tuple-element.84), channel_id=1, source_target_pairs={{0,8},{1,9},{2,10},{3,11},{4,12},{5,13},{6,14},{7,15},{8,0},{9,1},... | collective-permute-start | bytes 356360 | tf_op jit(solution)/shard_map/ppermute | solution.py:769
  16.9 1.8 %collective-permute-start.7 = (f32[232,128]{1,0:T(8,128)S(1)}, f32[232,128]{1,0:T(8,128)S(1)}, u32[]{:S(2)}, u32[]{:S(2)}) collective-permute-start(f32[232,128]{1,0:T(8,128)S(1)} %get-tuple-element.85), channel_id=1, source_target_pairs={{0,1},{1,0},{2,3},{3,2},{4,5},{5,4},{6,7},{7,6},{8,16},{9,17},{10,... | collective-permute-start | bytes 356360 | tf_op jit(solution)/shard_map/ppermute | solution.py:769
  19.8 1.9 %collective-permute-start.10 = (f32[48,2,128]{2,1,0:T(2,128)S(1)}, f32[48,2,128]{2,1,0:T(2,128)S(1)}, u32[]{:S(2)}, u32[]{:S(2)}) collective-permute-start(f32[48,2,128]{2,1,0:T(2,128)S(1)} %get-tuple-element.93), channel_id=1, source_target_pairs={{0,1},{1,0},{2,3},{3,2},{4,5},{5,4},{6,7},{7,6},{8,9},{9,8},{10,11... | collective-permute-start | bytes 147464 | tf_op jit(solution)/shard_map/ppermute | solution.py:769
  22.5 1.4 %collective-permute-done.9.refs_25_.refs_28_ = f32[144,2,128]{2,1,0:T(2,128)S(1)} collective-permute-done((f32[144,2,128]{2,1,0:T(2,128)S(1)}, f32[144,2,128]{2,1,0:T(2,128)S(1)}, u32[]{:S(2)}, u32[]{:S(2)}) %collective-permute-start.9) | collective-permute-done | bytes 147488 | tf_op jit(solution)/shard_map/ppermute | solution.py:769
  23.9 1.9 %shard_map.156 = (f32[3,16,16,128]{3,2,1,0:T(8,128)S(1)}, f32[3,8,8,256]{3,2,1,0:T(8,128)S(1)}, f32[8,128]{1,0:T(8,128)S(1)}) custom-call(f32[3,16,16,128]{3,2,1,0:T(8,128)S(1)} %get-tuple-element.81.refs_0_.prev, f32[3,8,8,256]{3,2,1,0:T(8,128)S(1)} %get-tuple-element.82.refs_1_.prev, f32[3,16,16,128]{3,2,1,0:T(8,128)S(1)} %copy-done, ...), custom_call_target="tpu_custom_call" | custom-call | flops 2000000 | bytes 1048576 | tf_op jit(solution)/shard_map/pallas_call | solution.py:689
  25.9 1.7 %shard_map.158 = (f32[3,16,16,128]{3,2,1,0:T(8,128)S(1)}, f32[3,8,8,256]{3,2,1,0:T(8,128)S(1)}, f32[8,128]{1,0:T(8,128)S(1)}, f32[136,128]{1,0:T(8,128)S(1)}, f32[136,128]{1,0:T(8,128)S(1)}) custom-call(f32[3,16,16,128]{3,2,1,0:T(8,128)S(1)} %get-tuple-element.81.refs_0_.prev, f32[3,8,8,256]{3,2,1,0:T(8,128)S(1)} %get-tuple-element.82.refs_1_.prev, ...), custom_call_target="tpu_custom_call" | custom-call | flops 2000000 | bytes 1048576 | tf_op jit(solution)/shard_map/pallas_call | solution.py:689
  27.6 4.7 %collective-permute-start.20 = (f32[136,128]{1,0:T(8,128)S(1)}, f32[136,128]{1,0:T(8,128)S(1)}, u32[]{:S(2)}, u32[]{:S(2)}) collective-permute-start(f32[136,128]{1,0:T(8,128)S(1)} %get-tuple-element.98), channel_id=1, source_target_pairs={{0,8},{1,9},{2,10},{3,11},{4,12},{5,13},{6,14},{7,15},{8,0},{9,1},... | collective-permute-start | bytes 208904 | tf_op jit(solution)/shard_map/ppermute | solution.py:769
  34.6 1.5 %collective-permute-start.22 = (f32[100,2,128]{2,1,0:T(2,128)S(1)}, f32[100,2,128]{2,1,0:T(2,128)S(1)}, u32[]{:S(2)}, u32[]{:S(2)}) collective-permute-start(f32[100,2,128]{2,1,0:T(2,128)S(1)} %get-tuple-element.100), channel_id=1, source_target_pairs={{0,1},{1,0},{2,3},{3,2},{4,5},{5,4},{6,7},{7,6},{8,9},{9,8},{10,11... | collective-permute-start | bytes 307208 | tf_op jit(solution)/shard_map/ppermute | solution.py:769
  36.1 10.5 %collective-permute-start.12 = (f32[8,128]{1,0:T(8,128)S(1)}, f32[8,128]{1,0:T(8,128)S(1)}, u32[]{:S(2)}, u32[]{:S(2)}) collective-permute-start(f32[8,128]{1,0:T(8,128)S(1)} %get-tuple-element.95), channel_id=1, source_target_pairs={{0,224},{1,225},{2,226},{3,227},{4,228},{5,229},{6,230},{7,231},{8... | collective-permute-start | bytes 12296 | tf_op jit(solution)/shard_map/ppermute | solution.py:769
  47.6 1.7 %collective-permute-start.13 = (f32[8,128]{1,0:T(8,128)S(1)}, f32[8,128]{1,0:T(8,128)S(1)}, u32[]{:S(2)}, u32[]{:S(2)}) collective-permute-start(f32[8,128]{1,0:T(8,128)S(1)} %add.43), channel_id=1, source_target_pairs={{0,1},{1,0},{2,3},{3,2},{4,5},{5,4},{6,7},{7,6},{8,9},{9,8},{10,11... | collective-permute-start | bytes 12296 | tf_op jit(solution)/shard_map/ppermute | solution.py:769
  50.1 2.4 %collective-permute-start.14 = (f32[8,128]{1,0:T(8,128)S(1)}, f32[8,128]{1,0:T(8,128)S(1)}, u32[]{:S(2)}, u32[]{:S(2)}) collective-permute-start(f32[8,128]{1,0:T(8,128)S(1)} %add.44), channel_id=1, source_target_pairs={{0,65},{1,64},{2,67},{3,66},{4,69},{5,68},{6,71},{7,70},{8,73},{9,... | collective-permute-start | bytes 12296 | tf_op jit(solution)/shard_map/ppermute | solution.py:769
  52.5 1.5 %collective-permute-done.14 = f32[8,128]{1,0:T(8,128)S(1)} collective-permute-done((f32[8,128]{1,0:T(8,128)S(1)}, f32[8,128]{1,0:T(8,128)S(1)}, u32[]{:S(2)}, u32[]{:S(2)}) %collective-permute-start.14) | collective-permute-done | bytes 4128 | tf_op jit(solution)/shard_map/ppermute | solution.py:769
  55.3 1.8 %collective-permute-done.15 = f32[8,128]{1,0:T(8,128)S(1)} collective-permute-done((f32[8,128]{1,0:T(8,128)S(1)}, f32[8,128]{1,0:T(8,128)S(1)}, u32[]{:S(2)}, u32[]{:S(2)}) %collective-permute-start.15) | collective-permute-done | bytes 4128 | tf_op jit(solution)/shard_map/ppermute | solution.py:769
  57.1 3.0 %collective-permute-done.16 = f32[8,128]{1,0:T(8,128)S(1)} collective-permute-done((f32[8,128]{1,0:T(8,128)S(1)}, f32[8,128]{1,0:T(8,128)S(1)}, u32[]{:S(2)}, u32[]{:S(2)}) %collective-permute-start.16) | collective-permute-done | bytes 4128 | tf_op jit(solution)/shard_map/ppermute | solution.py:769
  60.1 3.2 %collective-permute-start.17 = (f32[8,128]{1,0:T(8,128)S(1)}, f32[8,128]{1,0:T(8,128)S(1)}, u32[]{:S(2)}, u32[]{:S(2)}) collective-permute-start(f32[8,128]{1,0:T(8,128)S(1)} %add.47), channel_id=1, source_target_pairs={{0,33},{1,32},{2,35},{3,34},{4,37},{5,36},{6,39},{7,38},{8,41},{9,... | collective-permute-start | bytes 12296 | tf_op jit(solution)/shard_map/ppermute | solution.py:769
  64.6 2.1 %collective-permute-start.18 = (f32[8,128]{1,0:T(8,128)S(1)}, f32[8,128]{1,0:T(8,128)S(1)}, u32[]{:S(2)}, u32[]{:S(2)}) collective-permute-start(f32[8,128]{1,0:T(8,128)S(1)} %add.48), channel_id=1, source_target_pairs={{0,25},{1,24},{2,27},{3,26},{4,29},{5,28},{6,31},{7,30},{8,17},{9,... | collective-permute-start | bytes 12296 | tf_op jit(solution)/shard_map/ppermute | solution.py:769
  66.8 2.1 %collective-permute-done.18 = f32[8,128]{1,0:T(8,128)S(1)} collective-permute-done((f32[8,128]{1,0:T(8,128)S(1)}, f32[8,128]{1,0:T(8,128)S(1)}, u32[]{:S(2)}, u32[]{:S(2)}) %collective-permute-start.18) | collective-permute-done | bytes 4128 | tf_op jit(solution)/shard_map/ppermute | solution.py:769
  70.2 2.0 %shard_map.160 = f32[3,16,16,128]{3,2,1,0:T(8,128)} custom-call(f32[3,16,16,128]{3,2,1,0:T(8,128)S(1)} %get-tuple-element.96.refs_0_.fine, f32[3,8,8,256]{3,2,1,0:T(8,128)S(1)} %get-tuple-element.97.refs_1_.coarse, f32[3,16,16,128]{3,2,1,0:T(8,128)S(1)} %get-tuple-element.81.refs_0_.prev, s32[16,128]{1,0:T(8,128)S(1)} %pad.4.refs_4_.offs, ...), custom_call_target="tpu_custom_call" | custom-call | flops 2000000 | bytes 1048576 | tf_op jit(solution)/shard_map/pallas_call | solution.py:689
  72.2 1.5 %shard_map.161 = f32[3,8,8,256]{3,2,1,0:T(8,128)} custom-call(f32[3,16,16,128]{3,2,1,0:T(8,128)S(1)} %get-tuple-element.96.refs_0_.fine, f32[3,8,8,256]{3,2,1,0:T(8,128)S(1)} %get-tuple-element.97.refs_1_.coarse, f32[3,8,8,256]{3,2,1,0:T(8,128)S(1)} %get-tuple-element.82.refs_1_.prev, f32[8,8,256]{2,1,0:T(8,128)S(1)} %get-tuple-element.59.refs_10_.refs_0_, ...), custom_call_target="tpu_custom_call" | custom-call | flops 2000000 | bytes 1048576 | tf_op jit(solution)/shard_map/pallas_call | solution.py:689
  (78 shorter events, 15.5 us)
Async XLA Ops:
  1.9 5.0 %collective-permute-start = (f32[200,128]{1,0:T(8,128)S(1)}, f32[200,128]{1,0:T(8,128)S(1)}, u32[]{:S(2)}, u32[]{:S(2)}) collective-permute-start(f32[200,128]{1,0:T(8,128)S(1)} %get-tuple-element.68), channel_id=1, source_target_pairs={{0,8},{1,9},{2,10},{3,11},{4,12},{5,13},{6,14},{7,15},{8,0},{9,1},... | collective-permute-start | bytes 307208 | tf_op jit(solution)/shard_map/ppermute | solution.py:769
  4.0 2.9 %collective-permute-start.1 = (f32[200,128]{1,0:T(8,128)S(1)}, f32[200,128]{1,0:T(8,128)S(1)}, u32[]{:S(2)}, u32[]{:S(2)}) collective-permute-start(f32[200,128]{1,0:T(8,128)S(1)} %get-tuple-element.69), channel_id=1, source_target_pairs={{0,1},{1,0},{2,3},{3,2},{4,5},{5,4},{6,7},{7,6},{8,16},{9,17},{10,... | collective-permute-start | bytes 307208 | tf_op jit(solution)/shard_map/ppermute | solution.py:769
  5.4 5.7 %collective-permute-start.2 = (f32[132,2,128]{2,1,0:T(2,128)S(1)}, f32[132,2,128]{2,1,0:T(2,128)S(1)}, u32[]{:S(2)}, u32[]{:S(2)}) collective-permute-start(f32[132,2,128]{2,1,0:T(2,128)S(1)} %get-tuple-element.70), channel_id=1, source_target_pairs={{0,1},{1,0},{2,3},{3,2},{4,5},{5,4},{6,7},{7,6},{8,9},{9,8},{10,11... | collective-permute-start | bytes 405512 | tf_op jit(solution)/shard_map/ppermute | solution.py:769
  5.6 5.6 %collective-permute-start.3 = (f32[132,2,128]{2,1,0:T(2,128)S(1)}, f32[132,2,128]{2,1,0:T(2,128)S(1)}, u32[]{:S(2)}, u32[]{:S(2)}) collective-permute-start(f32[132,2,128]{2,1,0:T(2,128)S(1)} %get-tuple-element.71), channel_id=1, source_target_pairs={{0,7},{1,2},{2,1},{3,4},{4,3},{5,6},{6,5},{7,0},{8,15},{9,10},{10,... | collective-permute-start | bytes 405512 | tf_op jit(solution)/shard_map/ppermute | solution.py:769
  7.1 6.5 %collective-permute-start.4 = (f32[28,2,128]{2,1,0:T(2,128)S(1)}, f32[28,2,128]{2,1,0:T(2,128)S(1)}, u32[]{:S(2)}, u32[]{:S(2)}) collective-permute-start(f32[28,2,128]{2,1,0:T(2,128)S(1)} %get-tuple-element.79), channel_id=1, source_target_pairs={{0,1},{1,0},{2,3},{3,2},{4,5},{5,4},{6,7},{7,6},{8,9},{9,8},{10,11... | collective-permute-start | bytes 86024 | tf_op jit(solution)/shard_map/ppermute | solution.py:769
  10.0 3.5 %collective-permute-start.5 = (f32[28,2,128]{2,1,0:T(2,128)S(1)}, f32[28,2,128]{2,1,0:T(2,128)S(1)}, u32[]{:S(2)}, u32[]{:S(2)}) collective-permute-start(f32[28,2,128]{2,1,0:T(2,128)S(1)} %get-tuple-element.80), channel_id=1, source_target_pairs={{0,7},{1,2},{2,1},{3,4},{4,3},{5,6},{6,5},{7,0},{8,15},{9,10},{10,... | collective-permute-start | bytes 86024 | tf_op jit(solution)/shard_map/ppermute | solution.py:769
  15.1 4.6 %collective-permute-start.6 = (f32[232,128]{1,0:T(8,128)S(1)}, f32[232,128]{1,0:T(8,128)S(1)}, u32[]{:S(2)}, u32[]{:S(2)}) collective-permute-start(f32[232,128]{1,0:T(8,128)S(1)} %get-tuple-element.84), channel_id=1, source_target_pairs={{0,8},{1,9},{2,10},{3,11},{4,12},{5,13},{6,14},{7,15},{8,0},{9,1},... | collective-permute-start | bytes 356360 | tf_op jit(solution)/shard_map/ppermute | solution.py:769
  16.9 2.8 %collective-permute-start.7 = (f32[232,128]{1,0:T(8,128)S(1)}, f32[232,128]{1,0:T(8,128)S(1)}, u32[]{:S(2)}, u32[]{:S(2)}) collective-permute-start(f32[232,128]{1,0:T(8,128)S(1)} %get-tuple-element.85), channel_id=1, source_target_pairs={{0,1},{1,0},{2,3},{3,2},{4,5},{5,4},{6,7},{7,6},{8,16},{9,17},{10,... | collective-permute-start | bytes 356360 | tf_op jit(solution)/shard_map/ppermute | solution.py:769
  18.8 3.6 %collective-permute-start.8 = (f32[144,2,128]{2,1,0:T(2,128)S(1)}, f32[144,2,128]{2,1,0:T(2,128)S(1)}, u32[]{:S(2)}, u32[]{:S(2)}) collective-permute-start(f32[144,2,128]{2,1,0:T(2,128)S(1)} %get-tuple-element.86), channel_id=1, source_target_pairs={{0,1},{1,0},{2,3},{3,2},{4,5},{5,4},{6,7},{7,6},{8,9},{9,8},{10,11... | collective-permute-start | bytes 442376 | tf_op jit(solution)/shard_map/ppermute | solution.py:769
  18.9 5.0 %collective-permute-start.9 = (f32[144,2,128]{2,1,0:T(2,128)S(1)}, f32[144,2,128]{2,1,0:T(2,128)S(1)}, u32[]{:S(2)}, u32[]{:S(2)}) collective-permute-start(f32[144,2,128]{2,1,0:T(2,128)S(1)} %get-tuple-element.87), channel_id=1, source_target_pairs={{0,7},{1,2},{2,1},{3,4},{4,3},{5,6},{6,5},{7,0},{8,15},{9,10},{10,... | collective-permute-start | bytes 442376 | tf_op jit(solution)/shard_map/ppermute | solution.py:769
  19.8 6.0 %collective-permute-start.10 = (f32[48,2,128]{2,1,0:T(2,128)S(1)}, f32[48,2,128]{2,1,0:T(2,128)S(1)}, u32[]{:S(2)}, u32[]{:S(2)}) collective-permute-start(f32[48,2,128]{2,1,0:T(2,128)S(1)} %get-tuple-element.93), channel_id=1, source_target_pairs={{0,1},{1,0},{2,3},{3,2},{4,5},{5,4},{6,7},{7,6},{8,9},{9,8},{10,11... | collective-permute-start | bytes 147464 | tf_op jit(solution)/shard_map/ppermute | solution.py:769
  21.7 4.1 %collective-permute-start.11 = (f32[48,2,128]{2,1,0:T(2,128)S(1)}, f32[48,2,128]{2,1,0:T(2,128)S(1)}, u32[]{:S(2)}, u32[]{:S(2)}) collective-permute-start(f32[48,2,128]{2,1,0:T(2,128)S(1)} %get-tuple-element.94), channel_id=1, source_target_pairs={{0,7},{1,2},{2,1},{3,4},{4,3},{5,6},{6,5},{7,0},{8,15},{9,10},{10,... | collective-permute-start | bytes 147464 | tf_op jit(solution)/shard_map/ppermute | solution.py:769
  27.6 6.4 %collective-permute-start.20 = (f32[136,128]{1,0:T(8,128)S(1)}, f32[136,128]{1,0:T(8,128)S(1)}, u32[]{:S(2)}, u32[]{:S(2)}) collective-permute-start(f32[136,128]{1,0:T(8,128)S(1)} %get-tuple-element.98), channel_id=1, source_target_pairs={{0,8},{1,9},{2,10},{3,11},{4,12},{5,13},{6,14},{7,15},{8,0},{9,1},... | collective-permute-start | bytes 208904 | tf_op jit(solution)/shard_map/ppermute | solution.py:769
  32.2 2.2 %collective-permute-start.21 = (f32[136,128]{1,0:T(8,128)S(1)}, f32[136,128]{1,0:T(8,128)S(1)}, u32[]{:S(2)}, u32[]{:S(2)}) collective-permute-start(f32[136,128]{1,0:T(8,128)S(1)} %get-tuple-element.99), channel_id=1, source_target_pairs={{0,1},{1,0},{2,3},{3,2},{4,5},{5,4},{6,7},{7,6},{8,16},{9,17},{10,... | collective-permute-start | bytes 208904 | tf_op jit(solution)/shard_map/ppermute | solution.py:769
  34.6 35.6 %collective-permute-start.22 = (f32[100,2,128]{2,1,0:T(2,128)S(1)}, f32[100,2,128]{2,1,0:T(2,128)S(1)}, u32[]{:S(2)}, u32[]{:S(2)}) collective-permute-start(f32[100,2,128]{2,1,0:T(2,128)S(1)} %get-tuple-element.100), channel_id=1, source_target_pairs={{0,1},{1,0},{2,3},{3,2},{4,5},{5,4},{6,7},{7,6},{8,9},{9,8},{10,11... | collective-permute-start | bytes 307208 | tf_op jit(solution)/shard_map/ppermute | solution.py:769
  36.1 34.1 %collective-permute-start.23 = (f32[100,2,128]{2,1,0:T(2,128)S(1)}, f32[100,2,128]{2,1,0:T(2,128)S(1)}, u32[]{:S(2)}, u32[]{:S(2)}) collective-permute-start(f32[100,2,128]{2,1,0:T(2,128)S(1)} %get-tuple-element.101), channel_id=1, source_target_pairs={{0,7},{1,2},{2,1},{3,4},{4,3},{5,6},{6,5},{7,0},{8,15},{9,10},{10,... | collective-permute-start | bytes 307208 | tf_op jit(solution)/shard_map/ppermute | solution.py:769
  36.1 11.5 %collective-permute-start.12 = (f32[8,128]{1,0:T(8,128)S(1)}, f32[8,128]{1,0:T(8,128)S(1)}, u32[]{:S(2)}, u32[]{:S(2)}) collective-permute-start(f32[8,128]{1,0:T(8,128)S(1)} %get-tuple-element.95), channel_id=1, source_target_pairs={{0,224},{1,225},{2,226},{3,227},{4,228},{5,229},{6,230},{7,231},{8... | collective-permute-start | bytes 12296 | tf_op jit(solution)/shard_map/ppermute | solution.py:769
  47.6 2.5 %collective-permute-start.13 = (f32[8,128]{1,0:T(8,128)S(1)}, f32[8,128]{1,0:T(8,128)S(1)}, u32[]{:S(2)}, u32[]{:S(2)}) collective-permute-start(f32[8,128]{1,0:T(8,128)S(1)} %add.43), channel_id=1, source_target_pairs={{0,1},{1,0},{2,3},{3,2},{4,5},{5,4},{6,7},{7,6},{8,9},{9,8},{10,11... | collective-permute-start | bytes 12296 | tf_op jit(solution)/shard_map/ppermute | solution.py:769
  50.1 3.9 %collective-permute-start.14 = (f32[8,128]{1,0:T(8,128)S(1)}, f32[8,128]{1,0:T(8,128)S(1)}, u32[]{:S(2)}, u32[]{:S(2)}) collective-permute-start(f32[8,128]{1,0:T(8,128)S(1)} %add.44), channel_id=1, source_target_pairs={{0,65},{1,64},{2,67},{3,66},{4,69},{5,68},{6,71},{7,70},{8,73},{9,... | collective-permute-start | bytes 12296 | tf_op jit(solution)/shard_map/ppermute | solution.py:769
  54.0 3.0 %collective-permute-start.15 = (f32[8,128]{1,0:T(8,128)S(1)}, f32[8,128]{1,0:T(8,128)S(1)}, u32[]{:S(2)}, u32[]{:S(2)}) collective-permute-start(f32[8,128]{1,0:T(8,128)S(1)} %add.45), channel_id=1, source_target_pairs={{0,3},{1,2},{2,1},{3,0},{4,7},{5,6},{6,5},{7,4},{8,11},{9,10},{10,... | collective-permute-start | bytes 12296 | tf_op jit(solution)/shard_map/ppermute | solution.py:769
  57.1 3.0 %collective-permute-start.16 = (f32[8,128]{1,0:T(8,128)S(1)}, f32[8,128]{1,0:T(8,128)S(1)}, u32[]{:S(2)}, u32[]{:S(2)}) collective-permute-start(f32[8,128]{1,0:T(8,128)S(1)} %add.46), channel_id=1, source_target_pairs={{0,9},{1,8},{2,11},{3,10},{4,13},{5,12},{6,15},{7,14},{8,1},{9,0},... | collective-permute-start | bytes 12296 | tf_op jit(solution)/shard_map/ppermute | solution.py:769
  60.1 4.5 %collective-permute-start.17 = (f32[8,128]{1,0:T(8,128)S(1)}, f32[8,128]{1,0:T(8,128)S(1)}, u32[]{:S(2)}, u32[]{:S(2)}) collective-permute-start(f32[8,128]{1,0:T(8,128)S(1)} %add.47), channel_id=1, source_target_pairs={{0,33},{1,32},{2,35},{3,34},{4,37},{5,36},{6,39},{7,38},{8,41},{9,... | collective-permute-start | bytes 12296 | tf_op jit(solution)/shard_map/ppermute | solution.py:769
  64.6 4.2 %collective-permute-start.18 = (f32[8,128]{1,0:T(8,128)S(1)}, f32[8,128]{1,0:T(8,128)S(1)}, u32[]{:S(2)}, u32[]{:S(2)}) collective-permute-start(f32[8,128]{1,0:T(8,128)S(1)} %add.48), channel_id=1, source_target_pairs={{0,25},{1,24},{2,27},{3,26},{4,29},{5,28},{6,31},{7,30},{8,17},{9,... | collective-permute-start | bytes 12296 | tf_op jit(solution)/shard_map/ppermute | solution.py:769
  68.9 4.9 %collective-permute-start.19 = (f32[8,128]{1,0:T(8,128)S(1)}, f32[8,128]{1,0:T(8,128)S(1)}, u32[]{:S(2)}, u32[]{:S(2)}) collective-permute-start(f32[8,128]{1,0:T(8,128)S(1)} %add.49), channel_id=1, source_target_pairs={{0,7},{1,6},{2,5},{3,4},{4,3},{5,2},{6,1},{7,0},{8,15},{9,14},{10,... | collective-permute-start | bytes 12296 | tf_op jit(solution)/shard_map/ppermute | solution.py:769
  (13 other events, 42.4 us)
